TPU v7x, 32 devices: a 4x2x2 block of a 4x4x8 slice. The times are simulated.
32 devices in a mesh: dp: 4 (over y, z), tp: 8 (over x, core).
Axes of the slice: x: 4, y: 2, z: 2, core: 2. Of those that a mesh axis runs over, the one named last changes fastest.
The devices are a block of a 4x4x8 slice.
Arguments:
- x_tokens: bfloat16 [12, 768, 5120], P('dp', 'tp'), parts along dimension 0
- e_time: float32 [12, 3, 5120], P('dp'), parts along dimension 0
- m_block: float32 [3, 5120], replicated
- w_q: bfloat16 [5120, 5120], P(None, 'tp')
- b_q: float32 [5120], P('tp')
- w_k: bfloat16 [5120, 5120], P(None, 'tp')
- b_k: float32 [5120], P('tp')
- w_v: bfloat16 [5120, 5120], P(None, 'tp')
- b_v: float32 [5120], P('tp')
- w_o: bfloat16 [5120, 5120], P('tp')
- b_o: float32 [5120], replicated
- g_q: float32 [5120], P('tp')
- g_k: float32 [5120], P('tp')
- positions: int32 [3072, 3], P('dp'), parts along dimension 0
- d_out: bfloat16 [12, 768, 5120], P('dp', 'tp'), parts along dimension 0
Outputs:
- output 1: bfloat16 [12, 768, 5120], P('dp', 'tp'), parts along dimension 0
- output 2: bfloat16 [12, 768, 5120], P('dp', 'tp'), parts along dimension 0
- output 3: float32 [12, 3, 5120], P('dp'), parts along dimension 0
- output 4: float32 [12, 5120], P('dp'), parts along dimension 0
- output 5: bfloat16 [20480, 5120], P('dp', 'tp'), parts along dimension 0
- output 6: bfloat16 [20480, 5120], P('dp', 'tp'), parts along dimension 0
- output 7: bfloat16 [20480, 5120], P('dp', 'tp'), parts along dimension 0
- output 8: bfloat16 [20480, 5120], P(('dp', 'tp')), parts along dimension 0
- output 9: float32 [20480], P(('dp', 'tp')), parts along dimension 0
- output 10: float32 [20480], P(('dp', 'tp')), parts along dimension 0
There are 4 independent parts. A program takes and returns all parts, laid end to end along the dimension named above; an argument that names none is the same for every part.
All inputs are finite; a program needn't handle non-finite values.
Results may differ from a plain program's by a relative error of at most 0.02.
Values are sent between devices in bfloat16 or wider.
A program may use at most 768 MiB of HBM per device.

v0:
```python
import jax
import jax.numpy as jnp
from jax import lax
from jax.sharding import PartitionSpec as P

HEAD_DIM = 128
EPS_NORM = 1e-6
ROPE_BASE = 10000.0
ROW_CONTRACT = (((0,), (0,)), ((), ()))
COL_CONTRACT = (((1,), (1,)), ((), ()))


def rope_angles(positions):
    half_dim = HEAD_DIM // 2
    side_len = HEAD_DIM // 6
    first_len = half_dim - 2 * side_len
    pair_idx = jnp.arange(half_dim)
    section = (pair_idx >= first_len).astype(jnp.int32) + (pair_idx >= first_len + side_len).astype(jnp.int32)
    offset = jnp.where(section == 0, 0, jnp.where(section == 1, first_len, first_len + side_len))
    sec_width = jnp.where(section == 0, first_len, side_len)
    freq_vals = ROPE_BASE ** (-(pair_idx - offset).astype(jnp.float32) / sec_width.astype(jnp.float32))
    select = jnp.where(section[None, :] == jnp.arange(3)[:, None], freq_vals[None, :], 0.0)
    angles = jnp.sum(positions.astype(jnp.float32)[:, :, None] * select[None, :, :], axis=1)
    return jnp.cos(angles), jnp.sin(angles)


def rope_rotate(values, cos_part, sin_part):
    val_pairs = values.reshape(values.shape[:-1] + (values.shape[-1] // 2, 2))
    even_part = val_pairs[..., 0]
    odd_part = val_pairs[..., 1]
    rotated = jnp.stack([even_part * cos_part - odd_part * sin_part, even_part * sin_part + odd_part * cos_part], axis=-1)
    return rotated.reshape(values.shape)


def attend(q_rot, k_rot, v_heads):
    scores = jnp.einsum('bqhd,bkhd->bhqk', q_rot, k_rot, preferred_element_type=jnp.float32) * HEAD_DIM ** -0.5
    attn_probs = jax.nn.softmax(scores, axis=-1).astype(jnp.bfloat16)
    return jnp.einsum('bhqk,bkhd->bqhd', attn_probs, v_heads, preferred_element_type=jnp.float32).astype(jnp.bfloat16)


def solution(mesh):
    tp_size = mesh.shape['tp']

    def device_step(x_loc, e_loc, m_block, w_q, b_q, w_k, b_k, w_v, b_v, w_o, b_o, g_q, g_k, pos_part, dy_loc):
        batch_size, seq_loc, model_dim = x_loc.shape
        seq_len = seq_loc * tp_size
        rows_all = batch_size * seq_len
        heads_loc = w_q.shape[1] // HEAD_DIM
        head_shape = (batch_size, seq_len, heads_loc, HEAD_DIM)
        cos_tab, sin_tab = rope_angles(pos_part)
        cos_bcast = cos_tab[None, :, None, :]
        sin_bcast = sin_tab[None, :, None, :]

        mod_rows = m_block[None] + e_loc
        shift_row = mod_rows[:, 0][:, None]
        scale_one = 1.0 + mod_rows[:, 1][:, None]
        gate_row = mod_rows[:, 2][:, None]
        x_float = x_loc.astype(jnp.float32)
        centered = x_float - jnp.mean(x_float, axis=-1, keepdims=True)
        inv_std = lax.rsqrt(jnp.mean(centered * centered, axis=-1, keepdims=True) + EPS_NORM)
        x_norm = centered * inv_std
        y_loc = (x_norm * scale_one + shift_row).astype(jnp.bfloat16)
        y_full = lax.all_gather(y_loc, 'tp', axis=1, tiled=True).reshape(rows_all, model_dim)

        q_raw = jnp.dot(y_full, w_q, preferred_element_type=jnp.float32) + b_q
        k_raw = jnp.dot(y_full, w_k, preferred_element_type=jnp.float32) + b_k
        v_heads = (jnp.dot(y_full, w_v, preferred_element_type=jnp.float32) + b_v).astype(jnp.bfloat16).reshape(head_shape)
        sq_sums = lax.psum(jnp.stack([jnp.sum(q_raw * q_raw, axis=-1), jnp.sum(k_raw * k_raw, axis=-1)]), 'tp')
        inv_rms = lax.rsqrt(sq_sums / model_dim + EPS_NORM)[:, :, None]
        q_hat = q_raw * inv_rms[0]
        k_hat = k_raw * inv_rms[1]
        q_rot = rope_rotate((q_hat * g_q).reshape(head_shape), cos_bcast, sin_bcast).astype(jnp.bfloat16)
        k_rot = rope_rotate((k_hat * g_k).reshape(head_shape), cos_bcast, sin_bcast).astype(jnp.bfloat16)
        attn_out, attn_pull = jax.vjp(attend, q_rot, k_rot, v_heads)
        o_flat = attn_out.reshape(rows_all, heads_loc * HEAD_DIM)
        part_sum = jnp.dot(o_flat, w_o, preferred_element_type=jnp.float32).astype(jnp.bfloat16).reshape(batch_size, seq_len, model_dim)
        proj_loc = lax.psum_scatter(part_sum, 'tp', scatter_dimension=1, tiled=True).astype(jnp.float32) + b_o
        x_out = (x_float + gate_row * proj_loc).astype(jnp.bfloat16)

        dy_float = dy_loc.astype(jnp.float32)
        d_gate = jnp.sum(dy_float * proj_loc, axis=1)
        d_proj = lax.all_gather((dy_float * gate_row).astype(jnp.bfloat16), 'tp', axis=1, tiled=True).reshape(rows_all, model_dim)
        d_wo = lax.dot_general(o_flat, d_proj, ROW_CONTRACT, preferred_element_type=jnp.float32).astype(jnp.bfloat16)
        d_attn = lax.dot_general(d_proj, w_o, COL_CONTRACT, preferred_element_type=jnp.float32).astype(jnp.bfloat16).reshape(head_shape)
        dq_rot, dk_rot, dv_heads = attn_pull(d_attn)
        dq_hat = rope_rotate(dq_rot.astype(jnp.float32), cos_bcast, -sin_bcast).reshape(rows_all, -1)
        dk_hat = rope_rotate(dk_rot.astype(jnp.float32), cos_bcast, -sin_bcast).reshape(rows_all, -1)
        d_gq = jnp.sum(dq_hat * q_hat, axis=0)
        d_gk = jnp.sum(dk_hat * k_hat, axis=0)
        dq_scaled = dq_hat * g_q
        dk_scaled = dk_hat * g_k
        stat_grads = lax.psum(jnp.stack([jnp.sum(dq_scaled * q_hat, axis=-1), jnp.sum(dk_scaled * k_hat, axis=-1)]), 'tp')[:, :, None] / model_dim
        dq_raw = (inv_rms[0] * (dq_scaled - q_hat * stat_grads[0])).astype(jnp.bfloat16)
        dk_raw = (inv_rms[1] * (dk_scaled - k_hat * stat_grads[1])).astype(jnp.bfloat16)
        dv_flat = dv_heads.reshape(rows_all, -1)
        d_wq = lax.dot_general(y_full, dq_raw, ROW_CONTRACT, preferred_element_type=jnp.float32).astype(jnp.bfloat16)
        d_wk = lax.dot_general(y_full, dk_raw, ROW_CONTRACT, preferred_element_type=jnp.float32).astype(jnp.bfloat16)
        d_wv = lax.dot_general(y_full, dv_flat, ROW_CONTRACT, preferred_element_type=jnp.float32).astype(jnp.bfloat16)
        dy_part = (lax.dot_general(dq_raw, w_q, COL_CONTRACT, preferred_element_type=jnp.float32)
                   + lax.dot_general(dk_raw, w_k, COL_CONTRACT, preferred_element_type=jnp.float32)
                   + lax.dot_general(dv_flat, w_v, COL_CONTRACT, preferred_element_type=jnp.float32))
        dy_part = dy_part.astype(jnp.bfloat16).reshape(batch_size, seq_len, model_dim)
        d_y = lax.psum_scatter(dy_part, 'tp', scatter_dimension=1, tiled=True).astype(jnp.float32)
        d_mod = lax.psum(jnp.stack([jnp.sum(d_y, axis=1), jnp.sum(d_y * x_norm, axis=1), d_gate], axis=1), 'tp')
        d_norm = d_y * scale_one
        d_x = dy_float + inv_std * (d_norm - jnp.mean(d_norm, axis=-1, keepdims=True) - x_norm * jnp.mean(d_norm * x_norm, axis=-1, keepdims=True))
        return (x_out, d_x.astype(jnp.bfloat16), d_mod, jnp.sum(d_mod, axis=0), d_wq, d_wk, d_wv, d_wo, d_gq, d_gk)

    in_specs = (P('dp', 'tp', None), P('dp', None, None), P(None, None), P(None, 'tp'), P('tp'), P(None, 'tp'), P('tp'),
                P(None, 'tp'), P('tp'), P('tp', None), P(None), P('tp'), P('tp'), P('dp', None), P('dp', 'tp', None))
    out_specs = (P('dp', 'tp', None), P('dp', 'tp', None), P('dp', None, None), P('dp', None), P('dp', 'tp'), P('dp', 'tp'),
                 P('dp', 'tp'), P(('dp', 'tp'), None), P(('dp', 'tp')), P(('dp', 'tp')))
    return jax.shard_map(device_step, mesh=mesh, in_specs=in_specs, out_specs=out_specs, check_vma=False)
```

profile of v0, /device:TPU:81, one launch (start us, length us, event | category | flops | bytes accessed | tf_op | source)
XLA Modules:
  0.0 1011.0 jit_solution(6240101077187539472)
XLA Ops:
  7.3 2.5 convert_reduce_fusion.1
  9.8 2.8 fusion.21
  13.1 0.4 copy-done.11
  13.5 2.9 fusion.18
  16.6 0.6 copy-done.14
  17.2 4.1 fusion.24
  21.4 0.3 reduce-scatter.5.cloned.1.call-start
  21.9 0.7 fusion.57
  22.6 0.7 neg.24
  23.3 108.9 %all-gather.3.cloned.1.call-done = bf16[3,768,5120]{2,1,0:T(8,128)(2,1)} async-done(((bf16[3,96,5120]{2,1,0:T(8,128)(2,1)}), bf16[3,768,5120]{2,1,0:T(8,128)(2,1)}) %all-gather.3.cloned.1.call-update) | async-done | bytes 23592976 | tf_op jit(solution)/shard_map/all_gather | solution.py:63
  132.2 23.6 %add_convert_fusion.1 = bf16[2304,640]{1,0:T(8,128)(2,1)S(1)} fusion(bf16[2304,5120]{1,0:T(8,128)(2,1)} %bitcast.112, bf16[5120,640]{1,0:T(8,128)(2,1)} %param.22, f32[640]{0:T(1024)S(1)} %copy-done.32), kind=kOutput, calls=%fused_computation.60 | convolution fusion | flops 15102443520 | bytes 33098240 | tf_op jit(solution)/shard_map/dot_general | solution.py:67
  155.8 5.0 reshape.204
  160.8 85.5 %all-gather.5.cloned.1.call-done = bf16[3,768,5120]{2,1,0:T(8,128)(2,1)} async-done(((bf16[3,96,5120]{2,1,0:T(8,128)(2,1)}), bf16[3,768,5120]{2,1,0:T(8,128)(2,1)}) %all-gather.5.cloned.1.call-update) | async-done | bytes 23592976 | tf_op jit(solution)/shard_map/all_gather | solution.py:82
  246.3 24.5 %convolution_convert_fusion.6 = bf16[2304,640]{1,0:T(8,128)(2,1)} fusion(bf16[2304,5120]{1,0:T(8,128)(2,1)} %bitcast.110, bf16[640,5120]{1,0:T(8,128)(2,1)} %param.24), kind=kOutput, calls=%fused_computation.65 | convolution fusion | flops 15100968960 | bytes 33095680 | tf_op jit(solution)/shard_map/dot_general | solution.py:84
  270.8 4.0 copy.71
  274.8 4.6 reshape.187
  279.4 22.8 %multiply_reduce_fusion.5 = (f32[2304]{0:T(1024)S(1)}, f32[2304,640]{0,1:T(8,128)}) fusion(f32[640]{0:T(1024)S(1)} %copy-done.33, bf16[2304,5120]{1,0:T(8,128)(2,1)} %bitcast.113, bf16[5120,640]{1,0:T(8,128)(2,1)} %param.20), kind=kOutput, calls=%fused_computation.58 | convolution fusion | flops 15103916032 | bytes 36056576 | tf_op jit(solution)/shard_map/dot_general | solution.py:66
  302.2 22.6 %multiply_reduce_fusion.6 = (f32[2304]{0:T(1024)S(1)}, f32[2304,640]{0,1:T(8,128)}) fusion(f32[640]{0:T(1024)S(1)} %copy-done.34, bf16[2304,5120]{1,0:T(8,128)(2,1)} %bitcast.114, bf16[5120,640]{1,0:T(8,128)(2,1)} %param.18), kind=kOutput, calls=%fused_computation.59 | convolution fusion | flops 15103916032 | bytes 36056576 | tf_op jit(solution)/shard_map/dot_general | solution.py:65
  324.8 22.1 %psum.21 = f32[2,2304]{1,0:T(2,128)S(1)} all-reduce(f32[2,2304]{1,0:T(2,128)S(1)} %pad_maximum_fusion.5), channel_id=1, replica_groups=mesh['dp'=4,'tp'=8] {'tp'}, use_global_device_ids=true, to_apply=%region_4.5 | all-reduce | flops 4608 | bytes 36864 | tf_op jit(solution)/shard_map/psum | solution.py:68
  347.1 5.8 multiply_multiply_fusion.1
  352.9 9.8 reshape_reshape.12
  362.7 5.8 multiply_multiply_fusion
  368.5 9.9 reshape_reshape.13
  378.3 8.0 subtract_convert_fusion.1
  386.3 4.5 pad_maximum_fusion.2
  390.8 4.4 pad_maximum_fusion.3
  395.2 19.8 %fusion.58 = (f32[3,5,768]{2,1,0:T(8,128)S(1)}, f32[3,5,768,768]{2,3,1,0:T(8,128)}) fusion(bf16[3,768,5,128]{1,0,3,2:T(4,128)(2,1)} %bitcast.99, bf16[3,768,5,128]{1,0,3,2:T(4,128)(2,1)} %bitcast.97), kind=kOutput, calls=%fused_computation.125 | convolution fusion | flops 2291467008 | bytes 41333760 | tf_op jit(solution)/shard_map/jvp()/sub | solution.py:37
  415.0 25.7 %fusion.5 = (f32[3,5,768]{2,1,0:T(8,128)S(1)}, bf16[3,5,768,768]{2,3,1,0:T(8,128)(2,1)}, bf16[3,5,768,768]{2,3,1,0:T(8,128)(2,1)}) fusion(f32[3,5,768,768]{2,3,1,0:T(8,128)} %get-tuple-element.69, f32[3,5,768]{2,1,0:T(8,128)S(1)} %multiply_divide_fusion, f32[3,5,768]{2,1,0:T(8,128)S(1)} %get-tuple-element.68, bf16[3,5,128,768]{3,0,2,1:T(4,128)(2,1)} %bitcast.95, ...), kind=kOutput, calls=%fused_computation.8 | convolution fusion | flops 2326844160 | bytes 76815360 | tf_op jit(solution)/shard_map/transpose(jvp(bhqk,bkhd->bqhd))/dot_general | solution.py:38
  440.7 22.7 %convert_bitcast_fusion = f32[3,768,5,128]{1,3,2,0:T(8,128)} fusion(bf16[3,768,5,128]{1,0,3,2:T(4,128)(2,1)} %bitcast.98, f32[3,5,768,768]{2,3,1,0:T(8,128)} %get-tuple-element.69, bf16[3,5,768,768]{2,3,1,0:T(8,128)(2,1)} %get-tuple-element.70, f32[3,5,768]{2,1,0:T(8,128)S(1)} %neg.23, f32[3,5,768]{2,1,0:T(8,128)S(1)} %get-tuple-element.68), kind=kOutput, calls=%fused_computation.49 | convolution fusion | flops 2312110080 | bytes 62023680 | tf_op jit(solution)/shard_map/transpose(jvp(bqhd,bkhd->bhqk))/dot_general | solution.py:36
  463.5 22.7 %convert_bitcast_fusion.1 = f32[3,768,5,128]{1,3,2,0:T(8,128)} fusion(bf16[3,768,5,128]{1,0,3,2:T(4,128)(2,1)} %bitcast.100, f32[3,5,768,768]{2,3,1,0:T(8,128)} %get-tuple-element.69, bf16[3,5,768,768]{2,3,1,0:T(8,128)(2,1)} %get-tuple-element.70, f32[3,5,768]{2,1,0:T(8,128)S(1)} %neg.23, f32[3,5,768]{2,1,0:T(8,128)S(1)} %get-tuple-element.68), kind=kOutput, calls=%fused_computation.50 | convolution fusion | flops 2312110080 | bytes 62023680 | tf_op jit(solution)/shard_map/transpose(jvp(bqhd,bkhd->bhqk))/dot_general | solution.py:36
  486.2 10.7 %convert_bitcast_fusion.2 = bf16[3,768,5,128]{1,3,2,0:T(8,128)(2,1)S(1)} fusion(bf16[3,5,768,768]{2,3,1,0:T(8,128)(2,1)} %get-tuple-element.43, bf16[3,5,128,768]{3,0,2,1:T(4,128)(2,1)} %bitcast.96), kind=kOutput, calls=%fused_computation.76 | convolution fusion | flops 2266398720 | bytes 23592960 | tf_op jit(solution)/shard_map/transpose(jvp(bhqk,bkhd->bqhd))/dot_general | solution.py:38
  496.8 2.5 copy.82
  499.4 2.2 copy.106
  501.6 7.2 copy.96
  508.7 10.0 copy.97
  518.8 11.9 %multiply_subtract_fusion = (f32[3,768,5,64,1]{1,0,4,3,2:T(4,128)S(1)}, f32[3,768,5,64,1]{1,0,4,3,2:T(4,128)}, f32[3,768,5,64,1]{1,0,4,3,2:T(4,128)}, f32[3,768,5,64,1]{1,0,4,3,2:T(4,128)}) fusion(f32[3,768,5,64,2]{1,0,4,3,2:T(4,128)} %bitcast.90, f32[768,64]{0,1:T(8,128)S(1)} %copy-done.13, f32[768,64]{0,1:T(8,128)S(1)} %copy-done.10, ...), kind=kLoop, calls=%fused_computation.69 | loop fusion | flops 8847360 | bytes 23986176 | tf_op jit(solution)/shard_map/sub | solution.py:31
  530.7 7.0 pad_maximum_fusion.1
  537.7 4.6 copy.105
  542.4 2.5 multiply_reduce_fusion.1
  544.9 5.1 pad_maximum_fusion
  550.0 1.3 copy.104
  551.4 6.8 multiply_reduce_fusion.2
  558.2 23.9 %psum.22 = f32[2,2304]{1,0:T(2,128)S(1)} all-reduce(f32[2,2304]{1,0:T(2,128)S(1)} %pad_maximum_fusion.6), channel_id=1, replica_groups=mesh['dp'=4,'tp'=8] {'tp'}, use_global_device_ids=true, to_apply=%region_12.13 | all-reduce | flops 4608 | bytes 36864 | tf_op jit(solution)/shard_map/psum | solution.py:92
  582.2 7.4 multiply_convert_fusion.1
  589.5 5.5 multiply_convert_fusion
  595.0 27.6 %fusion.67 = f32[2304,5120]{1,0:T(8,128)} fusion(bf16[2304,640]{0,1:T(8,128)(2,1)} %multiply_convert_fusion.1, bf16[5120,640]{1,0:T(8,128)(2,1)} %param.18), kind=kOutput, calls=%fused_computation.126 | convolution fusion | flops 15099494400 | bytes 56688640 | tf_op jit(solution)/shard_map/dot_general | solution.py:99
  622.6 28.2 %fusion.68 = f32[2304,5120]{1,0:T(8,128)} fusion(bf16[2304,640]{0,1:T(8,128)(2,1)} %multiply_convert_fusion, bf16[5120,640]{1,0:T(8,128)(2,1)} %param.20), kind=kOutput, calls=%fused_computation.127 | convolution fusion | flops 15099494400 | bytes 56688640 | tf_op jit(solution)/shard_map/dot_general | solution.py:100
  650.9 42.4 %add_convert_fusion = bf16[2304,5120]{1,0:T(8,128)(2,1)} fusion(f32[2304,5120]{1,0:T(8,128)} %fusion.67, f32[2304,5120]{1,0:T(8,128)} %fusion.68, bf16[2304,640]{0,1:T(8,128)(2,1)S(1)} %bitcast.101, bf16[5120,640]{1,0:T(8,128)(2,1)} %param.22), kind=kOutput, calls=%fused_computation.1 | convolution fusion | flops 15134883840 | bytes 127467520 | tf_op jit(solution)/shard_map/dot_general | solution.py:101
  693.6 10.2 %convert_bitcast_fusion.3 = bf16[3,768,5,128]{1,3,2,0:T(8,128)(2,1)S(1)} fusion(bf16[3,5,768,768]{2,3,1,0:T(8,128)(2,1)} %get-tuple-element.43, bf16[3,768,5,128]{3,2,1,0:T(8,128)(2,1)} %reshape.204), kind=kOutput, calls=%fused_computation.77 | convolution fusion | flops 2266398720 | bytes 23592960 | tf_op jit(solution)/shard_map/jvp(bhqk,bkhd->bqhd)/dot_general | solution.py:38
  703.8 2.5 copy.70
  706.3 0.6 copy.103
  706.9 26.1 %convolution_convert_fusion = bf16[2304,5120]{1,0:T(8,128)(2,1)} fusion(bf16[2304,640]{0,1:T(8,128)(2,1)S(1)} %bitcast.103, bf16[640,5120]{1,0:T(8,128)(2,1)} %param.24), kind=kOutput, calls=%fused_computation.13 | convolution fusion | flops 15111290880 | bytes 33095680 | tf_op jit(solution)/shard_map/dot_general | solution.py:76
  733.2 23.4 %convolution_convert_fusion.2 = bf16[5120,640]{1,0:T(8,128)(2,1)} fusion(bf16[2304,5120]{1,0:T(8,128)(2,1)} %bitcast.115, bf16[2304,640]{0,1:T(8,128)(2,1)S(1)} %bitcast.102), kind=kOutput, calls=%fused_computation.28 | convolution fusion | flops 15102771200 | bytes 33095680 | tf_op jit(solution)/shard_map/dot_general | solution.py:98
  756.7 23.2 %convolution_convert_fusion.3 = bf16[5120,640]{1,0:T(8,128)(2,1)} fusion(bf16[2304,5120]{1,0:T(8,128)(2,1)} %bitcast.116, bf16[2304,640]{0,1:T(8,128)(2,1)S(1)} %copy-done.8), kind=kOutput, calls=%fused_computation.29 | convolution fusion | flops 15102771200 | bytes 33095680 | tf_op jit(solution)/shard_map/dot_general | solution.py:97
  779.9 23.5 %convolution_convert_fusion.4 = bf16[5120,640]{1,0:T(8,128)(2,1)} fusion(bf16[2304,5120]{1,0:T(8,128)(2,1)} %bitcast.117, bf16[2304,640]{0,1:T(8,128)(2,1)S(1)} %copy-done.7), kind=kOutput, calls=%fused_computation.30 | convolution fusion | flops 15102771200 | bytes 33095680 | tf_op jit(solution)/shard_map/dot_general | solution.py:96
  803.4 12.4 %reduce-scatter.5.cloned.1.call-done = bf16[3,96,5120]{2,1,0:T(8,128)(2,1)} async-done(((bf16[3,768,5120]{2,1,0:T(8,128)(2,1)}), bf16[3,96,5120]{2,1,0:T(8,128)(2,1)}) %reduce-scatter.5.cloned.1.call-update) | async-done | bytes 2949136 | tf_op jit(solution)/shard_map/reduce_scatter | solution.py:103
  815.8 4.4 fusion.27
  820.3 118.3 %reduce-scatter.3.cloned.1.call-done = bf16[3,96,5120]{2,1,0:T(8,128)(2,1)} async-done(((bf16[3,768,5120]{2,1,0:T(8,128)(2,1)}), bf16[3,96,5120]{2,1,0:T(8,128)(2,1)}) %reduce-scatter.3.cloned.1.call-update) | async-done | bytes 2949136 | tf_op jit(solution)/shard_map/reduce_scatter | solution.py:77
  938.6 9.0 fusion.26
  947.7 0.8 pad_maximum_fusion.4
  948.5 22.9 %convolution_convert_fusion.5 = bf16[640,5120]{1,0:T(8,128)(2,1)} fusion(bf16[2304,640]{0,1:T(8,128)(2,1)} %bitcast.104, bf16[2304,5120]{1,0:T(8,128)(2,1)} %bitcast.111), kind=kOutput, calls=%fused_computation.31 | convolution fusion | flops 15102771200 | bytes 33095680 | tf_op jit(solution)/shard_map/dot_general | solution.py:83
  971.4 29.0 %all-reduce.2.cloned.1.call-done = f32[3,3,5120]{2,0,1:T(4,128)} async-done(((f32[3,3,5120]{2,0,1:T(4,128)}), f32[3,3,5120]{2,0,1:T(4,128)}) %all-reduce.2.cloned.1.call-update) | async-done | bytes 184336 | tf_op jit(solution)/shard_map/psum | solution.py:104
  1000.4 1.8 copy.83
  1002.2 1.7 reduce_sum.171
  (112 shorter events, 1.8 us)
Async XLA Ops:
  7.2 6.3 copy-start
  7.2 5.3 copy-start.21
  7.2 5.3 copy-start.16
  7.2 125.0 %all-gather.3.cloned.1.call-start = ((), (), s32[]{:S(2)}) async-start(), calls=%async_computation.2 | async-start | bytes 26542080 | tf_op jit(solution)/shard_map/all_gather | solution.py:63
  9.8 3.1 copy-start.22
  12.6 0.5 copy-start.28
  12.8 0.6 copy-start.11
  16.4 5.3 copy-start.31
  16.4 115.8 %copy-start.32 = (f32[640]{0:T(1024)S(1)}, f32[640]{0:T(1024)}, u32[]{:S(2)}) copy-start(f32[640]{0:T(1024)} %param.23) | copy-start | bytes 7684
  16.5 229.8 %all-gather.5.cloned.1.call-start = ((), (), s32[]{:S(2)}) async-start(), calls=%async_computation.4 | async-start | bytes 26542080 | tf_op jit(solution)/shard_map/all_gather | solution.py:82
  16.6 0.6 copy-start.14
  21.4 794.4 %reduce-scatter.5.cloned.1.call-start = ((), (), s32[]{:S(2)}) async-start(), calls=%async_computation.5 | async-start | bytes 26542080 | tf_op jit(solution)/shard_map/reduce_scatter | solution.py:103
  22.6 355.8 %copy-start.9 = (f32[768,64]{0,1:T(8,128)}, f32[768,64]{0,1:T(8,128)S(1)}, u32[]{:S(2)}) copy-start(f32[768,64]{0,1:T(8,128)S(1)} %get-tuple-element.62) | copy-start | bytes 589828
  270.8 8.6 copy-start.33
  279.4 22.8 %copy-start.34 = (f32[640]{0:T(1024)S(1)}, f32[640]{0:T(1024)}, u32[]{:S(2)}) copy-start(f32[640]{0:T(1024)} %param.19) | copy-start | bytes 7684
  302.2 44.8 %copy-start.24 = (f32[640]{0:T(1024)S(1)}, f32[640]{0:T(1024)}, u32[]{:S(2)}) copy-start(f32[640]{0:T(1024)} %param.26) | copy-start | bytes 7684
  347.0 5.8 copy-start.19
  347.0 15.7 %copy-start.17 = (f32[2304]{0:T(1024)}, f32[2304]{0:T(1024)S(1)}, u32[]{:S(2)}) copy-start(f32[2304]{0:T(1024)S(1)} %get-tuple-element.41) | copy-start | bytes 27652
  352.8 9.8 copy-start.26
  496.8 4.7 copy-start.4
  508.7 10.0 copy-start.10
  508.7 10.0 copy-start.13
  508.7 33.6 %slice-start = ((s8[5898240]{0:T(1024)(128)(4,1)}), s8[4194304]{0:T(1024)(128)(4,1)S(1)}, s32[]{:S(2)}) async-start(s8[5898240]{0:T(1024)(128)(4,1)} %bitcast.79), calls=%async_computation.7 | async-start | bytes 8388608
  518.8 23.6 %slice-start.1 = ((s8[5898240]{0:T(1024)(128)(4,1)}), s8[1703936]{0:T(1024)(128)(4,1)S(1)}, s32[]{:S(2)}) async-start(s8[5898240]{0:T(1024)(128)(4,1)} %bitcast.79), calls=%async_computation.8 | async-start | bytes 3407872
  537.7 4.6 copy-start.18
  537.7 4.6 copy-start.27
  542.3 2.6 copy-start.2
  549.9 1.4 copy-start.20
  550.0 1.4 copy-start.25
  551.3 6.8 copy-start.3
  551.4 38.2 %slice-start.2 = ((s8[5898240]{0:T(1024)(128)(4,1)}), s8[1703936]{0:T(1024)(128)(4,1)S(1)}, s32[]{:S(2)}) async-start(s8[5898240]{0:T(1024)(128)(4,1)} %bitcast.81), calls=%async_computation.9 | async-start | bytes 3407872
  582.2 7.4 slice-start.3
  622.6 28.2 %copy-start.5 = (bf16[80,8,3,768]{3,1,2,0:T(8,128)(2,1)S(1)}, bf16[80,8,3,768]{3,1,2,0:T(8,128)(2,1)}, u32[]{:S(2)}) copy-start(bf16[80,8,3,768]{3,1,2,0:T(8,128)(2,1)} %copy.106) | copy-start | bytes 8847364
  693.3 245.3 %reduce-scatter.3.cloned.1.call-start = ((), (), s32[]{:S(2)}) async-start(), calls=%async_computation.3 | async-start | bytes 26542080 | tf_op jit(solution)/shard_map/reduce_scatter | solution.py:77
  706.9 26.1 %copy-start.6 = (bf16[80,8,3,768]{3,1,2,0:T(8,128)(2,1)}, bf16[80,8,3,768]{3,1,2,0:T(8,128)(2,1)S(1)}, u32[]{:S(2)}) copy-start(bf16[80,8,3,768]{3,1,2,0:T(8,128)(2,1)S(1)} %copy.103) | copy-start | bytes 8847364
  733.1 267.3 %all-reduce.2.cloned.1.call-start = ((), (), s32[]{:S(2)}) async-start(), calls=%async_computation.6 | async-start | bytes 491520 | tf_op jit(solution)/shard_map/psum | solution.py:104
  733.2 23.5 %copy-start.8 = (bf16[2304,640]{0,1:T(8,128)(2,1)S(1)}, bf16[2304,640]{0,1:T(8,128)(2,1)}, u32[]{:S(2)}) copy-start(bf16[2304,640]{0,1:T(8,128)(2,1)} %multiply_convert_fusion) | copy-start | bytes 8847364
  756.6 23.2 %copy-start.7 = (bf16[2304,640]{0,1:T(8,128)(2,1)S(1)}, bf16[2304,640]{0,1:T(8,128)(2,1)}, u32[]{:S(2)}) copy-start(bf16[2304,640]{0,1:T(8,128)(2,1)} %multiply_convert_fusion.1) | copy-start | bytes 8847364
  779.9 35.9 %copy-start.1 = (bf16[3,96,5120]{2,1,0:T(8,128)(2,1)S(1)}, bf16[3,96,5120]{2,1,0:T(8,128)(2,1)}, u32[]{:S(2)}) copy-start(bf16[3,96,5120]{2,1,0:T(8,128)(2,1)} %param.15) | copy-start | bytes 8847364
  779.9 35.9 %copy-start.12 = (f32[3,5120]{1,0:T(4,128)S(1)}, f32[3,5120]{1,0:T(4,128)}, u32[]{:S(2)}) copy-start(f32[3,5120]{1,0:T(4,128)} %copy-done.11) | copy-start | bytes 184324
  779.9 35.9 %copy-start.23 = (f32[3,96]{1,0:T(4,128)S(1)}, f32[3,96]{1,0:T(4,128)}, u32[]{:S(2)}) copy-start(f32[3,96]{1,0:T(4,128)} %copy-done.22) | copy-start | bytes 3460
  779.9 35.9 %copy-start.29 = (f32[3,96]{1,0:T(4,128)S(1)}, f32[3,96]{1,0:T(4,128)}, u32[]{:S(2)}) copy-start(f32[3,96]{1,0:T(4,128)} %copy-done.28) | copy-start | bytes 3460
  803.4 135.3 %copy-start.15 = (f32[3,1,5120]{2,0,1:T(4,128)S(1)}, f32[3,1,5120]{2,0,1:T(4,128)}, u32[]{:S(2)}) copy-start(f32[3,1,5120]{2,0,1:T(4,128)} %copy-done.14) | copy-start | bytes 184324
  803.4 135.3 %copy-start.30 = (f32[5120]{0:T(1024)S(1)}, f32[5120]{0:T(1024)}, u32[]{:S(2)}) copy-start(f32[5120]{0:T(1024)} %param.25) | copy-start | bytes 61444
Sparse Core Ops, SparseCore 0:
  16.6 115.5 all-gather.2
  134.4 111.8 all-gather.4
  693.5 122.2 reduce-scatter.4
  818.0 120.5 reduce-scatter.2
  948.6 51.7 all-reduce.1
where the time goes:
time: 1020 us; the launch traced here: 1010 us
  matrix products  423 us (41%)
  waiting for transfers between devices  354 us (35%)
  other arithmetic  104 us (10%)
  local copies, waits for them, and re-layouts  68.3 us (7%)
  blocking collectives  46 us (5%)
  between operations  14.9 us (1%)
    reduce_scatter x1, waiting for transfers between devices, device_step(): lax.psum_scatter(part_sum, 'tp', scatter_dimension=1, tiled=True)  118 us
    all_gather x1, waiting for transfers between devices, device_step(): lax.all_gather(y_loc, 'tp', axis=1, tiled=True).reshape(rows_all, model_dim)  109 us
    all_gather x1, waiting for transfers between devices, device_step(): lax.all_gather((dy_float * gate_row).astype(jnp.bfloat16), 'tp', axis=1,...  85.5 us
    dot_general x3, matrix products, attend(): jnp.einsum('bhqk,bkhd->bqhd', attn_probs, v_heads, preferred_element_type...  46.5 us
    dot_general x2, matrix products, attend(): jnp.einsum('bqhd,bkhd->bhqk', q_rot, k_rot, preferred_element_type=jnp.fl...  45.4 us
    dot_general x1, matrix products, device_step(): lax.dot_general(dv_flat, w_v, COL_CONTRACT, preferred_element_type=jnp.fl...  42.4 us
    psum x1, waiting for transfers between devices, device_step(): lax.psum(jnp.stack([jnp.sum(d_y, axis=1), jnp.sum(d_y * x_norm, axis=1),...  29 us
    dot_general x1, matrix products, device_step(): lax.dot_general(dk_raw, w_k, COL_CONTRACT, preferred_element_type=jnp.flo...  28.2 us
  transfers between devices with their start and end apart: 5, of which 5 were waited for; matrix products, arithmetic and copies ran while one was open for 17% of the time, Pallas kernels for 0%

commit v1 on v0

v1 whole, which is shorter than its diff:
```python
import functools

import jax
import jax.numpy as jnp
from jax import lax
from jax.experimental import pallas as pl
from jax.experimental.pallas import tpu as pltpu
from jax.sharding import PartitionSpec as P

HEAD_DIM = 128
EPS_NORM = 1e-6
ROPE_BASE = 10000.0
LOG2E = 1.4426950408889634
VMEM_LIMIT = 60 * 1024 * 1024
F32 = jnp.float32
BF16 = jnp.bfloat16
MESH_ID = pl.DeviceIdType.MESH
NT = (((1,), (1,)), ((), ()))
TN = (((0,), (0,)), ((), ()))


def params(*semantics, **kw):
    return pltpu.CompilerParams(dimension_semantics=semantics or None, vmem_limit_bytes=VMEM_LIMIT, **kw)


def cost(flops, nbytes):
    return pl.CostEstimate(flops=int(flops), bytes_accessed=int(nbytes), transcendentals=0)


def rope_tables(positions):
    half_dim = HEAD_DIM // 2
    side_len = HEAD_DIM // 6
    first_len = half_dim - 2 * side_len
    lane = jnp.arange(HEAD_DIM)
    pair_idx = lane // 2
    section = (pair_idx >= first_len).astype(jnp.int32) + (pair_idx >= first_len + side_len).astype(jnp.int32)
    offset = jnp.where(section == 0, 0, jnp.where(section == 1, first_len, first_len + side_len))
    sec_width = jnp.where(section == 0, first_len, side_len)
    freq_vals = ROPE_BASE ** (-(pair_idx - offset).astype(F32) / sec_width.astype(F32))
    select = jnp.where(section[None, :] == jnp.arange(3)[:, None], freq_vals[None, :], 0.0)
    angles = jnp.sum(positions.astype(F32)[:, :, None] * select[None, :, :], axis=1)
    return jnp.cos(angles), jnp.where((lane % 2 == 0)[None, :], -1.0, 1.0) * jnp.sin(angles)


def norm_stats(x):
    centered = x - jnp.mean(x, axis=-1, keepdims=True)
    inv_std = lax.rsqrt(jnp.mean(centered * centered, axis=-1, keepdims=True) + EPS_NORM)
    return centered * inv_std, inv_std


def ln_kernel(x_ref, m_ref, e_ref, y_ref):
    mod = m_ref[...] + e_ref[0]
    x_norm, _ = norm_stats(x_ref[0].astype(F32))
    y_ref[...] = (x_norm * (1.0 + mod[1:2]) + mod[0:1]).astype(BF16)


def ln_call(b, x_loc, m_block, e_loc):
    _, rows, dim = x_loc.shape
    return pl.pallas_call(
        ln_kernel, name=f"ln{b}", grid=(1,),
        out_shape=jax.ShapeDtypeStruct((rows, dim), BF16),
        in_specs=[pl.BlockSpec((1, rows, dim), lambda i: (b, 0, 0)), pl.BlockSpec((3, dim), lambda i: (0, 0)),
                  pl.BlockSpec((1, 3, dim), lambda i: (b, 0, 0))],
        out_specs=pl.BlockSpec((rows, dim), lambda i: (0, 0)),
        compiler_params=params("arbitrary"), cost_estimate=cost(rows * dim * 12, rows * dim * 4),
    )(x_loc, m_block, e_loc)


def gate_kernel(d_ref, m_ref, e_ref, o_ref):
    gate = m_ref[2:3] + e_ref[0, 2:3]
    o_ref[...] = (d_ref[0].astype(F32) * gate).astype(BF16)


def gate_call(b, dy_loc, m_block, e_loc):
    _, rows, dim = dy_loc.shape
    return pl.pallas_call(
        gate_kernel, name=f"gate{b}", grid=(1,),
        out_shape=jax.ShapeDtypeStruct((rows, dim), BF16),
        in_specs=[pl.BlockSpec((1, rows, dim), lambda i: (b, 0, 0)), pl.BlockSpec((3, dim), lambda i: (0, 0)),
                  pl.BlockSpec((1, 3, dim), lambda i: (b, 0, 0))],
        out_specs=pl.BlockSpec((rows, dim), lambda i: (0, 0)),
        compiler_params=params("arbitrary"), cost_estimate=cost(rows * dim * 4, rows * dim * 4),
    )(dy_loc, m_block, e_loc)


def to_row(acc):
    return jnp.sum(acc.T, axis=0, keepdims=True)


def lanes_of(row):
    return jnp.broadcast_to(row, (HEAD_DIM, row.shape[1])).T


def head_sum(values):
    out = values[:, :HEAD_DIM]
    for h in range(1, values.shape[1] // HEAD_DIM):
        out = out + values[:, h * HEAD_DIM:(h + 1) * HEAD_DIM]
    return out


def qkv_kernel(steps, y_ref, wq_ref, wk_ref, wv_ref, bq_ref, bk_ref, bv_ref, q_ref, k_ref, v_ref, ss_ref, acc):
    step = pl.program_id(0)
    cols = wq_ref.shape[1]

    @pl.when(step == 0)
    def _():
        acc[:, :cols] = jnp.broadcast_to(bq_ref[...], (acc.shape[0], cols))
        acc[:, cols:2 * cols] = jnp.broadcast_to(bk_ref[...], (acc.shape[0], cols))
        acc[:, 2 * cols:] = jnp.broadcast_to(bv_ref[...], (acc.shape[0], cols))

    w_all = jnp.concatenate([wq_ref[...], wk_ref[...], wv_ref[...]], axis=1)
    acc[...] += jnp.dot(y_ref[...], w_all, preferred_element_type=F32)

    @pl.when(step == steps - 1)
    def _():
        q = acc[:, :cols]
        k = acc[:, cols:2 * cols]
        q_ref[...] = q
        k_ref[...] = k
        v_ref[...] = acc[:, 2 * cols:].astype(BF16)
        row_q = to_row(head_sum(q * q))
        row_k = to_row(head_sum(k * k))
        ss_ref[...] = jnp.concatenate([row_q, row_k, jnp.zeros((6, row_q.shape[1]), F32)], axis=0)


def qkv_call(b, y, w_q, w_k, w_v, b_q, b_k, b_v):
    rows, dim = y.shape
    cols = w_q.shape[1]
    bk = min(512, dim)
    steps = dim // bk
    w_spec = pl.BlockSpec((bk, cols), lambda i: (i, 0))
    vec = pl.BlockSpec((1, cols), lambda i: (0, 0))
    full = pl.BlockSpec((rows, cols), lambda i: (0, 0))
    return pl.pallas_call(
        functools.partial(qkv_kernel, steps), name=f"qkv{b}", grid=(steps,),
        out_shape=[jax.ShapeDtypeStruct((rows, cols), F32), jax.ShapeDtypeStruct((rows, cols), F32),
                   jax.ShapeDtypeStruct((rows, cols), BF16), jax.ShapeDtypeStruct((8, rows), F32)],
        in_specs=[pl.BlockSpec((rows, bk), lambda i: (0, i)), w_spec, w_spec, w_spec, vec, vec, vec],
        out_specs=[full, full, full, pl.BlockSpec((8, rows), lambda i: (0, 0))],
        scratch_shapes=[pltpu.VMEM((rows, 3 * cols), F32)],
        compiler_params=params("arbitrary"),
        cost_estimate=cost(6 * rows * dim * cols, 2 * rows * dim + 6 * dim * cols + 10 * rows * cols),
    )(y, w_q, w_k, w_v, b_q[None], b_k[None], b_v[None])


def exchange_kernel(n, x_ref, o_ref, slots, send_sems, recv_sems):
    me = lax.axis_index('tp')
    barrier = pltpu.get_barrier_semaphore()
    for d in range(1, n):
        pl.semaphore_signal(barrier, inc=1, device_id={'tp': lax.rem(me + d, n)}, device_id_type=MESH_ID)
    pl.semaphore_wait(barrier, n - 1)
    copies = []
    for d in range(1, n):
        copy = pltpu.make_async_remote_copy(
            src_ref=x_ref, dst_ref=slots.at[me], send_sem=send_sems.at[d], recv_sem=recv_sems.at[me],
            device_id={'tp': lax.rem(me + d, n)}, device_id_type=MESH_ID)
        copy.start()
        copies.append(copy)
    slots[me] = x_ref[...]
    for copy in copies:
        copy.wait_send()
    for d in range(1, n):
        src = lax.rem(me + d, n)
        pltpu.make_async_remote_copy(
            src_ref=x_ref, dst_ref=slots.at[src], send_sem=send_sems.at[d], recv_sem=recv_sems.at[src],
            device_id={'tp': src}, device_id_type=MESH_ID).wait_recv()
    total = slots[0]
    for d in range(1, n):
        total = total + slots[d]
    o_ref[...] = total


def exchange_call(name, cid, n, x):
    spec = pl.BlockSpec(memory_space=pltpu.VMEM)
    return pl.pallas_call(
        functools.partial(exchange_kernel, n), name=name,
        out_shape=jax.ShapeDtypeStruct(x.shape, x.dtype), in_specs=[spec], out_specs=spec,
        scratch_shapes=[pltpu.VMEM((n,) + x.shape, x.dtype), pltpu.SemaphoreType.DMA((n,)), pltpu.SemaphoreType.DMA((n,))],
        compiler_params=pltpu.CompilerParams(collective_id=cid, has_side_effects=True),
        cost_estimate=cost(4_000_000_000, x.size * 4 * n),
    )(x)


def swap_pairs(x):
    lane = lax.broadcasted_iota(jnp.int32, x.shape, 1)
    return jnp.where(lane % 2 == 0, pltpu.roll(x, HEAD_DIM - 1, 1), pltpu.roll(x, 1, 1))


def attn_kernel(heads, dim, q_ref, k_ref, v_ref, do_ref, gq_ref, gk_ref, cos_ref, sin_ref, ss_ref,
                o_ref, dv_ref, dqs_ref, dks_ref, dgq_ref, dgk_ref, st_ref,
                inv_q, inv_k, acc_q, acc_k, p_all, ds_all, dq_all):
    head = pl.program_id(0)
    rows = q_ref.shape[0]
    blk = min(256, rows)
    scale = HEAD_DIM ** -0.5

    @pl.when(head == 0)
    def _():
        inv = lax.rsqrt(ss_ref[...] / dim + EPS_NORM)
        inv_q[...] = lanes_of(inv[0:1])
        inv_k[...] = lanes_of(inv[1:2])
        acc_q[...] = jnp.zeros_like(acc_q)
        acc_k[...] = jnp.zeros_like(acc_k)

    cos = cos_ref[...]
    sin = sin_ref[...]
    q_gain = q_ref[...] * inv_q[...] * gq_ref[...]
    k_gain = k_ref[...] * inv_k[...] * gk_ref[...]
    q_rot = (q_gain * cos + swap_pairs(q_gain) * sin).astype(BF16)
    k_rot = (k_gain * cos + swap_pairs(k_gain) * sin).astype(BF16)
    v = v_ref[...]
    do = do_ref[...]
    for i in range(rows // blk):
        sl = slice(i * blk, (i + 1) * blk)
        s = lax.dot_general(q_rot[sl], k_rot, NT, preferred_element_type=F32)
        top = jnp.max(s, axis=1, keepdims=True)
        p = jnp.exp2(s * (scale * LOG2E) - top * (scale * LOG2E))
        p = p * (1.0 / jnp.sum(p, axis=1, keepdims=True))
        p_bf = p.astype(BF16)
        p_all[sl] = p_bf
        o = jnp.dot(p_bf, v, preferred_element_type=F32)
        o_ref[sl] = o.astype(BF16)
        dp = lax.dot_general(do[sl], v, NT, preferred_element_type=F32)
        delta = jnp.sum(do[sl].astype(F32) * o, axis=1, keepdims=True)
        ds = (p * (dp - delta)).astype(BF16)
        ds_all[sl] = ds
        dq_all[sl] = jnp.dot(ds, k_rot, preferred_element_type=F32) * scale
    do_t = do.astype(F32).T.astype(BF16)
    q_t = q_rot.astype(F32).T.astype(BF16)
    dv_ref[...] = jnp.dot(do_t, p_all[...], preferred_element_type=F32).T.astype(BF16)
    dk_rot = (jnp.dot(q_t, ds_all[...], preferred_element_type=F32) * scale).T.astype(BF16).astype(F32)
    dq_rot = dq_all[...].astype(BF16).astype(F32)
    dq_hat = dq_rot * cos - swap_pairs(dq_rot) * sin
    dk_hat = dk_rot * cos - swap_pairs(dk_rot) * sin
    q_hat = q_ref[...] * inv_q[...]
    k_hat = k_ref[...] * inv_k[...]
    dgq_ref[...] = jnp.sum(dq_hat * q_hat, axis=0, keepdims=True)
    dgk_ref[...] = jnp.sum(dk_hat * k_hat, axis=0, keepdims=True)
    dq_s = dq_hat * gq_ref[...]
    dk_s = dk_hat * gk_ref[...]
    dqs_ref[...] = dq_s
    dks_ref[...] = dk_s
    acc_q[...] += dq_s * q_hat
    acc_k[...] += dk_s * k_hat

    @pl.when(head == heads - 1)
    def _():
        row_q = to_row(acc_q[...])
        row_k = to_row(acc_k[...])
        st_ref[...] = jnp.concatenate([row_q, row_k, jnp.zeros((6, row_q.shape[1]), F32)], axis=0)


def attn_call(b, dim, q, k, v, d_attn, g_q, g_k, cos_tab, sin_tab, ss):
    rows, cols = q.shape
    heads = cols // HEAD_DIM
    blk = pl.BlockSpec((rows, HEAD_DIM), lambda h: (0, h))
    vec = pl.BlockSpec((1, HEAD_DIM), lambda h: (0, h))
    tab = pl.BlockSpec((rows, HEAD_DIM), lambda h: (0, 0))
    small = pl.BlockSpec((8, rows), lambda h: (0, 0))
    shape = jax.ShapeDtypeStruct
    return pl.pallas_call(
        functools.partial(attn_kernel, heads, dim), name=f"attn{b}", grid=(heads,),
        out_shape=[shape((rows, cols), BF16), shape((rows, cols), BF16), shape((rows, cols), F32), shape((rows, cols), F32),
                   shape((1, cols), F32), shape((1, cols), F32), shape((8, rows), F32)],
        in_specs=[blk, blk, blk, blk, vec, vec, tab, tab, small],
        out_specs=[blk, blk, blk, blk, vec, vec, small],
        scratch_shapes=[pltpu.VMEM((rows, HEAD_DIM), F32)] * 4
        + [pltpu.VMEM((rows, rows), BF16)] * 2 + [pltpu.VMEM((rows, HEAD_DIM), F32)],
        compiler_params=params("arbitrary"),
        cost_estimate=cost(40 * rows * rows * cols, 24 * rows * cols),
    )(q, k, v, d_attn, g_q[None], g_k[None], cos_tab, sin_tab, ss)


def nn_kernel(a_ref, w_ref, o_ref):
    o_ref[...] = jnp.dot(a_ref[...], w_ref[...], preferred_element_type=F32).astype(BF16)


def nn_call(name, a, w):
    rows, depth = a.shape
    width = w.shape[1]
    bn = min(512, width)
    return pl.pallas_call(
        nn_kernel, name=name, grid=(width // bn,),
        out_shape=jax.ShapeDtypeStruct((rows, width), BF16),
        in_specs=[pl.BlockSpec((rows, depth), lambda i: (0, 0)), pl.BlockSpec((depth, bn), lambda i: (0, i))],
        out_specs=pl.BlockSpec((rows, bn), lambda i: (0, i)),
        compiler_params=params("arbitrary"),
        cost_estimate=cost(2 * rows * depth * width, 2 * (rows * depth + depth * width + rows * width)),
    )(a, w)


def nt_kernel(steps, a_ref, w_ref, o_ref, acc):
    step = pl.program_id(0)

    @pl.when(step == 0)
    def _():
        acc[...] = jnp.zeros_like(acc)

    acc[...] += lax.dot_general(a_ref[...], w_ref[...], NT, preferred_element_type=F32)

    @pl.when(step == steps - 1)
    def _():
        o_ref[...] = acc[...].astype(BF16)


def nt_call(name, a, w):
    rows, depth = a.shape
    width = w.shape[0]
    bk = min(512, depth)
    return pl.pallas_call(
        functools.partial(nt_kernel, depth // bk), name=name, grid=(depth // bk,),
        out_shape=jax.ShapeDtypeStruct((rows, width), BF16),
        in_specs=[pl.BlockSpec((rows, bk), lambda i: (0, i)), pl.BlockSpec((width, bk), lambda i: (0, i))],
        out_specs=pl.BlockSpec((rows, width), lambda i: (0, 0)),
        scratch_shapes=[pltpu.VMEM((rows, width), F32)],
        compiler_params=params("arbitrary"),
        cost_estimate=cost(2 * rows * depth * width, 2 * (rows * depth + depth * width + rows * width)),
    )(a, w)


def dy_kernel(dim, dqs_ref, dks_ref, q_ref, k_ref, dv_ref, ss_ref, st_ref, wq_ref, wk_ref, wv_ref, o_ref, g_ref):
    cols = dqs_ref.shape[1]

    @pl.when(pl.program_id(0) == 0)
    def _():
        inv = lax.rsqrt(ss_ref[...] / dim + EPS_NORM)
        for j, (d_ref, x_ref) in enumerate(((dqs_ref, q_ref), (dks_ref, k_ref))):
            inv_l = lanes_of(inv[j:j + 1])
            st_l = lanes_of(st_ref[j:j + 1] / dim)
            for h in range(cols // HEAD_DIM):
                sl = slice(h * HEAD_DIM, (h + 1) * HEAD_DIM)
                grad = inv_l * (d_ref[:, sl] - (x_ref[:, sl] * inv_l) * st_l)
                g_ref[:, j * cols + h * HEAD_DIM:j * cols + (h + 1) * HEAD_DIM] = grad.astype(BF16)
        g_ref[:, 2 * cols:] = dv_ref[...]

    w_all = jnp.concatenate([wq_ref[...], wk_ref[...], wv_ref[...]], axis=1)
    o_ref[...] = lax.dot_general(g_ref[...], w_all, NT, preferred_element_type=F32).astype(BF16)


def dy_call(b, dqs, dks, q, k, dv, ss, st, w_q, w_k, w_v):
    rows, cols = dqs.shape
    dim = w_q.shape[0]
    bn = min(512, dim)
    full = pl.BlockSpec((rows, cols), lambda i: (0, 0))
    small = pl.BlockSpec((8, rows), lambda i: (0, 0))
    w_spec = pl.BlockSpec((bn, cols), lambda i: (i, 0))
    return pl.pallas_call(
        functools.partial(dy_kernel, dim), name=f"dy{b}", grid=(dim // bn,),
        out_shape=[jax.ShapeDtypeStruct((rows, dim), BF16), jax.ShapeDtypeStruct((rows, 3 * cols), BF16)],
        in_specs=[full, full, full, full, full, small, small, w_spec, w_spec, w_spec],
        out_specs=[pl.BlockSpec((rows, bn), lambda i: (0, i)), pl.BlockSpec((rows, 3 * cols), lambda i: (0, 0))],
        compiler_params=params("arbitrary"),
        cost_estimate=cost(6 * rows * dim * cols, 2 * rows * dim + 6 * dim * cols + 20 * rows * cols),
    )(dqs, dks, q, k, dv, ss, st, w_q, w_k, w_v)


def dw_kernel(nb, *refs):
    y_refs, g_refs, outs = refs[:nb], refs[nb:2 * nb], refs[2 * nb:]
    acc = lax.dot_general(y_refs[0][...], g_refs[0][...], TN, preferred_element_type=F32)
    for b in range(1, nb):
        acc = acc + lax.dot_general(y_refs[b][...], g_refs[b][...], TN, preferred_element_type=F32)
    cols = outs[0].shape[1]
    for j, o_ref in enumerate(outs):
        o_ref[...] = acc[:, j * cols:(j + 1) * cols].astype(BF16)


def dw_call(ys, gs):
    nb = len(ys)
    rows, dim = ys[0].shape
    cols = gs[0].shape[1] // 3
    bm = min(512, dim)
    return pl.pallas_call(
        functools.partial(dw_kernel, nb), name="dw", grid=(dim // bm,),
        out_shape=[jax.ShapeDtypeStruct((dim, cols), BF16)] * 3,
        in_specs=[pl.BlockSpec((rows, bm), lambda i: (0, i))] * nb + [pl.BlockSpec((rows, 3 * cols), lambda i: (0, 0))] * nb,
        out_specs=[pl.BlockSpec((bm, cols), lambda i: (i, 0))] * 3,
        compiler_params=params("arbitrary"),
        cost_estimate=cost(6 * nb * rows * dim * cols, 2 * nb * rows * (dim + 3 * cols) + 6 * dim * cols),
    )(*ys, *gs)


def dwo_kernel(nb, *refs):
    o_refs, d_refs, out, turned = refs[:nb], refs[nb:2 * nb], refs[2 * nb], refs[2 * nb + 1]

    @pl.when(pl.program_id(0) == 0)
    def _():
        for b in range(nb):
            turned[b] = o_refs[b][...].T

    acc = jnp.dot(turned[0], d_refs[0][...], preferred_element_type=F32)
    for b in range(1, nb):
        acc = acc + jnp.dot(turned[b], d_refs[b][...], preferred_element_type=F32)
    out[...] = acc.astype(BF16)


def dwo_call(os, ds):
    nb = len(os)
    rows, cols = os[0].shape
    dim = ds[0].shape[1]
    bn = min(512, dim)
    return pl.pallas_call(
        functools.partial(dwo_kernel, nb), name="dwo", grid=(dim // bn,),
        out_shape=jax.ShapeDtypeStruct((cols, dim), BF16),
        in_specs=[pl.BlockSpec((rows, cols), lambda i: (0, 0))] * nb + [pl.BlockSpec((rows, bn), lambda i: (0, i))] * nb,
        out_specs=pl.BlockSpec((cols, bn), lambda i: (0, i)),
        scratch_shapes=[pltpu.VMEM((nb, cols, rows), BF16)],
        compiler_params=params("arbitrary"),
        cost_estimate=cost(2 * nb * rows * dim * cols, 2 * nb * rows * (dim + cols) + 2 * dim * cols),
    )(*os, *ds)


def out_kernel(x_ref, dy_ref, pr_ref, m_ref, e_ref, bo_ref, *rest):
    o_ref, dg_ref = rest[-2:]
    gate = m_ref[2:3] + e_ref[0, 2:3]
    proj = pr_ref[...].astype(F32) + bo_ref[...]
    o_ref[0] = (x_ref[0].astype(F32) + gate * proj).astype(BF16)
    dg_ref[...] = jnp.sum(dy_ref[0].astype(F32) * proj, axis=0, keepdims=True)


def dx_kernel(x_ref, dy_ref, g_ref, m_ref, e_ref, *rest):
    o_ref, dm_ref = rest[-2:]
    scale_one = 1.0 + (m_ref[1:2] + e_ref[0, 1:2])
    x_norm, inv_std = norm_stats(x_ref[0].astype(F32))
    d_y = g_ref[...].astype(F32)
    d_norm = d_y * scale_one
    d_x = dy_ref[0].astype(F32) + inv_std * (
        d_norm - jnp.mean(d_norm, axis=-1, keepdims=True) - x_norm * jnp.mean(d_norm * x_norm, axis=-1, keepdims=True))
    o_ref[0] = d_x.astype(BF16)
    dm_ref[0:1] = jnp.sum(d_y, axis=0, keepdims=True)
    dm_ref[1:2] = jnp.sum(d_y * x_norm, axis=0, keepdims=True)


def token_call(kernel, name, b, n_sums, x_loc, dy_loc, piece, m_block, e_loc, extra, whole):
    _, rows, dim = x_loc.shape
    row = pl.BlockSpec((1, rows, dim), lambda i: (b, 0, 0))
    specs = [row, row, pl.BlockSpec((rows, dim), lambda i: (0, 0)), pl.BlockSpec((3, dim), lambda i: (0, 0)),
             pl.BlockSpec((1, 3, dim), lambda i: (b, 0, 0))] + [pl.BlockSpec((1, dim), lambda i: (0, 0))] * len(extra)
    args = [x_loc, dy_loc, piece, m_block, e_loc, *extra]
    aliases = {}
    if whole is not None:
        aliases = {len(args): 0}
        specs.append(pl.BlockSpec(memory_space=pl.ANY))
        args.append(whole)
    return pl.pallas_call(
        kernel, name=f"{name}{b}", grid=(1,),
        out_shape=[jax.ShapeDtypeStruct(x_loc.shape, BF16), jax.ShapeDtypeStruct((n_sums, dim), F32)],
        in_specs=specs, out_specs=[row, pl.BlockSpec((n_sums, dim), lambda i: (0, 0))],
        input_output_aliases=aliases, compiler_params=params("arbitrary"),
        cost_estimate=cost(rows * dim * 20, rows * dim * 8),
    )(*args)


def solution(mesh):
    tp_size = mesh.shape['tp']

    def device_step(x_loc, e_loc, m_block, w_q, b_q, w_k, b_k, w_v, b_v, w_o, b_o, g_q, g_k, pos_part, dy_loc):
        nb, _, dim = x_loc.shape
        batch = range(nb)

        y_loc = [ln_call(b, x_loc, m_block, e_loc) for b in batch]
        dp_loc = [gate_call(b, dy_loc, m_block, e_loc) for b in batch]
        y_all = [lax.all_gather(y_loc[b], 'tp', axis=0, tiled=True) for b in batch]
        dp_all = [lax.all_gather(dp_loc[b], 'tp', axis=0, tiled=True) for b in batch]
        cos_tab, sin_tab = rope_tables(pos_part)

        qkv = []
        for b in batch:
            q, k, v, ss = qkv_call(b, y_all[b], w_q, w_k, w_v, b_q, b_k, b_v)
            qkv.append((q, k, v, exchange_call(f"sumsq{b}", b, tp_size, ss)))

        x_out, d_x = None, None
        o_all, grads, d_gq, d_gk, gate_sums, mod_sums, parts = [], [], [], [], [], [], []
        for b in batch:
            q, k, v, ss = qkv[b]
            d_attn = nt_call(f"dattn{b}", dp_all[b], w_o)
            o, dv, dqs, dks, dgq, dgk, st = attn_call(b, dim, q, k, v, d_attn, g_q, g_k, cos_tab, sin_tab, ss)
            o_all.append(o)
            d_gq.append(dgq)
            d_gk.append(dgk)
            part = nn_call(f"proj{b}", o, w_o)
            st, part = lax.optimization_barrier((st, part))
            st = exchange_call(f"stat{b}", nb + b, tp_size, st)
            dy_part, grad = dy_call(b, dqs, dks, q, k, dv, ss, st, w_q, w_k, w_v)
            grads.append(grad)
            parts.append((part, dy_part))
        d_wq, d_wk, d_wv = dw_call(y_all, grads)
        d_wo = dwo_call(o_all, dp_all)
        for b in batch:
            proj = lax.psum_scatter(parts[b][0], 'tp', scatter_dimension=0, tiled=True)
            if b:
                proj, mod_sums[b - 1] = lax.optimization_barrier((proj, mod_sums[b - 1]))
            x_out, dg = token_call(out_kernel, "xout", b, 1, x_loc, dy_loc, proj, m_block, e_loc, [b_o[None]], x_out)
            gate_sums.append(dg)
            d_y = lax.psum_scatter(parts[b][1], 'tp', scatter_dimension=0, tiled=True)
            d_x, dm = token_call(dx_kernel, "dx", b, 2, x_loc, dy_loc, d_y, m_block, e_loc, [], d_x)
            flat = jnp.concatenate([dm, gate_sums[b]], axis=0)
            mod_sums.append(exchange_call(f"dmod{b}", 2 * nb + b, tp_size, flat.reshape(8, -1)).reshape(3, dim))
        d_e = jnp.stack(mod_sums)
        return (x_out, d_x, d_e, jnp.sum(d_e, axis=0), d_wq, d_wk, d_wv, d_wo,
                sum(d_gq)[0], sum(d_gk)[0])

    in_specs = (P('dp', 'tp', None), P('dp', None, None), P(None, None), P(None, 'tp'), P('tp'), P(None, 'tp'), P('tp'),
                P(None, 'tp'), P('tp'), P('tp', None), P(None), P('tp'), P('tp'), P('dp', None), P('dp', 'tp', None))
    out_specs = (P('dp', 'tp', None), P('dp', 'tp', None), P('dp', None, None), P('dp', None), P('dp', 'tp'), P('dp', 'tp'),
                 P('dp', 'tp'), P(('dp', 'tp'), None), P(('dp', 'tp')), P(('dp', 'tp')))
    return jax.shard_map(device_step, mesh=mesh, in_specs=in_specs, out_specs=out_specs, check_vma=False)
```

time: 1020 us -> 640 us (0.63)
  Pallas kernels: 0 us -> 505 us
  matrix products: 423 us -> 0 us
  waiting for transfers between devices: 354 us -> 95.8 us
  other arithmetic: 104 us -> 7.02 us
  local copies, waits for them, and re-layouts: 68.3 us -> 9.01 us
  blocking collectives: 46 us -> 0 us
    pallas_call x0 -> x38, Pallas kernels: none -> 505 us  [the longest x9 95.6 us: exchange_call(): pl.pallas_call(functools.partial(exchange_kernel, n), name=name, out_shap...]
    dot_general x17 -> x0, matrix products: 403 us -> none  [the longest x3 46.5 us: attend(): jnp.einsum('bhqk,bkhd->bqhd', attn_probs, v_heads, preferred_element_type...]
    all_gather x2 -> x6, waiting for transfers between devices: 194 us -> 43.8 us  [the longest x3 28.5 us: device_step(): y_all = [lax.all_gather(y_loc[b], 'tp', axis=0, tiled=True) for b in batch]]
    reduce_scatter x2 -> x6, waiting for transfers between devices: 131 us -> 50.6 us  [the longest x3 45.5 us: device_step(): d_y = lax.psum_scatter(parts[b][1], 'tp', scatter_dimension=0, tiled=True)]
    psum x2 -> x0, blocking collectives: 46 us -> none  [the longest x1 23.9 us: device_step(): lax.psum(jnp.stack([jnp.sum(dq_scaled * q_hat, axis=-1), jnp.sum(dk_scale...]
    psum x1 -> x0, waiting for transfers between devices: 29 us -> none  [device_step(): lax.psum(jnp.stack([jnp.sum(d_y, axis=1), jnp.sum(d_y * x_norm, axis=1),...]
    another operation x8 -> x1, other arithmetic: 29.7 us -> 0.75 us  [device_step(): d_e = jnp.stack(mod_sums)]
    reduce_sum x8 -> x2, other arithmetic: 29.8 us -> 1.03 us  [the longest x1 0.67 us: device_step(): jnp.sum(d_e, axis=0)]
  transfers between devices with their start and end apart: 5 -> 12, of which waited for: 5 -> 4; matrix products, arithmetic and copies ran while one was open for 17% -> 2% of each run, Pallas kernels for 0% -> 77%
where the time goes in v1:
time: 640 us; the launch traced here: 633 us
  Pallas kernels  505 us (79%)
  waiting for transfers between devices  95.8 us (15%)
  between operations  14.7 us (2%)
  local copies, waits for them, and re-layouts  9.01 us (1%)
  other arithmetic  7.02 us (1%)
    pallas_call x9, Pallas kernels, exchange_call(): pl.pallas_call(functools.partial(exchange_kernel, n), name=name, out_shap...  95.6 us
    pallas_call x3, Pallas kernels, dy_call(): pl.pallas_call(functools.partial(dy_kernel, dim), name=f'dy{b}', grid=(di...  75.2 us
    pallas_call x3, Pallas kernels, qkv_call(): pl.pallas_call(functools.partial(qkv_kernel, steps), name=f'qkv{b}', grid...  69.8 us
    pallas_call x3, Pallas kernels, attn_call(): pl.pallas_call(functools.partial(attn_kernel, heads, dim), name=f'attn{b}...  66.8 us
    pallas_call x1, Pallas kernels, dw_call(): pl.pallas_call(functools.partial(dw_kernel, nb), name='dw', grid=(dim //...  56.7 us
    reduce_scatter x3, waiting for transfers between devices, device_step(): d_y = lax.psum_scatter(parts[b][1], 'tp', scatter_dimension=0, tiled=True)  45.5 us
    pallas_call x3, Pallas kernels, nt_call(): pl.pallas_call(functools.partial(nt_kernel, depth // bk), name=name, grid...  39.4 us
    pallas_call x3, Pallas kernels, nn_call(): pl.pallas_call(nn_kernel, name=name, grid=(width // bn,), out_shape=jax.S...  38.3 us
  transfers between devices with their start and end apart: 12, of which 4 were waited for; matrix products, arithmetic and copies ran while one was open for 2% of the time, Pallas kernels for 77%

profile of v1, /device:TPU:81, one launch (start us, length us, event | category | flops | bytes accessed | tf_op | source)
XLA Modules:
  0.0 633.1 jit_solution(16753209007547071978)
XLA Ops:
  7.3 3.2 ln0.1
  10.6 2.4 gate0.1
  13.1 3.2 ln1.1
  16.4 2.4 gate1.1
  19.0 3.2 ln2.1
  22.4 2.4 gate2.1
  24.8 0.5 reduce-scatter.11.cloned.1.call-start
  25.4 0.6 broadcast_in_dim.66.bq_ref
  26.0 0.6 broadcast_in_dim.67.bk_ref
  26.5 0.6 broadcast_in_dim.68.bv_ref
  27.1 0.6 broadcast_in_dim.69.gq_ref
  27.7 0.6 broadcast_in_dim.70.gk_ref
  28.7 2.2 sine_multiply_fusion
  30.9 28.5 %all-gather.15.cloned.1.call-done.y_ref.refs_0_ = bf16[768,5120]{1,0:T(8,128)(2,1)} async-done(((bf16[96,5120]{1,0:T(8,128)(2,1)}), bf16[768,5120]{1,0:T(8,128)(2,1)}) %all-gather.15.cloned.1.call-update) | async-done | bytes 7864336 | tf_op jit(solution)/shard_map/all_gather | solution.py:462
  59.4 23.3 %qkv0.1 = (f32[768,640]{1,0:T(8,128)}, f32[768,640]{1,0:T(8,128)}, bf16[768,640]{1,0:T(8,128)(2,1)}, f32[8,768]{1,0:T(8,128)}) custom-call(bf16[768,5120]{1,0:T(8,128)(2,1)} %all-gather.15.cloned.1.call-done.y_ref.refs_0_, bf16[5120,640]{1,0:T(8,128)(2,1)} %wq_ref.11, bf16[5120,640]{1,0:T(8,128)(2,1)} %wk_ref.11, bf16[5120,640]{1,0:T(8,128)(2,1)} %wv_ref.11, ...), custom_call_target="tpu_custom_call" | custom-call | flops 15099494400 | bytes 32440320 | tf_op jit(solution)/shard_map/qkv0/pallas_call | solution.py:134
  82.7 10.2 %sumsq0.1.ss_ref = f32[8,768]{1,0:T(8,128)} custom-call(f32[8,768]{1,0:T(8,128)} %get-tuple-element.95.x_ref), custom_call_target="tpu_custom_call" | custom-call | flops 4000000000 | bytes 196608 | tf_op jit(solution)/shard_map/sumsq0/pallas_call | solution.py:175
  92.8 15.3 %all-gather.17.cloned.1.call-done.a_ref.refs_3_ = bf16[768,5120]{1,0:T(8,128)(2,1)} async-done(((bf16[96,5120]{1,0:T(8,128)(2,1)}), bf16[768,5120]{1,0:T(8,128)(2,1)}) %all-gather.17.cloned.1.call-update) | async-done | bytes 7864336 | tf_op jit(solution)/shard_map/all_gather | solution.py:463
  108.1 13.2 %dattn0.1.do_ref = bf16[768,640]{1,0:T(8,128)(2,1)} custom-call(bf16[768,5120]{1,0:T(8,128)(2,1)} %all-gather.17.cloned.1.call-done.a_ref.refs_3_, bf16[640,5120]{1,0:T(8,128)(2,1)} %w_ref.11), custom_call_target="tpu_custom_call" | custom-call | flops 5033164800 | bytes 15400960 | tf_op jit(solution)/shard_map/dattn0/pallas_call | solution.py:310
  121.3 22.3 %attn0.1 = (bf16[768,640]{1,0:T(8,128)(2,1)}, bf16[768,640]{1,0:T(8,128)(2,1)}, f32[768,640]{1,0:T(8,128)}, f32[768,640]{1,0:T(8,128)}, f32[1,640]{1,0:T(1,128)}, /*index=5*/f32[1,640]{1,0:T(1,128)}, f32[8,768]{1,0:T(8,128)}) custom-call(f32[768,640]{1,0:T(8,128)} %get-tuple-element.92.q_ref, f32[768,640]{1,0:T(8,128)} %get-tuple-element.93.k_ref, ...), custom_call_target="tpu_custom_call" | custom-call | flops 15099494400 | bytes 11796480 | tf_op jit(solution)/shard_map/attn0/pallas_call | solution.py:261
  143.5 12.7 %proj0.1 = bf16[768,5120]{1,0:T(8,128)(2,1)} custom-call(bf16[768,640]{1,0:T(8,128)(2,1)} %get-tuple-element.100.a_ref.refs_0_, bf16[640,5120]{1,0:T(8,128)(2,1)} %w_ref.11), custom_call_target="tpu_custom_call" | custom-call | flops 5033164800 | bytes 15400960 | tf_op jit(solution)/shard_map/proj0/pallas_call | solution.py:282
  156.3 7.7 %stat0.1.st_ref = f32[8,768]{1,0:T(8,128)} custom-call(f32[8,768]{1,0:T(8,128)} %get-tuple-element.101.x_ref), custom_call_target="tpu_custom_call" | custom-call | flops 4000000000 | bytes 196608 | tf_op jit(solution)/shard_map/stat0/pallas_call | solution.py:175
  164.0 25.0 %dy0.1 = (bf16[768,5120]{1,0:T(8,128)(2,1)}, bf16[768,1920]{1,0:T(8,128)(2,1)}) custom-call(f32[768,640]{1,0:T(8,128)} %get-tuple-element.96.dqs_ref, f32[768,640]{1,0:T(8,128)} %get-tuple-element.97.dks_ref, f32[768,640]{1,0:T(8,128)} %get-tuple-element.92.q_ref, f32[768,640]{1,0:T(8,128)} %get-tuple-element.93.k_ref, ...), custom_call_target="tpu_custom_call" | custom-call | flops 15099494400 | bytes 37355520 | tf_op jit(solution)/shard_map/dy0/pallas_call | solution.py:347
  189.2 0.7 reduce-scatter.15.cloned.1.call-update
  190.2 23.3 %qkv1.1 = (f32[768,640]{1,0:T(8,128)}, f32[768,640]{1,0:T(8,128)}, bf16[768,640]{1,0:T(8,128)(2,1)}, f32[8,768]{1,0:T(8,128)}) custom-call(bf16[768,5120]{1,0:T(8,128)(2,1)} %all-gather.11.cloned.1.call-done.y_ref.refs_1_, bf16[5120,640]{1,0:T(8,128)(2,1)} %wq_ref.11, bf16[5120,640]{1,0:T(8,128)(2,1)} %wk_ref.11, bf16[5120,640]{1,0:T(8,128)(2,1)} %wv_ref.11, ...), custom_call_target="tpu_custom_call" | custom-call | flops 15099494400 | bytes 32440320 | tf_op jit(solution)/shard_map/qkv1/pallas_call | solution.py:134
  213.5 10.3 %sumsq1.1.ss_ref = f32[8,768]{1,0:T(8,128)} custom-call(f32[8,768]{1,0:T(8,128)} %get-tuple-element.84.x_ref), custom_call_target="tpu_custom_call" | custom-call | flops 4000000000 | bytes 196608 | tf_op jit(solution)/shard_map/sumsq1/pallas_call | solution.py:175
  223.8 13.1 %dattn1.1.do_ref = bf16[768,640]{1,0:T(8,128)(2,1)} custom-call(bf16[768,5120]{1,0:T(8,128)(2,1)} %all-gather.13.cloned.1.call-done.a_ref.refs_4_, bf16[640,5120]{1,0:T(8,128)(2,1)} %w_ref.11), custom_call_target="tpu_custom_call" | custom-call | flops 5033164800 | bytes 15400960 | tf_op jit(solution)/shard_map/dattn1/pallas_call | solution.py:310
  236.9 22.3 %attn1.1 = (bf16[768,640]{1,0:T(8,128)(2,1)}, bf16[768,640]{1,0:T(8,128)(2,1)}, f32[768,640]{1,0:T(8,128)}, f32[768,640]{1,0:T(8,128)}, f32[1,640]{1,0:T(1,128)}, /*index=5*/f32[1,640]{1,0:T(1,128)}, f32[8,768]{1,0:T(8,128)}) custom-call(f32[768,640]{1,0:T(8,128)} %get-tuple-element.81.q_ref, f32[768,640]{1,0:T(8,128)} %get-tuple-element.82.k_ref, ...), custom_call_target="tpu_custom_call" | custom-call | flops 15099494400 | bytes 11796480 | tf_op jit(solution)/shard_map/attn1/pallas_call | solution.py:261
  259.2 12.8 %proj1.1 = bf16[768,5120]{1,0:T(8,128)(2,1)} custom-call(bf16[768,640]{1,0:T(8,128)(2,1)} %get-tuple-element.89.a_ref.refs_1_, bf16[640,5120]{1,0:T(8,128)(2,1)} %w_ref.11), custom_call_target="tpu_custom_call" | custom-call | flops 5033164800 | bytes 15400960 | tf_op jit(solution)/shard_map/proj1/pallas_call | solution.py:282
  272.1 10.0 %stat1.1.st_ref = f32[8,768]{1,0:T(8,128)} custom-call(f32[8,768]{1,0:T(8,128)} %get-tuple-element.90.x_ref), custom_call_target="tpu_custom_call" | custom-call | flops 4000000000 | bytes 196608 | tf_op jit(solution)/shard_map/stat1/pallas_call | solution.py:175
  282.1 25.1 %dy1.1 = (bf16[768,5120]{1,0:T(8,128)(2,1)}, bf16[768,1920]{1,0:T(8,128)(2,1)}) custom-call(f32[768,640]{1,0:T(8,128)} %get-tuple-element.85.dqs_ref, f32[768,640]{1,0:T(8,128)} %get-tuple-element.86.dks_ref, f32[768,640]{1,0:T(8,128)} %get-tuple-element.81.q_ref, f32[768,640]{1,0:T(8,128)} %get-tuple-element.82.k_ref, ...), custom_call_target="tpu_custom_call" | custom-call | flops 15099494400 | bytes 37355520 | tf_op jit(solution)/shard_map/dy1/pallas_call | solution.py:347
  307.6 23.3 %qkv2.1 = (f32[768,640]{1,0:T(8,128)}, f32[768,640]{1,0:T(8,128)}, bf16[768,640]{1,0:T(8,128)(2,1)}, f32[8,768]{1,0:T(8,128)}) custom-call(bf16[768,5120]{1,0:T(8,128)(2,1)} %all-gather.7.cloned.1.call-done.y_ref.refs_2_, bf16[5120,640]{1,0:T(8,128)(2,1)} %wq_ref.11, bf16[5120,640]{1,0:T(8,128)(2,1)} %wk_ref.11, bf16[5120,640]{1,0:T(8,128)(2,1)} %wv_ref.11, ...), custom_call_target="tpu_custom_call" | custom-call | flops 15099494400 | bytes 32440320 | tf_op jit(solution)/shard_map/qkv2/pallas_call | solution.py:134
  330.8 8.9 %sumsq2.1.ss_ref = f32[8,768]{1,0:T(8,128)} custom-call(f32[8,768]{1,0:T(8,128)} %get-tuple-element.77.x_ref), custom_call_target="tpu_custom_call" | custom-call | flops 4000000000 | bytes 196608 | tf_op jit(solution)/shard_map/sumsq2/pallas_call | solution.py:175
  339.8 13.1 %dattn2.1.do_ref = bf16[768,640]{1,0:T(8,128)(2,1)} custom-call(bf16[768,5120]{1,0:T(8,128)(2,1)} %all-gather.9.cloned.1.call-done.a_ref.refs_5_, bf16[640,5120]{1,0:T(8,128)(2,1)} %w_ref.11), custom_call_target="tpu_custom_call" | custom-call | flops 5033164800 | bytes 15400960 | tf_op jit(solution)/shard_map/dattn2/pallas_call | solution.py:310
  352.9 22.3 %attn2.1 = (bf16[768,640]{1,0:T(8,128)(2,1)}, bf16[768,640]{1,0:T(8,128)(2,1)}, f32[768,640]{1,0:T(8,128)}, f32[768,640]{1,0:T(8,128)}, f32[1,640]{1,0:T(1,128)}, /*index=5*/f32[1,640]{1,0:T(1,128)}, f32[8,768]{1,0:T(8,128)}) custom-call(f32[768,640]{1,0:T(8,128)} %get-tuple-element.74.q_ref, f32[768,640]{1,0:T(8,128)} %get-tuple-element.75.k_ref, ...), custom_call_target="tpu_custom_call" | custom-call | flops 15099494400 | bytes 11796480 | tf_op jit(solution)/shard_map/attn2/pallas_call | solution.py:261
  375.2 12.8 %proj2.1 = bf16[768,5120]{1,0:T(8,128)(2,1)} custom-call(bf16[768,640]{1,0:T(8,128)(2,1)} %get-tuple-element.79.a_ref.refs_2_, bf16[640,5120]{1,0:T(8,128)(2,1)} %w_ref.11), custom_call_target="tpu_custom_call" | custom-call | flops 5033164800 | bytes 15400960 | tf_op jit(solution)/shard_map/proj2/pallas_call | solution.py:282
  388.5 8.9 %stat2.1.st_ref = f32[8,768]{1,0:T(8,128)} custom-call(f32[8,768]{1,0:T(8,128)} %get-tuple-element.118.x_ref), custom_call_target="tpu_custom_call" | custom-call | flops 4000000000 | bytes 196608 | tf_op jit(solution)/shard_map/stat2/pallas_call | solution.py:175
  397.4 25.1 %dy2.1 = (bf16[768,5120]{1,0:T(8,128)(2,1)}, bf16[768,1920]{1,0:T(8,128)(2,1)}) custom-call(f32[768,640]{1,0:T(8,128)} %get-tuple-element.115.dqs_ref, f32[768,640]{1,0:T(8,128)} %get-tuple-element.116.dks_ref, f32[768,640]{1,0:T(8,128)} %get-tuple-element.74.q_ref, f32[768,640]{1,0:T(8,128)} %get-tuple-element.75.k_ref, ...), custom_call_target="tpu_custom_call" | custom-call | flops 15099494400 | bytes 37355520 | tf_op jit(solution)/shard_map/dy2/pallas_call | solution.py:347
  422.6 0.6 copy-done.9
  423.2 0.6 add_reduce_fusion
  423.8 22.2 %dwo.1 = bf16[640,5120]{1,0:T(8,128)(2,1)} custom-call(bf16[768,640]{1,0:T(8,128)(2,1)} %get-tuple-element.100.a_ref.refs_0_, bf16[768,640]{1,0:T(8,128)(2,1)} %get-tuple-element.89.a_ref.refs_1_, bf16[768,640]{1,0:T(8,128)(2,1)} %get-tuple-element.79.a_ref.refs_2_, bf16[768,5120]{1,0:T(8,128)(2,1)} %all-gather.17.cloned.1.call-done.a_ref.refs_3_, ...), custom_call_target="tpu_custom_call" | custom-call | flops 15099494400 | bytes 33095680 | tf_op jit(solution)/shard_map/dwo/pallas_call | solution.py:401
  446.0 56.7 %dw.1 = (bf16[5120,640]{1,0:T(8,128)(2,1)}, bf16[5120,640]{1,0:T(8,128)(2,1)}, bf16[5120,640]{1,0:T(8,128)(2,1)}) custom-call(bf16[768,5120]{1,0:T(8,128)(2,1)} %all-gather.15.cloned.1.call-done.y_ref.refs_0_, bf16[768,5120]{1,0:T(8,128)(2,1)} %all-gather.11.cloned.1.call-done.y_ref.refs_1_, bf16[768,5120]{1,0:T(8,128)(2,1)} %all-gather.7.cloned.1.call-done.y_ref.refs_2_, ...), custom_call_target="tpu_custom_call" | custom-call | flops 45298483200 | bytes 52101120 | tf_op jit(solution)/shard_map/dw/pallas_call | solution.py:372
  502.7 4.7 dx0.1
  507.4 3.3 xout0.1
  510.7 0.8 pad_maximum_fusion.1
  511.5 0.7 reshape.120.x_ref
  512.1 13.8 %dmod0.1 = f32[8,1920]{1,0:T(8,128)} custom-call(f32[8,1920]{1,0:T(8,128)} %reshape.120.x_ref), custom_call_target="tpu_custom_call" | custom-call | flops 4000000000 | bytes 491520 | tf_op jit(solution)/shard_map/dmod0/pallas_call | solution.py:175
  525.9 0.9 reshape.121
  526.8 3.3 xout1.1
  530.1 4.7 dx1.1
  534.8 0.8 pad_maximum_fusion.2
  535.6 0.7 reshape.122.x_ref
  536.3 13.7 %dmod1.1 = f32[8,1920]{1,0:T(8,128)} custom-call(f32[8,1920]{1,0:T(8,128)} %reshape.122.x_ref), custom_call_target="tpu_custom_call" | custom-call | flops 4000000000 | bytes 491520 | tf_op jit(solution)/shard_map/dmod1/pallas_call | solution.py:175
  550.0 0.9 reshape.123
  550.9 5.1 reduce-scatter.7.cloned.1.call-done.pr_ref
  556.0 3.3 xout2.1
  559.3 45.4 %reduce-scatter.17.cloned.1.call-done.g_ref = bf16[96,5120]{1,0:T(8,128)(2,1)} async-done(((bf16[768,5120]{1,0:T(8,128)(2,1)}), bf16[96,5120]{1,0:T(8,128)(2,1)}) %reduce-scatter.17.cloned.1.call-update) | async-done | bytes 983056 | tf_op jit(solution)/shard_map/reduce_scatter | solution.py:494
  604.8 4.7 dx2.1
  609.4 0.8 pad_maximum_fusion.3
  610.3 0.7 reshape.124.x_ref
  610.9 12.0 %dmod2.1 = f32[8,1920]{1,0:T(8,128)} custom-call(f32[8,1920]{1,0:T(8,128)} %reshape.124.x_ref), custom_call_target="tpu_custom_call" | custom-call | flops 4000000000 | bytes 491520 | tf_op jit(solution)/shard_map/dmod2/pallas_call | solution.py:175
  623.0 0.9 reduce_sum.23
  623.8 0.9 stack_reshape.3
  624.7 0.7 add_add_fusion
  625.4 0.7 pad_maximum_fusion
  (65 shorter events, 2.7 us)
Async XLA Ops:
  7.2 52.2 %all-gather.15.cloned.1.call-start = ((), (), s32[]{:S(2)}) async-start(), calls=%async_computation.12 | async-start | bytes 8847360 | tf_op jit(solution)/shard_map/all_gather | solution.py:462
  10.5 97.6 %all-gather.17.cloned.1.call-start = ((), (), s32[]{:S(2)}) async-start(), calls=%async_computation.13 | async-start | bytes 8847360 | tf_op jit(solution)/shard_map/all_gather | solution.py:463
  13.0 177.2 %all-gather.11.cloned.1.call-start = ((), (), s32[]{:S(2)}) async-start(), calls=%async_computation.9 | async-start | bytes 8847360 | tf_op jit(solution)/shard_map/all_gather | solution.py:462
  16.4 207.4 %all-gather.13.cloned.1.call-start = ((), (), s32[]{:S(2)}) async-start(), calls=%async_computation.10 | async-start | bytes 8847360 | tf_op jit(solution)/shard_map/all_gather | solution.py:463
  18.9 288.7 %all-gather.7.cloned.1.call-start = ((), (), s32[]{:S(2)}) async-start(), calls=%async_computation.6 | async-start | bytes 8847360 | tf_op jit(solution)/shard_map/all_gather | solution.py:462
  22.2 3.2 copy-start.4
  22.2 3.8 copy-start.5
  22.2 4.4 copy-start.6
  22.2 4.9 copy-start.7
  22.2 5.5 copy-start.8
  22.2 6.1 copy-start.3
  22.3 317.5 %all-gather.9.cloned.1.call-start = ((), (), s32[]{:S(2)}) async-start(), calls=%async_computation.7 | async-start | bytes 8847360 | tf_op jit(solution)/shard_map/all_gather | solution.py:463
  24.8 477.8 %reduce-scatter.11.cloned.1.call-start = ((), (), s32[]{:S(2)}) async-start(), calls=%async_computation.14 | async-start | bytes 8847360 | tf_op jit(solution)/shard_map/reduce_scatter | solution.py:494
  189.1 318.2 %reduce-scatter.15.cloned.1.call-start = ((), (), s32[]{:S(2)}) async-start(), calls=%async_computation.16 | async-start | bytes 8847360 | tf_op jit(solution)/shard_map/reduce_scatter | solution.py:489
  189.9 336.9 %reduce-scatter.13.cloned.1.call-start = ((), (), s32[]{:S(2)}) async-start(), calls=%async_computation.15 | async-start | bytes 8847360 | tf_op jit(solution)/shard_map/reduce_scatter | solution.py:489
  272.0 258.1 %reduce-scatter.9.cloned.1.call-start = ((), (), s32[]{:S(2)}) async-start(), calls=%async_computation.11 | async-start | bytes 8847360 | tf_op jit(solution)/shard_map/reduce_scatter | solution.py:494
  307.3 248.7 %reduce-scatter.7.cloned.1.call-start = ((), (), s32[]{:S(2)}) async-start(), calls=%async_computation.8 | async-start | bytes 8847360 | tf_op jit(solution)/shard_map/reduce_scatter | solution.py:489
  388.0 216.8 %reduce-scatter.17.cloned.1.call-start = ((), (), s32[]{:S(2)}) async-start(), calls=%async_computation.17 | async-start | bytes 8847360 | tf_op jit(solution)/shard_map/reduce_scatter | solution.py:494
  422.5 0.7 copy-start.9
  422.5 0.7 copy-start.10
  422.5 0.7 copy-start.11
  422.5 0.7 copy-start.12
  422.5 0.7 copy-start.13
  422.5 0.7 copy-start.14
  507.4 3.3 copy-start
  530.1 4.7 copy-start.1
  604.8 4.7 copy-start.2
Sparse Core Ops, SparseCore 0:
  10.6 48.7 all-gather.14
  61.6 46.4 all-gather.16
  110.3 44.3 all-gather.10
  156.1 44.3 all-gather.12
  202.6 46.4 all-gather.6
  250.6 46.4 all-gather.8
  299.4 48.3 reduce-scatter.10
  350.1 48.6 reduce-scatter.14
  401.1 46.5 reduce-scatter.12
  449.9 46.5 reduce-scatter.8
  498.9 57.0 reduce-scatter.6
  558.2 46.5 reduce-scatter.16

commit v2 on v0

v2 whole, which is shorter than its diff:
```python
import functools

import jax
import jax.numpy as jnp
from jax import lax
from jax.experimental import pallas as pl
from jax.experimental.pallas import tpu as pltpu
from jax.sharding import PartitionSpec as P

HEAD_DIM = 128
EPS_NORM = 1e-6
ROPE_BASE = 10000.0
LOG2E = 1.4426950408889634
VMEM_LIMIT = 60 * 1024 * 1024
F32 = jnp.float32
BF16 = jnp.bfloat16
MESH_ID = pl.DeviceIdType.MESH
NT = (((1,), (1,)), ((), ()))
TN = (((0,), (0,)), ((), ()))


def params(*semantics, **kw):
    return pltpu.CompilerParams(dimension_semantics=semantics or None, vmem_limit_bytes=VMEM_LIMIT, **kw)


def cost(flops, nbytes):
    return pl.CostEstimate(flops=int(flops), bytes_accessed=int(nbytes), transcendentals=0)


def rope_tables(positions):
    half_dim = HEAD_DIM // 2
    side_len = HEAD_DIM // 6
    first_len = half_dim - 2 * side_len
    lane = jnp.arange(HEAD_DIM)
    pair_idx = lane // 2
    section = (pair_idx >= first_len).astype(jnp.int32) + (pair_idx >= first_len + side_len).astype(jnp.int32)
    offset = jnp.where(section == 0, 0, jnp.where(section == 1, first_len, first_len + side_len))
    sec_width = jnp.where(section == 0, first_len, side_len)
    freq_vals = ROPE_BASE ** (-(pair_idx - offset).astype(F32) / sec_width.astype(F32))
    select = jnp.where(section[None, :] == jnp.arange(3)[:, None], freq_vals[None, :], 0.0)
    angles = jnp.sum(positions.astype(F32)[:, :, None] * select[None, :, :], axis=1)
    return jnp.cos(angles), jnp.where((lane % 2 == 0)[None, :], -1.0, 1.0) * jnp.sin(angles)


def norm_stats(x):
    centered = x - jnp.mean(x, axis=-1, keepdims=True)
    inv_std = lax.rsqrt(jnp.mean(centered * centered, axis=-1, keepdims=True) + EPS_NORM)
    return centered * inv_std, inv_std


def to_row(acc):
    return jnp.sum(acc.T, axis=0, keepdims=True)


def lanes_of(row):
    return jnp.broadcast_to(row, (HEAD_DIM, row.shape[1])).T


def head_sum(values):
    out = values[:, :HEAD_DIM]
    for h in range(1, values.shape[1] // HEAD_DIM):
        out = out + values[:, h * HEAD_DIM:(h + 1) * HEAD_DIM]
    return out


class Place:
    def __init__(self, n):
        self.n = n
        self.me = lax.axis_index('tp')
        self.right = lax.rem(self.me + 2, n)
        self.left = lax.rem(self.me + n - 2, n)
        self.far = lax.rem(self.me + n // 2, n)
        self.chip = self.me // 2

    def partner(self, dev):
        return dev + 1 - 2 * lax.rem(dev, 2)

    def barrier(self, devices):
        sem = pltpu.get_barrier_semaphore()
        for dev in devices:
            pl.semaphore_signal(sem, inc=1, device_id={'tp': dev}, device_id_type=MESH_ID)
        pl.semaphore_wait(sem, len(devices))

    def everyone(self):
        return [lax.rem(self.me + d, self.n) for d in range(1, self.n)]

    def near(self):
        return [self.right, self.left, self.partner(self.me)]


class Gather:
    def __init__(self, place, full, rows, send, recv):
        self.at, self.full, self.rows, self.send, self.recv = place, full, rows, send, recv

    def part(self, b, dev, off, count):
        return self.full.at[b, pl.ds(pl.multiple_of(dev * self.rows + off, 16), count)]

    def copy(self, b, dev, off, count, s_idx, r_idx, target):
        ref = self.part(b, dev, off, count)
        return pltpu.make_async_remote_copy(src_ref=ref, dst_ref=ref, send_sem=self.send.at[b, s_idx], recv_sem=self.recv.at[b, r_idx],
                                            device_id={'tp': target}, device_id_type=MESH_ID)

    def start_own(self, b):
        p = self.at
        self.copy(b, p.me, 0, self.rows, 0, 0, p.right).start()
        self.copy(b, p.me, 0, self.rows, 1, 1, p.left).start()
        self.copy(b, p.me, 0, self.rows, 2, 4, p.partner(p.me)).start()

    def take_own(self, b):
        p = self.at
        self.copy(b, p.partner(p.me), 0, self.rows, 2, 4, p.me).wait_recv()

    def take_left(self, b):
        p, half = self.at, self.rows // 2
        self.copy(b, p.left, 0, self.rows, 0, 0, p.me).wait_recv()
        self.copy(b, p.left, 0, half, 3, 2, p.right).start()
        self.copy(b, p.left, 0, self.rows, 5, 5, p.partner(p.me)).start()
        self.copy(b, p.partner(p.left), 0, self.rows, 5, 5, p.me).wait_recv()

    def take_right(self, b):
        p, half = self.at, self.rows // 2
        self.copy(b, p.right, 0, self.rows, 1, 1, p.me).wait_recv()
        self.copy(b, p.right, half, half, 4, 3, p.left).start()
        self.copy(b, p.right, 0, self.rows, 6, 6, p.partner(p.me)).start()
        self.copy(b, p.partner(p.right), 0, self.rows, 6, 6, p.me).wait_recv()

    def take_far(self, b):
        p, half = self.at, self.rows // 2
        self.copy(b, p.far, 0, half, 3, 2, p.me).wait_recv()
        self.copy(b, p.far, 0, half, 7, 7, p.partner(p.me)).start()
        self.copy(b, p.far, half, half, 4, 3, p.me).wait_recv()
        self.copy(b, p.far, half, half, 8, 8, p.partner(p.me)).start()
        self.copy(b, p.partner(p.far), 0, half, 7, 7, p.me).wait_recv()
        self.copy(b, p.partner(p.far), half, half, 8, 8, p.me).wait_recv()

    def finish(self, b):
        p, half = self.at, self.rows // 2
        for s_idx, count in ((0, self.rows), (1, self.rows), (2, self.rows), (3, half), (4, half), (5, self.rows), (6, self.rows), (7, half), (8, half)):
            self.copy(b, p.me, 0, count, s_idx, s_idx, p.me).wait_send()

    def take_item(self, i, nb):
        j = i - nb
        b = jnp.where(i < nb, i, jnp.where(i < 3 * nb, j // 2, i - 3 * nb))
        is_left = (i >= nb) & (i < 3 * nb) & (lax.rem(j + 2 * nb, 2) == 0)
        is_right = (i >= nb) & (i < 3 * nb) & (lax.rem(j + 2 * nb, 2) == 1)
        pl.when(i < nb)(lambda: self.take_own(b))
        pl.when(is_left)(lambda: self.take_left(b))
        pl.when(is_right)(lambda: self.take_right(b))
        pl.when(i >= 3 * nb)(lambda: self.take_far(b))
        chips = self.at.n // 2
        off = jnp.where(i < nb, 0, jnp.where(is_left, chips - 1, jnp.where(is_right, 1, chips // 2)))
        chip = lax.rem(self.at.chip + off, chips)
        return b, pl.multiple_of(chip * (2 * self.rows), 32)


GATHER_SEMS = 9


def chunks_of(width, step):
    return [(c, min(c + step, width)) for c in range(0, width, step)]


def exchange(place, x_ref, slots, send_sems, recv_sems):
    n, me = place.n, place.me
    for d, dev in enumerate(place.everyone()):
        pltpu.make_async_remote_copy(src_ref=x_ref, dst_ref=slots.at[me], send_sem=send_sems.at[d], recv_sem=recv_sems.at[me],
                                     device_id={'tp': dev}, device_id_type=MESH_ID).start()
    slots[me] = x_ref[...]
    for d, dev in enumerate(place.everyone()):
        copy = pltpu.make_async_remote_copy(src_ref=x_ref, dst_ref=slots.at[dev], send_sem=send_sems.at[d], recv_sem=recv_sems.at[dev],
                                            device_id={'tp': dev}, device_id_type=MESH_ID)
        copy.wait_send()
        copy.wait_recv()
    total = slots[0]
    for d in range(1, n):
        total = total + slots[d]
    return total


def gather_qkv_kernel(n, x_ref, dy_ref, m_ref, e_ref, wq_ref, wk_ref, wv_ref, bias_ref,
                      y_full, d_full, q_out, k_out, v_out, ss_ref,
                      w_all, xin, stage, xbuf, zst, vst, sq, ss_row, slots,
                      w_sem, in_sem, st_sem, ld_sem, out_sem, g_send, g_recv, e_send, e_recv):
    nb, rows, dim = x_ref.shape
    cols = wq_ref.shape[1]
    place = Place(n)
    gather = Gather(place, y_full, rows, g_send, g_recv)
    w_copies = [pltpu.make_async_copy(w, w_all.at[:, pl.ds(j * cols, cols)], w_sem.at[j]) for j, w in enumerate((wq_ref, wk_ref, wv_ref))]
    load_x = pltpu.make_async_copy(x_ref, xin, in_sem)
    load_x.start()
    for c in w_copies:
        c.start()
    group = 16

    def mine(full, b):
        return full.at[b, pl.ds(pl.multiple_of(place.me * rows, 16), rows)]

    load_x.wait()
    place.barrier(place.everyone())

    def ln_step(b, _):
        shift = m_ref[0:1] + e_ref[b, 0:1]
        scale_one = 1.0 + (m_ref[1:2] + e_ref[b, 1:2])

        def ln_rows(r, _):
            sl = pl.ds(pl.multiple_of(r * group, group), group)
            x_norm, _ = norm_stats(xin[b, sl].astype(F32))
            stage[b, sl] = (x_norm * scale_one + shift).astype(BF16)
            return 0

        lax.fori_loop(0, rows // group, ln_rows, 0)
        out = pltpu.make_async_copy(stage.at[b], mine(y_full, b), st_sem)
        out.start()
        out.wait()
        gather.start_own(b)
        return 0

    lax.fori_loop(0, nb, ln_step, 0)
    load_dy = pltpu.make_async_copy(dy_ref, xin, in_sem)
    load_dy.start()

    def gate_step(b, _):
        gate = m_ref[2:3] + e_ref[b, 2:3]

        def gate_rows(r, _):
            sl = pl.ds(pl.multiple_of(r * group, group), group)
            stage[b, sl] = (xin[b, sl].astype(F32) * gate).astype(BF16)
            return 0

        lax.fori_loop(0, rows // group, gate_rows, 0)
        out = pltpu.make_async_copy(stage.at[b], mine(d_full, b), st_sem)
        out.start()
        out.wait()
        return 0

    for c in w_copies:
        c.wait()

    def outputs(b, row0, slot):
        dst = pl.ds(row0, 2 * rows)
        return [pltpu.make_async_copy(zst.at[slot, :, pl.ds(0, cols)], q_out.at[b, dst], out_sem.at[slot, 0]),
                pltpu.make_async_copy(zst.at[slot, :, pl.ds(cols, cols)], k_out.at[b, dst], out_sem.at[slot, 1]),
                pltpu.make_async_copy(vst.at[slot], v_out.at[b, dst], out_sem.at[slot, 2])]

    def item(i, _):
        b, row0 = gather.take_item(i, nb)
        slot = lax.rem(i, 2)
        load = pltpu.make_async_copy(y_full.at[b, pl.ds(row0, 2 * rows)], xbuf, ld_sem)
        load.start()

        @pl.when(i == nb)
        def _():
            load_dy.wait()
            lax.fori_loop(0, nb, gate_step, 0)

        @pl.when(i >= 2)
        def _():
            for c in outputs(0, 0, slot):
                c.wait()

        load.wait()
        for lo, hi in chunks_of(3 * cols, 512):
            zst[slot, :, lo:hi] = jnp.dot(xbuf[...], w_all[:, lo:hi], preferred_element_type=F32) + bias_ref[:, lo:hi]
        vst[slot] = zst[slot, :, 2 * cols:].astype(BF16)
        q = zst[slot, :, :cols]
        k = zst[slot, :, cols:2 * cols]
        sq[2 * b, pl.ds(row0, 2 * rows)] = head_sum(q * q)
        sq[2 * b + 1, pl.ds(row0, 2 * rows)] = head_sum(k * k)
        for c in outputs(b, row0, slot):
            c.start()
        return 0

    lax.fori_loop(0, 4 * nb, item, 0)
    ss_row[...] = jnp.zeros_like(ss_row)
    for j in range(2 * nb):
        ss_row[j:j + 1] = to_row(sq[j])
    for slot in range(2):
        for c in outputs(0, 0, slot):
            c.wait()
    for b in range(nb):
        gather.finish(b)
    ss_ref[...] = exchange(place, ss_row, slots, e_send, e_recv)


def gather_qkv_call(n, x_loc, dy_loc, m_block, e_loc, w_q, w_k, w_v, b_q, b_k, b_v):
    nb, rows, dim = x_loc.shape
    cols = w_q.shape[1]
    tokens = rows * n
    shape = jax.ShapeDtypeStruct
    any_spec = pl.BlockSpec(memory_space=pl.ANY)
    vmem = pl.BlockSpec(memory_space=pltpu.VMEM)
    dma = pltpu.SemaphoreType.DMA
    stat_rows = -(-2 * nb // 8) * 8
    return pl.pallas_call(
        functools.partial(gather_qkv_kernel, n), name="gather_qkv",
        out_shape=[shape((nb, tokens, dim), BF16), shape((nb, tokens, dim), BF16), shape((nb, tokens, cols), F32),
                   shape((nb, tokens, cols), F32), shape((nb, tokens, cols), BF16), shape((stat_rows, tokens), F32)],
        in_specs=[any_spec, any_spec, vmem, vmem, any_spec, any_spec, any_spec, vmem],
        out_specs=[any_spec] * 5 + [vmem],
        scratch_shapes=[
            pltpu.VMEM((dim, 3 * cols), BF16), pltpu.VMEM((nb, rows, dim), BF16), pltpu.VMEM((nb, rows, dim), BF16),
            pltpu.VMEM((2 * rows, dim), BF16), pltpu.VMEM((2, 2 * rows, 3 * cols), F32), pltpu.VMEM((2, 2 * rows, cols), BF16),
            pltpu.VMEM((2 * nb, tokens, HEAD_DIM), F32), pltpu.VMEM((stat_rows, tokens), F32), pltpu.VMEM((n, stat_rows, tokens), F32),
            dma((3,)), dma, dma, dma, dma((2, 3)), dma((nb, GATHER_SEMS)), dma((nb, GATHER_SEMS)), dma((n,)), dma((n,))],
        compiler_params=params(collective_id=0, has_side_effects=True),
        cost_estimate=cost(6 * nb * tokens * dim * cols, 6 * dim * cols + 14 * nb * tokens * cols),
    )(x_loc, dy_loc, m_block, e_loc, w_q, w_k, w_v, jnp.concatenate([b_q, b_k, b_v])[None])


def exchange_kernel(n, x_ref, o_ref, slots, send_sems, recv_sems):
    place = Place(n)
    place.barrier(place.everyone())
    o_ref[...] = exchange(place, x_ref, slots, send_sems, recv_sems)


def exchange_call(name, cid, n, x):
    spec = pl.BlockSpec(memory_space=pltpu.VMEM)
    return pl.pallas_call(
        functools.partial(exchange_kernel, n), name=name,
        out_shape=jax.ShapeDtypeStruct(x.shape, x.dtype), in_specs=[spec], out_specs=spec,
        scratch_shapes=[pltpu.VMEM((n,) + x.shape, x.dtype), pltpu.SemaphoreType.DMA((n,)), pltpu.SemaphoreType.DMA((n,))],
        compiler_params=pltpu.CompilerParams(collective_id=cid, has_side_effects=True),
        cost_estimate=cost(4_000_000_000, x.size * 4 * n),
    )(x)


def swap_pairs(x):
    lane = lax.broadcasted_iota(jnp.int32, x.shape, 1)
    return jnp.where(lane % 2 == 0, pltpu.roll(x, HEAD_DIM - 1, 1), pltpu.roll(x, 1, 1))


def rotate(x, cos, sin):
    return x * cos + swap_pairs(x) * sin


def softmax_block(s):
    c = HEAD_DIM ** -0.5 * LOG2E
    top = jnp.max(s, axis=1, keepdims=True)
    p = jnp.exp2(s * c - top * c)
    return p * (1.0 / jnp.sum(p, axis=1, keepdims=True))


def gather_attn_kernel(n, nb, heads, dim, q_ref, k_ref, v_ref, gq_ref, gk_ref, cos_ref, sin_ref, ss_ref, wo_ref, d_in,
                       d_full, o_out, da_out, dwo_out,
                       inv_q, inv_k, o_all, wo, xbuf, ast, turned, dbuf, acc, wst,
                       w_sem, ld_sem, out_sem, c_sem, o_sem, g_send, g_recv):
    step = pl.program_id(0)
    tokens = q_ref.shape[1]
    rows = tokens // n
    cols = heads * HEAD_DIM
    blk = min(256, tokens)
    place = Place(n)
    gather = Gather(place, d_full, rows, g_send, g_recv)
    load_w = pltpu.make_async_copy(wo_ref, wo, w_sem)

    @pl.when(step == 0)
    def _():
        load_w.start()
        place.barrier(place.near())

        def own(b, _):
            gather.start_own(b)
            return 0

        lax.fori_loop(0, nb, own, 0)

    @pl.when(step < nb * heads)
    def _():
        b = step // heads
        h = lax.rem(step, heads)

        @pl.when(h == 0)
        def _():
            inv_q[...] = lanes_of(lax.rsqrt(ss_ref[pl.ds(2 * b, 1)] / dim + EPS_NORM))
            inv_k[...] = lanes_of(lax.rsqrt(ss_ref[pl.ds(2 * b + 1, 1)] / dim + EPS_NORM))

        cos, sin = cos_ref[...], sin_ref[...]
        q_rot = rotate(q_ref[0] * inv_q[...] * gq_ref[...], cos, sin).astype(BF16)
        k_rot = rotate(k_ref[0] * inv_k[...] * gk_ref[...], cos, sin).astype(BF16)
        v = v_ref[0]
        lanes = pl.ds(pl.multiple_of(h * HEAD_DIM, HEAD_DIM), HEAD_DIM)
        for i in range(tokens // blk):
            s = lax.dot_general(q_rot[i * blk:(i + 1) * blk], k_rot, NT, preferred_element_type=F32)
            p = softmax_block(s).astype(BF16)
            o_all[b, i * blk:(i + 1) * blk, lanes] = jnp.dot(p, v, preferred_element_type=F32).astype(BF16)

    @pl.when(step == nb * heads)
    def _():
        o_copy = pltpu.make_async_copy(o_all, o_out, o_sem)
        o_copy.start()
        load_w.wait()
        bn = min(512, dim)
        n_chunks = dim // bn

        def outputs(b, row0, slot):
            return pltpu.make_async_copy(ast.at[slot], da_out.at[b, pl.ds(row0, 2 * rows)], out_sem.at[slot])

        def chunk(b, c):
            slot = lax.rem(c, 2)
            return pltpu.make_async_copy(d_full.at[b, :, pl.ds(pl.multiple_of(c * bn, bn), bn)], dbuf.at[slot], c_sem.at[slot])

        def item(i, _):
            b, row0 = gather.take_item(i, nb)
            slot = lax.rem(i, 2)
            load = pltpu.make_async_copy(d_full.at[b, pl.ds(row0, 2 * rows)], xbuf, ld_sem)
            load.start()

            @pl.when(i >= 2)
            def _():
                outputs(0, 0, slot).wait()

            load.wait()
            ast[slot] = lax.dot_general(xbuf[...], wo[...], NT, preferred_element_type=F32).astype(BF16)
            outputs(b, row0, slot).start()

            @pl.when(i >= 3 * nb)
            def _():
                chunk(b, 0).start()
                turned[...] = o_all[b].T

                def d_wo(c, _):
                    @pl.when(c + 1 < n_chunks)
                    def _():
                        chunk(b, c + 1).start()

                    chunk(b, c).wait()
                    sl = pl.ds(pl.multiple_of(c * bn, bn), bn)
                    part = jnp.dot(turned[...], dbuf[lax.rem(c, 2)], preferred_element_type=F32)

                    @pl.when(b == 0)
                    def _():
                        acc[:, sl] = part

                    @pl.when(b > 0)
                    def _():
                        acc[:, sl] += part

                    return 0

                lax.fori_loop(0, n_chunks, d_wo, 0)

            return 0

        lax.fori_loop(0, 4 * nb, item, 0)

        def flush(c, _):
            sl = pl.ds(pl.multiple_of(c * bn, bn), bn)
            slot = lax.rem(c, 2)

            @pl.when(c >= 2)
            def _():
                pltpu.make_async_copy(wst.at[slot], dwo_out.at[:, sl], c_sem.at[slot]).wait()

            wst[slot] = acc[:, sl].astype(BF16)
            pltpu.make_async_copy(wst.at[slot], dwo_out.at[:, sl], c_sem.at[slot]).start()
            return 0

        lax.fori_loop(0, n_chunks, flush, 0)
        for slot in range(min(2, n_chunks)):
            pltpu.make_async_copy(wst.at[slot], dwo_out.at[:, pl.ds(0, bn)], c_sem.at[slot]).wait()
        for slot in range(2):
            outputs(0, 0, slot).wait()
        o_copy.wait()
        for b in range(nb):
            gather.finish(b)


def gather_attn_call(n, q, k, v, g_q, g_k, cos_tab, sin_tab, ss, w_o, d_full):
    nb, tokens, cols = q.shape
    dim = w_o.shape[1]
    heads = cols // HEAD_DIM
    rows = tokens // n
    last = nb * heads - 1
    bn = min(512, dim)
    shape = jax.ShapeDtypeStruct
    dma = pltpu.SemaphoreType.DMA
    any_spec = pl.BlockSpec(memory_space=pl.ANY)

    def head_of(i):
        i = jnp.minimum(i, last)
        return i // heads, i % heads

    blk = pl.BlockSpec((1, tokens, HEAD_DIM), lambda i: (head_of(i)[0], 0, head_of(i)[1]))
    vec = pl.BlockSpec((1, HEAD_DIM), lambda i: (0, head_of(i)[1]))
    tab = pl.BlockSpec((tokens, HEAD_DIM), lambda i: (0, 0))
    return pl.pallas_call(
        functools.partial(gather_attn_kernel, n, nb, heads, dim), name="gather_attn", grid=(nb * heads + 1,),
        out_shape=[shape(d_full.shape, BF16), shape((nb, tokens, cols), BF16), shape((nb, tokens, cols), BF16), shape((cols, dim), BF16)],
        in_specs=[blk, blk, blk, vec, vec, tab, tab, pl.BlockSpec(ss.shape, lambda i: (0, 0)), any_spec, any_spec],
        out_specs=[any_spec] * 4,
        scratch_shapes=[
            pltpu.VMEM((tokens, HEAD_DIM), F32), pltpu.VMEM((tokens, HEAD_DIM), F32), pltpu.VMEM((nb, tokens, cols), BF16),
            pltpu.VMEM((cols, dim), BF16), pltpu.VMEM((2 * rows, dim), BF16), pltpu.VMEM((2, 2 * rows, cols), BF16),
            pltpu.VMEM((cols, tokens), BF16), pltpu.VMEM((2, tokens, bn), BF16), pltpu.VMEM((cols, dim), F32),
            pltpu.VMEM((2, cols, bn), BF16),
            dma, dma, dma((2,)), dma((2,)), dma, dma((nb, GATHER_SEMS)), dma((nb, GATHER_SEMS))],
        input_output_aliases={9: 0},
        compiler_params=params("arbitrary", collective_id=1, has_side_effects=True),
        cost_estimate=cost(4 * nb * tokens * dim * cols + 4 * nb * tokens * tokens * cols, 8 * nb * tokens * dim),
    )(q, k, v, g_q[None], g_k[None], cos_tab, sin_tab, ss, w_o, d_full)


def attn_bwd_kernel(heads, dim, q_ref, k_ref, v_ref, do_ref, gq_ref, gk_ref, cos_ref, sin_ref, ss_ref,
                    dv_ref, dqs_ref, dks_ref, dgq_ref, dgk_ref, st_ref,
                    inv_q, inv_k, acc_q, acc_k, p_all, ds_all, dq_all):
    b, head = pl.program_id(0), pl.program_id(1)
    tokens = q_ref.shape[1]
    blk = min(256, tokens)
    scale = HEAD_DIM ** -0.5

    @pl.when((head == 0) & (b == 0))
    def _():
        st_ref[...] = jnp.zeros_like(st_ref)

    @pl.when(head == 0)
    def _():
        inv_q[...] = lanes_of(lax.rsqrt(ss_ref[pl.ds(2 * b, 1)] / dim + EPS_NORM))
        inv_k[...] = lanes_of(lax.rsqrt(ss_ref[pl.ds(2 * b + 1, 1)] / dim + EPS_NORM))
        acc_q[...] = jnp.zeros_like(acc_q)
        acc_k[...] = jnp.zeros_like(acc_k)

    cos, sin = cos_ref[...], sin_ref[...]
    q_rot = rotate(q_ref[0] * inv_q[...] * gq_ref[...], cos, sin).astype(BF16)
    k_rot = rotate(k_ref[0] * inv_k[...] * gk_ref[...], cos, sin).astype(BF16)
    v = v_ref[0]
    do = do_ref[0]
    for i in range(tokens // blk):
        sl = slice(i * blk, (i + 1) * blk)
        p = softmax_block(lax.dot_general(q_rot[sl], k_rot, NT, preferred_element_type=F32))
        p_all[sl] = p.astype(BF16)
        dp = lax.dot_general(do[sl], v, NT, preferred_element_type=F32)
        delta = jnp.sum(dp * p, axis=1, keepdims=True)
        ds = (p * (dp - delta)).astype(BF16)
        ds_all[sl] = ds
        dq_all[sl] = jnp.dot(ds, k_rot, preferred_element_type=F32) * scale
    do_t = do.astype(F32).T.astype(BF16)
    q_t = q_rot.astype(F32).T.astype(BF16)
    dv_ref[0] = jnp.dot(do_t, p_all[...], preferred_element_type=F32).T.astype(BF16)
    dk_rot = (jnp.dot(q_t, ds_all[...], preferred_element_type=F32) * scale).T.astype(BF16).astype(F32)
    dq_rot = dq_all[...].astype(BF16).astype(F32)
    dq_hat = rotate(dq_rot, cos, -sin)
    dk_hat = rotate(dk_rot, cos, -sin)
    q_hat = q_ref[0] * inv_q[...]
    k_hat = k_ref[0] * inv_k[...]
    dgq_ref[0] = jnp.sum(dq_hat * q_hat, axis=0, keepdims=True)
    dgk_ref[0] = jnp.sum(dk_hat * k_hat, axis=0, keepdims=True)
    dq_s = dq_hat * gq_ref[...]
    dk_s = dk_hat * gk_ref[...]
    dqs_ref[0] = dq_s
    dks_ref[0] = dk_s
    acc_q[...] += dq_s * q_hat
    acc_k[...] += dk_s * k_hat

    @pl.when(head == heads - 1)
    def _():
        st_ref[pl.ds(2 * b, 1)] = to_row(acc_q[...])
        st_ref[pl.ds(2 * b + 1, 1)] = to_row(acc_k[...])


def attn_bwd_call(dim, q, k, v, d_attn, g_q, g_k, cos_tab, sin_tab, ss):
    nb, tokens, cols = q.shape
    heads = cols // HEAD_DIM
    blk = pl.BlockSpec((1, tokens, HEAD_DIM), lambda b, h: (b, 0, h))
    vec = pl.BlockSpec((1, HEAD_DIM), lambda b, h: (0, h))
    out_vec = pl.BlockSpec((1, 1, HEAD_DIM), lambda b, h: (b, 0, h))
    tab = pl.BlockSpec((tokens, HEAD_DIM), lambda b, h: (0, 0))
    small = pl.BlockSpec(ss.shape, lambda b, h: (0, 0))
    shape = jax.ShapeDtypeStruct
    whole = (nb, tokens, cols)
    return pl.pallas_call(
        functools.partial(attn_bwd_kernel, heads, dim), name="attn_bwd", grid=(nb, heads),
        out_shape=[shape(whole, BF16), shape(whole, F32), shape(whole, F32),
                   shape((nb, 1, cols), F32), shape((nb, 1, cols), F32), shape(ss.shape, F32)],
        in_specs=[blk, blk, blk, blk, vec, vec, tab, tab, small],
        out_specs=[blk, blk, blk, out_vec, out_vec, small],
        scratch_shapes=[pltpu.VMEM((tokens, HEAD_DIM), F32)] * 4
        + [pltpu.VMEM((tokens, tokens), BF16)] * 2 + [pltpu.VMEM((tokens, HEAD_DIM), F32)],
        compiler_params=params("arbitrary", "arbitrary"),
        cost_estimate=cost(36 * nb * tokens * tokens * cols, 24 * nb * tokens * cols),
    )(q, k, v, d_attn, g_q[None], g_k[None], cos_tab, sin_tab, ss)


def nn_kernel(a_ref, w_ref, o_ref):
    o_ref[...] = jnp.dot(a_ref[...], w_ref[...], preferred_element_type=F32).astype(BF16)


def nn_call(name, a, w):
    rows, depth = a.shape
    width = w.shape[1]
    bn = min(512, width)
    return pl.pallas_call(
        nn_kernel, name=name, grid=(width // bn,),
        out_shape=jax.ShapeDtypeStruct((rows, width), BF16),
        in_specs=[pl.BlockSpec((rows, depth), lambda i: (0, 0)), pl.BlockSpec((depth, bn), lambda i: (0, i))],
        out_specs=pl.BlockSpec((rows, bn), lambda i: (0, i)),
        compiler_params=params("arbitrary"),
        cost_estimate=cost(2 * rows * depth * width, 2 * (rows * depth + depth * width + rows * width)),
    )(a, w)


def dy_kernel(dim, dqs_ref, dks_ref, q_ref, k_ref, dv_ref, ss_ref, st_ref, wq_ref, wk_ref, wv_ref, o_ref, g_ref):
    b = pl.program_id(0)
    cols = dqs_ref.shape[2]

    @pl.when(pl.program_id(1) == 0)
    def _():
        for j, (d_ref, x_ref) in enumerate(((dqs_ref, q_ref), (dks_ref, k_ref))):
            inv_l = lanes_of(lax.rsqrt(ss_ref[pl.ds(2 * b + j, 1)] / dim + EPS_NORM))
            st_l = lanes_of(st_ref[pl.ds(2 * b + j, 1)] / dim)
            for h in range(cols // HEAD_DIM):
                sl = slice(h * HEAD_DIM, (h + 1) * HEAD_DIM)
                grad = inv_l * (d_ref[0, :, sl] - (x_ref[0, :, sl] * inv_l) * st_l)
                g_ref[0, :, j * cols + h * HEAD_DIM:j * cols + (h + 1) * HEAD_DIM] = grad.astype(BF16)
        g_ref[0, :, 2 * cols:] = dv_ref[0]

    w_all = jnp.concatenate([wq_ref[...], wk_ref[...], wv_ref[...]], axis=1)
    o_ref[0] = lax.dot_general(g_ref[0], w_all, NT, preferred_element_type=F32).astype(BF16)


def dy_call(dqs, dks, q, k, dv, ss, st, w_q, w_k, w_v):
    nb, rows, cols = dqs.shape
    dim = w_q.shape[0]
    bn = min(512, dim)
    full = pl.BlockSpec((1, rows, cols), lambda b, i: (b, 0, 0))
    small = pl.BlockSpec(ss.shape, lambda b, i: (0, 0))
    w_spec = pl.BlockSpec((bn, cols), lambda b, i: (i, 0))
    return pl.pallas_call(
        functools.partial(dy_kernel, dim), name="dy", grid=(nb, dim // bn),
        out_shape=[jax.ShapeDtypeStruct((nb, rows, dim), BF16), jax.ShapeDtypeStruct((nb, rows, 3 * cols), BF16)],
        in_specs=[full, full, full, full, full, small, small, w_spec, w_spec, w_spec],
        out_specs=[pl.BlockSpec((1, rows, bn), lambda b, i: (b, 0, i)), pl.BlockSpec((1, rows, 3 * cols), lambda b, i: (b, 0, 0))],
        compiler_params=params("arbitrary", "arbitrary"),
        cost_estimate=cost(6 * nb * rows * dim * cols, nb * (2 * rows * dim + 6 * dim * cols + 20 * rows * cols)),
    )(dqs, dks, q, k, dv, ss, st, w_q, w_k, w_v)


def dw_kernel(y_ref, g_ref, *outs):
    acc = lax.dot_general(y_ref[...], g_ref[...], TN, preferred_element_type=F32)
    cols = outs[0].shape[1]
    for j, o_ref in enumerate(outs):
        o_ref[...] = acc[:, j * cols:(j + 1) * cols].astype(BF16)


def dw_call(y, g):
    rows, dim = y.shape
    cols = g.shape[1] // 3
    bm = min(512, dim)
    return pl.pallas_call(
        dw_kernel, name="dw", grid=(dim // bm,),
        out_shape=[jax.ShapeDtypeStruct((dim, cols), BF16)] * 3,
        in_specs=[pl.BlockSpec((rows, bm), lambda i: (0, i)), pl.BlockSpec((rows, 3 * cols), lambda i: (0, 0))],
        out_specs=[pl.BlockSpec((bm, cols), lambda i: (i, 0))] * 3,
        compiler_params=params("arbitrary"),
        cost_estimate=cost(6 * rows * dim * cols, 2 * rows * (dim + 3 * cols) + 6 * dim * cols),
    )(y, g)


def out_kernel(x_ref, dy_ref, pr_ref, m_ref, e_ref, bo_ref, o_ref, dg_ref):
    gate = m_ref[2:3] + e_ref[0, 2:3]
    proj = pr_ref[0].astype(F32) + bo_ref[...]
    o_ref[0] = (x_ref[0].astype(F32) + gate * proj).astype(BF16)
    dg_ref[0] = jnp.sum(dy_ref[0].astype(F32) * proj, axis=0, keepdims=True)


def dx_kernel(x_ref, dy_ref, g_ref, m_ref, e_ref, o_ref, dm_ref):
    scale_one = 1.0 + (m_ref[1:2] + e_ref[0, 1:2])
    x_norm, inv_std = norm_stats(x_ref[0].astype(F32))
    d_y = g_ref[0].astype(F32)
    d_norm = d_y * scale_one
    d_x = dy_ref[0].astype(F32) + inv_std * (
        d_norm - jnp.mean(d_norm, axis=-1, keepdims=True) - x_norm * jnp.mean(d_norm * x_norm, axis=-1, keepdims=True))
    o_ref[0] = d_x.astype(BF16)
    dm_ref[0, 0:1] = jnp.sum(d_y, axis=0, keepdims=True)
    dm_ref[0, 1:2] = jnp.sum(d_y * x_norm, axis=0, keepdims=True)


def token_call(kernel, name, n_sums, x_loc, dy_loc, piece, m_block, e_loc, extra):
    nb, rows, dim = x_loc.shape
    row = pl.BlockSpec((1, rows, dim), lambda i: (i, 0, 0))
    specs = [row, row, row, pl.BlockSpec((3, dim), lambda i: (0, 0)),
             pl.BlockSpec((1, 3, dim), lambda i: (i, 0, 0))] + [pl.BlockSpec((1, dim), lambda i: (0, 0))] * len(extra)
    return pl.pallas_call(
        kernel, name=name, grid=(nb,),
        out_shape=[jax.ShapeDtypeStruct(x_loc.shape, BF16), jax.ShapeDtypeStruct((nb, n_sums, dim), F32)],
        in_specs=specs, out_specs=[row, pl.BlockSpec((1, n_sums, dim), lambda i: (i, 0, 0))],
        compiler_params=params("arbitrary"),
        cost_estimate=cost(nb * rows * dim * 20, nb * rows * dim * 8),
    )(x_loc, dy_loc, piece, m_block, e_loc, *extra)


def solution(mesh):
    tp_size = mesh.shape['tp']

    def device_step(x_loc, e_loc, m_block, w_q, b_q, w_k, b_k, w_v, b_v, w_o, b_o, g_q, g_k, pos_part, dy_loc):
        nb, _, dim = x_loc.shape
        cols = w_q.shape[1]
        cos_tab, sin_tab = rope_tables(pos_part)
        y_full, d_own, q, k, v, ss = gather_qkv_call(tp_size, x_loc, dy_loc, m_block, e_loc, w_q, w_k, w_v, b_q, b_k, b_v)
        d_full, o, d_attn, d_wo = gather_attn_call(tp_size, q, k, v, g_q, g_k, cos_tab, sin_tab, ss, w_o, d_own)
        rows_all = nb * q.shape[1]
        part = nn_call("proj", o.reshape(rows_all, cols), w_o).reshape(d_full.shape)
        proj = lax.psum_scatter(part, 'tp', scatter_dimension=1, tiled=True)
        d_attn, part = lax.optimization_barrier((d_attn, part))
        dv, dqs, dks, d_gq, d_gk, st = attn_bwd_call(dim, q, k, v, d_attn, g_q, g_k, cos_tab, sin_tab, ss)
        st = exchange_call("stat", 2, tp_size, st)
        dy_part, grad = dy_call(dqs, dks, q, k, dv, ss, st, w_q, w_k, w_v)
        dy_part, proj = lax.optimization_barrier((dy_part, proj))
        d_y = lax.psum_scatter(dy_part, 'tp', scatter_dimension=1, tiled=True)
        grad, dy_part = lax.optimization_barrier((grad, dy_part))
        d_wq, d_wk, d_wv = dw_call(y_full.reshape(rows_all, dim), grad.reshape(rows_all, 3 * cols))
        x_out, d_gate = token_call(out_kernel, "xout", 1, x_loc, dy_loc, proj, m_block, e_loc, [b_o[None]])
        d_x, d_mod = token_call(dx_kernel, "dx", 2, x_loc, dy_loc, d_y, m_block, e_loc, [])
        sums = jnp.concatenate([d_mod, d_gate], axis=1)
        d_e = exchange_call("dmod", 3, tp_size, sums.reshape(8, -1)).reshape(nb, 3, dim)
        return (x_out, d_x, d_e, jnp.sum(d_e, axis=0), d_wq, d_wk, d_wv, d_wo,
                jnp.sum(d_gq, axis=(0, 1)), jnp.sum(d_gk, axis=(0, 1)))

    in_specs = (P('dp', 'tp', None), P('dp', None, None), P(None, None), P(None, 'tp'), P('tp'), P(None, 'tp'), P('tp'),
                P(None, 'tp'), P('tp'), P('tp', None), P(None), P('tp'), P('tp'), P('dp', None), P('dp', 'tp', None))
    out_specs = (P('dp', 'tp', None), P('dp', 'tp', None), P('dp', None, None), P('dp', None), P('dp', 'tp'), P('dp', 'tp'),
                 P('dp', 'tp'), P(('dp', 'tp'), None), P(('dp', 'tp')), P(('dp', 'tp')))
    return jax.shard_map(device_step, mesh=mesh, in_specs=in_specs, out_specs=out_specs, check_vma=False)
```

time: 1020 us -> 611 us (0.60)
  Pallas kernels: 0 us -> 519 us
  matrix products: 423 us -> 0 us
  waiting for transfers between devices: 354 us -> 57.7 us
  other arithmetic: 104 us -> 6.94 us
  local copies, waits for them, and re-layouts: 68.3 us -> 11.6 us
  blocking collectives: 46 us -> 0 us
    pallas_call x0 -> x10, Pallas kernels: none -> 519 us  [the longest x1 140 us: gather_attn_call(): pl.pallas_call(functools.partial(gather_attn_kernel, n, nb, heads, dim),...]
    dot_general x17 -> x0, matrix products: 403 us -> none  [the longest x3 46.5 us: attend(): jnp.einsum('bhqk,bkhd->bqhd', attn_probs, v_heads, preferred_element_type...]
    all_gather x2 -> x0, waiting for transfers between devices: 194 us -> none  [the longest x1 109 us: device_step(): lax.all_gather(y_loc, 'tp', axis=1, tiled=True).reshape(rows_all, model_dim)]
    reduce_scatter x2, waiting for transfers between devices: 131 us -> 57.5 us  [the longest x1 57.5 us: device_step(): d_y = lax.psum_scatter(dy_part, 'tp', scatter_dimension=1, tiled=True)]
    psum x2 -> x0, blocking collectives: 46 us -> none  [the longest x1 23.9 us: device_step(): lax.psum(jnp.stack([jnp.sum(dq_scaled * q_hat, axis=-1), jnp.sum(dk_scale...]
    another operation x8 -> x0, other arithmetic: 29.7 us -> none  [the longest x4 21 us: rope_rotate(): jnp.stack([even_part * cos_part - odd_part * sin_part, even_part * sin_pa...]
    psum x1 -> x0, waiting for transfers between devices: 29 us -> none  [device_step(): lax.psum(jnp.stack([jnp.sum(d_y, axis=1), jnp.sum(d_y * x_norm, axis=1),...]
    reduce_sum x8 -> x4, other arithmetic: 29.8 us -> 2.29 us  [the longest x1 0.71 us: device_step(): jnp.sum(d_e, axis=0)]
  transfers between devices with their start and end apart: 5 -> 2, of which waited for: 5 -> 1; matrix products, arithmetic and copies ran while one was open for 17% -> 0% of each run, Pallas kernels for 0% -> 32%
where the time goes in v2:
time: 611 us; the launch traced here: 609 us
  Pallas kernels  519 us (85%)
  waiting for transfers between devices  57.7 us (9%)
  between operations  14.2 us (2%)
  local copies, waits for them, and re-layouts  11.6 us (2%)
  other arithmetic  6.94 us (1%)
    pallas_call x1, Pallas kernels, gather_attn_call(): pl.pallas_call(functools.partial(gather_attn_kernel, n, nb, heads, dim),...  140 us
    pallas_call x1, Pallas kernels, gather_qkv_call(): pl.pallas_call(functools.partial(gather_qkv_kernel, n), name='gather_qkv'...  126 us
    pallas_call x1, Pallas kernels, dy_call(): pl.pallas_call(functools.partial(dy_kernel, dim), name='dy', grid=(nb, di...  72.5 us
    reduce_scatter x1, waiting for transfers between devices, device_step(): d_y = lax.psum_scatter(dy_part, 'tp', scatter_dimension=1, tiled=True)  57.5 us
    pallas_call x1, Pallas kernels, dw_call(): pl.pallas_call(dw_kernel, name='dw', grid=(dim // bm,), out_shape=[jax.Sh...  55.9 us
    pallas_call x1, Pallas kernels, attn_bwd_call(): pl.pallas_call(functools.partial(attn_bwd_kernel, heads, dim), name='attn...  51.7 us
    pallas_call x2, Pallas kernels, exchange_call(): pl.pallas_call(functools.partial(exchange_kernel, n), name=name, out_shap...  31.6 us
    pallas_call x1, Pallas kernels, nn_call(): pl.pallas_call(nn_kernel, name=name, grid=(width // bn,), out_shape=jax.S...  23.9 us
  transfers between devices with their start and end apart: 2, of which 1 were waited for; matrix products, arithmetic and copies ran while one was open for 0% of the time, Pallas kernels for 32%

profile of v2, /device:TPU:81, one launch (start us, length us, event | category | flops | bytes accessed | tf_op | source)
XLA Modules:
  0.0 609.4 jit_solution(17315004588279145993)
XLA Ops:
  7.2 0.1 reduce-scatter.3.cloned.1.call-start
  7.3 1.3 broadcast_in_dim.51.gq_ref
  8.6 1.3 broadcast_in_dim.52.gk_ref
  9.8 0.7 pad_maximum_fusion.1
  10.6 0.6 broadcast_in_dim.50.bias_ref
  11.2 0.7 convert_element_type.37
  11.9 0.4 multiply_reduce_fusion
  12.3 2.2 sine_multiply_fusion
  14.4 126.4 %gather_qkv.1 = (bf16[3,768,5120]{2,1,0:T(8,128)(2,1)}, bf16[3,768,5120]{2,1,0:T(8,128)(2,1)}, f32[3,768,640]{2,1,0:T(8,128)}, f32[3,768,640]{2,1,0:T(8,128)}, b...) custom-call(bf16[3,96,5120]{2,1,0:T(8,128)(2,1)} %x_ref.5, bf16[3,96,5120]{2,1,0:T(8,128)(2,1)} %dy_ref.5, f32[3,5120]{1,0:T(4,128)} %m_ref.5, ...), custom_call_target="tpu_custom_call" | custom-call | flops 45298483200 | bytes 40304640 | tf_op jit(solution)/shard_map/gather_qkv/pallas_call | solution.py:294
  140.8 140.4 %gather_attn.1 = (bf16[3,768,5120]{2,1,0:T(8,128)(2,1)}, bf16[3,768,640]{2,1,0:T(8,128)(2,1)}, bf16[3,768,640]{2,1,0:T(8,128)(2,1)}, bf16[640,5120]{1,0:T(8,128)(2,1)}) custom-call(f32[3,768,640]{2,1,0:T(8,128)} %get-tuple-element.38.q_ref, f32[3,768,640]{2,1,0:T(8,128)} %get-tuple-element.39.k_ref, ...), custom_call_target="tpu_custom_call", output_to_operand_aliasing={{0}: (9, {})} | custom-call | flops 34728837120 | bytes 94371840 | tf_op jit(solution)/shard_map/gather_attn/pallas_call | solution.py:486
  281.2 23.9 %proj.1 = bf16[2304,5120]{1,0:T(8,128)(2,1)} custom-call(bf16[2304,640]{1,0:T(8,128)(2,1)} %bitcast.9, bf16[640,5120]{1,0:T(8,128)(2,1)} %w_ref.1), custom_call_target="tpu_custom_call" | custom-call | flops 15099494400 | bytes 33095680 | tf_op jit(solution)/shard_map/proj/pallas_call | solution.py:591
  305.1 0.1 reduce-scatter.3.cloned.1.call-update
  305.2 0.1 reduce-scatter.5.cloned.1.call-start
  305.2 51.7 %attn_bwd.1 = (bf16[3,768,640]{2,1,0:T(8,128)(2,1)}, f32[3,768,640]{2,1,0:T(8,128)}, f32[3,768,640]{2,1,0:T(8,128)}, f32[3,1,640]{2,1,0:T(1,128)}, f32[3,1,640]{2,1,0:T(1,128)}, /*index=5*/f32[8,768]{1,0:T(8,128)}) custom-call(f32[3,768,640]{2,1,0:T(8,128)} %get-tuple-element.38.q_ref, f32[3,768,640]{2,1,0:T(8,128)} %get-tuple-element.39.k_ref, ...), custom_call_target="tpu_custom_call" | custom-call | flops 40768634880 | bytes 35389440 | tf_op jit(solution)/shard_map/attn_bwd/pallas_call | solution.py:570
  357.0 8.9 %stat.1.st_ref = f32[8,768]{1,0:T(8,128)} custom-call(f32[8,768]{1,0:T(8,128)} %get-tuple-element.49.x_ref), custom_call_target="tpu_custom_call" | custom-call | flops 4000000000 | bytes 196608 | tf_op jit(solution)/shard_map/stat/pallas_call | solution.py:318
  365.9 72.5 %dy.1 = (bf16[3,768,5120]{2,1,0:T(8,128)(2,1)}, bf16[3,768,1920]{2,1,0:T(8,128)(2,1)}) custom-call(f32[3,768,640]{2,1,0:T(8,128)} %get-tuple-element.46.dqs_ref, f32[3,768,640]{2,1,0:T(8,128)} %get-tuple-element.47.dks_ref, f32[3,768,640]{2,1,0:T(8,128)} %get-tuple-element.38.q_ref, f32[3,768,640]{2,1,0:T(8,128)} %get-tuple-element.39.k_ref, ...), custom_call_target="tpu_custom_call" | custom-call | flops 45298483200 | bytes 112066560 | tf_op jit(solution)/shard_map/dy/pallas_call | solution.py:627
  438.4 0.0 reduce-scatter.3.cloned.1.call-done.pr_ref
  438.4 0.0 copy-start.3
  438.4 0.0 copy-start.2
  438.4 0.1 reduce-scatter.5.cloned.1.call-update
  438.5 0.6 copy-done.3
  439.1 0.6 reduce_sum.38
  439.7 0.0 copy-done.2
  439.7 0.6 reduce_sum.39
  440.3 6.7 %xout.1 = (bf16[3,96,5120]{2,1,0:T(8,128)(2,1)}, f32[3,1,5120]{2,1,0:T(1,128)}) custom-call(bf16[3,96,5120]{2,1,0:T(8,128)(2,1)} %x_ref.5, bf16[3,96,5120]{2,1,0:T(8,128)(2,1)} %dy_ref.5, bf16[3,96,5120]{2,1,0:T(8,128)(2,1)} %reduce-scatter.3.cloned.1.call-done.pr_ref, f32[3,5120]{1,0:T(4,128)} %m_ref.5, f32[3,3,5120]{2,1,0:T(4,128)} %e_ref.5, f32[1,5120]{1,0:T(1,128)} %bitcast.6), custom_call_target="tpu_custom_call" | custom-call | flops 29491200 | bytes 11796480 | tf_op jit(solution)/shard_map/xout/pallas_call | solution.py:682
  447.0 55.9 %dw.1 = (bf16[5120,640]{1,0:T(8,128)(2,1)}, bf16[5120,640]{1,0:T(8,128)(2,1)}, bf16[5120,640]{1,0:T(8,128)(2,1)}) custom-call(bf16[2304,5120]{1,0:T(8,128)(2,1)} %bitcast.7, bf16[2304,1920]{1,0:T(8,128)(2,1)} %bitcast.8), custom_call_target="tpu_custom_call" | custom-call | flops 45298483200 | bytes 52101120 | tf_op jit(solution)/shard_map/dw/pallas_call | solution.py:648
  502.9 0.0 copy-start.1
  502.9 57.5 %reduce-scatter.5.cloned.1.call-done.g_ref = bf16[3,96,5120]{2,1,0:T(8,128)(2,1)} async-done(((bf16[3,768,5120]{2,1,0:T(8,128)(2,1)}), bf16[3,96,5120]{2,1,0:T(8,128)(2,1)}) %reduce-scatter.5.cloned.1.call-update) | async-done | bytes 2949136 | tf_op jit(solution)/shard_map/reduce_scatter | solution.py:708
  560.5 9.8 %dx.1 = (bf16[3,96,5120]{2,1,0:T(8,128)(2,1)}, f32[3,2,5120]{2,1,0:T(2,128)}) custom-call(bf16[3,96,5120]{2,1,0:T(8,128)(2,1)} %x_ref.5, bf16[3,96,5120]{2,1,0:T(8,128)(2,1)} %dy_ref.5, bf16[3,96,5120]{2,1,0:T(8,128)(2,1)} %reduce-scatter.5.cloned.1.call-done.g_ref, f32[3,5120]{1,0:T(4,128)} %m_ref.5, f32[3,3,5120]{2,1,0:T(4,128)} %e_ref.5), custom_call_target="tpu_custom_call" | custom-call | flops 29491200 | bytes 11796480 | tf_op jit(solution)/shard_map/dx/pallas_call | solution.py:682
  570.2 0.0 copy-done.1
  570.2 1.0 pad_maximum_fusion
  571.2 0.8 reshape.119.x_ref
  572.0 22.8 %dmod.1 = f32[8,5760]{1,0:T(8,128)} custom-call(f32[8,5760]{1,0:T(8,128)} %reshape.119.x_ref), custom_call_target="tpu_custom_call" | custom-call | flops 4000000000 | bytes 1474560 | tf_op jit(solution)/shard_map/dmod/pallas_call | solution.py:318
  594.8 1.0 reshape.120
  595.8 0.0 copy-start
  595.8 0.7 reduce_sum.37
  596.5 6.1 copy.29
  602.6 0.0 copy-done
  (4 shorter events, 0.0 us)
Async XLA Ops:
  7.2 431.2 %reduce-scatter.3.cloned.1.call-start = ((), (), s32[]{:S(2)}) async-start(), calls=%async_computation.2 | async-start | bytes 26542080 | tf_op jit(solution)/shard_map/reduce_scatter | solution.py:702
  305.2 255.3 %reduce-scatter.5.cloned.1.call-start = ((), (), s32[]{:S(2)}) async-start(), calls=%async_computation.3 | async-start | bytes 26542080 | tf_op jit(solution)/shard_map/reduce_scatter | solution.py:708
  438.4 0.7 copy-start.3
  438.4 1.3 copy-start.2
  502.9 67.3 %copy-start.1 = (f32[3,1,5120]{2,1,0:T(1,128)S(1)}, f32[3,1,5120]{2,1,0:T(1,128)}, u32[]{:S(2)}) copy-start(f32[3,1,5120]{2,1,0:T(1,128)} %get-tuple-element.56) | copy-start | bytes 184324
  595.8 6.8 %copy-start = (f32[3,3,5120]{2,1,0:T(4,128)}, f32[3,3,5120]{2,1,0:T(4,128)S(1)}, u32[]{:S(2)}) copy-start(f32[3,3,5120]{2,1,0:T(4,128)S(1)} %reshape.120) | copy-start | bytes 552964
Sparse Core Ops, SparseCore 0:
  305.3 123.8 reduce-scatter.2
  438.6 121.7 reduce-scatter.4

commit v3 on v2

v3 whole, which is shorter than its diff:
```python
import functools

import jax
import jax.numpy as jnp
from jax import lax
from jax.experimental import pallas as pl
from jax.experimental.pallas import tpu as pltpu
from jax.sharding import PartitionSpec as P

HEAD_DIM = 128
EPS_NORM = 1e-6
ROPE_BASE = 10000.0
LOG2E = 1.4426950408889634
CHUNK = 512
VMEM_LIMIT = 60 * 1024 * 1024
F32 = jnp.float32
BF16 = jnp.bfloat16
MESH_ID = pl.DeviceIdType.MESH
NT = (((1,), (1,)), ((), ()))
TN = (((0,), (0,)), ((), ()))


def params(*semantics, **kw):
    return pltpu.CompilerParams(dimension_semantics=semantics or None, vmem_limit_bytes=VMEM_LIMIT, **kw)


def cost(flops, nbytes):
    return pl.CostEstimate(flops=int(flops), bytes_accessed=int(nbytes), transcendentals=0)


def rope_tables(positions):
    half_dim = HEAD_DIM // 2
    side_len = HEAD_DIM // 6
    first_len = half_dim - 2 * side_len
    lane = jnp.arange(HEAD_DIM)
    pair_idx = lane // 2
    section = (pair_idx >= first_len).astype(jnp.int32) + (pair_idx >= first_len + side_len).astype(jnp.int32)
    offset = jnp.where(section == 0, 0, jnp.where(section == 1, first_len, first_len + side_len))
    sec_width = jnp.where(section == 0, first_len, side_len)
    freq_vals = ROPE_BASE ** (-(pair_idx - offset).astype(F32) / sec_width.astype(F32))
    select = jnp.where(section[None, :] == jnp.arange(3)[:, None], freq_vals[None, :], 0.0)
    angles = jnp.sum(positions.astype(F32)[:, :, None] * select[None, :, :], axis=1)
    return jnp.cos(angles), jnp.where((lane % 2 == 0)[None, :], -1.0, 1.0) * jnp.sin(angles)


def norm_stats(x):
    centered = x - jnp.mean(x, axis=-1, keepdims=True)
    inv_std = lax.rsqrt(jnp.mean(centered * centered, axis=-1, keepdims=True) + EPS_NORM)
    return centered * inv_std, inv_std


def to_row(acc):
    return jnp.sum(acc.T, axis=0, keepdims=True)


def lanes_of(row):
    return jnp.broadcast_to(row, (HEAD_DIM, row.shape[1])).T


def head_sum(values):
    out = values[:, :HEAD_DIM]
    for h in range(1, values.shape[1] // HEAD_DIM):
        out = out + values[:, h * HEAD_DIM:(h + 1) * HEAD_DIM]
    return out


class Place:
    def __init__(self, n):
        self.n = n
        self.me = lax.axis_index('tp')
        self.right = lax.rem(self.me + 2, n)
        self.left = lax.rem(self.me + n - 2, n)
        self.far = lax.rem(self.me + n // 2, n)
        self.chip = self.me // 2

    def partner(self, dev):
        return dev + 1 - 2 * lax.rem(dev, 2)

    def barrier(self, devices):
        sem = pltpu.get_barrier_semaphore()
        for dev in devices:
            pl.semaphore_signal(sem, inc=1, device_id={'tp': dev}, device_id_type=MESH_ID)
        pl.semaphore_wait(sem, len(devices))

    def to_partner(self, src, dst, send_sem, recv_sem):
        return pltpu.make_async_remote_copy(src_ref=src, dst_ref=dst, send_sem=send_sem, recv_sem=recv_sem,
                                            device_id={'tp': self.partner(self.me)}, device_id_type=MESH_ID)

    def everyone(self):
        return [lax.rem(self.me + d, self.n) for d in range(1, self.n)]

    def near(self):
        return [self.right, self.left, self.partner(self.me)]


class Gather:
    def __init__(self, place, full, rows, send, recv):
        self.at, self.full, self.rows, self.send, self.recv = place, full, rows, send, recv

    def part(self, b, dev, off, count):
        return self.full.at[b, pl.ds(pl.multiple_of(dev * self.rows + off, 16), count)]

    def copy(self, b, dev, off, count, s_idx, r_idx, target):
        ref = self.part(b, dev, off, count)
        return pltpu.make_async_remote_copy(src_ref=ref, dst_ref=ref, send_sem=self.send.at[b, s_idx], recv_sem=self.recv.at[b, r_idx],
                                            device_id={'tp': target}, device_id_type=MESH_ID)

    def start_own(self, b):
        p = self.at
        self.copy(b, p.me, 0, self.rows, 0, 0, p.right).start()
        self.copy(b, p.me, 0, self.rows, 1, 1, p.left).start()
        self.copy(b, p.me, 0, self.rows, 2, 4, p.partner(p.me)).start()

    def take_own(self, b):
        p = self.at
        self.copy(b, p.partner(p.me), 0, self.rows, 2, 4, p.me).wait_recv()

    def take_left(self, b):
        p, half = self.at, self.rows // 2
        self.copy(b, p.left, 0, self.rows, 0, 0, p.me).wait_recv()
        self.copy(b, p.left, 0, half, 3, 2, p.right).start()
        self.copy(b, p.left, 0, self.rows, 5, 5, p.partner(p.me)).start()
        self.copy(b, p.partner(p.left), 0, self.rows, 5, 5, p.me).wait_recv()

    def take_right(self, b):
        p, half = self.at, self.rows // 2
        self.copy(b, p.right, 0, self.rows, 1, 1, p.me).wait_recv()
        self.copy(b, p.right, half, half, 4, 3, p.left).start()
        self.copy(b, p.right, 0, self.rows, 6, 6, p.partner(p.me)).start()
        self.copy(b, p.partner(p.right), 0, self.rows, 6, 6, p.me).wait_recv()

    def take_far(self, b):
        p, half = self.at, self.rows // 2
        self.copy(b, p.far, 0, half, 3, 2, p.me).wait_recv()
        self.copy(b, p.far, 0, half, 7, 7, p.partner(p.me)).start()
        self.copy(b, p.far, half, half, 4, 3, p.me).wait_recv()
        self.copy(b, p.far, half, half, 8, 8, p.partner(p.me)).start()
        self.copy(b, p.partner(p.far), 0, half, 7, 7, p.me).wait_recv()
        self.copy(b, p.partner(p.far), half, half, 8, 8, p.me).wait_recv()

    def finish(self, b):
        p, half = self.at, self.rows // 2
        for s_idx, count in ((0, self.rows), (1, self.rows), (2, self.rows), (3, half), (4, half), (5, self.rows), (6, self.rows), (7, half), (8, half)):
            self.copy(b, p.me, 0, count, s_idx, s_idx, p.me).wait_send()

    def item_place(self, i, nb):
        j = i - nb
        b = jnp.where(i < nb, i, jnp.where(i < 3 * nb, j // 2, i - 3 * nb))
        chips = self.at.n // 2
        side = jnp.where(lax.rem(j + 2 * nb, 2) == 0, chips - 1, 1)
        off = jnp.where(i < nb, 0, jnp.where(i < 3 * nb, side, chips // 2))
        return b, pl.multiple_of(lax.rem(self.at.chip + off, chips) * (2 * self.rows), 32)

    def take_item(self, i, nb):
        b, row0 = self.item_place(i, nb)
        odd = lax.rem(i + nb, 2)
        pl.when(i < nb)(lambda: self.take_own(b))
        pl.when((i >= nb) & (i < 3 * nb) & (odd == 0))(lambda: self.take_left(b))
        pl.when((i >= nb) & (i < 3 * nb) & (odd == 1))(lambda: self.take_right(b))
        pl.when(i >= 3 * nb)(lambda: self.take_far(b))
        return b, row0


GATHER_SEMS = 9


def chunks_of(width, step):
    return [(c, min(c + step, width)) for c in range(0, width, step)]


def exchange(place, x_ref, slots, send_sems, recv_sems):
    n, me = place.n, place.me
    for d, dev in enumerate(place.everyone()):
        pltpu.make_async_remote_copy(src_ref=x_ref, dst_ref=slots.at[me], send_sem=send_sems.at[d], recv_sem=recv_sems.at[me],
                                     device_id={'tp': dev}, device_id_type=MESH_ID).start()
    slots[me] = x_ref[...]
    for d, dev in enumerate(place.everyone()):
        copy = pltpu.make_async_remote_copy(src_ref=x_ref, dst_ref=slots.at[dev], send_sem=send_sems.at[d], recv_sem=recv_sems.at[dev],
                                            device_id={'tp': dev}, device_id_type=MESH_ID)
        copy.wait_send()
        copy.wait_recv()
    total = slots[0]
    for d in range(1, n):
        total = total + slots[d]
    return total


def gather_qkv_kernel(n, x_ref, dy_ref, m_ref, e_ref, wq_ref, wk_ref, wv_ref, bias_ref,
                      y_full, d_full, q_out, k_out, v_out, ss_ref,
                      w_all, xin, stage, xbuf, zst, vst, sq, ss_row, slots,
                      w_sem, in_sem, st_sem, ld_sem, out_sem, g_send, g_recv, e_send, e_recv):
    nb, rows, dim = x_ref.shape
    cols = wq_ref.shape[1]
    place = Place(n)
    gather = Gather(place, y_full, rows, g_send, g_recv)
    w_copies = [pltpu.make_async_copy(w, w_all.at[:, pl.ds(j * cols, cols)], w_sem.at[j]) for j, w in enumerate((wq_ref, wk_ref, wv_ref))]
    load_x = pltpu.make_async_copy(x_ref, xin, in_sem)
    load_x.start()
    for c in w_copies:
        c.start()
    group = 16

    def mine(full, b):
        return full.at[b, pl.ds(pl.multiple_of(place.me * rows, 16), rows)]

    load_x.wait()
    place.barrier(place.everyone())

    def ln_step(b, _):
        shift = m_ref[0:1] + e_ref[b, 0:1]
        scale_one = 1.0 + (m_ref[1:2] + e_ref[b, 1:2])

        def ln_rows(r, _):
            sl = pl.ds(pl.multiple_of(r * group, group), group)
            x_norm, _ = norm_stats(xin[b, sl].astype(F32))
            stage[b, sl] = (x_norm * scale_one + shift).astype(BF16)
            return 0

        lax.fori_loop(0, rows // group, ln_rows, 0)
        out = pltpu.make_async_copy(stage.at[b], mine(y_full, b), st_sem)
        out.start()
        out.wait()
        gather.start_own(b)
        return 0

    lax.fori_loop(0, nb, ln_step, 0)
    load_dy = pltpu.make_async_copy(dy_ref, xin, in_sem)
    load_dy.start()

    def gate_step(b, _):
        gate = m_ref[2:3] + e_ref[b, 2:3]

        def gate_rows(r, _):
            sl = pl.ds(pl.multiple_of(r * group, group), group)
            stage[b, sl] = (xin[b, sl].astype(F32) * gate).astype(BF16)
            return 0

        lax.fori_loop(0, rows // group, gate_rows, 0)
        out = pltpu.make_async_copy(stage.at[b], mine(d_full, b), st_sem)
        out.start()
        out.wait()
        return 0

    for c in w_copies:
        c.wait()

    def outputs(b, row0, slot):
        dst = pl.ds(row0, 2 * rows)
        return [pltpu.make_async_copy(zst.at[slot, :, pl.ds(0, cols)], q_out.at[b, dst], out_sem.at[slot, 0]),
                pltpu.make_async_copy(zst.at[slot, :, pl.ds(cols, cols)], k_out.at[b, dst], out_sem.at[slot, 1]),
                pltpu.make_async_copy(vst.at[slot], v_out.at[b, dst], out_sem.at[slot, 2])]

    def item(i, _):
        b, row0 = gather.take_item(i, nb)
        slot = lax.rem(i, 2)
        load = pltpu.make_async_copy(y_full.at[b, pl.ds(row0, 2 * rows)], xbuf, ld_sem)
        load.start()

        @pl.when(i == nb)
        def _():
            load_dy.wait()
            lax.fori_loop(0, nb, gate_step, 0)

        @pl.when(i >= 2)
        def _():
            for c in outputs(0, 0, slot):
                c.wait()

        load.wait()
        for lo, hi in chunks_of(3 * cols, 512):
            zst[slot, :, lo:hi] = jnp.dot(xbuf[...], w_all[:, lo:hi], preferred_element_type=F32) + bias_ref[:, lo:hi]
        vst[slot] = zst[slot, :, 2 * cols:].astype(BF16)
        q = zst[slot, :, :cols]
        k = zst[slot, :, cols:2 * cols]
        sq[2 * b, pl.ds(row0, 2 * rows)] = head_sum(q * q)
        sq[2 * b + 1, pl.ds(row0, 2 * rows)] = head_sum(k * k)
        for c in outputs(b, row0, slot):
            c.start()
        return 0

    lax.fori_loop(0, 4 * nb, item, 0)
    ss_row[...] = jnp.zeros_like(ss_row)
    for j in range(2 * nb):
        ss_row[j:j + 1] = to_row(sq[j])
    for slot in range(2):
        for c in outputs(0, 0, slot):
            c.wait()
    for b in range(nb):
        gather.finish(b)
    ss_ref[...] = exchange(place, ss_row, slots, e_send, e_recv)


def gather_qkv_call(n, x_loc, dy_loc, m_block, e_loc, w_q, w_k, w_v, b_q, b_k, b_v):
    nb, rows, dim = x_loc.shape
    cols = w_q.shape[1]
    tokens = rows * n
    shape = jax.ShapeDtypeStruct
    any_spec = pl.BlockSpec(memory_space=pl.ANY)
    vmem = pl.BlockSpec(memory_space=pltpu.VMEM)
    dma = pltpu.SemaphoreType.DMA
    stat_rows = -(-2 * nb // 8) * 8
    return pl.pallas_call(
        functools.partial(gather_qkv_kernel, n), name="gather_qkv",
        out_shape=[shape((nb, tokens, dim), BF16), shape((nb, tokens, dim), BF16), shape((nb, tokens, cols), F32),
                   shape((nb, tokens, cols), F32), shape((nb, tokens, cols), BF16), shape((stat_rows, tokens), F32)],
        in_specs=[any_spec, any_spec, vmem, vmem, any_spec, any_spec, any_spec, vmem],
        out_specs=[any_spec] * 5 + [vmem],
        scratch_shapes=[
            pltpu.VMEM((dim, 3 * cols), BF16), pltpu.VMEM((nb, rows, dim), BF16), pltpu.VMEM((nb, rows, dim), BF16),
            pltpu.VMEM((2 * rows, dim), BF16), pltpu.VMEM((2, 2 * rows, 3 * cols), F32), pltpu.VMEM((2, 2 * rows, cols), BF16),
            pltpu.VMEM((2 * nb, tokens, HEAD_DIM), F32), pltpu.VMEM((stat_rows, tokens), F32), pltpu.VMEM((n, stat_rows, tokens), F32),
            dma((3,)), dma, dma, dma, dma((2, 3)), dma((nb, GATHER_SEMS)), dma((nb, GATHER_SEMS)), dma((n,)), dma((n,))],
        compiler_params=params(collective_id=0, has_side_effects=True),
        cost_estimate=cost(6 * nb * tokens * dim * cols, 6 * dim * cols + 14 * nb * tokens * cols),
    )(x_loc, dy_loc, m_block, e_loc, w_q, w_k, w_v, jnp.concatenate([b_q, b_k, b_v])[None])


def all_sum_kernel(n, x_ref, o_ref, pieces, total, send_a, recv_a, send_b, recv_b):
    place = Place(n)
    me = place.me
    place.barrier(place.everyone())

    def first(d, dev, src):
        return pltpu.make_async_remote_copy(src_ref=x_ref.at[src], dst_ref=pieces.at[me], send_sem=send_a.at[d], recv_sem=recv_a.at[me],
                                            device_id={'tp': dev}, device_id_type=MESH_ID)

    for d, dev in enumerate(place.everyone()):
        first(d, dev, dev).start()
    pieces[me] = x_ref[me]
    for d, dev in enumerate(place.everyone()):
        pltpu.make_async_remote_copy(src_ref=x_ref.at[me], dst_ref=pieces.at[dev], send_sem=send_a.at[d], recv_sem=recv_a.at[dev],
                                     device_id={'tp': dev}, device_id_type=MESH_ID).wait_recv()
    acc = pieces[0]
    for d in range(1, n):
        acc = acc + pieces[d]
    total[...] = acc
    o_ref[me] = acc
    for d, dev in enumerate(place.everyone()):
        first(d, dev, dev).wait_send()
    for d, dev in enumerate(place.everyone()):
        pltpu.make_async_remote_copy(src_ref=total, dst_ref=o_ref.at[me], send_sem=send_b.at[d], recv_sem=recv_b.at[me],
                                     device_id={'tp': dev}, device_id_type=MESH_ID).start()
    for d, dev in enumerate(place.everyone()):
        copy = pltpu.make_async_remote_copy(src_ref=total, dst_ref=o_ref.at[dev], send_sem=send_b.at[d], recv_sem=recv_b.at[dev],
                                            device_id={'tp': dev}, device_id_type=MESH_ID)
        copy.wait_send()
        copy.wait_recv()


def all_sum_call(n, x):
    spec = pl.BlockSpec(memory_space=pltpu.VMEM)
    dma = pltpu.SemaphoreType.DMA
    return pl.pallas_call(
        functools.partial(all_sum_kernel, n), name="all_sum",
        out_shape=jax.ShapeDtypeStruct(x.shape, x.dtype), in_specs=[spec], out_specs=spec,
        scratch_shapes=[pltpu.VMEM(x.shape, x.dtype), pltpu.VMEM(x.shape[1:], x.dtype), dma((n,)), dma((n,)), dma((n,)), dma((n,))],
        compiler_params=pltpu.CompilerParams(collective_id=4, has_side_effects=True, vmem_limit_bytes=4 * 1024 * 1024),
        cost_estimate=cost(4_000_000_000, x.size * 8),
    )(x)


def swap_pairs(x):
    lane = lax.broadcasted_iota(jnp.int32, x.shape, 1)
    return jnp.where(lane % 2 == 0, pltpu.roll(x, HEAD_DIM - 1, 1), pltpu.roll(x, 1, 1))


def rotate(x, cos, sin):
    return x * cos + swap_pairs(x) * sin


def softmax_block(s):
    c = HEAD_DIM ** -0.5 * LOG2E
    top = jnp.max(s, axis=1, keepdims=True)
    p = jnp.exp2(s * c - top * c)
    return p * (1.0 / jnp.sum(p, axis=1, keepdims=True))


def gather_attn_kernel(n, nb, heads, dim, q_ref, k_ref, v_ref, gq_ref, gk_ref, cos_ref, sin_ref, ss_ref,
                       wq_ref, wk_ref, wv_ref, wo_ref, d_in,
                       d_full, o_out, o_p, da_out, wq_p, wk_p, wv_p, wo_p,
                       inv_q, inv_k, o_all, wo, xbuf, ast,
                       w_sem, ld_sem, out_sem, o_sem, g_send, g_recv, t_send, t_recv):
    step = pl.program_id(0)
    tokens = q_ref.shape[1]
    rows = tokens // n
    blk = min(256, tokens)
    place = Place(n)
    gather = Gather(place, d_full, rows, g_send, g_recv)
    pairs = ((wo_ref, wo_p), (wq_ref, wq_p), (wk_ref, wk_p), (wv_ref, wv_p), (o_out, o_p))

    def trade(j):
        return place.to_partner(*pairs[j], t_send.at[j], t_recv.at[j])


    @pl.when(step == 0)
    def _():
        pltpu.make_async_copy(wo_ref, wo, w_sem).start()
        place.barrier(place.near())

        def own(b, _):
            gather.start_own(b)
            return 0

        lax.fori_loop(0, nb, own, 0)
        for j in range(4):
            trade(j).start()

    @pl.when(step < nb * heads)
    def _():
        b = step // heads
        h = lax.rem(step, heads)

        @pl.when(h == 0)
        def _():
            inv_q[...] = lanes_of(lax.rsqrt(ss_ref[pl.ds(2 * b, 1)] / dim + EPS_NORM))
            inv_k[...] = lanes_of(lax.rsqrt(ss_ref[pl.ds(2 * b + 1, 1)] / dim + EPS_NORM))

        cos, sin = cos_ref[...], sin_ref[...]
        q_rot = rotate(q_ref[0] * inv_q[...] * gq_ref[...], cos, sin).astype(BF16)
        k_rot = rotate(k_ref[0] * inv_k[...] * gk_ref[...], cos, sin).astype(BF16)
        v = v_ref[0]
        lanes = pl.ds(pl.multiple_of(h * HEAD_DIM, HEAD_DIM), HEAD_DIM)
        for i in range(tokens // blk):
            s = lax.dot_general(q_rot[i * blk:(i + 1) * blk], k_rot, NT, preferred_element_type=F32)
            p = softmax_block(s).astype(BF16)
            o_all[b, i * blk:(i + 1) * blk, lanes] = jnp.dot(p, v, preferred_element_type=F32).astype(BF16)

    @pl.when(step == nb * heads)
    def _():
        o_copy = pltpu.make_async_copy(o_all, o_out, o_sem)
        o_copy.start()
        pltpu.make_async_copy(wo_ref, wo, w_sem).wait()

        def outputs(b, row0, slot):
            return pltpu.make_async_copy(ast.at[slot], da_out.at[b, pl.ds(row0, 2 * rows)], out_sem.at[slot])

        def load(b, row0, slot):
            return pltpu.make_async_copy(d_full.at[b, pl.ds(row0, 2 * rows)], xbuf.at[slot], ld_sem.at[slot])

        def take(i):
            b, row0 = gather.take_item(i, nb)
            load(b, row0, lax.rem(i, 2)).start()

        take(0)

        def item(i, _):
            slot = lax.rem(i, 2)

            @pl.when(i + 1 < 3 * nb)
            def _():
                take(i + 1)

            @pl.when(i >= 2)
            def _():
                outputs(0, 0, slot).wait()

            load(0, 0, slot).wait()
            ast[slot] = lax.dot_general(xbuf[slot], wo[...], NT, preferred_element_type=F32).astype(BF16)
            b, row0 = gather.item_place(i, nb)
            outputs(b, row0, slot).start()

            @pl.when(i == 0)
            def _():
                o_copy.wait()
                trade(4).start()

            @pl.when((i + 1 >= 3 * nb) & (i + 1 < 4 * nb))
            def _():
                take(i + 1)

            return 0

        lax.fori_loop(0, 4 * nb, item, 0)
        for slot in range(2):
            outputs(0, 0, slot).wait()
        for b in range(nb):
            gather.finish(b)
        for j in range(5):
            trade(j).wait()


def gather_attn_call(n, q, k, v, g_q, g_k, cos_tab, sin_tab, ss, w_q, w_k, w_v, w_o, d_full):
    nb, tokens, cols = q.shape
    dim = w_o.shape[1]
    heads = cols // HEAD_DIM
    rows = tokens // n
    last = nb * heads - 1
    shape = jax.ShapeDtypeStruct
    dma = pltpu.SemaphoreType.DMA
    any_spec = pl.BlockSpec(memory_space=pl.ANY)

    def head_of(i):
        i = jnp.minimum(i, last)
        return i // heads, i % heads

    blk = pl.BlockSpec((1, tokens, HEAD_DIM), lambda i: (head_of(i)[0], 0, head_of(i)[1]))
    vec = pl.BlockSpec((1, HEAD_DIM), lambda i: (0, head_of(i)[1]))
    tab = pl.BlockSpec((tokens, HEAD_DIM), lambda i: (0, 0))
    head_arr = shape((nb, tokens, cols), BF16)
    return pl.pallas_call(
        functools.partial(gather_attn_kernel, n, nb, heads, dim), name="gather_attn", grid=(nb * heads + 1,),
        out_shape=[shape(d_full.shape, BF16), head_arr, head_arr, head_arr] + [shape(w.shape, BF16) for w in (w_q, w_k, w_v, w_o)],
        in_specs=[blk, blk, blk, vec, vec, tab, tab, pl.BlockSpec(ss.shape, lambda i: (0, 0))] + [any_spec] * 5,
        out_specs=[any_spec] * 8,
        scratch_shapes=[
            pltpu.VMEM((tokens, HEAD_DIM), F32), pltpu.VMEM((tokens, HEAD_DIM), F32), pltpu.VMEM((nb, tokens, cols), BF16),
            pltpu.VMEM((cols, dim), BF16), pltpu.VMEM((2, 2 * rows, dim), BF16), pltpu.VMEM((2, 2 * rows, cols), BF16),
            dma, dma((2,)), dma((2,)), dma, dma((nb, GATHER_SEMS)), dma((nb, GATHER_SEMS)), dma((5,)), dma((5,))],
        input_output_aliases={12: 0},
        compiler_params=params("arbitrary", collective_id=1, has_side_effects=True),
        cost_estimate=cost(2 * nb * tokens * dim * cols + 4 * nb * tokens * tokens * cols, 8 * nb * tokens * dim),
    )(q, k, v, g_q[None], g_k[None], cos_tab, sin_tab, ss, w_q, w_k, w_v, w_o, d_full)


class Scatter:
    def __init__(self, place, part, recv_far, recv_side, send, recv):
        self.at, self.part, self.far, self.side, self.send, self.recv = place, part, recv_far, recv_side, send, recv
        self.rows = part.shape[2]
        self.half = self.rows // 2

    def copy(self, j, idx, src, dst, target):
        return pltpu.make_async_remote_copy(src_ref=src, dst_ref=dst, send_sem=self.send.at[j, idx], recv_sem=self.recv.at[j, idx],
                                            device_id={'tp': target}, device_id_type=MESH_ID)

    def message(self, j, idx):
        p, part, far, side = self.at, self.part, self.far, self.side
        first, second = pl.ds(0, self.half), pl.ds(self.half, self.rows - self.half)
        src, dst, target = (
            lambda: (part.at[j, 0, first], far.at[j, 0], p.right),
            lambda: (part.at[j, 0, second], far.at[j, 1], p.left),
            lambda: (part.at[j, 1, second], side.at[j, 0, second], p.right),
            lambda: (part.at[j, 2, first], side.at[j, 1, first], p.left),
            lambda: (part.at[j, 1, first], side.at[j, 0, first], p.right),
            lambda: (part.at[j, 2, second], side.at[j, 1, second], p.left))[idx]()
        return self.copy(j, idx, src, dst, target)

    def start(self, j):
        for idx in range(4):
            self.message(j, idx).start()

    def sums(self, j):
        h = self.half
        self.message(j, 0).wait_recv()
        self.part[j, 1, :h] = (self.part[j, 1, :h].astype(F32) + self.far[j, 0].astype(F32)).astype(BF16)
        self.message(j, 1).wait_recv()
        self.part[j, 2, h:] = (self.part[j, 2, h:].astype(F32) + self.far[j, 1].astype(F32)).astype(BF16)
        self.message(j, 4).start()
        self.message(j, 5).start()

    def final(self, j):
        for idx in range(2, 6):
            self.message(j, idx).wait_recv()
        total = self.part[j, 3].astype(F32) + self.side[j, 0].astype(F32) + self.side[j, 1].astype(F32)
        self.part[j, 3] = total.astype(BF16)

    def finish(self, j):
        for idx in range(6):
            self.message(j, idx).wait_send()

    @staticmethod
    def scratch(rows, dim):
        nc, dma = dim // CHUNK, pltpu.SemaphoreType.DMA
        return [pltpu.VMEM((nc, 4, rows, CHUNK), BF16), pltpu.VMEM((nc, 2, rows // 2, CHUNK), BF16),
                pltpu.VMEM((nc, 2, rows, CHUNK), BF16), dma((nc, 6)), dma((nc, 6))]


def scatter_outputs(part, out, sem, j):
    nb, rows, _ = out.shape
    cs = pl.ds(pl.multiple_of(j * CHUNK, CHUNK), CHUNK)
    return [pltpu.make_async_copy(part.at[j, 3, pl.ds(b * rows, rows)], out.at[b, :, cs], sem.at[b]) for b in range(nb)]


def scatter_end(scatter, out, sem, nc):
    def last(j, _):
        scatter.final(j)
        for c in scatter_outputs(scatter.part, out, sem, j):
            c.start()
        return 0

    lax.fori_loop(0, nc, last, 0)

    def drain(j, _):
        for c in scatter_outputs(scatter.part, out, sem, j):
            c.wait()
        scatter.finish(j)
        return 0

    lax.fori_loop(0, nc, drain, 0)


def pair_rows(place, nb, rows, mine, theirs, lhs, sem):
    width = mine.shape[2]
    out = []
    for d, dev in enumerate((place.far, place.right, place.left, place.me)):
        src_rows = pl.ds(pl.multiple_of(dev * rows, 16), rows)
        for b in range(nb):
            dst_rows = pl.ds((d * nb + b) * rows, rows)
            for j, src in enumerate((mine, theirs)):
                out.append(pltpu.make_async_copy(src.at[b, src_rows], lhs.at[dst_rows, pl.ds(j * width, width)], sem))
    return out


def proj_bwd_kernel(n, nb, heads, dim, q_ref, k_ref, v_ref, do_ref, gq_ref, gk_ref, cos_ref, sin_ref, ss_ref,
                    q_hbm, k_hbm, o_hbm, o_p, wo_hbm, wo_p, d_full,
                    proj_out, g_out, g_p, dqs_out, dks_out, dwo_out, dgq_ref, dgk_ref,
                    part, recv_far, recv_side, s_send, s_recv,
                    inv_q, inv_k, acc_q, acc_k, p_all, ds_all, dq_all, qs_st, ks_st, v_st, st_row, st_sum, slots,
                    ld_sem, w_sem, fl_sem, g_sem, go_sem, out_sem, e_send, e_recv, t_send, t_recv):
    step = pl.program_id(0)
    tokens = q_ref.shape[1]
    rows = tokens // n
    cols = heads * HEAD_DIM
    blk = min(256, tokens)
    nc = dim // CHUNK
    steps = nb * heads
    scale = HEAD_DIM ** -0.5
    place = Place(n)
    scatter = Scatter(place, part, recv_far, recv_side, s_send, s_recv)

    @pl.when(step == 0)
    def _():
        def project(lhs, wbuf):
            loads = pair_rows(place, nb, rows, o_hbm, o_p, lhs, ld_sem.at[0])
            for c in loads:
                c.start()

            def chunk(j):
                cs = pl.ds(pl.multiple_of(j * CHUNK, CHUNK), CHUNK)
                slot = lax.rem(j, 2)
                return [pltpu.make_async_copy(wo_hbm.at[:, cs], wbuf.at[slot, pl.ds(0, cols)], w_sem.at[slot, 0]),
                        pltpu.make_async_copy(wo_p.at[:, cs], wbuf.at[slot, pl.ds(cols, cols)], w_sem.at[slot, 1])]

            for c in chunk(0):
                c.start()
            place.barrier(place.everyone())
            for c in loads:
                c.wait()

            def body(j, _):
                @pl.when(j + 1 < nc)
                def _():
                    for c in chunk(j + 1):
                        c.start()

                for c in chunk(j):
                    c.wait()
                w = wbuf[lax.rem(j, 2)]
                half = 2 * nb * rows
                for d in range(2):
                    z = jnp.dot(lhs[d * half:(d + 1) * half], w, preferred_element_type=F32).astype(BF16)
                    part[j, 2 * d] = z[:half // 2]
                    part[j, 2 * d + 1] = z[half // 2:]
                scatter.start(j)
                return 0

            lax.fori_loop(0, nc, body, 0)

        pl.run_scoped(project, pltpu.VMEM((4 * nb * rows, 2 * cols), BF16), pltpu.VMEM((2, 2 * cols, CHUNK), BF16))

    def flush(b, h, slot):
        lanes = pl.ds(pl.multiple_of(h * HEAD_DIM, HEAD_DIM), HEAD_DIM)
        v_lanes = pl.ds(pl.multiple_of(2 * cols + h * HEAD_DIM, HEAD_DIM), HEAD_DIM)
        return [pltpu.make_async_copy(qs_st.at[slot], dqs_out.at[b, :, lanes], fl_sem.at[slot, 0]),
                pltpu.make_async_copy(ks_st.at[slot], dks_out.at[b, :, lanes], fl_sem.at[slot, 1]),
                pltpu.make_async_copy(v_st.at[slot], g_out.at[b, :, v_lanes], fl_sem.at[slot, 2])]

    for j in range(nc):
        at_step = 1 + j * (steps - 1) // max(nc - 1, 1)
        pl.when(step == at_step)(functools.partial(scatter.sums, j))

    @pl.when((step >= 1) & (step <= steps))
    def _():
        b = (step - 1) // heads
        head = lax.rem(step - 1, heads)
        slot = lax.rem(step, 2)

        @pl.when(step == 1)
        def _():
            st_row[...] = jnp.zeros_like(st_row)

        @pl.when(head == 0)
        def _():
            inv_q[...] = lanes_of(lax.rsqrt(ss_ref[pl.ds(2 * b, 1)] / dim + EPS_NORM))
            inv_k[...] = lanes_of(lax.rsqrt(ss_ref[pl.ds(2 * b + 1, 1)] / dim + EPS_NORM))
            acc_q[...] = jnp.zeros_like(acc_q)
            acc_k[...] = jnp.zeros_like(acc_k)

        @pl.when(step >= 3)
        def _():
            for c in flush(0, 0, slot):
                c.wait()

        cos, sin = cos_ref[...], sin_ref[...]
        q_rot = rotate(q_ref[0] * inv_q[...] * gq_ref[...], cos, sin).astype(BF16)
        k_rot = rotate(k_ref[0] * inv_k[...] * gk_ref[...], cos, sin).astype(BF16)
        v = v_ref[0]
        do = do_ref[0]
        for i in range(tokens // blk):
            sl = slice(i * blk, (i + 1) * blk)
            p = softmax_block(lax.dot_general(q_rot[sl], k_rot, NT, preferred_element_type=F32))
            p_all[sl] = p.astype(BF16)
            dp = lax.dot_general(do[sl], v, NT, preferred_element_type=F32)
            delta = jnp.sum(dp * p, axis=1, keepdims=True)
            ds = (p * (dp - delta)).astype(BF16)
            ds_all[sl] = ds
            dq_all[sl] = jnp.dot(ds, k_rot, preferred_element_type=F32) * scale
        do_t = do.astype(F32).T.astype(BF16)
        q_t = q_rot.astype(F32).T.astype(BF16)
        v_st[slot] = jnp.dot(do_t, p_all[...], preferred_element_type=F32).T.astype(BF16)
        dk_rot = (jnp.dot(q_t, ds_all[...], preferred_element_type=F32) * scale).T.astype(BF16).astype(F32)
        dq_rot = dq_all[...].astype(BF16).astype(F32)
        dq_hat = rotate(dq_rot, cos, -sin)
        dk_hat = rotate(dk_rot, cos, -sin)
        q_hat = q_ref[0] * inv_q[...]
        k_hat = k_ref[0] * inv_k[...]
        dgq_ref[0] = jnp.sum(dq_hat * q_hat, axis=0, keepdims=True)
        dgk_ref[0] = jnp.sum(dk_hat * k_hat, axis=0, keepdims=True)
        dq_s = dq_hat * gq_ref[...]
        dk_s = dk_hat * gk_ref[...]
        qs_st[slot] = dq_s
        ks_st[slot] = dk_s
        acc_q[...] += dq_s * q_hat
        acc_k[...] += dk_s * k_hat
        for c in flush(b, head, slot):
            c.start()

        @pl.when(head == heads - 1)
        def _():
            st_row[pl.ds(2 * b, 1)] = to_row(acc_q[...])
            st_row[pl.ds(2 * b + 1, 1)] = to_row(acc_k[...])

    @pl.when(step == steps + 1)
    def _():
        for s in (steps - 1, steps):
            for c in flush(0, 0, s % 2):
                c.wait()
        st_sum[...] = exchange(place, st_row, slots, e_send, e_recv)
        rb = min(256, tokens)
        per = tokens // rb
        trade = place.to_partner(g_out, g_p, t_send, t_recv)

        def norm_grad(fbuf, gbuf):
            def loads(i, slot):
                b, r0 = i // per, pl.multiple_of(lax.rem(i, per) * rb, rb)
                return [pltpu.make_async_copy(src.at[b, pl.ds(r0, rb)], fbuf.at[slot, m], g_sem.at[slot, m])
                        for m, src in enumerate((dqs_out, q_hbm, dks_out, k_hbm))]

            def store(i, slot):
                b, r0 = i // per, pl.multiple_of(lax.rem(i, per) * rb, rb)
                return pltpu.make_async_copy(gbuf.at[slot], g_out.at[b, pl.ds(r0, rb), pl.ds(0, 2 * cols)], go_sem.at[slot])

            for c in loads(0, 0):
                c.start()

            def body(i, _):
                slot = lax.rem(i, 2)
                b, r0 = i // per, pl.multiple_of(lax.rem(i, per) * rb, rb)

                @pl.when(i + 1 < nb * per)
                def _():
                    for c in loads(i + 1, lax.rem(i + 1, 2)):
                        c.start()

                @pl.when(r0 == 0)
                def _():
                    inv_q[...] = lanes_of(lax.rsqrt(ss_ref[pl.ds(2 * b, 1)] / dim + EPS_NORM))
                    inv_k[...] = lanes_of(lax.rsqrt(ss_ref[pl.ds(2 * b + 1, 1)] / dim + EPS_NORM))
                    acc_q[...] = lanes_of(st_sum[pl.ds(2 * b, 1)] / dim)
                    acc_k[...] = lanes_of(st_sum[pl.ds(2 * b + 1, 1)] / dim)

                @pl.when(i >= 2)
                def _():
                    store(0, slot).wait()

                for c in loads(i, slot):
                    c.wait()
                sl = pl.ds(r0, rb)
                for m, (inv, st) in enumerate(((inv_q, acc_q), (inv_k, acc_k))):
                    inv_l, st_l = inv[sl], st[sl]
                    for h in range(heads):
                        hs = slice(h * HEAD_DIM, (h + 1) * HEAD_DIM)
                        grad = inv_l * (fbuf[slot, 2 * m, :, hs] - (fbuf[slot, 2 * m + 1, :, hs] * inv_l) * st_l)
                        gbuf[slot, :, m * cols + h * HEAD_DIM:m * cols + (h + 1) * HEAD_DIM] = grad.astype(BF16)
                store(i, slot).start()
                return 0

            lax.fori_loop(0, nb * per, body, 0)
            for s in range(min(2, nb * per)):
                store(0, s).wait()

        pl.run_scoped(norm_grad, pltpu.VMEM((2, 4, rb, cols), F32), pltpu.VMEM((2, rb, 2 * cols), BF16))
        trade.start()

        def weight_grad(turned, obuf, dbuf, wst):
            bn = min(512, dim)
            n_chunks = dim // bn

            def chunk(c):
                slot = lax.rem(c, 2)
                return pltpu.make_async_copy(d_full.at[:, :, pl.ds(pl.multiple_of(c * bn, bn), bn)], dbuf.at[slot], go_sem.at[slot])

            def store(c):
                slot = lax.rem(c, 2)
                return pltpu.make_async_copy(wst.at[slot], dwo_out.at[:, pl.ds(pl.multiple_of(c * bn, bn), bn)], w_sem.at[slot, 0])

            load_o = pltpu.make_async_copy(o_hbm, obuf, ld_sem.at[0])
            load_o.start()
            chunk(0).start()
            load_o.wait()
            for b in range(nb):
                turned[:, b * tokens:(b + 1) * tokens] = obuf[b].T

            def body(c, _):
                slot = lax.rem(c, 2)

                @pl.when(c + 1 < n_chunks)
                def _():
                    chunk(c + 1).start()

                @pl.when(c >= 2)
                def _():
                    store(c).wait()

                chunk(c).wait()
                d = dbuf[slot].reshape(nb * tokens, bn)
                wst[slot] = jnp.dot(turned[...], d, preferred_element_type=F32).astype(BF16)
                store(c).start()
                return 0

            lax.fori_loop(0, n_chunks, body, 0)
            for s in range(min(2, n_chunks)):
                store(s).wait()

        bn = min(512, dim)
        pl.run_scoped(weight_grad, pltpu.VMEM((cols, nb * tokens), BF16), pltpu.VMEM((nb, tokens, cols), BF16),
                      pltpu.VMEM((2, nb, tokens, bn), BF16), pltpu.VMEM((2, cols, bn), BF16))
        scatter_end(scatter, proj_out, out_sem, nc)
        trade.wait()


def proj_bwd_call(n, q, k, v, d_attn, g_q, g_k, cos_tab, sin_tab, ss, o, o_p, w_o, wo_p, d_full):
    nb, tokens, cols = q.shape
    dim = w_o.shape[1]
    heads = cols // HEAD_DIM
    rows = tokens // n
    steps = nb * heads
    shape = jax.ShapeDtypeStruct
    dma = pltpu.SemaphoreType.DMA
    any_spec = pl.BlockSpec(memory_space=pl.ANY)

    def head_of(i):
        i = jnp.clip(i - 1, 0, steps - 1)
        return i // heads, i % heads

    blk = pl.BlockSpec((1, tokens, HEAD_DIM), lambda i: (head_of(i)[0], 0, head_of(i)[1]))
    vec = pl.BlockSpec((1, HEAD_DIM), lambda i: (0, head_of(i)[1]))
    out_vec = pl.BlockSpec((1, 1, HEAD_DIM), lambda i: (head_of(i)[0], 0, head_of(i)[1]))
    tab = pl.BlockSpec((tokens, HEAD_DIM), lambda i: (0, 0))
    whole = (nb, tokens, cols)
    lane_tile = pltpu.VMEM((tokens, HEAD_DIM), F32)
    return pl.pallas_call(
        functools.partial(proj_bwd_kernel, n, nb, heads, dim), name="proj_bwd", grid=(steps + 2,),
        out_shape=[shape((nb, rows, dim), BF16), shape((nb, tokens, 3 * cols), BF16), shape((nb, tokens, 3 * cols), BF16),
                   shape(whole, F32), shape(whole, F32), shape((cols, dim), BF16), shape((nb, 1, cols), F32), shape((nb, 1, cols), F32)],
        in_specs=[blk, blk, blk, blk, vec, vec, tab, tab, pl.BlockSpec(ss.shape, lambda i: (0, 0))] + [any_spec] * 7,
        out_specs=[any_spec] * 6 + [out_vec, out_vec],
        scratch_shapes=Scatter.scratch(nb * rows, dim) + [lane_tile] * 4 + [pltpu.VMEM((tokens, tokens), BF16)] * 2 + [
            lane_tile, pltpu.VMEM((2, tokens, HEAD_DIM), F32), pltpu.VMEM((2, tokens, HEAD_DIM), F32),
            pltpu.VMEM((2, tokens, HEAD_DIM), BF16), pltpu.VMEM(ss.shape, F32), pltpu.VMEM(ss.shape, F32), pltpu.VMEM((n,) + ss.shape, F32),
            dma((1,)), dma((2, 2)), dma((2, 3)), dma((2, 4)), dma((2,)), dma((nb,)), dma((n,)), dma((n,)), dma, dma],
        compiler_params=params("arbitrary", collective_id=2, has_side_effects=True),
        cost_estimate=cost(4 * nb * tokens * dim * cols + 36 * nb * tokens * tokens * cols, 30 * nb * tokens * cols),
    )(q, k, v, d_attn, g_q[None], g_k[None], cos_tab, sin_tab, ss, q, k, o, o_p, w_o, wo_p, d_full)


def dy_dw_kernel(n, nb, dim, g_hbm, g_p, wq_hbm, wk_hbm, wv_hbm, wq_p, wk_p, wv_p, y_full,
                 dy_out, dwq_out, dwk_out, dwv_out,
                 part, recv_far, recv_side, s_send, s_recv, ld_sem, w_sem, y_sem, o_sem, out_sem):
    tokens = g_hbm.shape[1]
    rows = tokens // n
    cols = g_hbm.shape[2] // 3
    nc = dim // CHUNK
    place = Place(n)
    scatter = Scatter(place, part, recv_far, recv_side, s_send, s_recv)
    lag = 2

    def chain(lhs, wbuf):
        loads = pair_rows(place, nb, rows, g_hbm, g_p, lhs, ld_sem)
        for c in loads:
            c.start()

        def chunk(j):
            slot = lax.rem(j, 2)
            src = pl.ds(pl.multiple_of(j * CHUNK, CHUNK), CHUNK)
            return [pltpu.make_async_copy(w.at[src], wbuf.at[slot, :, pl.ds(m * cols, cols)], w_sem.at[slot, m])
                    for m, w in enumerate((wq_hbm, wk_hbm, wv_hbm, wq_p, wk_p, wv_p))]

        for c in chunk(0):
            c.start()
        place.barrier(place.near()[:2])
        for c in loads:
            c.wait()

        def body(j, _):
            @pl.when(j + 1 < nc)
            def _():
                for c in chunk(j + 1):
                    c.start()

            for c in chunk(j):
                c.wait()
            w = wbuf[lax.rem(j, 2)]
            half = 2 * nb * rows
            for d in range(2):
                z = lax.dot_general(lhs[d * half:(d + 1) * half], w, NT, preferred_element_type=F32).astype(BF16)
                part[j, 2 * d] = z[:half // 2]
                part[j, 2 * d + 1] = z[half // 2:]
            scatter.start(j)

            @pl.when(j >= lag)
            def _():
                scatter.sums(j - lag)

            return 0

        lax.fori_loop(0, nc, body, 0)

    pl.run_scoped(chain, pltpu.VMEM((4 * nb * rows, 6 * cols), BF16), pltpu.VMEM((2, CHUNK, 6 * cols), BF16))

    def weight_grad(g, ybuf, wst):
        bm = min(512, dim)
        n_chunks = dim // bm

        def chunk(c):
            slot = lax.rem(c, 2)
            return pltpu.make_async_copy(y_full.at[:, :, pl.ds(pl.multiple_of(c * bm, bm), bm)], ybuf.at[slot], y_sem.at[slot])

        def store(c):
            slot = lax.rem(c, 2)
            dst = pl.ds(pl.multiple_of(c * bm, bm), bm)
            return [pltpu.make_async_copy(wst.at[slot, :, pl.ds(m * cols, cols)], out.at[dst], o_sem.at[slot, m])
                    for m, out in enumerate((dwq_out, dwk_out, dwv_out))]

        load_g = pltpu.make_async_copy(g_hbm, g, ld_sem)
        load_g.start()
        chunk(0).start()
        load_g.wait()

        def body(c, _):
            slot = lax.rem(c, 2)

            @pl.when(c + 1 < n_chunks)
            def _():
                chunk(c + 1).start()

            @pl.when(c >= 2)
            def _():
                for s in store(c):
                    s.wait()

            chunk(c).wait()
            for m in range(lag):
                late = nc - lag + m
                pl.when(c == min(1 + 2 * m, n_chunks - 1))(functools.partial(scatter.sums, max(late, 0)) if late >= 0 else (lambda: None))
            wst[slot] = lax.dot_general(ybuf[slot].reshape(nb * tokens, bm), g[...].reshape(nb * tokens, 3 * cols), TN,
                                        preferred_element_type=F32).astype(BF16)
            for s in store(c):
                s.start()
            return 0

        lax.fori_loop(0, n_chunks, body, 0)
        for s in range(min(2, n_chunks)):
            for c in store(s):
                c.wait()

    bm = min(512, dim)
    pl.run_scoped(weight_grad, pltpu.VMEM((nb, tokens, 3 * cols), BF16), pltpu.VMEM((2, nb, tokens, bm), BF16),
                  pltpu.VMEM((2, bm, 3 * cols), BF16))
    scatter_end(scatter, dy_out, out_sem, nc)


def dy_dw_call(n, g, g_p, w_q, w_k, w_v, wq_p, wk_p, wv_p, y_full):
    nb, tokens, wide = g.shape
    dim = y_full.shape[2]
    cols = wide // 3
    rows = tokens // n
    shape = jax.ShapeDtypeStruct
    dma = pltpu.SemaphoreType.DMA
    any_spec = pl.BlockSpec(memory_space=pl.ANY)
    return pl.pallas_call(
        functools.partial(dy_dw_kernel, n, nb, dim), name="dy_dw",
        out_shape=[shape((nb, rows, dim), BF16)] + [shape((dim, cols), BF16)] * 3,
        in_specs=[any_spec] * 9, out_specs=[any_spec] * 4,
        scratch_shapes=Scatter.scratch(nb * rows, dim) + [dma, dma((2, 6)), dma((2,)), dma((2, 3)), dma((nb,))],
        compiler_params=params(collective_id=3, has_side_effects=True),
        cost_estimate=cost(12 * nb * tokens * dim * cols, 30 * nb * tokens * cols),
    )(g, g_p, w_q, w_k, w_v, wq_p, wk_p, wv_p, y_full)


def token_kernel(x_ref, dy_ref, pr_ref, g_ref, m_ref, e_ref, bo_ref, xo_ref, dx_ref, dm_ref):
    mod = m_ref[...] + e_ref[0]
    x = x_ref[0].astype(F32)
    d_out = dy_ref[0].astype(F32)
    proj = pr_ref[0].astype(F32) + bo_ref[...]
    xo_ref[0] = (x + mod[2:3] * proj).astype(BF16)
    x_norm, inv_std = norm_stats(x)
    d_y = g_ref[0].astype(F32)
    d_norm = d_y * (1.0 + mod[1:2])
    d_x = d_out + inv_std * (
        d_norm - jnp.mean(d_norm, axis=-1, keepdims=True) - x_norm * jnp.mean(d_norm * x_norm, axis=-1, keepdims=True))
    dx_ref[0] = d_x.astype(BF16)
    dm_ref[0, 0:1] = jnp.sum(d_y, axis=0, keepdims=True)
    dm_ref[0, 1:2] = jnp.sum(d_y * x_norm, axis=0, keepdims=True)
    dm_ref[0, 2:3] = jnp.sum(d_out * proj, axis=0, keepdims=True)


def token_call(x_loc, dy_loc, proj, d_y, m_block, e_loc, b_o):
    nb, rows, dim = x_loc.shape
    row = pl.BlockSpec((1, rows, dim), lambda i: (i, 0, 0))
    mod = pl.BlockSpec((1, 3, dim), lambda i: (i, 0, 0))
    return pl.pallas_call(
        token_kernel, name="tokens", grid=(nb,),
        out_shape=[jax.ShapeDtypeStruct(x_loc.shape, BF16), jax.ShapeDtypeStruct(x_loc.shape, BF16),
                   jax.ShapeDtypeStruct((nb, 3, dim), F32)],
        in_specs=[row, row, row, row, pl.BlockSpec((3, dim), lambda i: (0, 0)), mod, pl.BlockSpec((1, dim), lambda i: (0, 0))],
        out_specs=[row, row, mod],
        compiler_params=params("arbitrary"),
        cost_estimate=cost(nb * rows * dim * 30, nb * rows * dim * 12),
    )(x_loc, dy_loc, proj, d_y, m_block, e_loc, b_o[None])


def solution(mesh):
    tp_size = mesh.shape['tp']

    def device_step(x_loc, e_loc, m_block, w_q, b_q, w_k, b_k, w_v, b_v, w_o, b_o, g_q, g_k, pos_part, dy_loc):
        nb, _, dim = x_loc.shape
        cos_tab, sin_tab = rope_tables(pos_part)
        y_full, d_own, q, k, v, ss = gather_qkv_call(tp_size, x_loc, dy_loc, m_block, e_loc, w_q, w_k, w_v, b_q, b_k, b_v)
        d_full, o, o_p, d_attn, wq_p, wk_p, wv_p, wo_p = gather_attn_call(
            tp_size, q, k, v, g_q, g_k, cos_tab, sin_tab, ss, w_q, w_k, w_v, w_o, d_own)
        proj, g, g_p, _, _, d_wo, d_gq, d_gk = proj_bwd_call(
            tp_size, q, k, v, d_attn, g_q, g_k, cos_tab, sin_tab, ss, o, o_p, w_o, wo_p, d_full)
        d_y, d_wq, d_wk, d_wv = dy_dw_call(tp_size, g, g_p, w_q, w_k, w_v, wq_p, wk_p, wv_p, y_full)
        x_out, d_x, d_mod = token_call(x_loc, dy_loc, proj, d_y, m_block, e_loc, b_o)
        d_e = all_sum_call(tp_size, d_mod.reshape(tp_size, -1, HEAD_DIM)).reshape(nb, 3, dim)
        return (x_out, d_x, d_e, jnp.sum(d_e, axis=0), d_wq, d_wk, d_wv, d_wo,
                jnp.sum(d_gq, axis=(0, 1)), jnp.sum(d_gk, axis=(0, 1)))

    in_specs = (P('dp', 'tp', None), P('dp', None, None), P(None, None), P(None, 'tp'), P('tp'), P(None, 'tp'), P('tp'),
                P(None, 'tp'), P('tp'), P('tp', None), P(None), P('tp'), P('tp'), P('dp', None), P('dp', 'tp', None))
    out_specs = (P('dp', 'tp', None), P('dp', 'tp', None), P('dp', None, None), P('dp', None), P('dp', 'tp'), P('dp', 'tp'),
                 P('dp', 'tp'), P(('dp', 'tp'), None), P(('dp', 'tp')), P(('dp', 'tp')))
    return jax.shard_map(device_step, mesh=mesh, in_specs=in_specs, out_specs=out_specs, check_vma=False)
```

time: 611 us -> 568 us (0.930)
  waiting for transfers between devices: 57.7 us -> 0 us
  Pallas kernels: 519 us -> 537 us
  between operations: 14.2 us -> 0.77 us
  local copies, waits for them, and re-layouts: 11.6 us -> 23.2 us
    reduce_scatter x2 -> x0, waiting for transfers between devices: 57.5 us -> none  [the longest x1 57.5 us: device_step(): d_y = lax.psum_scatter(dy_part, 'tp', scatter_dimension=1, tiled=True)]
    pallas_call x8 -> x4, Pallas kernels: 252 us -> 302 us  [the longest x1 143 us: proj_bwd_call(): pl.pallas_call(functools.partial(proj_bwd_kernel, n, nb, heads, dim), nam...]
    pallas_call x1, Pallas kernels: 140 us -> 108 us  [gather_attn_call(): pl.pallas_call(functools.partial(gather_attn_kernel, n, nb, heads, dim),...]
    unnamed x9 -> x18, local copies, waits for them, and re-layouts: 6.71 us -> 18.9 us
  transfers between devices with their start and end apart: 2 -> 0, of which waited for: 1 -> 0; matrix products, arithmetic and copies ran while one was open for 0% -> 0% of each run, Pallas kernels for 32% -> 0%
where the time goes in v3:
time: 568 us; the launch traced here: 567 us
  Pallas kernels  537 us (95%)
  local copies, waits for them, and re-layouts  23.2 us (4%)
  other arithmetic  5.93 us (1%)
    pallas_call x1, Pallas kernels, proj_bwd_call(): pl.pallas_call(functools.partial(proj_bwd_kernel, n, nb, heads, dim), nam...  143 us
    pallas_call x1, Pallas kernels, dy_dw_call(): pl.pallas_call(functools.partial(dy_dw_kernel, n, nb, dim), name='dy_dw',...  135 us
    pallas_call x1, Pallas kernels, gather_qkv_call(): pl.pallas_call(functools.partial(gather_qkv_kernel, n), name='gather_qkv'...  126 us
    pallas_call x1, Pallas kernels, gather_attn_call(): pl.pallas_call(functools.partial(gather_attn_kernel, n, nb, heads, dim),...  108 us
    unnamed x18, local copies, waits for them, and re-layouts  18.9 us
    pallas_call x1, Pallas kernels, token_call(): pl.pallas_call(token_kernel, name='tokens', grid=(nb,), out_shape=[jax.Sh...  12.8 us
    pallas_call x1, Pallas kernels, all_sum_call(): pl.pallas_call(functools.partial(all_sum_kernel, n), name='all_sum', out_...  12 us

profile of v3, /device:TPU:81, one launch (start us, length us, event | category | flops | bytes accessed | tf_op | source)
XLA Modules:
  0.0 566.8 jit_solution(13889347722410779332)
XLA Ops:
  0.7 1.3 broadcast_in_dim.51.gq_ref
  2.0 1.3 broadcast_in_dim.52.gk_ref
  3.2 0.7 pad_maximum_fusion
  4.0 0.6 broadcast_in_dim.50.bias_ref
  4.6 0.7 convert_element_type.37
  5.3 0.4 multiply_reduce_fusion
  5.6 2.2 sine_multiply_fusion
  7.8 126.4 %gather_qkv.1 = (bf16[3,768,5120]{2,1,0:T(8,128)(2,1)}, bf16[3,768,5120]{2,1,0:T(8,128)(2,1)}, f32[3,768,640]{2,1,0:T(8,128)}, f32[3,768,640]{2,1,0:T(8,128)}, b...) custom-call(bf16[3,96,5120]{2,1,0:T(8,128)(2,1)} %x_ref.3, bf16[3,96,5120]{2,1,0:T(8,128)(2,1)} %dy_ref.3, f32[3,5120]{1,0:T(4,128)} %m_ref.3, ...), custom_call_target="tpu_custom_call" | custom-call | flops 45298483200 | bytes 40304640 | tf_op jit(solution)/shard_map/gather_qkv/pallas_call | solution.py:302
  134.2 108.0 %gather_attn.1 = (bf16[3,768,5120]{2,1,0:T(8,128)(2,1)}, bf16[3,768,640]{2,1,0:T(8,128)(2,1)}, bf16[3,768,640]{2,1,0:T(8,128)(2,1)}, bf16[3,768,640]{2,1,0:T(8,1...) custom-call(f32[3,768,640]{2,1,0:T(8,128)} %get-tuple-element.37.q_r, ...), custom_call_target="tpu_custom_call", output_to_operand_aliasing={{0}: (12, {})} | custom-call | flops 19629342720 | bytes 94371840 | tf_op jit(solution)/shard_map/gather_attn/pallas_call | solution.py:500
  242.3 142.9 %proj_bwd.1 = (bf16[3,96,5120]{2,1,0:T(8,128)(2,1)}, bf16[3,768,1920]{2,1,0:T(8,128)(2,1)}, bf16[3,768,1920]{2,1,0:T(8,128)(2,1)}, f32[3,768,640]{2,1,0:T(8,128)...) custom-call(f32[3,768,640]{2,1,0:T(8,128)} %get-tuple-element.37.q_ref.q_hbm, ...), custom_call_target="tpu_custom_call" | custom-call | flops 70967623680 | bytes 44236800 | tf_op jit(solution)/shard_map/proj_bwd/pallas_call | solution.py:861
  385.2 0.0 copy-start.2
  385.2 0.0 copy-start.1
  385.2 134.8 %dy_dw.1 = (bf16[3,96,5120]{2,1,0:T(8,128)(2,1)}, bf16[5120,640]{1,0:T(8,128)(2,1)}, bf16[5120,640]{1,0:T(8,128)(2,1)}, bf16[5120,640]{1,0:T(8,128)(2,1)}) custom-call(bf16[3,768,1920]{2,1,0:T(8,128)(2,1)} %get-tuple-element.48.g_hbm, bf16[3,768,1920]{2,1,0:T(8,128)(2,1)} %get-tuple-element.49.g_p, bf16[5120,640]{1,0:T(8,128)(2,1)} %wq_hbm.1, ...), custom_call_target="tpu_custom_call" | custom-call | flops 90596966400 | bytes 44236800 | tf_op jit(solution)/shard_map/dy_dw/pallas_call | solution.py:990
  520.1 0.0 copy-done.2
  520.1 0.6 reduce_sum.38
  520.7 0.0 copy-done.1
  520.7 0.6 reduce_sum.39
  521.3 12.8 %tokens.1 = (bf16[3,96,5120]{2,1,0:T(8,128)(2,1)}, bf16[3,96,5120]{2,1,0:T(8,128)(2,1)}, f32[3,3,5120]{2,1,0:T(4,128)}) custom-call(bf16[3,96,5120]{2,1,0:T(8,128)(2,1)} %x_ref.3, bf16[3,96,5120]{2,1,0:T(8,128)(2,1)} %dy_ref.3, bf16[3,96,5120]{2,1,0:T(8,128)(2,1)} %get-tuple-element.47.pr_ref, bf16[3,96,5120]{2,1,0:T(8,128)(2,1)} %get-tuple-element.54.g_ref, ...), custom_call_target="tpu_custom_call" | custom-call | flops 44236800 | bytes 17694720 | tf_op jit(solution)/shard_map/tokens/pallas_call | solution.py:1021
  534.0 1.0 reshape.105.x_ref
  535.1 12.0 %all_sum.1 = f32[8,45,128]{2,1,0:T(8,128)S(1)} custom-call(f32[8,45,128]{2,1,0:T(8,128)S(1)} %reshape.105.x_ref), custom_call_target="tpu_custom_call" | custom-call | flops 4000000000 | bytes 368640 | tf_op jit(solution)/shard_map/all_sum/pallas_call | solution.py:353
  547.1 0.1 reshape.106
  547.2 0.0 copy-start
  547.2 0.7 reduce_sum.37
  547.9 0.0 slice-start.2
  547.9 6.4 %copy.33 = bf16[5120,640]{1,0:T(8,128)(2,1)} copy(bf16[5120,640]{1,0:T(8,128)(2,1)} %get-tuple-element.80) | data formatting | bytes 13107200
  554.3 0.0 copy-done
  554.3 0.0 slice-start.3
  554.3 0.0 slice-start
  554.3 6.4 %copy.34 = bf16[5120,640]{1,0:T(8,128)(2,1)} copy(bf16[5120,640]{1,0:T(8,128)(2,1)} %get-tuple-element.81) | data formatting | bytes 13107200
  560.6 0.0 slice-done.2
  560.6 0.0 slice-done.3
  560.6 0.0 slice-start.1
  560.6 3.0 copy.35
  563.7 0.0 slice-done
  563.7 0.3 slice-done.1
  564.0 2.8 copy.36
  (6 shorter events, 0.0 us)
Async XLA Ops:
  385.2 134.9 %copy-start.2 = (f32[3,1,640]{2,1,0:T(1,128)S(1)}, f32[3,1,640]{2,1,0:T(1,128)}, u32[]{:S(2)}) copy-start(f32[3,1,640]{2,1,0:T(1,128)} %get-tuple-element.62) | copy-start | bytes 23044
  385.2 135.5 %copy-start.1 = (f32[3,1,640]{2,1,0:T(1,128)S(1)}, f32[3,1,640]{2,1,0:T(1,128)}, u32[]{:S(2)}) copy-start(f32[3,1,640]{2,1,0:T(1,128)} %get-tuple-element.63) | copy-start | bytes 23044
  547.2 7.1 %copy-start = (f32[3,3,5120]{2,1,0:T(4,128)}, f32[3,3,5120]{2,1,0:T(4,128)S(1)}, u32[]{:S(2)}) copy-start(f32[3,3,5120]{2,1,0:T(4,128)S(1)} %reshape.106) | copy-start | bytes 552964
  547.9 12.7 %slice-start.2 = ((s8[6553600]{0:T(1024)(128)(4,1)}), s8[4194304]{0:T(1024)(128)(4,1)S(1)}, s32[]{:S(2)}) async-start(s8[6553600]{0:T(1024)(128)(4,1)} %bitcast.3), calls=%async_computation.2 | async-start | bytes 8388608
  554.3 6.4 %slice-start.3 = ((s8[6553600]{0:T(1024)(128)(4,1)}), s8[2359296]{0:T(1024)(128)(4,1)S(1)}, s32[]{:S(2)}) async-start(s8[6553600]{0:T(1024)(128)(4,1)} %bitcast.3), calls=%async_computation.3 | async-start | bytes 4718592
  554.3 9.4 %slice-start = ((s8[6553600]{0:T(1024)(128)(4,1)}), s8[4194304]{0:T(1024)(128)(4,1)S(1)}, s32[]{:S(2)}) async-start(s8[6553600]{0:T(1024)(128)(4,1)} %bitcast.1), calls=%async_computation | async-start | bytes 8388608
  560.6 3.4 slice-start.1

commit v4 on v3

--- a/solution.py
+++ b/solution.py
@@ -2,6 +2,7 @@
 
 import jax
 import jax.numpy as jnp
+import numpy as np
 from jax import lax
 from jax.experimental import pallas as pl
 from jax.experimental.pallas import tpu as pltpu
@@ -28,19 +29,17 @@
     return pl.CostEstimate(flops=int(flops), bytes_accessed=int(nbytes), transcendentals=0)
 
 
-def rope_tables(positions):
+def rope_freqs():
     half_dim = HEAD_DIM // 2
     side_len = HEAD_DIM // 6
     first_len = half_dim - 2 * side_len
-    lane = jnp.arange(HEAD_DIM)
-    pair_idx = lane // 2
-    section = (pair_idx >= first_len).astype(jnp.int32) + (pair_idx >= first_len + side_len).astype(jnp.int32)
-    offset = jnp.where(section == 0, 0, jnp.where(section == 1, first_len, first_len + side_len))
-    sec_width = jnp.where(section == 0, first_len, side_len)
-    freq_vals = ROPE_BASE ** (-(pair_idx - offset).astype(F32) / sec_width.astype(F32))
-    select = jnp.where(section[None, :] == jnp.arange(3)[:, None], freq_vals[None, :], 0.0)
-    angles = jnp.sum(positions.astype(F32)[:, :, None] * select[None, :, :], axis=1)
-    return jnp.cos(angles), jnp.where((lane % 2 == 0)[None, :], -1.0, 1.0) * jnp.sin(angles)
+    pair_idx = np.arange(HEAD_DIM) // 2
+    section = (pair_idx >= first_len).astype(np.int32) + (pair_idx >= first_len + side_len).astype(np.int32)
+    offset = np.where(section == 0, 0, np.where(section == 1, first_len, first_len + side_len))
+    sec_width = np.where(section == 0, first_len, side_len)
+    exponent = -(pair_idx - offset).astype(np.float32) / sec_width.astype(np.float32)
+    freq_vals = np.power(np.float32(ROPE_BASE), exponent)
+    return np.where(section[None, :] == np.arange(3)[:, None], freq_vals[None, :], np.float32(0.0)).astype(np.float32)
 
 
 def norm_stats(x):
@@ -168,26 +167,31 @@
     return [(c, min(c + step, width)) for c in range(0, width, step)]
 
 
-def exchange(place, x_ref, slots, send_sems, recv_sems):
-    n, me = place.n, place.me
-    for d, dev in enumerate(place.everyone()):
-        pltpu.make_async_remote_copy(src_ref=x_ref, dst_ref=slots.at[me], send_sem=send_sems.at[d], recv_sem=recv_sems.at[me],
-                                     device_id={'tp': dev}, device_id_type=MESH_ID).start()
-    slots[me] = x_ref[...]
-    for d, dev in enumerate(place.everyone()):
-        copy = pltpu.make_async_remote_copy(src_ref=x_ref, dst_ref=slots.at[dev], send_sem=send_sems.at[d], recv_sem=recv_sems.at[dev],
+class Exchange:
+    def __init__(self, place, x_ref, slots, send_sems, recv_sems):
+        self.at, self.x, self.slots, self.send, self.recv = place, x_ref, slots, send_sems, recv_sems
+
+    def copy(self, d, dev, src):
+        return pltpu.make_async_remote_copy(src_ref=self.x, dst_ref=self.slots.at[src], send_sem=self.send.at[d], recv_sem=self.recv.at[src],
                                             device_id={'tp': dev}, device_id_type=MESH_ID)
-        copy.wait_send()
-        copy.wait_recv()
-    total = slots[0]
-    for d in range(1, n):
-        total = total + slots[d]
-    return total
-
-
-def gather_qkv_kernel(n, x_ref, dy_ref, m_ref, e_ref, wq_ref, wk_ref, wv_ref, bias_ref,
-                      y_full, d_full, q_out, k_out, v_out, ss_ref,
-                      w_all, xin, stage, xbuf, zst, vst, sq, ss_row, slots,
+
+    def start(self):
+        for d, dev in enumerate(self.at.everyone()):
+            self.copy(d, dev, self.at.me).start()
+        self.slots[self.at.me] = self.x[...]
+
+    def finish(self):
+        for d, dev in enumerate(self.at.everyone()):
+            self.copy(d, dev, dev).wait()
+        total = self.slots[0]
+        for d in range(1, self.at.n):
+            total = total + self.slots[d]
+        return total
+
+
+def gather_qkv_kernel(n, x_ref, dy_ref, m_ref, e_ref, wq_ref, wk_ref, wv_ref, bq_ref, bk_ref, bv_ref, gq_ref, gk_ref, pos_ref, freq_ref,
+                      y_full, d_full, q_out, k_out, v_out, ss_ref, cos_ref, sin_ref, gain_ref,
+                      bias_ref, w_all, xin, stage, xbuf, zst, vst, sq, ss_row, slots,
                       w_sem, in_sem, st_sem, ld_sem, out_sem, g_send, g_recv, e_send, e_recv):
     nb, rows, dim = x_ref.shape
     cols = wq_ref.shape[1]
@@ -226,6 +230,23 @@
     lax.fori_loop(0, nb, ln_step, 0)
     load_dy = pltpu.make_async_copy(dy_ref, xin, in_sem)
     load_dy.start()
+    for j, ref in enumerate((bq_ref, bk_ref, bv_ref)):
+        bias_ref[:, j * cols:(j + 1) * cols] = ref[...].reshape(1, cols)
+    for j, ref in enumerate((gq_ref, gk_ref)):
+        gain_ref[j:j + 1] = ref[...].reshape(1, cols)
+
+    def tables():
+        lane = lax.broadcasted_iota(jnp.int32, (128, HEAD_DIM), 1)
+
+        def rows_of(r, _):
+            sl = pl.ds(pl.multiple_of(r * 128, 128), 128)
+            pos = pos_ref[sl].astype(F32)
+            angle = pos[:, 0:1] * freq_ref[0:1] + pos[:, 1:2] * freq_ref[1:2] + pos[:, 2:3] * freq_ref[2:3]
+            cos_ref[sl] = jnp.cos(angle)
+            sin_ref[sl] = jnp.where(lane % 2 == 0, -1.0, 1.0) * jnp.sin(angle)
+            return 0
+
+        lax.fori_loop(0, pos_ref.shape[0] // 128, rows_of, 0)
 
     def gate_step(b, _):
         gate = m_ref[2:3] + e_ref[b, 2:3]
@@ -260,6 +281,7 @@
         def _():
             load_dy.wait()
             lax.fori_loop(0, nb, gate_step, 0)
+            tables()
 
         @pl.when(i >= 2)
         def _():
@@ -282,15 +304,17 @@
     ss_row[...] = jnp.zeros_like(ss_row)
     for j in range(2 * nb):
         ss_row[j:j + 1] = to_row(sq[j])
+    sums = Exchange(place, ss_row, slots, e_send, e_recv)
+    sums.start()
     for slot in range(2):
         for c in outputs(0, 0, slot):
             c.wait()
     for b in range(nb):
         gather.finish(b)
-    ss_ref[...] = exchange(place, ss_row, slots, e_send, e_recv)
-
-
-def gather_qkv_call(n, x_loc, dy_loc, m_block, e_loc, w_q, w_k, w_v, b_q, b_k, b_v):
+    ss_ref[...] = sums.finish()
+
+
+def gather_qkv_call(n, x_loc, dy_loc, m_block, e_loc, w_q, w_k, w_v, b_q, b_k, b_v, g_q, g_k, positions):
     nb, rows, dim = x_loc.shape
     cols = w_q.shape[1]
     tokens = rows * n
@@ -302,17 +326,19 @@
     return pl.pallas_call(
         functools.partial(gather_qkv_kernel, n), name="gather_qkv",
         out_shape=[shape((nb, tokens, dim), BF16), shape((nb, tokens, dim), BF16), shape((nb, tokens, cols), F32),
-                   shape((nb, tokens, cols), F32), shape((nb, tokens, cols), BF16), shape((stat_rows, tokens), F32)],
-        in_specs=[any_spec, any_spec, vmem, vmem, any_spec, any_spec, any_spec, vmem],
-        out_specs=[any_spec] * 5 + [vmem],
+                   shape((nb, tokens, cols), F32), shape((nb, tokens, cols), BF16), shape((stat_rows, tokens), F32),
+                   shape((tokens, HEAD_DIM), F32), shape((tokens, HEAD_DIM), F32), shape((2, cols), F32)],
+        in_specs=[any_spec, any_spec, vmem, vmem, any_spec, any_spec, any_spec] + [vmem] * 7,
+        out_specs=[any_spec] * 5 + [vmem] * 4,
         scratch_shapes=[
+            pltpu.VMEM((1, 3 * cols), F32),
             pltpu.VMEM((dim, 3 * cols), BF16), pltpu.VMEM((nb, rows, dim), BF16), pltpu.VMEM((nb, rows, dim), BF16),
             pltpu.VMEM((2 * rows, dim), BF16), pltpu.VMEM((2, 2 * rows, 3 * cols), F32), pltpu.VMEM((2, 2 * rows, cols), BF16),
             pltpu.VMEM((2 * nb, tokens, HEAD_DIM), F32), pltpu.VMEM((stat_rows, tokens), F32), pltpu.VMEM((n, stat_rows, tokens), F32),
             dma((3,)), dma, dma, dma, dma((2, 3)), dma((nb, GATHER_SEMS)), dma((nb, GATHER_SEMS)), dma((n,)), dma((n,))],
         compiler_params=params(collective_id=0, has_side_effects=True),
         cost_estimate=cost(6 * nb * tokens * dim * cols, 6 * dim * cols + 14 * nb * tokens * cols),
-    )(x_loc, dy_loc, m_block, e_loc, w_q, w_k, w_v, jnp.concatenate([b_q, b_k, b_v])[None])
+    )(x_loc, dy_loc, m_block, e_loc, w_q, w_k, w_v, b_q, b_k, b_v, g_q, g_k, positions, jnp.asarray(rope_freqs()))
 
 
 def all_sum_kernel(n, x_ref, o_ref, pieces, total, send_a, recv_a, send_b, recv_b):
@@ -375,7 +401,7 @@
     return p * (1.0 / jnp.sum(p, axis=1, keepdims=True))
 
 
-def gather_attn_kernel(n, nb, heads, dim, q_ref, k_ref, v_ref, gq_ref, gk_ref, cos_ref, sin_ref, ss_ref,
+def gather_attn_kernel(n, nb, heads, dim, q_ref, k_ref, v_ref, gain_ref, cos_ref, sin_ref, ss_ref,
                        wq_ref, wk_ref, wv_ref, wo_ref, d_in,
                        d_full, o_out, o_p, da_out, wq_p, wk_p, wv_p, wo_p,
                        inv_q, inv_k, o_all, wo, xbuf, ast,
@@ -416,8 +442,8 @@
             inv_k[...] = lanes_of(lax.rsqrt(ss_ref[pl.ds(2 * b + 1, 1)] / dim + EPS_NORM))
 
         cos, sin = cos_ref[...], sin_ref[...]
-        q_rot = rotate(q_ref[0] * inv_q[...] * gq_ref[...], cos, sin).astype(BF16)
-        k_rot = rotate(k_ref[0] * inv_k[...] * gk_ref[...], cos, sin).astype(BF16)
+        q_rot = rotate(q_ref[0] * inv_q[...] * gain_ref[0:1], cos, sin).astype(BF16)
+        k_rot = rotate(k_ref[0] * inv_k[...] * gain_ref[1:2], cos, sin).astype(BF16)
         v = v_ref[0]
         lanes = pl.ds(pl.multiple_of(h * HEAD_DIM, HEAD_DIM), HEAD_DIM)
         for i in range(tokens // blk):
@@ -479,7 +505,7 @@
             trade(j).wait()
 
 
-def gather_attn_call(n, q, k, v, g_q, g_k, cos_tab, sin_tab, ss, w_q, w_k, w_v, w_o, d_full):
+def gather_attn_call(n, q, k, v, gains, cos_tab, sin_tab, ss, w_q, w_k, w_v, w_o, d_full):
     nb, tokens, cols = q.shape
     dim = w_o.shape[1]
     heads = cols // HEAD_DIM
@@ -494,22 +520,22 @@
         return i // heads, i % heads
 
     blk = pl.BlockSpec((1, tokens, HEAD_DIM), lambda i: (head_of(i)[0], 0, head_of(i)[1]))
-    vec = pl.BlockSpec((1, HEAD_DIM), lambda i: (0, head_of(i)[1]))
+    vec = pl.BlockSpec((2, HEAD_DIM), lambda i: (0, head_of(i)[1]))
     tab = pl.BlockSpec((tokens, HEAD_DIM), lambda i: (0, 0))
     head_arr = shape((nb, tokens, cols), BF16)
     return pl.pallas_call(
         functools.partial(gather_attn_kernel, n, nb, heads, dim), name="gather_attn", grid=(nb * heads + 1,),
         out_shape=[shape(d_full.shape, BF16), head_arr, head_arr, head_arr] + [shape(w.shape, BF16) for w in (w_q, w_k, w_v, w_o)],
-        in_specs=[blk, blk, blk, vec, vec, tab, tab, pl.BlockSpec(ss.shape, lambda i: (0, 0))] + [any_spec] * 5,
+        in_specs=[blk, blk, blk, vec, tab, tab, pl.BlockSpec(ss.shape, lambda i: (0, 0))] + [any_spec] * 5,
         out_specs=[any_spec] * 8,
         scratch_shapes=[
             pltpu.VMEM((tokens, HEAD_DIM), F32), pltpu.VMEM((tokens, HEAD_DIM), F32), pltpu.VMEM((nb, tokens, cols), BF16),
             pltpu.VMEM((cols, dim), BF16), pltpu.VMEM((2, 2 * rows, dim), BF16), pltpu.VMEM((2, 2 * rows, cols), BF16),
             dma, dma((2,)), dma((2,)), dma, dma((nb, GATHER_SEMS)), dma((nb, GATHER_SEMS)), dma((5,)), dma((5,))],
-        input_output_aliases={12: 0},
+        input_output_aliases={11: 0},
         compiler_params=params("arbitrary", collective_id=1, has_side_effects=True),
         cost_estimate=cost(2 * nb * tokens * dim * cols + 4 * nb * tokens * tokens * cols, 8 * nb * tokens * dim),
-    )(q, k, v, g_q[None], g_k[None], cos_tab, sin_tab, ss, w_q, w_k, w_v, w_o, d_full)
+    )(q, k, v, gains, cos_tab, sin_tab, ss, w_q, w_k, w_v, w_o, d_full)
 
 
 class Scatter:
@@ -534,9 +560,14 @@
             lambda: (part.at[j, 2, second], side.at[j, 1, second], p.left))[idx]()
         return self.copy(j, idx, src, dst, target)
 
-    def start(self, j):
-        for idx in range(4):
+    def start_far(self, j):
+        for idx in (0, 1):
             self.message(j, idx).start()
+
+    def start_side(self, j, _):
+        for idx in (2, 3):
+            self.message(j, idx).start()
+        return 0
 
     def sums(self, j):
         h = self.half
@@ -600,7 +631,7 @@
     return out
 
 
-def proj_bwd_kernel(n, nb, heads, dim, q_ref, k_ref, v_ref, do_ref, gq_ref, gk_ref, cos_ref, sin_ref, ss_ref,
+def proj_bwd_kernel(n, nb, heads, dim, q_ref, k_ref, v_ref, do_ref, gain_ref, cos_ref, sin_ref, ss_ref,
                     q_hbm, k_hbm, o_hbm, o_p, wo_hbm, wo_p, d_full,
                     proj_out, g_out, g_p, dqs_out, dks_out, dwo_out, dgq_ref, dgk_ref,
                     part, recv_far, recv_side, s_send, s_recv,
@@ -650,7 +681,7 @@
                     z = jnp.dot(lhs[d * half:(d + 1) * half], w, preferred_element_type=F32).astype(BF16)
                     part[j, 2 * d] = z[:half // 2]
                     part[j, 2 * d + 1] = z[half // 2:]
-                scatter.start(j)
+                scatter.start_far(j)
                 return 0
 
             lax.fori_loop(0, nc, body, 0)
@@ -691,8 +722,8 @@
                 c.wait()
 
         cos, sin = cos_ref[...], sin_ref[...]
-        q_rot = rotate(q_ref[0] * inv_q[...] * gq_ref[...], cos, sin).astype(BF16)
-        k_rot = rotate(k_ref[0] * inv_k[...] * gk_ref[...], cos, sin).astype(BF16)
+        q_rot = rotate(q_ref[0] * inv_q[...] * gain_ref[0:1], cos, sin).astype(BF16)
+        k_rot = rotate(k_ref[0] * inv_k[...] * gain_ref[1:2], cos, sin).astype(BF16)
         v = v_ref[0]
         do = do_ref[0]
         for i in range(tokens // blk):
@@ -715,8 +746,8 @@
         k_hat = k_ref[0] * inv_k[...]
         dgq_ref[0] = jnp.sum(dq_hat * q_hat, axis=0, keepdims=True)
         dgk_ref[0] = jnp.sum(dk_hat * k_hat, axis=0, keepdims=True)
-        dq_s = dq_hat * gq_ref[...]
-        dk_s = dk_hat * gk_ref[...]
+        dq_s = dq_hat * gain_ref[0:1]
+        dk_s = dk_hat * gain_ref[1:2]
         qs_st[slot] = dq_s
         ks_st[slot] = dk_s
         acc_q[...] += dq_s * q_hat
@@ -734,7 +765,10 @@
         for s in (steps - 1, steps):
             for c in flush(0, 0, s % 2):
                 c.wait()
-        st_sum[...] = exchange(place, st_row, slots, e_send, e_recv)
+        stats = Exchange(place, st_row, slots, e_send, e_recv)
+        stats.start()
+        lax.fori_loop(0, nc, scatter.start_side, 0)
+        st_sum[...] = stats.finish()
         rb = min(256, tokens)
         per = tokens // rb
         trade = place.to_partner(g_out, g_p, t_send, t_recv)
@@ -838,7 +872,7 @@
         trade.wait()
 
 
-def proj_bwd_call(n, q, k, v, d_attn, g_q, g_k, cos_tab, sin_tab, ss, o, o_p, w_o, wo_p, d_full):
+def proj_bwd_call(n, q, k, v, d_attn, gains, cos_tab, sin_tab, ss, o, o_p, w_o, wo_p, d_full):
     nb, tokens, cols = q.shape
     dim = w_o.shape[1]
     heads = cols // HEAD_DIM
@@ -853,7 +887,7 @@
         return i // heads, i % heads
 
     blk = pl.BlockSpec((1, tokens, HEAD_DIM), lambda i: (head_of(i)[0], 0, head_of(i)[1]))
-    vec = pl.BlockSpec((1, HEAD_DIM), lambda i: (0, head_of(i)[1]))
+    vec = pl.BlockSpec((2, HEAD_DIM), lambda i: (0, head_of(i)[1]))
     out_vec = pl.BlockSpec((1, 1, HEAD_DIM), lambda i: (head_of(i)[0], 0, head_of(i)[1]))
     tab = pl.BlockSpec((tokens, HEAD_DIM), lambda i: (0, 0))
     whole = (nb, tokens, cols)
@@ -862,7 +896,7 @@
         functools.partial(proj_bwd_kernel, n, nb, heads, dim), name="proj_bwd", grid=(steps + 2,),
         out_shape=[shape((nb, rows, dim), BF16), shape((nb, tokens, 3 * cols), BF16), shape((nb, tokens, 3 * cols), BF16),
                    shape(whole, F32), shape(whole, F32), shape((cols, dim), BF16), shape((nb, 1, cols), F32), shape((nb, 1, cols), F32)],
-        in_specs=[blk, blk, blk, blk, vec, vec, tab, tab, pl.BlockSpec(ss.shape, lambda i: (0, 0))] + [any_spec] * 7,
+        in_specs=[blk, blk, blk, blk, vec, tab, tab, pl.BlockSpec(ss.shape, lambda i: (0, 0))] + [any_spec] * 7,
         out_specs=[any_spec] * 6 + [out_vec, out_vec],
         scratch_shapes=Scatter.scratch(nb * rows, dim) + [lane_tile] * 4 + [pltpu.VMEM((tokens, tokens), BF16)] * 2 + [
             lane_tile, pltpu.VMEM((2, tokens, HEAD_DIM), F32), pltpu.VMEM((2, tokens, HEAD_DIM), F32),
@@ -870,7 +904,7 @@
             dma((1,)), dma((2, 2)), dma((2, 3)), dma((2, 4)), dma((2,)), dma((nb,)), dma((n,)), dma((n,)), dma, dma],
         compiler_params=params("arbitrary", collective_id=2, has_side_effects=True),
         cost_estimate=cost(4 * nb * tokens * dim * cols + 36 * nb * tokens * tokens * cols, 30 * nb * tokens * cols),
-    )(q, k, v, d_attn, g_q[None], g_k[None], cos_tab, sin_tab, ss, q, k, o, o_p, w_o, wo_p, d_full)
+    )(q, k, v, d_attn, gains, cos_tab, sin_tab, ss, q, k, o, o_p, w_o, wo_p, d_full)
 
 
 def dy_dw_kernel(n, nb, dim, g_hbm, g_p, wq_hbm, wk_hbm, wv_hbm, wq_p, wk_p, wv_p, y_full,
@@ -882,7 +916,7 @@
     nc = dim // CHUNK
     place = Place(n)
     scatter = Scatter(place, part, recv_far, recv_side, s_send, s_recv)
-    lag = 2
+    lag = 4
 
     def chain(lhs, wbuf):
         loads = pair_rows(place, nb, rows, g_hbm, g_p, lhs, ld_sem)
@@ -915,7 +949,7 @@
                 z = lax.dot_general(lhs[d * half:(d + 1) * half], w, NT, preferred_element_type=F32).astype(BF16)
                 part[j, 2 * d] = z[:half // 2]
                 part[j, 2 * d + 1] = z[half // 2:]
-            scatter.start(j)
+            scatter.start_far(j)
 
             @pl.when(j >= lag)
             def _():
@@ -924,6 +958,7 @@
             return 0
 
         lax.fori_loop(0, nc, body, 0)
+        lax.fori_loop(0, nc, scatter.start_side, 0)
 
     pl.run_scoped(chain, pltpu.VMEM((4 * nb * rows, 6 * cols), BF16), pltpu.VMEM((2, CHUNK, 6 * cols), BF16))
 
@@ -961,7 +996,7 @@
             chunk(c).wait()
             for m in range(lag):
                 late = nc - lag + m
-                pl.when(c == min(1 + 2 * m, n_chunks - 1))(functools.partial(scatter.sums, max(late, 0)) if late >= 0 else (lambda: None))
+                pl.when(c == min(m, n_chunks - 1))(functools.partial(scatter.sums, max(late, 0)) if late >= 0 else (lambda: None))
             wst[slot] = lax.dot_general(ybuf[slot].reshape(nb * tokens, bm), g[...].reshape(nb * tokens, 3 * cols), TN,
                                         preferred_element_type=F32).astype(BF16)
             for s in store(c):
@@ -997,36 +1032,105 @@
     )(g, g_p, w_q, w_k, w_v, wq_p, wk_p, wv_p, y_full)
 
 
-def token_kernel(x_ref, dy_ref, pr_ref, g_ref, m_ref, e_ref, bo_ref, xo_ref, dx_ref, dm_ref):
+def token_kernel(n_copies, x_ref, dy_ref, pr_ref, g_ref, m_ref, e_ref, bo_ref, *refs):
+    srcs, (xo_ref, dx_ref, dm_ref), dsts = refs[:4], refs[4:7], refs[7:11]
+    bufs, (acc, in_sem, out_sem) = refs[11:15], refs[15:]
+    group = 16
+    step = pl.program_id(0)
+    rows = x_ref.shape[1]
+    groups = rows // group
+    depth = bufs[0].shape[0]
+    lag = depth - 1
+
+    def move(c, out):
+        copies = []
+        for j, (src, dst, buf) in enumerate(zip(srcs, dsts, bufs)):
+            size = buf.shape[1]
+            sl = pl.ds(pl.multiple_of(c * size, 16), size)
+            slot = lax.rem(c, depth)
+            copies.append(pltpu.make_async_copy(buf.at[slot], dst.at[sl], out_sem.at[slot, j]) if out
+                          else pltpu.make_async_copy(src.at[sl], buf.at[slot], in_sem.at[slot, j]))
+        return copies
+
+    def advance(i):
+        @pl.when(i < n_copies)
+        def _():
+            @pl.when(i >= depth)
+            def _():
+                for c in move(i - depth, True):
+                    c.wait()
+
+            for c in move(i, False):
+                c.start()
+
+        @pl.when((i >= lag) & (i < n_copies + lag))
+        def _():
+            for c in move(i - lag, False):
+                c.wait()
+            for c in move(i - lag, True):
+                c.start()
+
     mod = m_ref[...] + e_ref[0]
-    x = x_ref[0].astype(F32)
-    d_out = dy_ref[0].astype(F32)
-    proj = pr_ref[0].astype(F32) + bo_ref[...]
-    xo_ref[0] = (x + mod[2:3] * proj).astype(BF16)
-    x_norm, inv_std = norm_stats(x)
-    d_y = g_ref[0].astype(F32)
-    d_norm = d_y * (1.0 + mod[1:2])
-    d_x = d_out + inv_std * (
-        d_norm - jnp.mean(d_norm, axis=-1, keepdims=True) - x_norm * jnp.mean(d_norm * x_norm, axis=-1, keepdims=True))
-    dx_ref[0] = d_x.astype(BF16)
-    dm_ref[0, 0:1] = jnp.sum(d_y, axis=0, keepdims=True)
-    dm_ref[0, 1:2] = jnp.sum(d_y * x_norm, axis=0, keepdims=True)
-    dm_ref[0, 2:3] = jnp.sum(d_out * proj, axis=0, keepdims=True)
-
-
-def token_call(x_loc, dy_loc, proj, d_y, m_block, e_loc, b_o):
+    shift_bo = bo_ref[...].reshape(1, bo_ref.shape[0])
+    acc[...] = jnp.zeros_like(acc)
+
+    def body(r, _):
+        advance(step * groups + r)
+        sl = pl.ds(pl.multiple_of(r * group, group), group)
+        x = x_ref[0, sl].astype(F32)
+        d_out = dy_ref[0, sl].astype(F32)
+        proj = pr_ref[0, sl].astype(F32) + shift_bo
+        xo_ref[0, sl] = (x + mod[2:3] * proj).astype(BF16)
+        gate_part = d_out * proj
+        x_norm, inv_std = norm_stats(x)
+        d_y = g_ref[0, sl].astype(F32)
+        d_norm = d_y * (1.0 + mod[1:2])
+        d_x = d_out + inv_std * (
+            d_norm - jnp.mean(d_norm, axis=-1, keepdims=True) - x_norm * jnp.mean(d_norm * x_norm, axis=-1, keepdims=True))
+        dx_ref[0, sl] = d_x.astype(BF16)
+        scale_part = d_y * x_norm
+        acc[0] += d_y[:8] + d_y[8:]
+        acc[1] += scale_part[:8] + scale_part[8:]
+        acc[2] += gate_part[:8] + gate_part[8:]
+        return 0
+
+    lax.fori_loop(0, groups, body, 0)
+    for j in range(3):
+        dm_ref[0, j:j + 1] = jnp.sum(acc[j], axis=0, keepdims=True)
+
+    @pl.when(step == pl.num_programs(0) - 1)
+    def _():
+        total = pl.num_programs(0) * groups
+
+        def rest(i, _):
+            advance(i)
+            return 0
+
+        lax.fori_loop(total, jnp.maximum(total, n_copies + lag), rest, 0)
+        for c in range(max(n_copies - depth, 0), n_copies):
+            for copy in move(c, True):
+                copy.wait()
+
+
+def token_call(x_loc, dy_loc, proj, d_y, m_block, e_loc, b_o, grads):
     nb, rows, dim = x_loc.shape
+    n_copies = dim // min(512, dim)
     row = pl.BlockSpec((1, rows, dim), lambda i: (i, 0, 0))
     mod = pl.BlockSpec((1, 3, dim), lambda i: (i, 0, 0))
+    any_spec = pl.BlockSpec(memory_space=pl.ANY)
+    dma = pltpu.SemaphoreType.DMA
+    depth = 4
     return pl.pallas_call(
-        token_kernel, name="tokens", grid=(nb,),
+        functools.partial(token_kernel, n_copies), name="tokens", grid=(nb,),
         out_shape=[jax.ShapeDtypeStruct(x_loc.shape, BF16), jax.ShapeDtypeStruct(x_loc.shape, BF16),
-                   jax.ShapeDtypeStruct((nb, 3, dim), F32)],
-        in_specs=[row, row, row, row, pl.BlockSpec((3, dim), lambda i: (0, 0)), mod, pl.BlockSpec((1, dim), lambda i: (0, 0))],
-        out_specs=[row, row, mod],
+                   jax.ShapeDtypeStruct((nb, 3, dim), F32)] + [jax.ShapeDtypeStruct(w.shape, BF16) for w in grads],
+        in_specs=[row, row, row, row, pl.BlockSpec((3, dim), lambda i: (0, 0)), mod, pl.BlockSpec(memory_space=pltpu.VMEM)] + [any_spec] * 4,
+        out_specs=[row, row, mod] + [any_spec] * 4,
+        scratch_shapes=[pltpu.VMEM((depth, w.shape[0] // n_copies, w.shape[1]), BF16) for w in grads]
+        + [pltpu.VMEM((3, 8, dim), F32), dma((depth, 4)), dma((depth, 4))],
         compiler_params=params("arbitrary"),
         cost_estimate=cost(nb * rows * dim * 30, nb * rows * dim * 12),
-    )(x_loc, dy_loc, proj, d_y, m_block, e_loc, b_o[None])
+    )(x_loc, dy_loc, proj, d_y, m_block, e_loc, b_o, *grads)
 
 
 def solution(mesh):
@@ -1034,14 +1138,15 @@
 
     def device_step(x_loc, e_loc, m_block, w_q, b_q, w_k, b_k, w_v, b_v, w_o, b_o, g_q, g_k, pos_part, dy_loc):
         nb, _, dim = x_loc.shape
-        cos_tab, sin_tab = rope_tables(pos_part)
-        y_full, d_own, q, k, v, ss = gather_qkv_call(tp_size, x_loc, dy_loc, m_block, e_loc, w_q, w_k, w_v, b_q, b_k, b_v)
+        y_full, d_own, q, k, v, ss, cos_tab, sin_tab, gains = gather_qkv_call(
+            tp_size, x_loc, dy_loc, m_block, e_loc, w_q, w_k, w_v, b_q, b_k, b_v, g_q, g_k, pos_part)
         d_full, o, o_p, d_attn, wq_p, wk_p, wv_p, wo_p = gather_attn_call(
-            tp_size, q, k, v, g_q, g_k, cos_tab, sin_tab, ss, w_q, w_k, w_v, w_o, d_own)
+            tp_size, q, k, v, gains, cos_tab, sin_tab, ss, w_q, w_k, w_v, w_o, d_own)
         proj, g, g_p, _, _, d_wo, d_gq, d_gk = proj_bwd_call(
-            tp_size, q, k, v, d_attn, g_q, g_k, cos_tab, sin_tab, ss, o, o_p, w_o, wo_p, d_full)
+            tp_size, q, k, v, d_attn, gains, cos_tab, sin_tab, ss, o, o_p, w_o, wo_p, d_full)
         d_y, d_wq, d_wk, d_wv = dy_dw_call(tp_size, g, g_p, w_q, w_k, w_v, wq_p, wk_p, wv_p, y_full)
-        x_out, d_x, d_mod = token_call(x_loc, dy_loc, proj, d_y, m_block, e_loc, b_o)
+        x_out, d_x, d_mod, d_wq, d_wk, d_wv, d_wo = token_call(
+            x_loc, dy_loc, proj, d_y, m_block, e_loc, b_o, (d_wq, d_wk, d_wv, d_wo))
         d_e = all_sum_call(tp_size, d_mod.reshape(tp_size, -1, HEAD_DIM)).reshape(nb, 3, dim)
         return (x_out, d_x, d_e, jnp.sum(d_e, axis=0), d_wq, d_wk, d_wv, d_wo,
                 jnp.sum(d_gq, axis=(0, 1)), jnp.sum(d_gk, axis=(0, 1)))

time: 568 us -> 512 us (0.901)
  Pallas kernels: 537 us -> 505 us
  local copies, waits for them, and re-layouts: 23.2 us -> 2.79 us
    pallas_call x1, Pallas kernels: 143 us -> 117 us  [proj_bwd_call(): pl.pallas_call(functools.partial(proj_bwd_kernel, n, nb, heads, dim), nam...]
    pallas_call x1, Pallas kernels: 135 us -> 116 us  [dy_dw_call(): pl.pallas_call(functools.partial(dy_dw_kernel, n, nb, dim), name='dy_dw',...]
    unnamed x18 -> x7, local copies, waits for them, and re-layouts: 18.9 us -> 1.65 us
    pallas_call x1, Pallas kernels: 12.8 us -> 27.4 us  [token_call(): pl.pallas_call(functools.partial(token_kernel, n_copies), name='tokens',...]
where the time goes in v4:
time: 512 us; the launch traced here: 511 us
  Pallas kernels  505 us (99%)
    pallas_call x1, Pallas kernels, gather_qkv_call(): pl.pallas_call(functools.partial(gather_qkv_kernel, n), name='gather_qkv'...  126 us
    pallas_call x1, Pallas kernels, proj_bwd_call(): pl.pallas_call(functools.partial(proj_bwd_kernel, n, nb, heads, dim), nam...  117 us
    pallas_call x1, Pallas kernels, dy_dw_call(): pl.pallas_call(functools.partial(dy_dw_kernel, n, nb, dim), name='dy_dw',...  116 us
    pallas_call x1, Pallas kernels, gather_attn_call(): pl.pallas_call(functools.partial(gather_attn_kernel, n, nb, heads, dim),...  108 us
    pallas_call x1, Pallas kernels, token_call(): pl.pallas_call(functools.partial(token_kernel, n_copies), name='tokens',...  27.4 us
    pallas_call x1, Pallas kernels, all_sum_call(): pl.pallas_call(functools.partial(all_sum_kernel, n), name='all_sum', out_...  11.2 us

profile of v4, /device:TPU:81, one launch (start us, length us, event | category | flops | bytes accessed | tf_op | source)
XLA Modules:
  0.0 510.8 jit_solution(8814176530747836137)
XLA Ops:
  0.6 1.6 copy.28.pos_ref
  2.3 126.5 %gather_qkv.1 = (bf16[3,768,5120]{2,1,0:T(8,128)(2,1)}, bf16[3,768,5120]{2,1,0:T(8,128)(2,1)}, f32[3,768,640]{2,1,0:T(8,128)}, f32[3,768,640]{2,1,0:T(8,128)}, b...) custom-call(bf16[3,96,5120]{2,1,0:T(8,128)(2,1)} %x_ref.3, ...), custom_call_target="tpu_custom_call" | custom-call | flops 45298483200 | bytes 40304640 | tf_op jit(solution)/shard_map/gather_qkv/pallas_call | solution.py:326
  128.8 108.0 %gather_attn.1 = (bf16[3,768,5120]{2,1,0:T(8,128)(2,1)}, bf16[3,768,640]{2,1,0:T(8,128)(2,1)}, bf16[3,768,640]{2,1,0:T(8,128)(2,1)}, bf16[3,768,640]{2,1,0:T(8,1...) custom-call(f32[3,768,640]{2,1,0:T(8,128)} %get-tuple-element.44.q_r, ...), custom_call_target="tpu_custom_call", output_to_operand_aliasing={{0}: (11, {})} | custom-call | flops 19629342720 | bytes 94371840 | tf_op jit(solution)/shard_map/gather_attn/pallas_call | solution.py:526
  236.7 116.8 %proj_bwd.1 = (bf16[3,96,5120]{2,1,0:T(8,128)(2,1)}, bf16[3,768,1920]{2,1,0:T(8,128)(2,1)}, bf16[3,768,1920]{2,1,0:T(8,128)(2,1)}, f32[3,768,640]{2,1,0:T(8,128)...) custom-call(f32[3,768,640]{2,1,0:T(8,128)} %get-tuple-element.44.q_ref.q_hbm, ...), custom_call_target="tpu_custom_call" | custom-call | flops 70967623680 | bytes 44236800 | tf_op jit(solution)/shard_map/proj_bwd/pallas_call | solution.py:895
  353.6 0.0 copy-start.2
  353.6 0.0 copy-start.1
  353.6 115.5 %dy_dw.1 = (bf16[3,96,5120]{2,1,0:T(8,128)(2,1)}, bf16[5120,640]{1,0:T(8,128)(2,1)}, bf16[5120,640]{1,0:T(8,128)(2,1)}, bf16[5120,640]{1,0:T(8,128)(2,1)}) custom-call(bf16[3,768,1920]{2,1,0:T(8,128)(2,1)} %get-tuple-element.58.g_hbm, bf16[3,768,1920]{2,1,0:T(8,128)(2,1)} %get-tuple-element.59.g_p, bf16[5120,640]{1,0:T(8,128)(2,1)} %wq_hbm.1, ...), custom_call_target="tpu_custom_call" | custom-call | flops 90596966400 | bytes 44236800 | tf_op jit(solution)/shard_map/dy_dw/pallas_call | solution.py:1025
  469.1 0.0 copy-done.2
  469.1 0.6 reduce_sum.28
  469.8 0.0 copy-done.1
  469.8 0.6 reduce_sum.29
  470.4 27.4 %tokens.1 = (bf16[3,96,5120]{2,1,0:T(8,128)(2,1)}, bf16[3,96,5120]{2,1,0:T(8,128)(2,1)}, f32[3,3,5120]{2,1,0:T(4,128)}, bf16[5120,640]{1,0:T(8,128)(2,1)}, bf16[...) custom-call(bf16[3,96,5120]{2,1,0:T(8,128)(2,1)} %x_ref.3, ...), custom_call_target="tpu_custom_call" | custom-call | flops 44236800 | bytes 17694720 | tf_op jit(solution)/shard_map/tokens/pallas_call | solution.py:1123
  497.8 1.1 reshape.26.x_ref
  498.8 11.2 %all_sum.1 = f32[8,45,128]{2,1,0:T(8,128)S(1)} custom-call(f32[8,45,128]{2,1,0:T(8,128)S(1)} %reshape.26.x_ref), custom_call_target="tpu_custom_call" | custom-call | flops 4000000000 | bytes 368640 | tf_op jit(solution)/shard_map/all_sum/pallas_call | solution.py:379
  510.0 0.1 reshape.27
  510.1 0.0 copy-start
  510.1 0.7 reduce_sum.27
  510.8 0.0 copy-done
Async XLA Ops:
  353.6 115.6 %copy-start.2 = (f32[3,1,640]{2,1,0:T(1,128)S(1)}, f32[3,1,640]{2,1,0:T(1,128)}, u32[]{:S(2)}) copy-start(f32[3,1,640]{2,1,0:T(1,128)} %get-tuple-element.76) | copy-start | bytes 23044
  353.6 116.2 %copy-start.1 = (f32[3,1,640]{2,1,0:T(1,128)S(1)}, f32[3,1,640]{2,1,0:T(1,128)}, u32[]{:S(2)}) copy-start(f32[3,1,640]{2,1,0:T(1,128)} %get-tuple-element.77) | copy-start | bytes 23044
  510.1 0.7 copy-start

commit v5 on v4

--- a/solution.py
+++ b/solution.py
@@ -93,8 +93,8 @@
 
 
 class Gather:
-    def __init__(self, place, full, rows, send, recv):
-        self.at, self.full, self.rows, self.send, self.recv = place, full, rows, send, recv
+    def __init__(self, place, full, rows, send, recv, early=0):
+        self.at, self.full, self.rows, self.send, self.recv, self.early = place, full, rows, send, recv, early
 
     def part(self, b, dev, off, count):
         return self.full.at[b, pl.ds(pl.multiple_of(dev * self.rows + off, 16), count)]
@@ -110,22 +110,49 @@
         self.copy(b, p.me, 0, self.rows, 1, 1, p.left).start()
         self.copy(b, p.me, 0, self.rows, 2, 4, p.partner(p.me)).start()
 
+    def whole_blocks_in(self, b):
+        p = self.at
+        self.copy(b, p.partner(p.me), 0, self.rows, 2, 4, p.me).wait_recv()
+        self.copy(b, p.left, 0, self.rows, 0, 0, p.me).wait_recv()
+        self.copy(b, p.right, 0, self.rows, 1, 1, p.me).wait_recv()
+        for s_idx in range(3):
+            self.copy(b, p.me, 0, self.rows, s_idx, s_idx, p.me).wait_send()
+
+    def pass_left(self, b):
+        p, half = self.at, self.rows // 2
+        self.copy(b, p.left, 0, half, 3, 2, p.right).start()
+        self.copy(b, p.left, 0, self.rows, 5, 5, p.partner(p.me)).start()
+
+    def pass_right(self, b):
+        p, half = self.at, self.rows // 2
+        self.copy(b, p.right, half, half, 4, 3, p.left).start()
+        self.copy(b, p.right, 0, self.rows, 6, 6, p.partner(p.me)).start()
+
     def take_own(self, b):
         p = self.at
-        self.copy(b, p.partner(p.me), 0, self.rows, 2, 4, p.me).wait_recv()
+
+        @pl.when(b >= self.early)
+        def _():
+            self.copy(b, p.partner(p.me), 0, self.rows, 2, 4, p.me).wait_recv()
 
     def take_left(self, b):
-        p, half = self.at, self.rows // 2
-        self.copy(b, p.left, 0, self.rows, 0, 0, p.me).wait_recv()
-        self.copy(b, p.left, 0, half, 3, 2, p.right).start()
-        self.copy(b, p.left, 0, self.rows, 5, 5, p.partner(p.me)).start()
+        p = self.at
+
+        @pl.when(b >= self.early)
+        def _():
+            self.copy(b, p.left, 0, self.rows, 0, 0, p.me).wait_recv()
+            self.pass_left(b)
+
         self.copy(b, p.partner(p.left), 0, self.rows, 5, 5, p.me).wait_recv()
 
     def take_right(self, b):
-        p, half = self.at, self.rows // 2
-        self.copy(b, p.right, 0, self.rows, 1, 1, p.me).wait_recv()
-        self.copy(b, p.right, half, half, 4, 3, p.left).start()
-        self.copy(b, p.right, 0, self.rows, 6, 6, p.partner(p.me)).start()
+        p = self.at
+
+        @pl.when(b >= self.early)
+        def _():
+            self.copy(b, p.right, 0, self.rows, 1, 1, p.me).wait_recv()
+            self.pass_right(b)
+
         self.copy(b, p.partner(p.right), 0, self.rows, 6, 6, p.me).wait_recv()
 
     def take_far(self, b):
@@ -139,7 +166,8 @@
 
     def finish(self, b):
         p, half = self.at, self.rows // 2
-        for s_idx, count in ((0, self.rows), (1, self.rows), (2, self.rows), (3, half), (4, half), (5, self.rows), (6, self.rows), (7, half), (8, half)):
+        counts = (self.rows, self.rows, self.rows, half, half, self.rows, self.rows, half, half)
+        for s_idx, count in list(enumerate(counts))[3 if b < self.early else 0:]:
             self.copy(b, p.me, 0, count, s_idx, s_idx, p.me).wait_send()
 
     def item_place(self, i, nb):
@@ -161,6 +189,8 @@
 
 
 GATHER_SEMS = 9
+EARLY_ROWS = 1
+EARLY_CHUNKS = 4
 
 
 def chunks_of(width, step):
@@ -192,11 +222,12 @@
 def gather_qkv_kernel(n, x_ref, dy_ref, m_ref, e_ref, wq_ref, wk_ref, wv_ref, bq_ref, bk_ref, bv_ref, gq_ref, gk_ref, pos_ref, freq_ref,
                       y_full, d_full, q_out, k_out, v_out, ss_ref, cos_ref, sin_ref, gain_ref,
                       bias_ref, w_all, xin, stage, xbuf, zst, vst, sq, ss_row, slots,
-                      w_sem, in_sem, st_sem, ld_sem, out_sem, g_send, g_recv, e_send, e_recv):
+                      w_sem, in_sem, st_sem, ld_sem, out_sem, g_send, g_recv, d_send, d_recv, e_send, e_recv):
     nb, rows, dim = x_ref.shape
     cols = wq_ref.shape[1]
     place = Place(n)
     gather = Gather(place, y_full, rows, g_send, g_recv)
+    gather_d = Gather(place, d_full, rows, d_send, d_recv)
     w_copies = [pltpu.make_async_copy(w, w_all.at[:, pl.ds(j * cols, cols)], w_sem.at[j]) for j, w in enumerate((wq_ref, wk_ref, wv_ref))]
     load_x = pltpu.make_async_copy(x_ref, xin, in_sem)
     load_x.start()
@@ -276,6 +307,11 @@
         slot = lax.rem(i, 2)
         load = pltpu.make_async_copy(y_full.at[b, pl.ds(row0, 2 * rows)], xbuf, ld_sem)
         load.start()
+
+        @pl.when(i == 3 * nb - 1)
+        def _():
+            for d in range(EARLY_ROWS):
+                gather_d.start_own(d)
 
         @pl.when(i == nb)
         def _():
@@ -311,6 +347,8 @@
             c.wait()
     for b in range(nb):
         gather.finish(b)
+    for d in range(EARLY_ROWS):
+        gather_d.whole_blocks_in(d)
     ss_ref[...] = sums.finish()
 
 
@@ -335,7 +373,8 @@
             pltpu.VMEM((dim, 3 * cols), BF16), pltpu.VMEM((nb, rows, dim), BF16), pltpu.VMEM((nb, rows, dim), BF16),
             pltpu.VMEM((2 * rows, dim), BF16), pltpu.VMEM((2, 2 * rows, 3 * cols), F32), pltpu.VMEM((2, 2 * rows, cols), BF16),
             pltpu.VMEM((2 * nb, tokens, HEAD_DIM), F32), pltpu.VMEM((stat_rows, tokens), F32), pltpu.VMEM((n, stat_rows, tokens), F32),
-            dma((3,)), dma, dma, dma, dma((2, 3)), dma((nb, GATHER_SEMS)), dma((nb, GATHER_SEMS)), dma((n,)), dma((n,))],
+            dma((3,)), dma, dma, dma, dma((2, 3)), dma((nb, GATHER_SEMS)), dma((nb, GATHER_SEMS)),
+            dma((EARLY_ROWS, GATHER_SEMS)), dma((EARLY_ROWS, GATHER_SEMS)), dma((n,)), dma((n,))],
         compiler_params=params(collective_id=0, has_side_effects=True),
         cost_estimate=cost(6 * nb * tokens * dim * cols, 6 * dim * cols + 14 * nb * tokens * cols),
     )(x_loc, dy_loc, m_block, e_loc, w_q, w_k, w_v, b_q, b_k, b_v, g_q, g_k, positions, jnp.asarray(rope_freqs()))
@@ -401,146 +440,10 @@
     return p * (1.0 / jnp.sum(p, axis=1, keepdims=True))
 
 
-def gather_attn_kernel(n, nb, heads, dim, q_ref, k_ref, v_ref, gain_ref, cos_ref, sin_ref, ss_ref,
-                       wq_ref, wk_ref, wv_ref, wo_ref, d_in,
-                       d_full, o_out, o_p, da_out, wq_p, wk_p, wv_p, wo_p,
-                       inv_q, inv_k, o_all, wo, xbuf, ast,
-                       w_sem, ld_sem, out_sem, o_sem, g_send, g_recv, t_send, t_recv):
-    step = pl.program_id(0)
-    tokens = q_ref.shape[1]
-    rows = tokens // n
-    blk = min(256, tokens)
-    place = Place(n)
-    gather = Gather(place, d_full, rows, g_send, g_recv)
-    pairs = ((wo_ref, wo_p), (wq_ref, wq_p), (wk_ref, wk_p), (wv_ref, wv_p), (o_out, o_p))
-
-    def trade(j):
-        return place.to_partner(*pairs[j], t_send.at[j], t_recv.at[j])
-
-
-    @pl.when(step == 0)
-    def _():
-        pltpu.make_async_copy(wo_ref, wo, w_sem).start()
-        place.barrier(place.near())
-
-        def own(b, _):
-            gather.start_own(b)
-            return 0
-
-        lax.fori_loop(0, nb, own, 0)
-        for j in range(4):
-            trade(j).start()
-
-    @pl.when(step < nb * heads)
-    def _():
-        b = step // heads
-        h = lax.rem(step, heads)
-
-        @pl.when(h == 0)
-        def _():
-            inv_q[...] = lanes_of(lax.rsqrt(ss_ref[pl.ds(2 * b, 1)] / dim + EPS_NORM))
-            inv_k[...] = lanes_of(lax.rsqrt(ss_ref[pl.ds(2 * b + 1, 1)] / dim + EPS_NORM))
-
-        cos, sin = cos_ref[...], sin_ref[...]
-        q_rot = rotate(q_ref[0] * inv_q[...] * gain_ref[0:1], cos, sin).astype(BF16)
-        k_rot = rotate(k_ref[0] * inv_k[...] * gain_ref[1:2], cos, sin).astype(BF16)
-        v = v_ref[0]
-        lanes = pl.ds(pl.multiple_of(h * HEAD_DIM, HEAD_DIM), HEAD_DIM)
-        for i in range(tokens // blk):
-            s = lax.dot_general(q_rot[i * blk:(i + 1) * blk], k_rot, NT, preferred_element_type=F32)
-            p = softmax_block(s).astype(BF16)
-            o_all[b, i * blk:(i + 1) * blk, lanes] = jnp.dot(p, v, preferred_element_type=F32).astype(BF16)
-
-    @pl.when(step == nb * heads)
-    def _():
-        o_copy = pltpu.make_async_copy(o_all, o_out, o_sem)
-        o_copy.start()
-        pltpu.make_async_copy(wo_ref, wo, w_sem).wait()
-
-        def outputs(b, row0, slot):
-            return pltpu.make_async_copy(ast.at[slot], da_out.at[b, pl.ds(row0, 2 * rows)], out_sem.at[slot])
-
-        def load(b, row0, slot):
-            return pltpu.make_async_copy(d_full.at[b, pl.ds(row0, 2 * rows)], xbuf.at[slot], ld_sem.at[slot])
-
-        def take(i):
-            b, row0 = gather.take_item(i, nb)
-            load(b, row0, lax.rem(i, 2)).start()
-
-        take(0)
-
-        def item(i, _):
-            slot = lax.rem(i, 2)
-
-            @pl.when(i + 1 < 3 * nb)
-            def _():
-                take(i + 1)
-
-            @pl.when(i >= 2)
-            def _():
-                outputs(0, 0, slot).wait()
-
-            load(0, 0, slot).wait()
-            ast[slot] = lax.dot_general(xbuf[slot], wo[...], NT, preferred_element_type=F32).astype(BF16)
-            b, row0 = gather.item_place(i, nb)
-            outputs(b, row0, slot).start()
-
-            @pl.when(i == 0)
-            def _():
-                o_copy.wait()
-                trade(4).start()
-
-            @pl.when((i + 1 >= 3 * nb) & (i + 1 < 4 * nb))
-            def _():
-                take(i + 1)
-
-            return 0
-
-        lax.fori_loop(0, 4 * nb, item, 0)
-        for slot in range(2):
-            outputs(0, 0, slot).wait()
-        for b in range(nb):
-            gather.finish(b)
-        for j in range(5):
-            trade(j).wait()
-
-
-def gather_attn_call(n, q, k, v, gains, cos_tab, sin_tab, ss, w_q, w_k, w_v, w_o, d_full):
-    nb, tokens, cols = q.shape
-    dim = w_o.shape[1]
-    heads = cols // HEAD_DIM
-    rows = tokens // n
-    last = nb * heads - 1
-    shape = jax.ShapeDtypeStruct
-    dma = pltpu.SemaphoreType.DMA
-    any_spec = pl.BlockSpec(memory_space=pl.ANY)
-
-    def head_of(i):
-        i = jnp.minimum(i, last)
-        return i // heads, i % heads
-
-    blk = pl.BlockSpec((1, tokens, HEAD_DIM), lambda i: (head_of(i)[0], 0, head_of(i)[1]))
-    vec = pl.BlockSpec((2, HEAD_DIM), lambda i: (0, head_of(i)[1]))
-    tab = pl.BlockSpec((tokens, HEAD_DIM), lambda i: (0, 0))
-    head_arr = shape((nb, tokens, cols), BF16)
-    return pl.pallas_call(
-        functools.partial(gather_attn_kernel, n, nb, heads, dim), name="gather_attn", grid=(nb * heads + 1,),
-        out_shape=[shape(d_full.shape, BF16), head_arr, head_arr, head_arr] + [shape(w.shape, BF16) for w in (w_q, w_k, w_v, w_o)],
-        in_specs=[blk, blk, blk, vec, tab, tab, pl.BlockSpec(ss.shape, lambda i: (0, 0))] + [any_spec] * 5,
-        out_specs=[any_spec] * 8,
-        scratch_shapes=[
-            pltpu.VMEM((tokens, HEAD_DIM), F32), pltpu.VMEM((tokens, HEAD_DIM), F32), pltpu.VMEM((nb, tokens, cols), BF16),
-            pltpu.VMEM((cols, dim), BF16), pltpu.VMEM((2, 2 * rows, dim), BF16), pltpu.VMEM((2, 2 * rows, cols), BF16),
-            dma, dma((2,)), dma((2,)), dma, dma((nb, GATHER_SEMS)), dma((nb, GATHER_SEMS)), dma((5,)), dma((5,))],
-        input_output_aliases={11: 0},
-        compiler_params=params("arbitrary", collective_id=1, has_side_effects=True),
-        cost_estimate=cost(2 * nb * tokens * dim * cols + 4 * nb * tokens * tokens * cols, 8 * nb * tokens * dim),
-    )(q, k, v, gains, cos_tab, sin_tab, ss, w_q, w_k, w_v, w_o, d_full)
-
-
 class Scatter:
-    def __init__(self, place, part, recv_far, recv_side, send, recv):
+    def __init__(self, place, part, recv_far, recv_side, send, recv, far_src=None, early=0):
         self.at, self.part, self.far, self.side, self.send, self.recv = place, part, recv_far, recv_side, send, recv
+        self.far_src, self.early = part if far_src is None else far_src, early
         self.rows = part.shape[2]
         self.half = self.rows // 2
 
@@ -552,17 +455,18 @@
         p, part, far, side = self.at, self.part, self.far, self.side
         first, second = pl.ds(0, self.half), pl.ds(self.half, self.rows - self.half)
         src, dst, target = (
-            lambda: (part.at[j, 0, first], far.at[j, 0], p.right),
-            lambda: (part.at[j, 0, second], far.at[j, 1], p.left),
+            lambda: (self.far_src.at[j, 0, first], far.at[j, 0], p.right),
+            lambda: (self.far_src.at[j, 0, second], far.at[j, 1], p.left),
             lambda: (part.at[j, 1, second], side.at[j, 0, second], p.right),
             lambda: (part.at[j, 2, first], side.at[j, 1, first], p.left),
             lambda: (part.at[j, 1, first], side.at[j, 0, first], p.right),
             lambda: (part.at[j, 2, second], side.at[j, 1, second], p.left))[idx]()
         return self.copy(j, idx, src, dst, target)
 
-    def start_far(self, j):
+    def start_far(self, j, _=0):
         for idx in (0, 1):
             self.message(j, idx).start()
+        return 0
 
     def start_side(self, j, _):
         for idx in (2, 3):
@@ -571,9 +475,12 @@
 
     def sums(self, j):
         h = self.half
-        self.message(j, 0).wait_recv()
+        arrived = isinstance(j, int) and j < self.early
+        if not arrived:
+            self.message(j, 0).wait_recv()
         self.part[j, 1, :h] = (self.part[j, 1, :h].astype(F32) + self.far[j, 0].astype(F32)).astype(BF16)
-        self.message(j, 1).wait_recv()
+        if not arrived:
+            self.message(j, 1).wait_recv()
         self.part[j, 2, h:] = (self.part[j, 2, h:].astype(F32) + self.far[j, 1].astype(F32)).astype(BF16)
         self.message(j, 4).start()
         self.message(j, 5).start()
@@ -585,7 +492,12 @@
         self.part[j, 3] = total.astype(BF16)
 
     def finish(self, j):
-        for idx in range(6):
+        @pl.when(j >= self.early)
+        def _():
+            for idx in range(2):
+                self.message(j, idx).wait_send()
+
+        for idx in range(2, 6):
             self.message(j, idx).wait_send()
 
     @staticmethod
@@ -631,8 +543,222 @@
     return out
 
 
-def proj_bwd_kernel(n, nb, heads, dim, q_ref, k_ref, v_ref, do_ref, gain_ref, cos_ref, sin_ref, ss_ref,
-                    q_hbm, k_hbm, o_hbm, o_p, wo_hbm, wo_p, d_full,
+def gather_attn_kernel(n, nb, heads, dim, q_ref, k_ref, v_ref, gain_ref, cos_ref, sin_ref, ss_ref,
+                       wq_ref, wk_ref, wv_ref, wo_ref, d_in,
+                       d_full, o_out, o_p, da_out, wq_p, wk_p, wv_p, wo_p, part_out, far_in,
+                       inv_q, inv_k, o_all, wo, xbuf, ast,
+                       w_sem, ld_sem, out_sem, o_sem, p_sem, l_sem, g_send, g_recv, t_send, t_recv, s_send, s_recv):
+    step = pl.program_id(0)
+    tokens = q_ref.shape[1]
+    rows = tokens // n
+    blk = min(256, tokens)
+    place = Place(n)
+    gather = Gather(place, d_full, rows, g_send, g_recv, early=EARLY_ROWS)
+    cols = heads * HEAD_DIM
+    nc = dim // CHUNK
+    early_chunks = min(EARLY_CHUNKS, nc)
+    scatter = Scatter(place, part_out, far_in, None, s_send, s_recv)
+    pairs = ((wo_ref, wo_p), (wq_ref, wq_p), (wk_ref, wk_p), (wv_ref, wv_p), (o_out, o_p))
+
+    def trade(j):
+        return place.to_partner(*pairs[j], t_send.at[j], t_recv.at[j])
+
+
+    @pl.when(step == 0)
+    def _():
+        pltpu.make_async_copy(wo_ref, wo, w_sem).start()
+        place.barrier(place.near())
+
+        for b in range(EARLY_ROWS):
+            gather.pass_left(b)
+            gather.pass_right(b)
+
+        def own(b, _):
+            gather.start_own(b)
+            return 0
+
+        lax.fori_loop(EARLY_ROWS, nb, own, 0)
+        for j in range(4):
+            trade(j).start()
+
+    @pl.when(step < nb * heads)
+    def _():
+        b = step // heads
+        h = lax.rem(step, heads)
+
+        @pl.when(h == 0)
+        def _():
+            inv_q[...] = lanes_of(lax.rsqrt(ss_ref[pl.ds(2 * b, 1)] / dim + EPS_NORM))
+            inv_k[...] = lanes_of(lax.rsqrt(ss_ref[pl.ds(2 * b + 1, 1)] / dim + EPS_NORM))
+
+        cos, sin = cos_ref[...], sin_ref[...]
+        q_rot = rotate(q_ref[0] * inv_q[...] * gain_ref[0:1], cos, sin).astype(BF16)
+        k_rot = rotate(k_ref[0] * inv_k[...] * gain_ref[1:2], cos, sin).astype(BF16)
+        v = v_ref[0]
+        lanes = pl.ds(pl.multiple_of(h * HEAD_DIM, HEAD_DIM), HEAD_DIM)
+        for i in range(tokens // blk):
+            s = lax.dot_general(q_rot[i * blk:(i + 1) * blk], k_rot, NT, preferred_element_type=F32)
+            p = softmax_block(s).astype(BF16)
+            o_all[b, i * blk:(i + 1) * blk, lanes] = jnp.dot(p, v, preferred_element_type=F32).astype(BF16)
+
+    @pl.when(step == nb * heads)
+    def _():
+        o_copy = pltpu.make_async_copy(o_all, o_out, o_sem)
+        o_copy.start()
+        pltpu.make_async_copy(wo_ref, wo, w_sem).wait()
+
+        def outputs(b, row0, slot):
+            return pltpu.make_async_copy(ast.at[slot], da_out.at[b, pl.ds(row0, 2 * rows)], out_sem.at[slot])
+
+        def load(b, row0, slot):
+            return pltpu.make_async_copy(d_full.at[b, pl.ds(row0, 2 * rows)], xbuf.at[slot], ld_sem.at[slot])
+
+        def project(lhs, wbuf, stage):
+            loads = pair_rows(place, nb, rows, o_out, o_p, lhs, l_sem.at[0])
+            for c in loads:
+                c.start()
+
+            def chunk(j):
+                cs = pl.ds(pl.multiple_of(j * CHUNK, CHUNK), CHUNK)
+                slot = lax.rem(j, 2)
+                return [pltpu.make_async_copy(wo_ref.at[:, cs], wbuf.at[slot, pl.ds(0, cols)], p_sem.at[slot, 0]),
+                        pltpu.make_async_copy(wo_p.at[:, cs], wbuf.at[slot, pl.ds(cols, cols)], p_sem.at[slot, 1])]
+
+            def store(j):
+                slot = lax.rem(j, 2)
+                return pltpu.make_async_copy(stage.at[slot], part_out.at[j], p_sem.at[slot, 2])
+
+            def stored(j):
+                store(j).wait()
+
+                @pl.when(j < early_chunks)
+                def _():
+                    scatter.start_far(j)
+
+            for c in chunk(0):
+                c.start()
+            for c in loads:
+                c.wait()
+
+            def body(j, _):
+                slot = lax.rem(j, 2)
+
+                @pl.when(j + 1 < nc)
+                def _():
+                    for c in chunk(j + 1):
+                        c.start()
+
+                for c in chunk(j):
+                    c.wait()
+                half = 2 * nb * rows
+                for d in range(2):
+                    z = jnp.dot(lhs[d * half:(d + 1) * half], wbuf[slot], preferred_element_type=F32).astype(BF16)
+                    stage[slot, 2 * d] = z[:half // 2]
+                    stage[slot, 2 * d + 1] = z[half // 2:]
+                store(j).start()
+
+                @pl.when(j >= 1)
+                def _():
+                    stored(j - 1)
+
+                return 0
+
+            lax.fori_loop(0, nc, body, 0)
+            stored(nc - 1)
+
+        def take(i):
+            b, row0 = gather.take_item(i, nb)
+            load(b, row0, lax.rem(i, 2)).start()
+
+        take(0)
+
+        def item(i, _):
+            slot = lax.rem(i, 2)
+
+            @pl.when(i + 1 < 3 * nb)
+            def _():
+                take(i + 1)
+
+            @pl.when(i >= 2)
+            def _():
+                outputs(0, 0, slot).wait()
+
+            load(0, 0, slot).wait()
+            ast[slot] = lax.dot_general(xbuf[slot], wo[...], NT, preferred_element_type=F32).astype(BF16)
+            b, row0 = gather.item_place(i, nb)
+            outputs(b, row0, slot).start()
+
+            @pl.when(i == 0)
+            def _():
+                o_copy.wait()
+                trade(4).start()
+
+            @pl.when(i + 1 == 3 * nb)
+            def _():
+                trade(4).wait_recv()
+                trade(0).wait_recv()
+                pl.run_scoped(project, pltpu.VMEM((4 * nb * rows, 2 * cols), BF16), pltpu.VMEM((2, 2 * cols, CHUNK), BF16),
+                              pltpu.VMEM((2, 4, nb * rows, CHUNK), BF16))
+
+            @pl.when((i + 1 >= 3 * nb) & (i + 1 < 4 * nb))
+            def _():
+                take(i + 1)
+
+            return 0
+
+        lax.fori_loop(0, 4 * nb, item, 0)
+        for slot in range(2):
+            outputs(0, 0, slot).wait()
+        for b in range(nb):
+            gather.finish(b)
+        trade(0).wait_send()
+        trade(4).wait_send()
+        for j in range(1, 4):
+            trade(j).wait()
+        for j in range(early_chunks):
+            for idx in (0, 1):
+                scatter.message(j, idx).wait()
+
+
+def gather_attn_call(n, q, k, v, gains, cos_tab, sin_tab, ss, w_q, w_k, w_v, w_o, d_full):
+    nb, tokens, cols = q.shape
+    dim = w_o.shape[1]
+    heads = cols // HEAD_DIM
+    rows = tokens // n
+    last = nb * heads - 1
+    nc = dim // CHUNK
+    early = min(EARLY_CHUNKS, nc)
+    shape = jax.ShapeDtypeStruct
+    dma = pltpu.SemaphoreType.DMA
+    any_spec = pl.BlockSpec(memory_space=pl.ANY)
+
+    def head_of(i):
+        i = jnp.minimum(i, last)
+        return i // heads, i % heads
+
+    blk = pl.BlockSpec((1, tokens, HEAD_DIM), lambda i: (head_of(i)[0], 0, head_of(i)[1]))
+    vec = pl.BlockSpec((2, HEAD_DIM), lambda i: (0, head_of(i)[1]))
+    tab = pl.BlockSpec((tokens, HEAD_DIM), lambda i: (0, 0))
+    head_arr = shape((nb, tokens, cols), BF16)
+    return pl.pallas_call(
+        functools.partial(gather_attn_kernel, n, nb, heads, dim), name="gather_attn", grid=(nb * heads + 1,),
+        out_shape=[shape(d_full.shape, BF16), head_arr, head_arr, head_arr] + [shape(w.shape, BF16) for w in (w_q, w_k, w_v, w_o)]
+        + [shape((nc, 4, nb * rows, CHUNK), BF16), shape((early, 2, nb * rows // 2, CHUNK), BF16)],
+        in_specs=[blk, blk, blk, vec, tab, tab, pl.BlockSpec(ss.shape, lambda i: (0, 0))] + [any_spec] * 5,
+        out_specs=[any_spec] * 10,
+        scratch_shapes=[
+            pltpu.VMEM((tokens, HEAD_DIM), F32), pltpu.VMEM((tokens, HEAD_DIM), F32), pltpu.VMEM((nb, tokens, cols), BF16),
+            pltpu.VMEM((cols, dim), BF16), pltpu.VMEM((2, 2 * rows, dim), BF16), pltpu.VMEM((2, 2 * rows, cols), BF16),
+            dma, dma((2,)), dma((2,)), dma, dma((2, 3)), dma((1,)), dma((nb, GATHER_SEMS)), dma((nb, GATHER_SEMS)), dma((5,)), dma((5,)),
+            dma((early, 6)), dma((early, 6))],
+        input_output_aliases={11: 0},
+        compiler_params=params("arbitrary", collective_id=1, has_side_effects=True),
+        cost_estimate=cost(4 * nb * tokens * dim * cols + 4 * nb * tokens * tokens * cols, 8 * nb * tokens * dim),
+    )(q, k, v, gains, cos_tab, sin_tab, ss, w_q, w_k, w_v, w_o, d_full)
+
+
+def attn_bwd_kernel(n, nb, heads, dim, q_ref, k_ref, v_ref, do_ref, gain_ref, cos_ref, sin_ref, ss_ref,
+                    q_hbm, k_hbm, o_hbm, part_in, far_in, d_full,
                     proj_out, g_out, g_p, dqs_out, dks_out, dwo_out, dgq_ref, dgk_ref,
                     part, recv_far, recv_side, s_send, s_recv,
                     inv_q, inv_k, acc_q, acc_k, p_all, ds_all, dq_all, qs_st, ks_st, v_st, st_row, st_sum, slots,
@@ -646,47 +772,24 @@
     steps = nb * heads
     scale = HEAD_DIM ** -0.5
     place = Place(n)
-    scatter = Scatter(place, part, recv_far, recv_side, s_send, s_recv)
+    early = far_in.shape[0]
+    scatter = Scatter(place, part, recv_far, recv_side, s_send, s_recv, far_src=part_in, early=early)
+
+    def stored():
+        return [pltpu.make_async_copy(part_in, part, ld_sem.at[0]),
+                pltpu.make_async_copy(far_in, recv_far.at[pl.ds(0, early)], ld_sem.at[1])]
 
     @pl.when(step == 0)
     def _():
-        def project(lhs, wbuf):
-            loads = pair_rows(place, nb, rows, o_hbm, o_p, lhs, ld_sem.at[0])
-            for c in loads:
-                c.start()
-
-            def chunk(j):
-                cs = pl.ds(pl.multiple_of(j * CHUNK, CHUNK), CHUNK)
-                slot = lax.rem(j, 2)
-                return [pltpu.make_async_copy(wo_hbm.at[:, cs], wbuf.at[slot, pl.ds(0, cols)], w_sem.at[slot, 0]),
-                        pltpu.make_async_copy(wo_p.at[:, cs], wbuf.at[slot, pl.ds(cols, cols)], w_sem.at[slot, 1])]
-
-            for c in chunk(0):
-                c.start()
-            place.barrier(place.everyone())
-            for c in loads:
-                c.wait()
-
-            def body(j, _):
-                @pl.when(j + 1 < nc)
-                def _():
-                    for c in chunk(j + 1):
-                        c.start()
-
-                for c in chunk(j):
-                    c.wait()
-                w = wbuf[lax.rem(j, 2)]
-                half = 2 * nb * rows
-                for d in range(2):
-                    z = jnp.dot(lhs[d * half:(d + 1) * half], w, preferred_element_type=F32).astype(BF16)
-                    part[j, 2 * d] = z[:half // 2]
-                    part[j, 2 * d + 1] = z[half // 2:]
-                scatter.start_far(j)
-                return 0
-
-            lax.fori_loop(0, nc, body, 0)
-
-        pl.run_scoped(project, pltpu.VMEM((4 * nb * rows, 2 * cols), BF16), pltpu.VMEM((2, 2 * cols, CHUNK), BF16))
+        place.barrier(place.everyone())
+        lax.fori_loop(early, nc, scatter.start_far, 0)
+        for c in stored():
+            c.start()
+
+    @pl.when(step == 1)
+    def _():
+        for c in stored():
+            c.wait()
 
     def flush(b, h, slot):
         lanes = pl.ds(pl.multiple_of(h * HEAD_DIM, HEAD_DIM), HEAD_DIM)
@@ -696,16 +799,16 @@
                 pltpu.make_async_copy(v_st.at[slot], g_out.at[b, :, v_lanes], fl_sem.at[slot, 2])]
 
     for j in range(nc):
-        at_step = 1 + j * (steps - 1) // max(nc - 1, 1)
+        at_step = 1 + j * (steps - 2) // max(nc - 1, 1)
         pl.when(step == at_step)(functools.partial(scatter.sums, j))
 
-    @pl.when((step >= 1) & (step <= steps))
+    @pl.when(step < steps)
     def _():
-        b = (step - 1) // heads
-        head = lax.rem(step - 1, heads)
+        b = step // heads
+        head = lax.rem(step, heads)
         slot = lax.rem(step, 2)
 
-        @pl.when(step == 1)
+        @pl.when(step == 0)
         def _():
             st_row[...] = jnp.zeros_like(st_row)
 
@@ -716,7 +819,7 @@
             acc_q[...] = jnp.zeros_like(acc_q)
             acc_k[...] = jnp.zeros_like(acc_k)
 
-        @pl.when(step >= 3)
+        @pl.when(step >= 2)
         def _():
             for c in flush(0, 0, slot):
                 c.wait()
@@ -760,10 +863,10 @@
             st_row[pl.ds(2 * b, 1)] = to_row(acc_q[...])
             st_row[pl.ds(2 * b + 1, 1)] = to_row(acc_k[...])
 
-    @pl.when(step == steps + 1)
+    @pl.when(step == steps)
     def _():
-        for s in (steps - 1, steps):
-            for c in flush(0, 0, s % 2):
+        for s in range(2):
+            for c in flush(0, 0, s):
                 c.wait()
         stats = Exchange(place, st_row, slots, e_send, e_recv)
         stats.start()
@@ -872,9 +975,9 @@
         trade.wait()
 
 
-def proj_bwd_call(n, q, k, v, d_attn, gains, cos_tab, sin_tab, ss, o, o_p, w_o, wo_p, d_full):
+def attn_bwd_call(n, q, k, v, d_attn, gains, cos_tab, sin_tab, ss, o, part, far, d_full):
     nb, tokens, cols = q.shape
-    dim = w_o.shape[1]
+    dim = d_full.shape[2]
     heads = cols // HEAD_DIM
     rows = tokens // n
     steps = nb * heads
@@ -883,7 +986,7 @@
     any_spec = pl.BlockSpec(memory_space=pl.ANY)
 
     def head_of(i):
-        i = jnp.clip(i - 1, 0, steps - 1)
+        i = jnp.minimum(i, steps - 1)
         return i // heads, i % heads
 
     blk = pl.BlockSpec((1, tokens, HEAD_DIM), lambda i: (head_of(i)[0], 0, head_of(i)[1]))
@@ -893,18 +996,18 @@
     whole = (nb, tokens, cols)
     lane_tile = pltpu.VMEM((tokens, HEAD_DIM), F32)
     return pl.pallas_call(
-        functools.partial(proj_bwd_kernel, n, nb, heads, dim), name="proj_bwd", grid=(steps + 2,),
+        functools.partial(attn_bwd_kernel, n, nb, heads, dim), name="attn_bwd", grid=(steps + 1,),
         out_shape=[shape((nb, rows, dim), BF16), shape((nb, tokens, 3 * cols), BF16), shape((nb, tokens, 3 * cols), BF16),
                    shape(whole, F32), shape(whole, F32), shape((cols, dim), BF16), shape((nb, 1, cols), F32), shape((nb, 1, cols), F32)],
-        in_specs=[blk, blk, blk, blk, vec, tab, tab, pl.BlockSpec(ss.shape, lambda i: (0, 0))] + [any_spec] * 7,
+        in_specs=[blk, blk, blk, blk, vec, tab, tab, pl.BlockSpec(ss.shape, lambda i: (0, 0))] + [any_spec] * 6,
         out_specs=[any_spec] * 6 + [out_vec, out_vec],
         scratch_shapes=Scatter.scratch(nb * rows, dim) + [lane_tile] * 4 + [pltpu.VMEM((tokens, tokens), BF16)] * 2 + [
             lane_tile, pltpu.VMEM((2, tokens, HEAD_DIM), F32), pltpu.VMEM((2, tokens, HEAD_DIM), F32),
             pltpu.VMEM((2, tokens, HEAD_DIM), BF16), pltpu.VMEM(ss.shape, F32), pltpu.VMEM(ss.shape, F32), pltpu.VMEM((n,) + ss.shape, F32),
-            dma((1,)), dma((2, 2)), dma((2, 3)), dma((2, 4)), dma((2,)), dma((nb,)), dma((n,)), dma((n,)), dma, dma],
+            dma((2,)), dma((2, 2)), dma((2, 3)), dma((2, 4)), dma((2,)), dma((nb,)), dma((n,)), dma((n,)), dma, dma],
         compiler_params=params("arbitrary", collective_id=2, has_side_effects=True),
         cost_estimate=cost(4 * nb * tokens * dim * cols + 36 * nb * tokens * tokens * cols, 30 * nb * tokens * cols),
-    )(q, k, v, d_attn, gains, cos_tab, sin_tab, ss, q, k, o, o_p, w_o, wo_p, d_full)
+    )(q, k, v, d_attn, gains, cos_tab, sin_tab, ss, q, k, o, part, far, d_full)
 
 
 def dy_dw_kernel(n, nb, dim, g_hbm, g_p, wq_hbm, wk_hbm, wv_hbm, wq_p, wk_p, wv_p, y_full,
@@ -1140,10 +1243,10 @@
         nb, _, dim = x_loc.shape
         y_full, d_own, q, k, v, ss, cos_tab, sin_tab, gains = gather_qkv_call(
             tp_size, x_loc, dy_loc, m_block, e_loc, w_q, w_k, w_v, b_q, b_k, b_v, g_q, g_k, pos_part)
-        d_full, o, o_p, d_attn, wq_p, wk_p, wv_p, wo_p = gather_attn_call(
+        d_full, o, _, d_attn, wq_p, wk_p, wv_p, _, part, far = gather_attn_call(
             tp_size, q, k, v, gains, cos_tab, sin_tab, ss, w_q, w_k, w_v, w_o, d_own)
-        proj, g, g_p, _, _, d_wo, d_gq, d_gk = proj_bwd_call(
-            tp_size, q, k, v, d_attn, gains, cos_tab, sin_tab, ss, o, o_p, w_o, wo_p, d_full)
+        proj, g, g_p, _, _, d_wo, d_gq, d_gk = attn_bwd_call(
+            tp_size, q, k, v, d_attn, gains, cos_tab, sin_tab, ss, o, part, far, d_full)
         d_y, d_wq, d_wk, d_wv = dy_dw_call(tp_size, g, g_p, w_q, w_k, w_v, wq_p, wk_p, wv_p, y_full)
         x_out, d_x, d_mod, d_wq, d_wk, d_wv, d_wo = token_call(
             x_loc, dy_loc, proj, d_y, m_block, e_loc, b_o, (d_wq, d_wk, d_wv, d_wo))

time: 512 us -> 511 us (level)
    pallas_call x1, Pallas kernels: 117 us -> 101 us  [attn_bwd_call(): pl.pallas_call(functools.partial(attn_bwd_kernel, n, nb, heads, dim), nam...]
    pallas_call x1, Pallas kernels: 126 us -> 136 us  [gather_qkv_call(): pl.pallas_call(functools.partial(gather_qkv_kernel, n), name='gather_qkv'...]
where the time goes in v5:
time: 511 us; the launch traced here: 510 us
  Pallas kernels  504 us (99%)
    pallas_call x1, Pallas kernels, gather_qkv_call(): pl.pallas_call(functools.partial(gather_qkv_kernel, n), name='gather_qkv'...  136 us
    pallas_call x1, Pallas kernels, dy_dw_call(): pl.pallas_call(functools.partial(dy_dw_kernel, n, nb, dim), name='dy_dw',...  115 us
    pallas_call x1, Pallas kernels, gather_attn_call(): pl.pallas_call(functools.partial(gather_attn_kernel, n, nb, heads, dim),...  113 us
    pallas_call x1, Pallas kernels, attn_bwd_call(): pl.pallas_call(functools.partial(attn_bwd_kernel, n, nb, heads, dim), nam...  101 us
    pallas_call x1, Pallas kernels, token_call(): pl.pallas_call(functools.partial(token_kernel, n_copies), name='tokens',...  27.4 us
    pallas_call x1, Pallas kernels, all_sum_call(): pl.pallas_call(functools.partial(all_sum_kernel, n), name='all_sum', out_...  12.2 us

profile of v5, /device:TPU:81, one launch (start us, length us, event | category | flops | bytes accessed | tf_op | source)
XLA Modules:
  0.0 509.5 jit_solution(10617647511153076862)
XLA Ops:
  0.6 1.6 copy.28.pos_ref
  2.3 136.0 %gather_qkv.1 = (bf16[3,768,5120]{2,1,0:T(8,128)(2,1)}, bf16[3,768,5120]{2,1,0:T(8,128)(2,1)}, f32[3,768,640]{2,1,0:T(8,128)}, f32[3,768,640]{2,1,0:T(8,128)}, b...) custom-call(bf16[3,96,5120]{2,1,0:T(8,128)(2,1)} %x_ref.3, ...), custom_call_target="tpu_custom_call" | custom-call | flops 45298483200 | bytes 40304640 | tf_op jit(solution)/shard_map/gather_qkv/pallas_call | solution.py:364
  138.3 113.1 %gather_attn.1 = (bf16[3,768,5120]{2,1,0:T(8,128)(2,1)}, bf16[3,768,640]{2,1,0:T(8,128)(2,1)}, bf16[3,768,640]{2,1,0:T(8,128)(2,1)}, bf16[3,768,640]{2,1,0:T(8,1...) custom-call(f32[3,768,640]{2,1,0:T(8,128)} %get-tuple-element.44.q_r, ...), custom_call_target="tpu_custom_call", output_to_operand_aliasing={{0}: (11, {})} | custom-call | flops 34728837120 | bytes 94371840 | tf_op jit(solution)/shard_map/gather_attn/pallas_call | solution.py:743
  251.4 100.9 %attn_bwd.1 = (bf16[3,96,5120]{2,1,0:T(8,128)(2,1)}, bf16[3,768,1920]{2,1,0:T(8,128)(2,1)}, bf16[3,768,1920]{2,1,0:T(8,128)(2,1)}, f32[3,768,640]{2,1,0:T(8,128)...) custom-call(f32[3,768,640]{2,1,0:T(8,128)} %get-tuple-element.44.q_ref.q_hbm, ...), custom_call_target="tpu_custom_call" | custom-call | flops 70967623680 | bytes 44236800 | tf_op jit(solution)/shard_map/attn_bwd/pallas_call | solution.py:998
  352.3 0.0 copy-start.2
  352.3 0.0 copy-start.1
  352.3 114.5 %dy_dw.1 = (bf16[3,96,5120]{2,1,0:T(8,128)(2,1)}, bf16[5120,640]{1,0:T(8,128)(2,1)}, bf16[5120,640]{1,0:T(8,128)(2,1)}, bf16[5120,640]{1,0:T(8,128)(2,1)}) custom-call(bf16[3,768,1920]{2,1,0:T(8,128)(2,1)} %get-tuple-element.58.g_hbm, bf16[3,768,1920]{2,1,0:T(8,128)(2,1)} %get-tuple-element.59.g_p, bf16[5120,640]{1,0:T(8,128)(2,1)} %wq_hbm.1, ...), custom_call_target="tpu_custom_call" | custom-call | flops 90596966400 | bytes 44236800 | tf_op jit(solution)/shard_map/dy_dw/pallas_call | solution.py:1128
  466.8 0.0 copy-done.2
  466.9 0.6 reduce_sum.28
  467.5 0.0 copy-done.1
  467.5 0.6 reduce_sum.29
  468.1 27.4 %tokens.1 = (bf16[3,96,5120]{2,1,0:T(8,128)(2,1)}, bf16[3,96,5120]{2,1,0:T(8,128)(2,1)}, f32[3,3,5120]{2,1,0:T(4,128)}, bf16[5120,640]{1,0:T(8,128)(2,1)}, bf16[...) custom-call(bf16[3,96,5120]{2,1,0:T(8,128)(2,1)} %x_ref.3, ...), custom_call_target="tpu_custom_call" | custom-call | flops 44236800 | bytes 17694720 | tf_op jit(solution)/shard_map/tokens/pallas_call | solution.py:1226
  495.5 1.1 reshape.26.x_ref
  496.5 12.2 %all_sum.1 = f32[8,45,128]{2,1,0:T(8,128)S(1)} custom-call(f32[8,45,128]{2,1,0:T(8,128)S(1)} %reshape.26.x_ref), custom_call_target="tpu_custom_call" | custom-call | flops 4000000000 | bytes 368640 | tf_op jit(solution)/shard_map/all_sum/pallas_call | solution.py:418
  508.7 0.1 reshape.27
  508.8 0.0 copy-start
  508.8 0.7 reduce_sum.27
  509.5 0.0 copy-done
Async XLA Ops:
  352.3 114.6 %copy-start.2 = (f32[3,1,640]{2,1,0:T(1,128)S(1)}, f32[3,1,640]{2,1,0:T(1,128)}, u32[]{:S(2)}) copy-start(f32[3,1,640]{2,1,0:T(1,128)} %get-tuple-element.76) | copy-start | bytes 23044
  352.3 115.2 %copy-start.1 = (f32[3,1,640]{2,1,0:T(1,128)S(1)}, f32[3,1,640]{2,1,0:T(1,128)}, u32[]{:S(2)}) copy-start(f32[3,1,640]{2,1,0:T(1,128)} %get-tuple-element.77) | copy-start | bytes 23044
  508.8 0.7 copy-start

commit v6 on v5

--- a/solution.py
+++ b/solution.py
@@ -75,11 +75,13 @@
     def partner(self, dev):
         return dev + 1 - 2 * lax.rem(dev, 2)
 
+    def arrive(self, devices):
+        for dev in devices:
+            pl.semaphore_signal(pltpu.get_barrier_semaphore(), inc=1, device_id={'tp': dev}, device_id_type=MESH_ID)
+
     def barrier(self, devices):
-        sem = pltpu.get_barrier_semaphore()
-        for dev in devices:
-            pl.semaphore_signal(sem, inc=1, device_id={'tp': dev}, device_id_type=MESH_ID)
-        pl.semaphore_wait(sem, len(devices))
+        self.arrive(devices)
+        pl.semaphore_wait(pltpu.get_barrier_semaphore(), len(devices))
 
     def to_partner(self, src, dst, send_sem, recv_sem):
         return pltpu.make_async_remote_copy(src_ref=src, dst_ref=dst, send_sem=send_sem, recv_sem=recv_sem,
@@ -188,6 +190,30 @@
         return b, row0
 
 
+class RowTrade:
+    def __init__(self, place, src, dst, rows, send, recv):
+        self.at, self.src, self.dst, self.rows, self.send, self.recv = place, src, dst, rows, send, recv
+
+    def copies(self, parity):
+        p = self.at
+        for b in range(self.src.shape[0]):
+            for k in range(p.n // 2):
+                sl = pl.ds(pl.multiple_of((2 * k + parity) * self.rows, 16), self.rows)
+                yield p.to_partner(self.src.at[b, sl], self.dst.at[b, sl], self.send.at[b, k], self.recv.at[b, k])
+
+    def start(self):
+        for c in self.copies(1 - lax.rem(self.at.me, 2)):
+            c.start()
+
+    def wait_recv(self):
+        for c in self.copies(lax.rem(self.at.me, 2)):
+            c.wait_recv()
+
+    def wait_send(self):
+        for c in self.copies(1 - lax.rem(self.at.me, 2)):
+            c.wait_send()
+
+
 GATHER_SEMS = 9
 EARLY_ROWS = 1
 EARLY_CHUNKS = 4
@@ -219,18 +245,24 @@
         return total
 
 
-def gather_qkv_kernel(n, x_ref, dy_ref, m_ref, e_ref, wq_ref, wk_ref, wv_ref, bq_ref, bk_ref, bv_ref, gq_ref, gk_ref, pos_ref, freq_ref,
-                      y_full, d_full, q_out, k_out, v_out, ss_ref, cos_ref, sin_ref, gain_ref,
+def gather_qkv_kernel(n, x_ref, dy_ref, m_ref, e_ref, wq_ref, wk_ref, wv_ref, wo_ref, bq_ref, bk_ref, bv_ref, gq_ref, gk_ref, pos_ref,
+                      freq_ref, y_full, d_full, q_out, k_out, v_out, wo_p, ss_ref, cos_ref, sin_ref, gain_ref,
                       bias_ref, w_all, xin, stage, xbuf, zst, vst, sq, ss_row, slots,
-                      w_sem, in_sem, st_sem, ld_sem, out_sem, g_send, g_recv, d_send, d_recv, e_send, e_recv):
+                      w_sem, in_sem, st_sem, ld_sem, out_sem, g_send, g_recv, d_send, d_recv, e_send, e_recv, t_send, t_recv):
     nb, rows, dim = x_ref.shape
     cols = wq_ref.shape[1]
     place = Place(n)
     gather = Gather(place, y_full, rows, g_send, g_recv)
     gather_d = Gather(place, d_full, rows, d_send, d_recv)
     w_copies = [pltpu.make_async_copy(w, w_all.at[:, pl.ds(j * cols, cols)], w_sem.at[j]) for j, w in enumerate((wq_ref, wk_ref, wv_ref))]
-    load_x = pltpu.make_async_copy(x_ref, xin, in_sem)
-    load_x.start()
+    place.arrive(place.everyone())
+    trade = place.to_partner(wo_ref, wo_p, t_send, t_recv)
+
+    def load_x(b):
+        return pltpu.make_async_copy(x_ref.at[b], xin.at[b], in_sem.at[b])
+
+    for b in range(nb):
+        load_x(b).start()
     for c in w_copies:
         c.start()
     group = 16
@@ -238,10 +270,8 @@
     def mine(full, b):
         return full.at[b, pl.ds(pl.multiple_of(place.me * rows, 16), rows)]
 
-    load_x.wait()
-    place.barrier(place.everyone())
-
     def ln_step(b, _):
+        load_x(b).wait()
         shift = m_ref[0:1] + e_ref[b, 0:1]
         scale_one = 1.0 + (m_ref[1:2] + e_ref[b, 1:2])
 
@@ -254,12 +284,17 @@
         lax.fori_loop(0, rows // group, ln_rows, 0)
         out = pltpu.make_async_copy(stage.at[b], mine(y_full, b), st_sem)
         out.start()
+
+        @pl.when(b == 0)
+        def _():
+            pl.semaphore_wait(pltpu.get_barrier_semaphore(), n - 1)
+
         out.wait()
         gather.start_own(b)
         return 0
 
     lax.fori_loop(0, nb, ln_step, 0)
-    load_dy = pltpu.make_async_copy(dy_ref, xin, in_sem)
+    load_dy = pltpu.make_async_copy(dy_ref, xin, in_sem.at[0])
     load_dy.start()
     for j, ref in enumerate((bq_ref, bk_ref, bv_ref)):
         bias_ref[:, j * cols:(j + 1) * cols] = ref[...].reshape(1, cols)
@@ -271,13 +306,13 @@
 
         def rows_of(r, _):
             sl = pl.ds(pl.multiple_of(r * 128, 128), 128)
-            pos = pos_ref[sl].astype(F32)
-            angle = pos[:, 0:1] * freq_ref[0:1] + pos[:, 1:2] * freq_ref[1:2] + pos[:, 2:3] * freq_ref[2:3]
+            pos = [lanes_of(pos_ref[m:m + 1, sl].astype(F32)) for m in range(3)]
+            angle = pos[0] * freq_ref[0:1] + pos[1] * freq_ref[1:2] + pos[2] * freq_ref[2:3]
             cos_ref[sl] = jnp.cos(angle)
             sin_ref[sl] = jnp.where(lane % 2 == 0, -1.0, 1.0) * jnp.sin(angle)
             return 0
 
-        lax.fori_loop(0, pos_ref.shape[0] // 128, rows_of, 0)
+        lax.fori_loop(0, pos_ref.shape[1] // 128, rows_of, 0)
 
     def gate_step(b, _):
         gate = m_ref[2:3] + e_ref[b, 2:3]
@@ -316,6 +351,7 @@
         @pl.when(i == nb)
         def _():
             load_dy.wait()
+            trade.start()
             lax.fori_loop(0, nb, gate_step, 0)
             tables()
 
@@ -349,10 +385,11 @@
         gather.finish(b)
     for d in range(EARLY_ROWS):
         gather_d.whole_blocks_in(d)
+    trade.wait()
     ss_ref[...] = sums.finish()
 
 
-def gather_qkv_call(n, x_loc, dy_loc, m_block, e_loc, w_q, w_k, w_v, b_q, b_k, b_v, g_q, g_k, positions):
+def gather_qkv_call(n, x_loc, dy_loc, m_block, e_loc, w_q, w_k, w_v, w_o, b_q, b_k, b_v, g_q, g_k, positions):
     nb, rows, dim = x_loc.shape
     cols = w_q.shape[1]
     tokens = rows * n
@@ -364,20 +401,20 @@
     return pl.pallas_call(
         functools.partial(gather_qkv_kernel, n), name="gather_qkv",
         out_shape=[shape((nb, tokens, dim), BF16), shape((nb, tokens, dim), BF16), shape((nb, tokens, cols), F32),
-                   shape((nb, tokens, cols), F32), shape((nb, tokens, cols), BF16), shape((stat_rows, tokens), F32),
+                   shape((nb, tokens, cols), F32), shape((nb, tokens, cols), BF16), shape(w_o.shape, BF16), shape((stat_rows, tokens), F32),
                    shape((tokens, HEAD_DIM), F32), shape((tokens, HEAD_DIM), F32), shape((2, cols), F32)],
-        in_specs=[any_spec, any_spec, vmem, vmem, any_spec, any_spec, any_spec] + [vmem] * 7,
-        out_specs=[any_spec] * 5 + [vmem] * 4,
+        in_specs=[any_spec, any_spec, vmem, vmem] + [any_spec] * 4 + [vmem] * 7,
+        out_specs=[any_spec] * 6 + [vmem] * 4,
         scratch_shapes=[
             pltpu.VMEM((1, 3 * cols), F32),
             pltpu.VMEM((dim, 3 * cols), BF16), pltpu.VMEM((nb, rows, dim), BF16), pltpu.VMEM((nb, rows, dim), BF16),
             pltpu.VMEM((2 * rows, dim), BF16), pltpu.VMEM((2, 2 * rows, 3 * cols), F32), pltpu.VMEM((2, 2 * rows, cols), BF16),
             pltpu.VMEM((2 * nb, tokens, HEAD_DIM), F32), pltpu.VMEM((stat_rows, tokens), F32), pltpu.VMEM((n, stat_rows, tokens), F32),
-            dma((3,)), dma, dma, dma, dma((2, 3)), dma((nb, GATHER_SEMS)), dma((nb, GATHER_SEMS)),
-            dma((EARLY_ROWS, GATHER_SEMS)), dma((EARLY_ROWS, GATHER_SEMS)), dma((n,)), dma((n,))],
+            dma((3,)), dma((nb,)), dma, dma, dma((2, 3)), dma((nb, GATHER_SEMS)), dma((nb, GATHER_SEMS)),
+            dma((EARLY_ROWS, GATHER_SEMS)), dma((EARLY_ROWS, GATHER_SEMS)), dma((n,)), dma((n,)), dma, dma],
         compiler_params=params(collective_id=0, has_side_effects=True),
         cost_estimate=cost(6 * nb * tokens * dim * cols, 6 * dim * cols + 14 * nb * tokens * cols),
-    )(x_loc, dy_loc, m_block, e_loc, w_q, w_k, w_v, b_q, b_k, b_v, g_q, g_k, positions, jnp.asarray(rope_freqs()))
+    )(x_loc, dy_loc, m_block, e_loc, w_q, w_k, w_v, w_o, b_q, b_k, b_v, g_q, g_k, positions.T, jnp.asarray(rope_freqs()))
 
 
 def all_sum_kernel(n, x_ref, o_ref, pieces, total, send_a, recv_a, send_b, recv_b):
@@ -539,15 +576,15 @@
         for b in range(nb):
             dst_rows = pl.ds((d * nb + b) * rows, rows)
             for j, src in enumerate((mine, theirs)):
-                out.append(pltpu.make_async_copy(src.at[b, src_rows], lhs.at[dst_rows, pl.ds(j * width, width)], sem))
+                out.append(pltpu.make_async_copy(src.at[b, src_rows], lhs.at[dst_rows, pl.ds(j * width, width)], sem.at[d // 2]))
     return out
 
 
 def gather_attn_kernel(n, nb, heads, dim, q_ref, k_ref, v_ref, gain_ref, cos_ref, sin_ref, ss_ref,
-                       wq_ref, wk_ref, wv_ref, wo_ref, d_in,
-                       d_full, o_out, o_p, da_out, wq_p, wk_p, wv_p, wo_p, part_out, far_in,
+                       wq_ref, wo_ref, wo_p, d_in,
+                       d_full, o_out, o_p, da_out, wq_p, part_out, far_in,
                        inv_q, inv_k, o_all, wo, xbuf, ast,
-                       w_sem, ld_sem, out_sem, o_sem, p_sem, l_sem, g_send, g_recv, t_send, t_recv, s_send, s_recv):
+                       w_sem, ld_sem, out_sem, o_sem, p_sem, l_sem, g_send, g_recv, t_send, t_recv, r_send, r_recv, s_send, s_recv):
     step = pl.program_id(0)
     tokens = q_ref.shape[1]
     rows = tokens // n
@@ -558,10 +595,10 @@
     nc = dim // CHUNK
     early_chunks = min(EARLY_CHUNKS, nc)
     scatter = Scatter(place, part_out, far_in, None, s_send, s_recv)
-    pairs = ((wo_ref, wo_p), (wq_ref, wq_p), (wk_ref, wk_p), (wv_ref, wv_p), (o_out, o_p))
-
-    def trade(j):
-        return place.to_partner(*pairs[j], t_send.at[j], t_recv.at[j])
+    trade_o = RowTrade(place, o_out, o_p, rows, r_send, r_recv)
+
+    def trade_w():
+        return place.to_partner(wq_ref, wq_p, t_send, t_recv)
 
 
     @pl.when(step == 0)
@@ -578,8 +615,7 @@
             return 0
 
         lax.fori_loop(EARLY_ROWS, nb, own, 0)
-        for j in range(4):
-            trade(j).start()
+        trade_w().start()
 
     @pl.when(step < nb * heads)
     def _():
@@ -614,7 +650,7 @@
             return pltpu.make_async_copy(d_full.at[b, pl.ds(row0, 2 * rows)], xbuf.at[slot], ld_sem.at[slot])
 
         def project(lhs, wbuf, stage):
-            loads = pair_rows(place, nb, rows, o_out, o_p, lhs, l_sem.at[0])
+            loads = pair_rows(place, nb, rows, o_out, o_p, lhs, l_sem)
             for c in loads:
                 c.start()
 
@@ -691,12 +727,11 @@
             @pl.when(i == 0)
             def _():
                 o_copy.wait()
-                trade(4).start()
+                trade_o.start()
 
             @pl.when(i + 1 == 3 * nb)
             def _():
-                trade(4).wait_recv()
-                trade(0).wait_recv()
+                trade_o.wait_recv()
                 pl.run_scoped(project, pltpu.VMEM((4 * nb * rows, 2 * cols), BF16), pltpu.VMEM((2, 2 * cols, CHUNK), BF16),
                               pltpu.VMEM((2, 4, nb * rows, CHUNK), BF16))
 
@@ -711,16 +746,14 @@
             outputs(0, 0, slot).wait()
         for b in range(nb):
             gather.finish(b)
-        trade(0).wait_send()
-        trade(4).wait_send()
-        for j in range(1, 4):
-            trade(j).wait()
+        trade_o.wait_send()
+        trade_w().wait()
         for j in range(early_chunks):
             for idx in (0, 1):
                 scatter.message(j, idx).wait()
 
 
-def gather_attn_call(n, q, k, v, gains, cos_tab, sin_tab, ss, w_q, w_k, w_v, w_o, d_full):
+def gather_attn_call(n, q, k, v, gains, cos_tab, sin_tab, ss, w_q, w_o, wo_p, d_full):
     nb, tokens, cols = q.shape
     dim = w_o.shape[1]
     heads = cols // HEAD_DIM
@@ -742,27 +775,27 @@
     head_arr = shape((nb, tokens, cols), BF16)
     return pl.pallas_call(
         functools.partial(gather_attn_kernel, n, nb, heads, dim), name="gather_attn", grid=(nb * heads + 1,),
-        out_shape=[shape(d_full.shape, BF16), head_arr, head_arr, head_arr] + [shape(w.shape, BF16) for w in (w_q, w_k, w_v, w_o)]
+        out_shape=[shape(d_full.shape, BF16), head_arr, head_arr, head_arr, shape(w_q.shape, BF16)]
         + [shape((nc, 4, nb * rows, CHUNK), BF16), shape((early, 2, nb * rows // 2, CHUNK), BF16)],
-        in_specs=[blk, blk, blk, vec, tab, tab, pl.BlockSpec(ss.shape, lambda i: (0, 0))] + [any_spec] * 5,
-        out_specs=[any_spec] * 10,
+        in_specs=[blk, blk, blk, vec, tab, tab, pl.BlockSpec(ss.shape, lambda i: (0, 0))] + [any_spec] * 4,
+        out_specs=[any_spec] * 7,
         scratch_shapes=[
             pltpu.VMEM((tokens, HEAD_DIM), F32), pltpu.VMEM((tokens, HEAD_DIM), F32), pltpu.VMEM((nb, tokens, cols), BF16),
             pltpu.VMEM((cols, dim), BF16), pltpu.VMEM((2, 2 * rows, dim), BF16), pltpu.VMEM((2, 2 * rows, cols), BF16),
-            dma, dma((2,)), dma((2,)), dma, dma((2, 3)), dma((1,)), dma((nb, GATHER_SEMS)), dma((nb, GATHER_SEMS)), dma((5,)), dma((5,)),
-            dma((early, 6)), dma((early, 6))],
-        input_output_aliases={11: 0},
+            dma, dma((2,)), dma((2,)), dma, dma((2, 3)), dma((2,)), dma((nb, GATHER_SEMS)), dma((nb, GATHER_SEMS)), dma, dma,
+            dma((nb, n // 2)), dma((nb, n // 2)), dma((early, 6)), dma((early, 6))],
+        input_output_aliases={10: 0},
         compiler_params=params("arbitrary", collective_id=1, has_side_effects=True),
         cost_estimate=cost(4 * nb * tokens * dim * cols + 4 * nb * tokens * tokens * cols, 8 * nb * tokens * dim),
-    )(q, k, v, gains, cos_tab, sin_tab, ss, w_q, w_k, w_v, w_o, d_full)
+    )(q, k, v, gains, cos_tab, sin_tab, ss, w_q, w_o, wo_p, d_full)
 
 
 def attn_bwd_kernel(n, nb, heads, dim, q_ref, k_ref, v_ref, do_ref, gain_ref, cos_ref, sin_ref, ss_ref,
-                    q_hbm, k_hbm, o_hbm, part_in, far_in, d_full,
-                    proj_out, g_out, g_p, dqs_out, dks_out, dwo_out, dgq_ref, dgk_ref,
+                    q_hbm, k_hbm, o_hbm, part_in, far_in, d_full, wk_hbm, wv_hbm,
+                    proj_out, g_out, g_p, dqs_out, dks_out, dwo_out, wk_p, wv_p, dgq_ref, dgk_ref,
                     part, recv_far, recv_side, s_send, s_recv,
                     inv_q, inv_k, acc_q, acc_k, p_all, ds_all, dq_all, qs_st, ks_st, v_st, st_row, st_sum, slots,
-                    ld_sem, w_sem, fl_sem, g_sem, go_sem, out_sem, e_send, e_recv, t_send, t_recv):
+                    ld_sem, w_sem, fl_sem, g_sem, go_sem, out_sem, e_send, e_recv, t_send, t_recv, r_send, r_recv):
     step = pl.program_id(0)
     tokens = q_ref.shape[1]
     rows = tokens // n
@@ -779,12 +812,17 @@
         return [pltpu.make_async_copy(part_in, part, ld_sem.at[0]),
                 pltpu.make_async_copy(far_in, recv_far.at[pl.ds(0, early)], ld_sem.at[1])]
 
+    def trade_w(j):
+        return place.to_partner((wk_hbm, wv_hbm)[j], (wk_p, wv_p)[j], t_send.at[j], t_recv.at[j])
+
     @pl.when(step == 0)
     def _():
         place.barrier(place.everyone())
         lax.fori_loop(early, nc, scatter.start_far, 0)
         for c in stored():
             c.start()
+        for j in range(2):
+            trade_w(j).start()
 
     @pl.when(step == 1)
     def _():
@@ -874,7 +912,7 @@
         st_sum[...] = stats.finish()
         rb = min(256, tokens)
         per = tokens // rb
-        trade = place.to_partner(g_out, g_p, t_send, t_recv)
+        trade = RowTrade(place, g_out, g_p, rows, r_send, r_recv)
 
         def norm_grad(fbuf, gbuf):
             def loads(i, slot):
@@ -972,10 +1010,13 @@
         pl.run_scoped(weight_grad, pltpu.VMEM((cols, nb * tokens), BF16), pltpu.VMEM((nb, tokens, cols), BF16),
                       pltpu.VMEM((2, nb, tokens, bn), BF16), pltpu.VMEM((2, cols, bn), BF16))
         scatter_end(scatter, proj_out, out_sem, nc)
-        trade.wait()
-
-
-def attn_bwd_call(n, q, k, v, d_attn, gains, cos_tab, sin_tab, ss, o, part, far, d_full):
+        trade.wait_recv()
+        trade.wait_send()
+        for j in range(2):
+            trade_w(j).wait()
+
+
+def attn_bwd_call(n, q, k, v, d_attn, gains, cos_tab, sin_tab, ss, o, part, far, d_full, w_k, w_v):
     nb, tokens, cols = q.shape
     dim = d_full.shape[2]
     heads = cols // HEAD_DIM
@@ -998,16 +1039,18 @@
     return pl.pallas_call(
         functools.partial(attn_bwd_kernel, n, nb, heads, dim), name="attn_bwd", grid=(steps + 1,),
         out_shape=[shape((nb, rows, dim), BF16), shape((nb, tokens, 3 * cols), BF16), shape((nb, tokens, 3 * cols), BF16),
-                   shape(whole, F32), shape(whole, F32), shape((cols, dim), BF16), shape((nb, 1, cols), F32), shape((nb, 1, cols), F32)],
-        in_specs=[blk, blk, blk, blk, vec, tab, tab, pl.BlockSpec(ss.shape, lambda i: (0, 0))] + [any_spec] * 6,
-        out_specs=[any_spec] * 6 + [out_vec, out_vec],
+                   shape(whole, F32), shape(whole, F32), shape((cols, dim), BF16),
+                   shape(w_k.shape, BF16), shape(w_v.shape, BF16), shape((nb, 1, cols), F32), shape((nb, 1, cols), F32)],
+        in_specs=[blk, blk, blk, blk, vec, tab, tab, pl.BlockSpec(ss.shape, lambda i: (0, 0))] + [any_spec] * 8,
+        out_specs=[any_spec] * 8 + [out_vec, out_vec],
         scratch_shapes=Scatter.scratch(nb * rows, dim) + [lane_tile] * 4 + [pltpu.VMEM((tokens, tokens), BF16)] * 2 + [
             lane_tile, pltpu.VMEM((2, tokens, HEAD_DIM), F32), pltpu.VMEM((2, tokens, HEAD_DIM), F32),
             pltpu.VMEM((2, tokens, HEAD_DIM), BF16), pltpu.VMEM(ss.shape, F32), pltpu.VMEM(ss.shape, F32), pltpu.VMEM((n,) + ss.shape, F32),
-            dma((2,)), dma((2, 2)), dma((2, 3)), dma((2, 4)), dma((2,)), dma((nb,)), dma((n,)), dma((n,)), dma, dma],
+            dma((2,)), dma((2, 2)), dma((2, 3)), dma((2, 4)), dma((2,)), dma((nb,)), dma((n,)), dma((n,)), dma((2,)), dma((2,)),
+            dma((nb, n // 2)), dma((nb, n // 2))],
         compiler_params=params("arbitrary", collective_id=2, has_side_effects=True),
         cost_estimate=cost(4 * nb * tokens * dim * cols + 36 * nb * tokens * tokens * cols, 30 * nb * tokens * cols),
-    )(q, k, v, d_attn, gains, cos_tab, sin_tab, ss, q, k, o, part, far, d_full)
+    )(q, k, v, d_attn, gains, cos_tab, sin_tab, ss, q, k, o, part, far, d_full, w_k, w_v)
 
 
 def dy_dw_kernel(n, nb, dim, g_hbm, g_p, wq_hbm, wk_hbm, wv_hbm, wq_p, wk_p, wv_p, y_full,
@@ -1035,8 +1078,6 @@
         for c in chunk(0):
             c.start()
         place.barrier(place.near()[:2])
-        for c in loads:
-            c.wait()
 
         def body(j, _):
             @pl.when(j + 1 < nc)
@@ -1046,13 +1087,19 @@
 
             for c in chunk(j):
                 c.wait()
-            w = wbuf[lax.rem(j, 2)]
+            slot = lax.rem(j, 2)
             half = 2 * nb * rows
             for d in range(2):
-                z = lax.dot_general(lhs[d * half:(d + 1) * half], w, NT, preferred_element_type=F32).astype(BF16)
+                @pl.when(j == 0)
+                def _(d=d):
+                    for c in loads[d * len(loads) // 2:(d + 1) * len(loads) // 2]:
+                        c.wait()
+
+                z = lax.dot_general(lhs[d * half:(d + 1) * half], wbuf[slot], NT, preferred_element_type=F32).astype(BF16)
                 part[j, 2 * d] = z[:half // 2]
                 part[j, 2 * d + 1] = z[half // 2:]
-            scatter.start_far(j)
+                if d == 0:
+                    scatter.start_far(j)
 
             @pl.when(j >= lag)
             def _():
@@ -1079,7 +1126,7 @@
             return [pltpu.make_async_copy(wst.at[slot, :, pl.ds(m * cols, cols)], out.at[dst], o_sem.at[slot, m])
                     for m, out in enumerate((dwq_out, dwk_out, dwv_out))]
 
-        load_g = pltpu.make_async_copy(g_hbm, g, ld_sem)
+        load_g = pltpu.make_async_copy(g_hbm, g, ld_sem.at[0])
         load_g.start()
         chunk(0).start()
         load_g.wait()
@@ -1129,15 +1176,15 @@
         functools.partial(dy_dw_kernel, n, nb, dim), name="dy_dw",
         out_shape=[shape((nb, rows, dim), BF16)] + [shape((dim, cols), BF16)] * 3,
         in_specs=[any_spec] * 9, out_specs=[any_spec] * 4,
-        scratch_shapes=Scatter.scratch(nb * rows, dim) + [dma, dma((2, 6)), dma((2,)), dma((2, 3)), dma((nb,))],
+        scratch_shapes=Scatter.scratch(nb * rows, dim) + [dma((2,)), dma((2, 6)), dma((2,)), dma((2, 3)), dma((nb,))],
         compiler_params=params(collective_id=3, has_side_effects=True),
         cost_estimate=cost(12 * nb * tokens * dim * cols, 30 * nb * tokens * cols),
     )(g, g_p, w_q, w_k, w_v, wq_p, wk_p, wv_p, y_full)
 
 
-def token_kernel(n_copies, x_ref, dy_ref, pr_ref, g_ref, m_ref, e_ref, bo_ref, *refs):
-    srcs, (xo_ref, dx_ref, dm_ref), dsts = refs[:4], refs[4:7], refs[7:11]
-    bufs, (acc, in_sem, out_sem) = refs[11:15], refs[15:]
+def token_kernel(n_copies, x_ref, dy_ref, pr_ref, g_ref, m_ref, e_ref, bo_ref, gq_ref, gk_ref, *refs):
+    srcs, (xo_ref, dx_ref, dm_ref, dgq_ref, dgk_ref), dsts = refs[:4], refs[4:9], refs[9:13]
+    bufs, (acc, in_sem, out_sem) = refs[13:17], refs[17:]
     group = 16
     step = pl.program_id(0)
     rows = x_ref.shape[1]
@@ -1174,6 +1221,8 @@
                 c.start()
 
     mod = m_ref[...] + e_ref[0]
+    for src, dst in ((gq_ref, dgq_ref), (gk_ref, dgk_ref)):
+        dst[...] = jnp.sum(src[...], axis=(0, 1))
     shift_bo = bo_ref[...].reshape(1, bo_ref.shape[0])
     acc[...] = jnp.zeros_like(acc)
 
@@ -1215,7 +1264,7 @@
                 copy.wait()
 
 
-def token_call(x_loc, dy_loc, proj, d_y, m_block, e_loc, b_o, grads):
+def token_call(x_loc, dy_loc, proj, d_y, m_block, e_loc, b_o, d_gq, d_gk, grads):
     nb, rows, dim = x_loc.shape
     n_copies = dim // min(512, dim)
     row = pl.BlockSpec((1, rows, dim), lambda i: (i, 0, 0))
@@ -1226,14 +1275,14 @@
     return pl.pallas_call(
         functools.partial(token_kernel, n_copies), name="tokens", grid=(nb,),
         out_shape=[jax.ShapeDtypeStruct(x_loc.shape, BF16), jax.ShapeDtypeStruct(x_loc.shape, BF16),
-                   jax.ShapeDtypeStruct((nb, 3, dim), F32)] + [jax.ShapeDtypeStruct(w.shape, BF16) for w in grads],
-        in_specs=[row, row, row, row, pl.BlockSpec((3, dim), lambda i: (0, 0)), mod, pl.BlockSpec(memory_space=pltpu.VMEM)] + [any_spec] * 4,
-        out_specs=[row, row, mod] + [any_spec] * 4,
+                   jax.ShapeDtypeStruct((nb, 3, dim), F32)] + [jax.ShapeDtypeStruct(d_gq.shape[2:], F32)] * 2 + [jax.ShapeDtypeStruct(w.shape, BF16) for w in grads],
+        in_specs=[row, row, row, row, pl.BlockSpec((3, dim), lambda i: (0, 0)), mod] + [pl.BlockSpec(memory_space=pltpu.VMEM)] * 3 + [any_spec] * 4,
+        out_specs=[row, row, mod] + [pl.BlockSpec(memory_space=pltpu.VMEM)] * 2 + [any_spec] * 4,
         scratch_shapes=[pltpu.VMEM((depth, w.shape[0] // n_copies, w.shape[1]), BF16) for w in grads]
         + [pltpu.VMEM((3, 8, dim), F32), dma((depth, 4)), dma((depth, 4))],
         compiler_params=params("arbitrary"),
         cost_estimate=cost(nb * rows * dim * 30, nb * rows * dim * 12),
-    )(x_loc, dy_loc, proj, d_y, m_block, e_loc, b_o, *grads)
+    )(x_loc, dy_loc, proj, d_y, m_block, e_loc, b_o, d_gq, d_gk, *grads)
 
 
 def solution(mesh):
@@ -1241,18 +1290,17 @@
 
     def device_step(x_loc, e_loc, m_block, w_q, b_q, w_k, b_k, w_v, b_v, w_o, b_o, g_q, g_k, pos_part, dy_loc):
         nb, _, dim = x_loc.shape
-        y_full, d_own, q, k, v, ss, cos_tab, sin_tab, gains = gather_qkv_call(
-            tp_size, x_loc, dy_loc, m_block, e_loc, w_q, w_k, w_v, b_q, b_k, b_v, g_q, g_k, pos_part)
-        d_full, o, _, d_attn, wq_p, wk_p, wv_p, _, part, far = gather_attn_call(
-            tp_size, q, k, v, gains, cos_tab, sin_tab, ss, w_q, w_k, w_v, w_o, d_own)
-        proj, g, g_p, _, _, d_wo, d_gq, d_gk = attn_bwd_call(
-            tp_size, q, k, v, d_attn, gains, cos_tab, sin_tab, ss, o, part, far, d_full)
+        y_full, d_own, q, k, v, wo_p, ss, cos_tab, sin_tab, gains = gather_qkv_call(
+            tp_size, x_loc, dy_loc, m_block, e_loc, w_q, w_k, w_v, w_o, b_q, b_k, b_v, g_q, g_k, pos_part)
+        d_full, o, _, d_attn, wq_p, part, far = gather_attn_call(
+            tp_size, q, k, v, gains, cos_tab, sin_tab, ss, w_q, w_o, wo_p, d_own)
+        proj, g, g_p, _, _, d_wo, wk_p, wv_p, d_gq, d_gk = attn_bwd_call(
+            tp_size, q, k, v, d_attn, gains, cos_tab, sin_tab, ss, o, part, far, d_full, w_k, w_v)
         d_y, d_wq, d_wk, d_wv = dy_dw_call(tp_size, g, g_p, w_q, w_k, w_v, wq_p, wk_p, wv_p, y_full)
-        x_out, d_x, d_mod, d_wq, d_wk, d_wv, d_wo = token_call(
-            x_loc, dy_loc, proj, d_y, m_block, e_loc, b_o, (d_wq, d_wk, d_wv, d_wo))
+        x_out, d_x, d_mod, d_gq, d_gk, d_wq, d_wk, d_wv, d_wo = token_call(
+            x_loc, dy_loc, proj, d_y, m_block, e_loc, b_o, d_gq, d_gk, (d_wq, d_wk, d_wv, d_wo))
         d_e = all_sum_call(tp_size, d_mod.reshape(tp_size, -1, HEAD_DIM)).reshape(nb, 3, dim)
-        return (x_out, d_x, d_e, jnp.sum(d_e, axis=0), d_wq, d_wk, d_wv, d_wo,
-                jnp.sum(d_gq, axis=(0, 1)), jnp.sum(d_gk, axis=(0, 1)))
+        return x_out, d_x, d_e, jnp.sum(d_e, axis=0), d_wq, d_wk, d_wv, d_wo, d_gq, d_gk
 
     in_specs = (P('dp', 'tp', None), P('dp', None, None), P(None, None), P(None, 'tp'), P('tp'), P(None, 'tp'), P('tp'),
                 P(None, 'tp'), P('tp'), P('tp', None), P(None), P('tp'), P('tp'), P('dp', None), P('dp', 'tp', None))

time: 511 us -> 501 us (0.980)
  Pallas kernels: 504 us -> 497 us
    pallas_call x1, Pallas kernels: 136 us -> 130 us  [gather_qkv_call(): pl.pallas_call(functools.partial(gather_qkv_kernel, n), name='gather_qkv'...]
where the time goes in v6:
time: 501 us; the launch traced here: 499 us
  Pallas kernels  497 us (99%)
    pallas_call x1, Pallas kernels, gather_qkv_call(): pl.pallas_call(functools.partial(gather_qkv_kernel, n), name='gather_qkv'...  130 us
    pallas_call x1, Pallas kernels, dy_dw_call(): pl.pallas_call(functools.partial(dy_dw_kernel, n, nb, dim), name='dy_dw',...  116 us
    pallas_call x1, Pallas kernels, gather_attn_call(): pl.pallas_call(functools.partial(gather_attn_kernel, n, nb, heads, dim),...  112 us
    pallas_call x1, Pallas kernels, attn_bwd_call(): pl.pallas_call(functools.partial(attn_bwd_kernel, n, nb, heads, dim), nam...  101 us
    pallas_call x1, Pallas kernels, token_call(): pl.pallas_call(functools.partial(token_kernel, n_copies), name='tokens',...  27 us
    pallas_call x1, Pallas kernels, all_sum_call(): pl.pallas_call(functools.partial(all_sum_kernel, n), name='all_sum', out_...  10.6 us

profile of v6, /device:TPU:81, one launch (start us, length us, event | category | flops | bytes accessed | tf_op | source)
XLA Modules:
  0.0 499.4 jit_solution(2446267262420832578)
XLA Ops:
  0.6 129.8 %gather_qkv.1 = (bf16[3,768,5120]{2,1,0:T(8,128)(2,1)}, bf16[3,768,5120]{2,1,0:T(8,128)(2,1)}, f32[3,768,640]{2,1,0:T(8,128)}, f32[3,768,640]{2,1,0:T(8,128)}, b...) custom-call(bf16[3,96,5120]{2,1,0:T(8,128)(2,1)} %x_ref.3, ...), custom_call_target="tpu_custom_call" | custom-call | flops 45298483200 | bytes 40304640 | tf_op jit(solution)/shard_map/gather_qkv/pallas_call | solution.py:401
  130.5 112.1 %gather_attn.1 = (bf16[3,768,5120]{2,1,0:T(8,128)(2,1)}, bf16[3,768,640]{2,1,0:T(8,128)(2,1)}, bf16[3,768,640]{2,1,0:T(8,128)(2,1)}, bf16[3,768,640]{2,1,0:T(8,1...) custom-call(f32[3,768,640]{2,1,0:T(8,128)} %get-tuple-element.47.q_r, ...), custom_call_target="tpu_custom_call", output_to_operand_aliasing={{0}: (10, {})} | custom-call | flops 34728837120 | bytes 94371840 | tf_op jit(solution)/shard_map/gather_attn/pallas_call | solution.py:776
  242.6 101.2 %attn_bwd.1 = (bf16[3,96,5120]{2,1,0:T(8,128)(2,1)}, bf16[3,768,1920]{2,1,0:T(8,128)(2,1)}, bf16[3,768,1920]{2,1,0:T(8,128)(2,1)}, f32[3,768,640]{2,1,0:T(8,128)...) custom-call(f32[3,768,640]{2,1,0:T(8,128)} %get-tuple-element.47.q_r, ...), custom_call_target="tpu_custom_call" | custom-call | flops 70967623680 | bytes 44236800 | tf_op jit(solution)/shard_map/attn_bwd/pallas_call | solution.py:1039
  343.7 116.2 %dy_dw.1 = (bf16[3,96,5120]{2,1,0:T(8,128)(2,1)}, bf16[5120,640]{1,0:T(8,128)(2,1)}, bf16[5120,640]{1,0:T(8,128)(2,1)}, bf16[5120,640]{1,0:T(8,128)(2,1)}) custom-call(bf16[3,768,1920]{2,1,0:T(8,128)(2,1)} %get-tuple-element.62.g_hbm, bf16[3,768,1920]{2,1,0:T(8,128)(2,1)} %get-tuple-element.63.g_p, bf16[5120,640]{1,0:T(8,128)(2,1)} %wq_hbm.1, ...), custom_call_target="tpu_custom_call" | custom-call | flops 90596966400 | bytes 44236800 | tf_op jit(solution)/shard_map/dy_dw/pallas_call | solution.py:1175
  459.9 27.0 %tokens.1 = (bf16[3,96,5120]{2,1,0:T(8,128)(2,1)}, bf16[3,96,5120]{2,1,0:T(8,128)(2,1)}, f32[3,3,5120]{2,1,0:T(4,128)}, f32[640]{0:T(1024)}, f32[640]{0:T(1024)}...) custom-call(bf16[3,96,5120]{2,1,0:T(8,128)(2,1)} %x_ref.3, ...), custom_call_target="tpu_custom_call" | custom-call | flops 44236800 | bytes 17694720 | tf_op jit(solution)/shard_map/tokens/pallas_call | solution.py:1275
  486.9 1.1 reshape.26.x_ref
  488.0 10.6 %all_sum.1 = f32[8,45,128]{2,1,0:T(8,128)S(1)} custom-call(f32[8,45,128]{2,1,0:T(8,128)S(1)} %reshape.26.x_ref), custom_call_target="tpu_custom_call" | custom-call | flops 4000000000 | bytes 368640 | tf_op jit(solution)/shard_map/all_sum/pallas_call | solution.py:455
  498.5 0.1 reshape.27
  498.6 0.0 copy-start
  498.6 0.7 reduce_sum.9
  499.3 0.0 copy-done
Async XLA Ops:
  498.6 0.7 copy-start

commit v7 on v6

--- a/solution.py
+++ b/solution.py
@@ -217,6 +217,7 @@
 GATHER_SEMS = 9
 EARLY_ROWS = 1
 EARLY_CHUNKS = 4
+EARLY_DY = 4
 
 
 def chunks_of(width, step):
@@ -246,8 +247,8 @@
 
 
 def gather_qkv_kernel(n, x_ref, dy_ref, m_ref, e_ref, wq_ref, wk_ref, wv_ref, wo_ref, bq_ref, bk_ref, bv_ref, gq_ref, gk_ref, pos_ref,
-                      freq_ref, y_full, d_full, q_out, k_out, v_out, wo_p, ss_ref, cos_ref, sin_ref, gain_ref,
-                      bias_ref, w_all, xin, stage, xbuf, zst, vst, sq, ss_row, slots,
+                      freq_ref, y_full, d_full, q_out, k_out, v_out, wo_p, wo_t, ss_ref, cos_ref, sin_ref, gain_ref,
+                      bias_ref, w_all, xin, stage, xbuf, zst, vst, sq, ss_row, slots, wo_in, wo_st, wo_sem,
                       w_sem, in_sem, st_sem, ld_sem, out_sem, g_send, g_recv, d_send, d_recv, e_send, e_recv, t_send, t_recv):
     nb, rows, dim = x_ref.shape
     cols = wq_ref.shape[1]
@@ -314,6 +315,40 @@
 
         lax.fori_loop(0, pos_ref.shape[1] // 128, rows_of, 0)
 
+    def turn_wo():
+        width = wo_in.shape[2]
+        n_chunks = dim // width
+
+        def load(c):
+            slot = lax.rem(c, 2)
+            return pltpu.make_async_copy(wo_ref.at[:, pl.ds(pl.multiple_of(c * width, width), width)], wo_in.at[slot], wo_sem.at[slot, 0])
+
+        def store(c):
+            slot = lax.rem(c, 2)
+            return pltpu.make_async_copy(wo_st.at[slot], wo_t.at[pl.ds(pl.multiple_of(c * width, width), width)], wo_sem.at[slot, 1])
+
+        load(0).start()
+
+        def body(c, _):
+            slot = lax.rem(c, 2)
+
+            @pl.when(c + 1 < n_chunks)
+            def _():
+                load(c + 1).start()
+
+            @pl.when(c >= 2)
+            def _():
+                store(c).wait()
+
+            load(c).wait()
+            wo_st[slot] = wo_in[slot].T
+            store(c).start()
+            return 0
+
+        lax.fori_loop(0, n_chunks, body, 0)
+        for c in range(min(2, n_chunks)):
+            store(c).wait()
+
     def gate_step(b, _):
         gate = m_ref[2:3] + e_ref[b, 2:3]
 
@@ -354,6 +389,7 @@
             trade.start()
             lax.fori_loop(0, nb, gate_step, 0)
             tables()
+            turn_wo()
 
         @pl.when(i >= 2)
         def _():
@@ -401,15 +437,16 @@
     return pl.pallas_call(
         functools.partial(gather_qkv_kernel, n), name="gather_qkv",
         out_shape=[shape((nb, tokens, dim), BF16), shape((nb, tokens, dim), BF16), shape((nb, tokens, cols), F32),
-                   shape((nb, tokens, cols), F32), shape((nb, tokens, cols), BF16), shape(w_o.shape, BF16), shape((stat_rows, tokens), F32),
+                   shape((nb, tokens, cols), F32), shape((nb, tokens, cols), BF16), shape(w_o.shape, BF16), shape((dim, cols), BF16), shape((stat_rows, tokens), F32),
                    shape((tokens, HEAD_DIM), F32), shape((tokens, HEAD_DIM), F32), shape((2, cols), F32)],
         in_specs=[any_spec, any_spec, vmem, vmem] + [any_spec] * 4 + [vmem] * 7,
-        out_specs=[any_spec] * 6 + [vmem] * 4,
+        out_specs=[any_spec] * 7 + [vmem] * 4,
         scratch_shapes=[
             pltpu.VMEM((1, 3 * cols), F32),
             pltpu.VMEM((dim, 3 * cols), BF16), pltpu.VMEM((nb, rows, dim), BF16), pltpu.VMEM((nb, rows, dim), BF16),
             pltpu.VMEM((2 * rows, dim), BF16), pltpu.VMEM((2, 2 * rows, 3 * cols), F32), pltpu.VMEM((2, 2 * rows, cols), BF16),
             pltpu.VMEM((2 * nb, tokens, HEAD_DIM), F32), pltpu.VMEM((stat_rows, tokens), F32), pltpu.VMEM((n, stat_rows, tokens), F32),
+            pltpu.VMEM((2, cols, min(512, dim)), BF16), pltpu.VMEM((2, min(512, dim), cols), BF16), dma((2, 2)),
             dma((3,)), dma((nb,)), dma, dma, dma((2, 3)), dma((nb, GATHER_SEMS)), dma((nb, GATHER_SEMS)),
             dma((EARLY_ROWS, GATHER_SEMS)), dma((EARLY_ROWS, GATHER_SEMS)), dma((n,)), dma((n,)), dma, dma],
         compiler_params=params(collective_id=0, has_side_effects=True),
@@ -470,11 +507,14 @@
     return x * cos + swap_pairs(x) * sin
 
 
+SCORE_SCALE = HEAD_DIM ** -0.5 * LOG2E
+
+
 def softmax_block(s):
-    c = HEAD_DIM ** -0.5 * LOG2E
     top = jnp.max(s, axis=1, keepdims=True)
-    p = jnp.exp2(s * c - top * c)
-    return p * (1.0 / jnp.sum(p, axis=1, keepdims=True))
+    p = jnp.exp2(s * SCORE_SCALE - top * SCORE_SCALE)
+    total = jnp.sum(p, axis=1, keepdims=True)
+    return p * (1.0 / total), top * SCORE_SCALE + jnp.log(total) * LOG2E
 
 
 class Scatter:
@@ -512,15 +552,20 @@
 
     def sums(self, j):
         h = self.half
-        arrived = isinstance(j, int) and j < self.early
-        if not arrived:
+
+        @pl.when(j >= self.early)
+        def _():
             self.message(j, 0).wait_recv()
+            self.message(j, 1).wait_recv()
+
         self.part[j, 1, :h] = (self.part[j, 1, :h].astype(F32) + self.far[j, 0].astype(F32)).astype(BF16)
-        if not arrived:
-            self.message(j, 1).wait_recv()
         self.part[j, 2, h:] = (self.part[j, 2, h:].astype(F32) + self.far[j, 1].astype(F32)).astype(BF16)
         self.message(j, 4).start()
         self.message(j, 5).start()
+
+    def sums_step(self, j, _):
+        self.sums(j)
+        return 0
 
     def final(self, j):
         for idx in range(2, 6):
@@ -581,14 +626,14 @@
 
 
 def gather_attn_kernel(n, nb, heads, dim, q_ref, k_ref, v_ref, gain_ref, cos_ref, sin_ref, ss_ref,
-                       wq_ref, wo_ref, wo_p, d_in,
-                       d_full, o_out, o_p, da_out, wq_p, part_out, far_in,
+                       wq_ref, wo_ref, wo_p, wo_t, d_in,
+                       d_full, o_out, o_p, da_out, wq_p, part_out, far_in, qr_ref, kr_ref, lse_ref, o32_ref,
                        inv_q, inv_k, o_all, wo, xbuf, ast,
                        w_sem, ld_sem, out_sem, o_sem, p_sem, l_sem, g_send, g_recv, t_send, t_recv, r_send, r_recv, s_send, s_recv):
     step = pl.program_id(0)
     tokens = q_ref.shape[1]
     rows = tokens // n
-    blk = min(256, tokens)
+    blk = min(384, tokens)
     place = Place(n)
     gather = Gather(place, d_full, rows, g_send, g_recv, early=EARLY_ROWS)
     cols = heads * HEAD_DIM
@@ -603,7 +648,7 @@
 
     @pl.when(step == 0)
     def _():
-        pltpu.make_async_copy(wo_ref, wo, w_sem).start()
+        pltpu.make_async_copy(wo_t, wo, w_sem).start()
         place.barrier(place.near())
 
         for b in range(EARLY_ROWS):
@@ -632,16 +677,27 @@
         k_rot = rotate(k_ref[0] * inv_k[...] * gain_ref[1:2], cos, sin).astype(BF16)
         v = v_ref[0]
         lanes = pl.ds(pl.multiple_of(h * HEAD_DIM, HEAD_DIM), HEAD_DIM)
+        qr_ref[0], kr_ref[0] = q_rot, k_rot
+
+        def scores(i):
+            return lax.dot_general(q_rot[i * blk:(i + 1) * blk], k_rot, NT, preferred_element_type=F32)
+
+        ahead = scores(0)
         for i in range(tokens // blk):
-            s = lax.dot_general(q_rot[i * blk:(i + 1) * blk], k_rot, NT, preferred_element_type=F32)
-            p = softmax_block(s).astype(BF16)
-            o_all[b, i * blk:(i + 1) * blk, lanes] = jnp.dot(p, v, preferred_element_type=F32).astype(BF16)
+            s = ahead
+            if (i + 1) * blk < tokens:
+                ahead = scores(i + 1)
+            p, lse = softmax_block(s)
+            lse_ref[0, i * blk:(i + 1) * blk] = jnp.broadcast_to(lse, (blk, HEAD_DIM))
+            o = jnp.dot(p.astype(BF16), v, preferred_element_type=F32)
+            o32_ref[0, i * blk:(i + 1) * blk] = o
+            o_all[b, i * blk:(i + 1) * blk, lanes] = o.astype(BF16)
 
     @pl.when(step == nb * heads)
     def _():
         o_copy = pltpu.make_async_copy(o_all, o_out, o_sem)
         o_copy.start()
-        pltpu.make_async_copy(wo_ref, wo, w_sem).wait()
+        pltpu.make_async_copy(wo_t, wo, w_sem).wait()
 
         def outputs(b, row0, slot):
             return pltpu.make_async_copy(ast.at[slot], da_out.at[b, pl.ds(row0, 2 * rows)], out_sem.at[slot])
@@ -711,7 +767,7 @@
         def item(i, _):
             slot = lax.rem(i, 2)
 
-            @pl.when(i + 1 < 3 * nb)
+            @pl.when((i + 1 != 3 * nb) & (i + 1 < 4 * nb - 1))
             def _():
                 take(i + 1)
 
@@ -720,7 +776,7 @@
                 outputs(0, 0, slot).wait()
 
             load(0, 0, slot).wait()
-            ast[slot] = lax.dot_general(xbuf[slot], wo[...], NT, preferred_element_type=F32).astype(BF16)
+            ast[slot] = jnp.dot(xbuf[slot], wo[...], preferred_element_type=F32).astype(BF16)
             b, row0 = gather.item_place(i, nb)
             outputs(b, row0, slot).start()
 
@@ -735,7 +791,7 @@
                 pl.run_scoped(project, pltpu.VMEM((4 * nb * rows, 2 * cols), BF16), pltpu.VMEM((2, 2 * cols, CHUNK), BF16),
                               pltpu.VMEM((2, 4, nb * rows, CHUNK), BF16))
 
-            @pl.when((i + 1 >= 3 * nb) & (i + 1 < 4 * nb))
+            @pl.when((i + 1 == 3 * nb) | (i + 1 == 4 * nb - 1))
             def _():
                 take(i + 1)
 
@@ -753,7 +809,7 @@
                 scatter.message(j, idx).wait()
 
 
-def gather_attn_call(n, q, k, v, gains, cos_tab, sin_tab, ss, w_q, w_o, wo_p, d_full):
+def gather_attn_call(n, q, k, v, gains, cos_tab, sin_tab, ss, w_q, w_o, wo_p, wo_t, d_full):
     nb, tokens, cols = q.shape
     dim = w_o.shape[1]
     heads = cols // HEAD_DIM
@@ -776,26 +832,43 @@
     return pl.pallas_call(
         functools.partial(gather_attn_kernel, n, nb, heads, dim), name="gather_attn", grid=(nb * heads + 1,),
         out_shape=[shape(d_full.shape, BF16), head_arr, head_arr, head_arr, shape(w_q.shape, BF16)]
-        + [shape((nc, 4, nb * rows, CHUNK), BF16), shape((early, 2, nb * rows // 2, CHUNK), BF16)],
-        in_specs=[blk, blk, blk, vec, tab, tab, pl.BlockSpec(ss.shape, lambda i: (0, 0))] + [any_spec] * 4,
-        out_specs=[any_spec] * 7,
+        + [shape((nc, 4, nb * rows, CHUNK), BF16), shape((early, 2, nb * rows // 2, CHUNK), BF16), head_arr, head_arr,
+           shape((nb, tokens, cols), F32), shape((nb, tokens, cols), F32)],
+        in_specs=[blk, blk, blk, vec, tab, tab, pl.BlockSpec(ss.shape, lambda i: (0, 0))] + [any_spec] * 5,
+        out_specs=[any_spec] * 7 + [blk] * 4,
         scratch_shapes=[
             pltpu.VMEM((tokens, HEAD_DIM), F32), pltpu.VMEM((tokens, HEAD_DIM), F32), pltpu.VMEM((nb, tokens, cols), BF16),
-            pltpu.VMEM((cols, dim), BF16), pltpu.VMEM((2, 2 * rows, dim), BF16), pltpu.VMEM((2, 2 * rows, cols), BF16),
+            pltpu.VMEM((dim, cols), BF16), pltpu.VMEM((2, 2 * rows, dim), BF16), pltpu.VMEM((2, 2 * rows, cols), BF16),
             dma, dma((2,)), dma((2,)), dma, dma((2, 3)), dma((2,)), dma((nb, GATHER_SEMS)), dma((nb, GATHER_SEMS)), dma, dma,
             dma((nb, n // 2)), dma((nb, n // 2)), dma((early, 6)), dma((early, 6))],
-        input_output_aliases={10: 0},
+        input_output_aliases={11: 0},
         compiler_params=params("arbitrary", collective_id=1, has_side_effects=True),
         cost_estimate=cost(4 * nb * tokens * dim * cols + 4 * nb * tokens * tokens * cols, 8 * nb * tokens * dim),
-    )(q, k, v, gains, cos_tab, sin_tab, ss, w_q, w_o, wo_p, d_full)
-
-
-def attn_bwd_kernel(n, nb, heads, dim, q_ref, k_ref, v_ref, do_ref, gain_ref, cos_ref, sin_ref, ss_ref,
-                    q_hbm, k_hbm, o_hbm, part_in, far_in, d_full, wk_hbm, wv_hbm,
-                    proj_out, g_out, g_p, dqs_out, dks_out, dwo_out, wk_p, wv_p, dgq_ref, dgk_ref,
+    )(q, k, v, gains, cos_tab, sin_tab, ss, w_q, w_o, wo_p, wo_t, d_full)
+
+
+class DyChunks:
+    def __init__(self, lhs, wbuf, weights, w_sem):
+        self.lhs, self.wbuf, self.weights, self.sem = lhs, wbuf, weights, w_sem
+
+    def loads(self, j):
+        slot = lax.rem(j, 2)
+        src = pl.ds(pl.multiple_of(j * CHUNK, CHUNK), CHUNK)
+        width = self.weights[0].shape[1]
+        return [pltpu.make_async_copy(w.at[src], self.wbuf.at[slot, :, pl.ds(m * width, width)], self.sem.at[slot, m])
+                for m, w in enumerate(self.weights)]
+
+    def dot(self, j, d):
+        half = self.lhs.shape[0] // 2
+        return lax.dot_general(self.lhs[d * half:(d + 1) * half], self.wbuf[lax.rem(j, 2)], NT, preferred_element_type=F32).astype(BF16)
+
+
+def attn_bwd_kernel(n, nb, heads, dim, q_ref, k_ref, qr_ref, kr_ref, v_ref, do_ref, o_ref, lse_ref, gain_ref, cos_ref, sin_ref, ss_ref,
+                    q_hbm, k_hbm, o_hbm, part_in, far_in, d_full, wq_hbm, wk_hbm, wv_hbm, wq_p,
+                    proj_out, g_out, g_p, dqs_out, dks_out, dwo_out, wk_p, wv_p, part_dy, far_dy, dgq_ref, dgk_ref,
                     part, recv_far, recv_side, s_send, s_recv,
                     inv_q, inv_k, acc_q, acc_k, p_all, ds_all, dq_all, qs_st, ks_st, v_st, st_row, st_sum, slots,
-                    ld_sem, w_sem, fl_sem, g_sem, go_sem, out_sem, e_send, e_recv, t_send, t_recv, r_send, r_recv):
+                    ld_sem, w_sem, fl_sem, g_sem, go_sem, out_sem, e_send, e_recv, t_send, t_recv, r_send, r_recv, c_sem, y_send, y_recv):
     step = pl.program_id(0)
     tokens = q_ref.shape[1]
     rows = tokens // n
@@ -836,8 +909,9 @@
                 pltpu.make_async_copy(ks_st.at[slot], dks_out.at[b, :, lanes], fl_sem.at[slot, 1]),
                 pltpu.make_async_copy(v_st.at[slot], g_out.at[b, :, v_lanes], fl_sem.at[slot, 2])]
 
-    for j in range(nc):
-        at_step = 1 + j * (steps - 2) // max(nc - 1, 1)
+    mid = nc // 2
+    for j in range(mid):
+        at_step = 1 + j * (steps - 2) // max(mid - 1, 1)
         pl.when(step == at_step)(functools.partial(scatter.sums, j))
 
     @pl.when(step < steps)
@@ -863,16 +937,23 @@
                 c.wait()
 
         cos, sin = cos_ref[...], sin_ref[...]
-        q_rot = rotate(q_ref[0] * inv_q[...] * gain_ref[0:1], cos, sin).astype(BF16)
-        k_rot = rotate(k_ref[0] * inv_k[...] * gain_ref[1:2], cos, sin).astype(BF16)
-        v = v_ref[0]
-        do = do_ref[0]
+        q_rot, k_rot, v, do = qr_ref[0], kr_ref[0], v_ref[0], do_ref[0]
+
+        def scores(i):
+            sl = slice(i * blk, (i + 1) * blk)
+            return (lax.dot_general(q_rot[sl], k_rot, NT, preferred_element_type=F32),
+                    lax.dot_general(do[sl], v, NT, preferred_element_type=F32))
+
+        ahead = scores(0)
         for i in range(tokens // blk):
             sl = slice(i * blk, (i + 1) * blk)
-            p = softmax_block(lax.dot_general(q_rot[sl], k_rot, NT, preferred_element_type=F32))
+            s, dp = ahead
+            if (i + 1) * blk < tokens:
+                ahead = scores(i + 1)
+            lse = jnp.concatenate([lse_ref[0, sl]] * (tokens // HEAD_DIM), axis=1)
+            p = jnp.exp2(s * SCORE_SCALE - lse)
             p_all[sl] = p.astype(BF16)
-            dp = lax.dot_general(do[sl], v, NT, preferred_element_type=F32)
-            delta = jnp.sum(dp * p, axis=1, keepdims=True)
+            delta = jnp.sum(do[sl].astype(F32) * o_ref[0, sl], axis=1, keepdims=True)
             ds = (p * (dp - delta)).astype(BF16)
             ds_all[sl] = ds
             dq_all[sl] = jnp.dot(ds, k_rot, preferred_element_type=F32) * scale
@@ -908,6 +989,7 @@
                 c.wait()
         stats = Exchange(place, st_row, slots, e_send, e_recv)
         stats.start()
+        lax.fori_loop(mid, nc, scatter.sums_step, 0)
         lax.fori_loop(0, nc, scatter.start_side, 0)
         st_sum[...] = stats.finish()
         rb = min(256, tokens)
@@ -1009,14 +1091,61 @@
         bn = min(512, dim)
         pl.run_scoped(weight_grad, pltpu.VMEM((cols, nb * tokens), BF16), pltpu.VMEM((nb, tokens, cols), BF16),
                       pltpu.VMEM((2, nb, tokens, bn), BF16), pltpu.VMEM((2, cols, bn), BF16))
+        trade.wait_recv()
+        for j in range(2):
+            trade_w(j).wait_recv()
+
+        n_dy = part_dy.shape[0]
+        scatter_y = Scatter(place, part_dy, far_dy, None, y_send, y_recv)
+
+        def first_dy(lhs, wbuf, pst):
+            loads = pair_rows(place, nb, rows, g_out, g_p, lhs, ld_sem)
+            for c in loads:
+                c.start()
+            dy = DyChunks(lhs, wbuf, (wq_hbm, wk_hbm, wv_hbm, wq_p, wk_p, wv_p), c_sem)
+            for c in dy.loads(0):
+                c.start()
+            for c in loads:
+                c.wait()
+
+            def body(j, _):
+                @pl.when(j + 1 < n_dy)
+                def _():
+                    for c in dy.loads(j + 1):
+                        c.start()
+
+                for c in dy.loads(j):
+                    c.wait()
+                store = pltpu.make_async_copy(pst, part_dy.at[j], go_sem.at[0])
+
+                @pl.when(j >= 1)
+                def _():
+                    store.wait()
+                    scatter_y.start_far(j - 1)
+
+                for d in range(2):
+                    z = dy.dot(j, d)
+                    pst[2 * d] = z[:nb * rows]
+                    pst[2 * d + 1] = z[nb * rows:]
+                store.start()
+                return 0
+
+            lax.fori_loop(0, n_dy, body, 0)
+            pltpu.make_async_copy(pst, part_dy.at[n_dy - 1], go_sem.at[0]).wait()
+            scatter_y.start_far(n_dy - 1)
+
+        pl.run_scoped(first_dy, pltpu.VMEM((4 * nb * rows, 6 * cols), BF16), pltpu.VMEM((2, CHUNK, 6 * cols), BF16),
+                      pltpu.VMEM((4, nb * rows, CHUNK), BF16))
         scatter_end(scatter, proj_out, out_sem, nc)
-        trade.wait_recv()
         trade.wait_send()
         for j in range(2):
-            trade_w(j).wait()
-
-
-def attn_bwd_call(n, q, k, v, d_attn, gains, cos_tab, sin_tab, ss, o, part, far, d_full, w_k, w_v):
+            trade_w(j).wait_send()
+        for j in range(n_dy):
+            for idx in (0, 1):
+                scatter_y.message(j, idx).wait()
+
+
+def attn_bwd_call(n, q, k, q_rot, k_rot, v, d_attn, o, o32, lse, gains, cos_tab, sin_tab, ss, part, far, d_full, w_q, w_k, w_v, wq_p):
     nb, tokens, cols = q.shape
     dim = d_full.shape[2]
     heads = cols // HEAD_DIM
@@ -1036,83 +1165,88 @@
     tab = pl.BlockSpec((tokens, HEAD_DIM), lambda i: (0, 0))
     whole = (nb, tokens, cols)
     lane_tile = pltpu.VMEM((tokens, HEAD_DIM), F32)
+    n_dy = min(EARLY_DY, dim // CHUNK)
     return pl.pallas_call(
         functools.partial(attn_bwd_kernel, n, nb, heads, dim), name="attn_bwd", grid=(steps + 1,),
         out_shape=[shape((nb, rows, dim), BF16), shape((nb, tokens, 3 * cols), BF16), shape((nb, tokens, 3 * cols), BF16),
                    shape(whole, F32), shape(whole, F32), shape((cols, dim), BF16),
-                   shape(w_k.shape, BF16), shape(w_v.shape, BF16), shape((nb, 1, cols), F32), shape((nb, 1, cols), F32)],
-        in_specs=[blk, blk, blk, blk, vec, tab, tab, pl.BlockSpec(ss.shape, lambda i: (0, 0))] + [any_spec] * 8,
-        out_specs=[any_spec] * 8 + [out_vec, out_vec],
+                   shape(w_k.shape, BF16), shape(w_v.shape, BF16), shape((n_dy,) + part.shape[1:], BF16), shape((n_dy,) + far.shape[1:], BF16),
+                   shape((nb, 1, cols), F32), shape((nb, 1, cols), F32)],
+        in_specs=[blk] * 8 + [vec, tab, tab, pl.BlockSpec(ss.shape, lambda i: (0, 0))] + [any_spec] * 10,
+        out_specs=[any_spec] * 10 + [out_vec, out_vec],
         scratch_shapes=Scatter.scratch(nb * rows, dim) + [lane_tile] * 4 + [pltpu.VMEM((tokens, tokens), BF16)] * 2 + [
             lane_tile, pltpu.VMEM((2, tokens, HEAD_DIM), F32), pltpu.VMEM((2, tokens, HEAD_DIM), F32),
             pltpu.VMEM((2, tokens, HEAD_DIM), BF16), pltpu.VMEM(ss.shape, F32), pltpu.VMEM(ss.shape, F32), pltpu.VMEM((n,) + ss.shape, F32),
             dma((2,)), dma((2, 2)), dma((2, 3)), dma((2, 4)), dma((2,)), dma((nb,)), dma((n,)), dma((n,)), dma((2,)), dma((2,)),
-            dma((nb, n // 2)), dma((nb, n // 2))],
+            dma((nb, n // 2)), dma((nb, n // 2)), dma((2, 6)), dma((n_dy, 6)), dma((n_dy, 6))],
         compiler_params=params("arbitrary", collective_id=2, has_side_effects=True),
         cost_estimate=cost(4 * nb * tokens * dim * cols + 36 * nb * tokens * tokens * cols, 30 * nb * tokens * cols),
-    )(q, k, v, d_attn, gains, cos_tab, sin_tab, ss, q, k, o, part, far, d_full, w_k, w_v)
-
-
-def dy_dw_kernel(n, nb, dim, g_hbm, g_p, wq_hbm, wk_hbm, wv_hbm, wq_p, wk_p, wv_p, y_full,
+    )(q, k, q_rot, k_rot, v, d_attn, o32, lse, gains, cos_tab, sin_tab, ss, q, k, o, part, far, d_full, w_q, w_k, w_v, wq_p)
+
+
+def dy_dw_kernel(n, nb, dim, g_hbm, g_p, wq_hbm, wk_hbm, wv_hbm, wq_p, wk_p, wv_p, y_full, part_in, far_in,
                  dy_out, dwq_out, dwk_out, dwv_out,
-                 part, recv_far, recv_side, s_send, s_recv, ld_sem, w_sem, y_sem, o_sem, out_sem):
+                 part, recv_far, recv_side, s_send, s_recv, g, ld_sem, w_sem, y_sem, o_sem, out_sem):
     tokens = g_hbm.shape[1]
     rows = tokens // n
     cols = g_hbm.shape[2] // 3
     nc = dim // CHUNK
+    early = far_in.shape[0]
+    lag = 3
     place = Place(n)
-    scatter = Scatter(place, part, recv_far, recv_side, s_send, s_recv)
-    lag = 4
+    scatter = Scatter(place, part, recv_far, recv_side, s_send, s_recv, early=early)
+    stored = [pltpu.make_async_copy(part_in, part.at[pl.ds(0, early)], ld_sem.at[2]),
+              pltpu.make_async_copy(far_in, recv_far.at[pl.ds(0, early)], ld_sem.at[3])]
+    load_g = pltpu.make_async_copy(g_hbm, g, ld_sem.at[4])
 
     def chain(lhs, wbuf):
+        for c in stored:
+            c.start()
         loads = pair_rows(place, nb, rows, g_hbm, g_p, lhs, ld_sem)
-        for c in loads:
-            c.start()
-
-        def chunk(j):
-            slot = lax.rem(j, 2)
-            src = pl.ds(pl.multiple_of(j * CHUNK, CHUNK), CHUNK)
-            return [pltpu.make_async_copy(w.at[src], wbuf.at[slot, :, pl.ds(m * cols, cols)], w_sem.at[slot, m])
-                    for m, w in enumerate((wq_hbm, wk_hbm, wv_hbm, wq_p, wk_p, wv_p))]
-
-        for c in chunk(0):
-            c.start()
+        dy = DyChunks(lhs, wbuf, (wq_hbm, wk_hbm, wv_hbm, wq_p, wk_p, wv_p), w_sem)
+        if early < nc:
+            for c in loads:
+                c.start()
+            for c in dy.loads(early):
+                c.start()
         place.barrier(place.near()[:2])
+        for c in stored:
+            c.wait()
+        lax.fori_loop(0, early, scatter.sums_step, 0)
+        load_g.start()
 
         def body(j, _):
             @pl.when(j + 1 < nc)
             def _():
-                for c in chunk(j + 1):
+                for c in dy.loads(j + 1):
                     c.start()
 
-            for c in chunk(j):
+            for c in dy.loads(j):
                 c.wait()
-            slot = lax.rem(j, 2)
-            half = 2 * nb * rows
             for d in range(2):
-                @pl.when(j == 0)
+                @pl.when(j == early)
                 def _(d=d):
                     for c in loads[d * len(loads) // 2:(d + 1) * len(loads) // 2]:
                         c.wait()
 
-                z = lax.dot_general(lhs[d * half:(d + 1) * half], wbuf[slot], NT, preferred_element_type=F32).astype(BF16)
-                part[j, 2 * d] = z[:half // 2]
-                part[j, 2 * d + 1] = z[half // 2:]
+                z = dy.dot(j, d)
+                part[j, 2 * d] = z[:nb * rows]
+                part[j, 2 * d + 1] = z[nb * rows:]
                 if d == 0:
                     scatter.start_far(j)
 
-            @pl.when(j >= lag)
+            @pl.when(j >= early + lag)
             def _():
                 scatter.sums(j - lag)
 
             return 0
 
-        lax.fori_loop(0, nc, body, 0)
+        lax.fori_loop(early, nc, body, 0)
         lax.fori_loop(0, nc, scatter.start_side, 0)
 
     pl.run_scoped(chain, pltpu.VMEM((4 * nb * rows, 6 * cols), BF16), pltpu.VMEM((2, CHUNK, 6 * cols), BF16))
 
-    def weight_grad(g, ybuf, wst):
+    def weight_grad(ybuf, wst):
         bm = min(512, dim)
         n_chunks = dim // bm
 
@@ -1126,8 +1260,6 @@
             return [pltpu.make_async_copy(wst.at[slot, :, pl.ds(m * cols, cols)], out.at[dst], o_sem.at[slot, m])
                     for m, out in enumerate((dwq_out, dwk_out, dwv_out))]
 
-        load_g = pltpu.make_async_copy(g_hbm, g, ld_sem.at[0])
-        load_g.start()
         chunk(0).start()
         load_g.wait()
 
@@ -1145,8 +1277,9 @@
 
             chunk(c).wait()
             for m in range(lag):
-                late = nc - lag + m
-                pl.when(c == min(m, n_chunks - 1))(functools.partial(scatter.sums, max(late, 0)) if late >= 0 else (lambda: None))
+                late = max(nc - lag, early) + m
+                if late < nc:
+                    pl.when(c == min(m, n_chunks - 1))(functools.partial(scatter.sums, late))
             wst[slot] = lax.dot_general(ybuf[slot].reshape(nb * tokens, bm), g[...].reshape(nb * tokens, 3 * cols), TN,
                                         preferred_element_type=F32).astype(BF16)
             for s in store(c):
@@ -1159,12 +1292,11 @@
                 c.wait()
 
     bm = min(512, dim)
-    pl.run_scoped(weight_grad, pltpu.VMEM((nb, tokens, 3 * cols), BF16), pltpu.VMEM((2, nb, tokens, bm), BF16),
-                  pltpu.VMEM((2, bm, 3 * cols), BF16))
+    pl.run_scoped(weight_grad, pltpu.VMEM((2, nb, tokens, bm), BF16), pltpu.VMEM((2, bm, 3 * cols), BF16))
     scatter_end(scatter, dy_out, out_sem, nc)
 
 
-def dy_dw_call(n, g, g_p, w_q, w_k, w_v, wq_p, wk_p, wv_p, y_full):
+def dy_dw_call(n, g, g_p, w_q, w_k, w_v, wq_p, wk_p, wv_p, y_full, part, far):
     nb, tokens, wide = g.shape
     dim = y_full.shape[2]
     cols = wide // 3
@@ -1175,11 +1307,11 @@
     return pl.pallas_call(
         functools.partial(dy_dw_kernel, n, nb, dim), name="dy_dw",
         out_shape=[shape((nb, rows, dim), BF16)] + [shape((dim, cols), BF16)] * 3,
-        in_specs=[any_spec] * 9, out_specs=[any_spec] * 4,
-        scratch_shapes=Scatter.scratch(nb * rows, dim) + [dma((2,)), dma((2, 6)), dma((2,)), dma((2, 3)), dma((nb,))],
+        in_specs=[any_spec] * 11, out_specs=[any_spec] * 4,
+        scratch_shapes=Scatter.scratch(nb * rows, dim) + [pltpu.VMEM((nb, tokens, 3 * cols), BF16), dma((5,)), dma((2, 6)), dma((2,)), dma((2, 3)), dma((nb,))],
         compiler_params=params(collective_id=3, has_side_effects=True),
         cost_estimate=cost(12 * nb * tokens * dim * cols, 30 * nb * tokens * cols),
-    )(g, g_p, w_q, w_k, w_v, wq_p, wk_p, wv_p, y_full)
+    )(g, g_p, w_q, w_k, w_v, wq_p, wk_p, wv_p, y_full, part, far)
 
 
 def token_kernel(n_copies, x_ref, dy_ref, pr_ref, g_ref, m_ref, e_ref, bo_ref, gq_ref, gk_ref, *refs):
@@ -1290,13 +1422,13 @@
 
     def device_step(x_loc, e_loc, m_block, w_q, b_q, w_k, b_k, w_v, b_v, w_o, b_o, g_q, g_k, pos_part, dy_loc):
         nb, _, dim = x_loc.shape
-        y_full, d_own, q, k, v, wo_p, ss, cos_tab, sin_tab, gains = gather_qkv_call(
+        y_full, d_own, q, k, v, wo_p, wo_t, ss, cos_tab, sin_tab, gains = gather_qkv_call(
             tp_size, x_loc, dy_loc, m_block, e_loc, w_q, w_k, w_v, w_o, b_q, b_k, b_v, g_q, g_k, pos_part)
-        d_full, o, _, d_attn, wq_p, part, far = gather_attn_call(
-            tp_size, q, k, v, gains, cos_tab, sin_tab, ss, w_q, w_o, wo_p, d_own)
-        proj, g, g_p, _, _, d_wo, wk_p, wv_p, d_gq, d_gk = attn_bwd_call(
-            tp_size, q, k, v, d_attn, gains, cos_tab, sin_tab, ss, o, part, far, d_full, w_k, w_v)
-        d_y, d_wq, d_wk, d_wv = dy_dw_call(tp_size, g, g_p, w_q, w_k, w_v, wq_p, wk_p, wv_p, y_full)
+        d_full, o, _, d_attn, wq_p, part, far, q_rot, k_rot, lse, o32 = gather_attn_call(
+            tp_size, q, k, v, gains, cos_tab, sin_tab, ss, w_q, w_o, wo_p, wo_t, d_own)
+        proj, g, g_p, _, _, d_wo, wk_p, wv_p, part, far, d_gq, d_gk = attn_bwd_call(
+            tp_size, q, k, q_rot, k_rot, v, d_attn, o, o32, lse, gains, cos_tab, sin_tab, ss, part, far, d_full, w_q, w_k, w_v, wq_p)
+        d_y, d_wq, d_wk, d_wv = dy_dw_call(tp_size, g, g_p, w_q, w_k, w_v, wq_p, wk_p, wv_p, y_full, part, far)
         x_out, d_x, d_mod, d_gq, d_gk, d_wq, d_wk, d_wv, d_wo = token_call(
             x_loc, dy_loc, proj, d_y, m_block, e_loc, b_o, d_gq, d_gk, (d_wq, d_wk, d_wv, d_wo))
         d_e = all_sum_call(tp_size, d_mod.reshape(tp_size, -1, HEAD_DIM)).reshape(nb, 3, dim)

time: 501 us -> 489 us (0.976)
  Pallas kernels: 497 us -> 485 us
    pallas_call x1, Pallas kernels: 116 us -> 94.7 us  [dy_dw_call(): pl.pallas_call(functools.partial(dy_dw_kernel, n, nb, dim), name='dy_dw',...]
    pallas_call x1, Pallas kernels: 101 us -> 114 us  [attn_bwd_call(): pl.pallas_call(functools.partial(attn_bwd_kernel, n, nb, heads, dim), nam...]
    pallas_call x1, Pallas kernels: 112 us -> 107 us  [gather_attn_call(): pl.pallas_call(functools.partial(gather_attn_kernel, n, nb, heads, dim),...]
where the time goes in v7:
time: 489 us; the launch traced here: 487 us
  Pallas kernels  485 us (99%)
    pallas_call x1, Pallas kernels, gather_qkv_call(): pl.pallas_call(functools.partial(gather_qkv_kernel, n), name='gather_qkv'...  130 us
    pallas_call x1, Pallas kernels, attn_bwd_call(): pl.pallas_call(functools.partial(attn_bwd_kernel, n, nb, heads, dim), nam...  114 us
    pallas_call x1, Pallas kernels, gather_attn_call(): pl.pallas_call(functools.partial(gather_attn_kernel, n, nb, heads, dim),...  107 us
    pallas_call x1, Pallas kernels, dy_dw_call(): pl.pallas_call(functools.partial(dy_dw_kernel, n, nb, dim), name='dy_dw',...  94.7 us
    pallas_call x1, Pallas kernels, token_call(): pl.pallas_call(functools.partial(token_kernel, n_copies), name='tokens',...  27 us
    pallas_call x1, Pallas kernels, all_sum_call(): pl.pallas_call(functools.partial(all_sum_kernel, n), name='all_sum', out_...  12.1 us

profile of v7, /device:TPU:81, one launch (start us, length us, event | category | flops | bytes accessed | tf_op | source)
XLA Modules:
  0.0 487.2 jit_solution(13410536556256552712)
XLA Ops:
  0.6 129.8 %gather_qkv.1 = (bf16[3,768,5120]{2,1,0:T(8,128)(2,1)}, bf16[3,768,5120]{2,1,0:T(8,128)(2,1)}, f32[3,768,640]{2,1,0:T(8,128)}, f32[3,768,640]{2,1,0:T(8,128)}, b...) custom-call(bf16[3,96,5120]{2,1,0:T(8,128)(2,1)} %x_ref.3, ...), custom_call_target="tpu_custom_call" | custom-call | flops 45298483200 | bytes 40304640 | tf_op jit(solution)/shard_map/gather_qkv/pallas_call | solution.py:437
  130.5 106.6 %gather_attn.1 = (bf16[3,768,5120]{2,1,0:T(8,128)(2,1)}, bf16[3,768,640]{2,1,0:T(8,128)(2,1)}, bf16[3,768,640]{2,1,0:T(8,128)(2,1)}, bf16[3,768,640]{2,1,0:T(8,1...) custom-call(f32[3,768,640]{2,1,0:T(8,128)} %get-tuple-element.54.q_r, ...), custom_call_target="tpu_custom_call", output_to_operand_aliasing={{0}: (11, {})} | custom-call | flops 34728837120 | bytes 94371840 | tf_op jit(solution)/shard_map/gather_attn/pallas_call | solution.py:832
  237.1 114.4 %attn_bwd.1 = (bf16[3,96,5120]{2,1,0:T(8,128)(2,1)}, bf16[3,768,1920]{2,1,0:T(8,128)(2,1)}, bf16[3,768,1920]{2,1,0:T(8,128)(2,1)}, f32[3,768,640]{2,1,0:T(8,128)...) custom-call(f32[3,768,640]{2,1,0:T(8,128)} %get-tuple-element.54.q_r, ...), custom_call_target="tpu_custom_call" | custom-call | flops 70967623680 | bytes 44236800 | tf_op jit(solution)/shard_map/attn_bwd/pallas_call | solution.py:1169
  351.5 94.7 %dy_dw.1 = (bf16[3,96,5120]{2,1,0:T(8,128)(2,1)}, bf16[5120,640]{1,0:T(8,128)(2,1)}, bf16[5120,640]{1,0:T(8,128)(2,1)}, bf16[5120,640]{1,0:T(8,128)(2,1)}) custom-call(bf16[3,768,1920]{2,1,0:T(8,128)(2,1)} %get-tuple-element.75.g_hbm, bf16[3,768,1920]{2,1,0:T(8,128)(2,1)} %get-tuple-element.76.g_p, bf16[5120,640]{1,0:T(8,128)(2,1)} %wq_hbm.3, ...), custom_call_target="tpu_custom_call" | custom-call | flops 90596966400 | bytes 44236800 | tf_op jit(solution)/shard_map/dy_dw/pallas_call | solution.py:1307
  446.2 27.0 %tokens.1 = (bf16[3,96,5120]{2,1,0:T(8,128)(2,1)}, bf16[3,96,5120]{2,1,0:T(8,128)(2,1)}, f32[3,3,5120]{2,1,0:T(4,128)}, f32[640]{0:T(1024)}, f32[640]{0:T(1024)}...) custom-call(bf16[3,96,5120]{2,1,0:T(8,128)(2,1)} %x_ref.3, ...), custom_call_target="tpu_custom_call" | custom-call | flops 44236800 | bytes 17694720 | tf_op jit(solution)/shard_map/tokens/pallas_call | solution.py:1407
  473.2 1.1 reshape.26.x_ref
  474.2 12.1 %all_sum.1 = f32[8,45,128]{2,1,0:T(8,128)S(1)} custom-call(f32[8,45,128]{2,1,0:T(8,128)S(1)} %reshape.26.x_ref), custom_call_target="tpu_custom_call" | custom-call | flops 4000000000 | bytes 368640 | tf_op jit(solution)/shard_map/all_sum/pallas_call | solution.py:492
  486.4 0.1 reshape.27
  486.5 0.0 copy-start
  486.5 0.7 reduce_sum.9
  487.2 0.0 copy-done
Async XLA Ops:
  486.5 0.7 copy-start

commit v8 on v7

--- a/solution.py
+++ b/solution.py
@@ -130,42 +130,6 @@
         self.copy(b, p.right, half, half, 4, 3, p.left).start()
         self.copy(b, p.right, 0, self.rows, 6, 6, p.partner(p.me)).start()
 
-    def take_own(self, b):
-        p = self.at
-
-        @pl.when(b >= self.early)
-        def _():
-            self.copy(b, p.partner(p.me), 0, self.rows, 2, 4, p.me).wait_recv()
-
-    def take_left(self, b):
-        p = self.at
-
-        @pl.when(b >= self.early)
-        def _():
-            self.copy(b, p.left, 0, self.rows, 0, 0, p.me).wait_recv()
-            self.pass_left(b)
-
-        self.copy(b, p.partner(p.left), 0, self.rows, 5, 5, p.me).wait_recv()
-
-    def take_right(self, b):
-        p = self.at
-
-        @pl.when(b >= self.early)
-        def _():
-            self.copy(b, p.right, 0, self.rows, 1, 1, p.me).wait_recv()
-            self.pass_right(b)
-
-        self.copy(b, p.partner(p.right), 0, self.rows, 6, 6, p.me).wait_recv()
-
-    def take_far(self, b):
-        p, half = self.at, self.rows // 2
-        self.copy(b, p.far, 0, half, 3, 2, p.me).wait_recv()
-        self.copy(b, p.far, 0, half, 7, 7, p.partner(p.me)).start()
-        self.copy(b, p.far, half, half, 4, 3, p.me).wait_recv()
-        self.copy(b, p.far, half, half, 8, 8, p.partner(p.me)).start()
-        self.copy(b, p.partner(p.far), 0, half, 7, 7, p.me).wait_recv()
-        self.copy(b, p.partner(p.far), half, half, 8, 8, p.me).wait_recv()
-
     def finish(self, b):
         p, half = self.at, self.rows // 2
         counts = (self.rows, self.rows, self.rows, half, half, self.rows, self.rows, half, half)
@@ -180,23 +144,66 @@
         off = jnp.where(i < nb, 0, jnp.where(i < 3 * nb, side, chips // 2))
         return b, pl.multiple_of(lax.rem(self.at.chip + off, chips) * (2 * self.rows), 32)
 
-    def take_item(self, i, nb):
+    def kinds(self, i, nb):
+        odd = lax.rem(i + nb, 2)
+        side = (i >= nb) & (i < 3 * nb)
+        return i < nb, side & (odd == 0), side & (odd == 1), i >= 3 * nb
+
+    def arrive(self, i, nb):
+        p, half = self.at, self.rows // 2
+        b, _ = self.item_place(i, nb)
+        _, is_left, is_right, is_far = self.kinds(i, nb)
+
+        @pl.when(is_left & (b >= self.early))
+        def _():
+            self.copy(b, p.left, 0, self.rows, 0, 0, p.me).wait_recv()
+            self.pass_left(b)
+
+        @pl.when(is_right & (b >= self.early))
+        def _():
+            self.copy(b, p.right, 0, self.rows, 1, 1, p.me).wait_recv()
+            self.pass_right(b)
+
+        @pl.when(is_far)
+        def _():
+            self.copy(b, p.far, 0, half, 3, 2, p.me).wait_recv()
+            self.copy(b, p.far, 0, half, 7, 7, p.partner(p.me)).start()
+            self.copy(b, p.far, half, half, 4, 3, p.me).wait_recv()
+            self.copy(b, p.far, half, half, 8, 8, p.partner(p.me)).start()
+
+    def ready(self, i, nb):
+        p, half = self.at, self.rows // 2
         b, row0 = self.item_place(i, nb)
-        odd = lax.rem(i + nb, 2)
-        pl.when(i < nb)(lambda: self.take_own(b))
-        pl.when((i >= nb) & (i < 3 * nb) & (odd == 0))(lambda: self.take_left(b))
-        pl.when((i >= nb) & (i < 3 * nb) & (odd == 1))(lambda: self.take_right(b))
-        pl.when(i >= 3 * nb)(lambda: self.take_far(b))
+        is_own, is_left, is_right, is_far = self.kinds(i, nb)
+
+        @pl.when(is_own & (b >= self.early))
+        def _():
+            self.copy(b, p.partner(p.me), 0, self.rows, 2, 4, p.me).wait_recv()
+
+        @pl.when(is_left)
+        def _():
+            self.copy(b, p.partner(p.left), 0, self.rows, 5, 5, p.me).wait_recv()
+
+        @pl.when(is_right)
+        def _():
+            self.copy(b, p.partner(p.right), 0, self.rows, 6, 6, p.me).wait_recv()
+
+        @pl.when(is_far)
+        def _():
+            self.copy(b, p.partner(p.far), 0, half, 7, 7, p.me).wait_recv()
+            self.copy(b, p.partner(p.far), half, half, 8, 8, p.me).wait_recv()
+
         return b, row0
 
 
 class RowTrade:
-    def __init__(self, place, src, dst, rows, send, recv):
+    def __init__(self, place, src, dst, rows, send, recv, rows_of=None):
         self.at, self.src, self.dst, self.rows, self.send, self.recv = place, src, dst, rows, send, recv
+        self.batch = range(src.shape[0]) if rows_of is None else rows_of
 
     def copies(self, parity):
         p = self.at
-        for b in range(self.src.shape[0]):
+        for b in self.batch:
             for k in range(p.n // 2):
                 sl = pl.ds(pl.multiple_of((2 * k + parity) * self.rows, 16), self.rows)
                 yield p.to_partner(self.src.at[b, sl], self.dst.at[b, sl], self.send.at[b, k], self.recv.at[b, k])
@@ -216,7 +223,7 @@
 
 GATHER_SEMS = 9
 EARLY_ROWS = 1
-EARLY_CHUNKS = 4
+EARLY_CHUNKS = 3
 EARLY_DY = 4
 
 
@@ -372,13 +379,20 @@
                 pltpu.make_async_copy(zst.at[slot, :, pl.ds(cols, cols)], k_out.at[b, dst], out_sem.at[slot, 1]),
                 pltpu.make_async_copy(vst.at[slot], v_out.at[b, dst], out_sem.at[slot, 2])]
 
+    def load(b, row0, slot):
+        return pltpu.make_async_copy(y_full.at[b, pl.ds(row0, 2 * rows)], xbuf.at[slot], ld_sem.at[slot])
+
+    load(*gather.ready(0, nb), 0).start()
+
     def item(i, _):
-        b, row0 = gather.take_item(i, nb)
         slot = lax.rem(i, 2)
-        load = pltpu.make_async_copy(y_full.at[b, pl.ds(row0, 2 * rows)], xbuf, ld_sem)
-        load.start()
-
-        @pl.when(i == 3 * nb - 1)
+        b, row0 = gather.item_place(i, nb)
+
+        @pl.when(i + 1 < 4 * nb)
+        def _():
+            gather.arrive(i + 1, nb)
+
+        @pl.when(i + 1 == 3 * nb - 1)
         def _():
             for d in range(EARLY_ROWS):
                 gather_d.start_own(d)
@@ -396,9 +410,15 @@
             for c in outputs(0, 0, slot):
                 c.wait()
 
-        load.wait()
-        for lo, hi in chunks_of(3 * cols, 512):
-            zst[slot, :, lo:hi] = jnp.dot(xbuf[...], w_all[:, lo:hi], preferred_element_type=F32) + bias_ref[:, lo:hi]
+        load(0, 0, slot).wait()
+        spans = chunks_of(3 * cols, 512)
+        for m, (lo, hi) in enumerate(spans):
+            if m == len(spans) - 1:
+                @pl.when(i + 1 < 4 * nb)
+                def _():
+                    load(*gather.ready(i + 1, nb), lax.rem(i + 1, 2)).start()
+
+            zst[slot, :, lo:hi] = jnp.dot(xbuf[slot], w_all[:, lo:hi], preferred_element_type=F32) + bias_ref[:, lo:hi]
         vst[slot] = zst[slot, :, 2 * cols:].astype(BF16)
         q = zst[slot, :, :cols]
         k = zst[slot, :, cols:2 * cols]
@@ -444,10 +464,10 @@
         scratch_shapes=[
             pltpu.VMEM((1, 3 * cols), F32),
             pltpu.VMEM((dim, 3 * cols), BF16), pltpu.VMEM((nb, rows, dim), BF16), pltpu.VMEM((nb, rows, dim), BF16),
-            pltpu.VMEM((2 * rows, dim), BF16), pltpu.VMEM((2, 2 * rows, 3 * cols), F32), pltpu.VMEM((2, 2 * rows, cols), BF16),
+            pltpu.VMEM((2, 2 * rows, dim), BF16), pltpu.VMEM((2, 2 * rows, 3 * cols), F32), pltpu.VMEM((2, 2 * rows, cols), BF16),
             pltpu.VMEM((2 * nb, tokens, HEAD_DIM), F32), pltpu.VMEM((stat_rows, tokens), F32), pltpu.VMEM((n, stat_rows, tokens), F32),
             pltpu.VMEM((2, cols, min(512, dim)), BF16), pltpu.VMEM((2, min(512, dim), cols), BF16), dma((2, 2)),
-            dma((3,)), dma((nb,)), dma, dma, dma((2, 3)), dma((nb, GATHER_SEMS)), dma((nb, GATHER_SEMS)),
+            dma((3,)), dma((nb,)), dma, dma((2,)), dma((2, 3)), dma((nb, GATHER_SEMS)), dma((nb, GATHER_SEMS)),
             dma((EARLY_ROWS, GATHER_SEMS)), dma((EARLY_ROWS, GATHER_SEMS)), dma((n,)), dma((n,)), dma, dma],
         compiler_params=params(collective_id=0, has_side_effects=True),
         cost_estimate=cost(6 * nb * tokens * dim * cols, 6 * dim * cols + 14 * nb * tokens * cols),
@@ -639,6 +659,7 @@
     cols = heads * HEAD_DIM
     nc = dim // CHUNK
     early_chunks = min(EARLY_CHUNKS, nc)
+    mid = nc // 2
     scatter = Scatter(place, part_out, far_in, None, s_send, s_recv)
     trade_o = RowTrade(place, o_out, o_p, rows, r_send, r_recv)
 
@@ -723,7 +744,7 @@
             def stored(j):
                 store(j).wait()
 
-                @pl.when(j < early_chunks)
+                @pl.when((j < early_chunks) & (j >= mid))
                 def _():
                     scatter.start_far(j)
 
@@ -753,23 +774,34 @@
                 def _():
                     stored(j - 1)
 
+                @pl.when(j == mid)
+                def _():
+                    gather.arrive(3 * nb - 2, nb)
+                    gather.arrive(3 * nb - 1, nb)
+                    lax.fori_loop(0, min(early_chunks, mid), scatter.start_far, 0)
+
                 return 0
 
             lax.fori_loop(0, nc, body, 0)
             stored(nc - 1)
 
-        def take(i):
-            b, row0 = gather.take_item(i, nb)
+        def fetch(i):
+            b, row0 = gather.ready(i, nb)
             load(b, row0, lax.rem(i, 2)).start()
 
-        take(0)
+        fetch(0)
+        gather.arrive(jnp.int32(1), nb)
 
         def item(i, _):
             slot = lax.rem(i, 2)
 
-            @pl.when((i + 1 != 3 * nb) & (i + 1 < 4 * nb - 1))
+            @pl.when((i + 2 != 3 * nb - 2) & (i + 2 != 3 * nb - 1) & (i + 2 < 4 * nb))
             def _():
-                take(i + 1)
+                gather.arrive(i + 2, nb)
+
+            @pl.when((i + 1 != 3 * nb - 2) & (i + 1 < 4 * nb))
+            def _():
+                fetch(i + 1)
 
             @pl.when(i >= 2)
             def _():
@@ -785,15 +817,12 @@
                 o_copy.wait()
                 trade_o.start()
 
-            @pl.when(i + 1 == 3 * nb)
+            @pl.when(i + 1 == 3 * nb - 2)
             def _():
                 trade_o.wait_recv()
                 pl.run_scoped(project, pltpu.VMEM((4 * nb * rows, 2 * cols), BF16), pltpu.VMEM((2, 2 * cols, CHUNK), BF16),
                               pltpu.VMEM((2, 4, nb * rows, CHUNK), BF16))
-
-            @pl.when((i + 1 == 3 * nb) | (i + 1 == 4 * nb - 1))
-            def _():
-                take(i + 1)
+                fetch(i + 1)
 
             return 0
 
@@ -867,7 +896,7 @@
                     q_hbm, k_hbm, o_hbm, part_in, far_in, d_full, wq_hbm, wk_hbm, wv_hbm, wq_p,
                     proj_out, g_out, g_p, dqs_out, dks_out, dwo_out, wk_p, wv_p, part_dy, far_dy, dgq_ref, dgk_ref,
                     part, recv_far, recv_side, s_send, s_recv,
-                    inv_q, inv_k, acc_q, acc_k, p_all, ds_all, dq_all, qs_st, ks_st, v_st, st_row, st_sum, slots,
+                    inv_q, inv_k, acc_q, acc_k, p_all, ds_all, dq_all, qs_st, ks_st, v_st, st_row, st_sum, slots, fbuf, gbuf, lanes_s,
                     ld_sem, w_sem, fl_sem, g_sem, go_sem, out_sem, e_send, e_recv, t_send, t_recv, r_send, r_recv, c_sem, y_send, y_recv):
     step = pl.program_id(0)
     tokens = q_ref.shape[1]
@@ -891,7 +920,6 @@
     @pl.when(step == 0)
     def _():
         place.barrier(place.everyone())
-        lax.fori_loop(early, nc, scatter.start_far, 0)
         for c in stored():
             c.start()
         for j in range(2):
@@ -909,10 +937,78 @@
                 pltpu.make_async_copy(ks_st.at[slot], dks_out.at[b, :, lanes], fl_sem.at[slot, 1]),
                 pltpu.make_async_copy(v_st.at[slot], g_out.at[b, :, v_lanes], fl_sem.at[slot, 2])]
 
-    mid = nc // 2
-    for j in range(mid):
-        at_step = 1 + j * (steps - 2) // max(mid - 1, 1)
-        pl.when(step == at_step)(functools.partial(scatter.sums, j))
+    mid = early
+    events = []
+    late = list(range(mid))
+    for m, j in enumerate(range(early, nc)):
+        events.append(functools.partial(scatter.start_far, j))
+        if m >= 2 and m % 2 == 0 and late:
+            events.append(functools.partial(scatter.sums, late.pop(0)))
+    events += [functools.partial(scatter.sums, j) for j in late]
+    for m, event in enumerate(events):
+        @pl.when(step == m * (steps - 1) // len(events))
+        def _(event=event):
+            event()
+
+    rb = min(256, tokens)
+    per = tokens // rb
+
+    def stats(b):
+        return Exchange(place, st_row.at[b], slots.at[b], e_send.at[b], e_recv.at[b])
+
+    def grad_loads(b, i):
+        r0 = pl.multiple_of(i * rb, rb)
+        return [pltpu.make_async_copy(src.at[b, pl.ds(r0, rb)], fbuf.at[m], g_sem.at[m])
+                for m, src in enumerate((dqs_out, q_hbm, dks_out, k_hbm))]
+
+    def grad_store(b, i):
+        r0 = pl.multiple_of(i * rb, rb)
+        return pltpu.make_async_copy(gbuf, g_out.at[b, pl.ds(r0, rb), pl.ds(0, 2 * cols)], go_sem.at[0])
+
+    def trade(b):
+        return RowTrade(place, g_out, g_p, rows, r_send, r_recv, rows_of=(b,))
+
+    def grad_block(b, i):
+        for c in grad_loads(b, i):
+            c.wait()
+        sl = pl.ds(pl.multiple_of(i * rb, rb), rb)
+        for m in range(2):
+            inv_l = lanes_s[2 * m, sl]
+            st_l = lanes_s[2 * m + 1, sl]
+            for h in range(heads):
+                hs = slice(h * HEAD_DIM, (h + 1) * HEAD_DIM)
+                grad = inv_l * (fbuf[2 * m, :, hs] - (fbuf[2 * m + 1, :, hs] * inv_l) * st_l)
+                gbuf[:, m * cols + h * HEAD_DIM:m * cols + (h + 1) * HEAD_DIM] = grad.astype(BF16)
+        grad_store(b, i).start()
+
+    def grad_begin(b):
+        st_sum[...] = stats(b).finish()
+        for m in range(2):
+            lanes_s[2 * m] = lanes_of(lax.rsqrt(ss_ref[pl.ds(2 * b + m, 1)] / dim + EPS_NORM))
+            lanes_s[2 * m + 1] = lanes_of(st_sum[m:m + 1] / dim)
+
+    first = heads - per
+    b_old = step // heads - 1
+    i_old = lax.rem(step, heads) - first
+
+    @pl.when((step >= heads) & (step < steps) & (i_old >= 0))
+    def _():
+        @pl.when(i_old == 0)
+        def _():
+            grad_begin(b_old)
+
+        @pl.when(i_old > 0)
+        def _():
+            grad_store(0, 0).wait()
+
+        for c in grad_loads(b_old, i_old):
+            c.start()
+
+    @pl.when((step >= 2 * heads) & (lax.rem(step, heads) == 0))
+    def _():
+        grad_store(0, 0).wait()
+        for b in range(nb - 1):
+            pl.when(step == (b + 2) * heads)(trade(b).start)
 
     @pl.when(step < steps)
     def _():
@@ -979,74 +1075,39 @@
 
         @pl.when(head == heads - 1)
         def _():
-            st_row[pl.ds(2 * b, 1)] = to_row(acc_q[...])
-            st_row[pl.ds(2 * b + 1, 1)] = to_row(acc_k[...])
+            st_row[b, 0:1] = to_row(acc_q[...])
+            st_row[b, 1:2] = to_row(acc_k[...])
+            for m in range(nb):
+                pl.when(b == m)(stats(m).start)
+
+    @pl.when((step >= heads) & (step < steps) & (i_old >= 0))
+    def _():
+        grad_block(b_old, i_old)
 
     @pl.when(step == steps)
     def _():
         for s in range(2):
             for c in flush(0, 0, s):
                 c.wait()
-        stats = Exchange(place, st_row, slots, e_send, e_recv)
-        stats.start()
         lax.fori_loop(mid, nc, scatter.sums_step, 0)
         lax.fori_loop(0, nc, scatter.start_side, 0)
-        st_sum[...] = stats.finish()
-        rb = min(256, tokens)
-        per = tokens // rb
-        trade = RowTrade(place, g_out, g_p, rows, r_send, r_recv)
-
-        def norm_grad(fbuf, gbuf):
-            def loads(i, slot):
-                b, r0 = i // per, pl.multiple_of(lax.rem(i, per) * rb, rb)
-                return [pltpu.make_async_copy(src.at[b, pl.ds(r0, rb)], fbuf.at[slot, m], g_sem.at[slot, m])
-                        for m, src in enumerate((dqs_out, q_hbm, dks_out, k_hbm))]
-
-            def store(i, slot):
-                b, r0 = i // per, pl.multiple_of(lax.rem(i, per) * rb, rb)
-                return pltpu.make_async_copy(gbuf.at[slot], g_out.at[b, pl.ds(r0, rb), pl.ds(0, 2 * cols)], go_sem.at[slot])
-
-            for c in loads(0, 0):
-                c.start()
-
-            def body(i, _):
-                slot = lax.rem(i, 2)
-                b, r0 = i // per, pl.multiple_of(lax.rem(i, per) * rb, rb)
-
-                @pl.when(i + 1 < nb * per)
-                def _():
-                    for c in loads(i + 1, lax.rem(i + 1, 2)):
-                        c.start()
-
-                @pl.when(r0 == 0)
-                def _():
-                    inv_q[...] = lanes_of(lax.rsqrt(ss_ref[pl.ds(2 * b, 1)] / dim + EPS_NORM))
-                    inv_k[...] = lanes_of(lax.rsqrt(ss_ref[pl.ds(2 * b + 1, 1)] / dim + EPS_NORM))
-                    acc_q[...] = lanes_of(st_sum[pl.ds(2 * b, 1)] / dim)
-                    acc_k[...] = lanes_of(st_sum[pl.ds(2 * b + 1, 1)] / dim)
-
-                @pl.when(i >= 2)
-                def _():
-                    store(0, slot).wait()
-
-                for c in loads(i, slot):
-                    c.wait()
-                sl = pl.ds(r0, rb)
-                for m, (inv, st) in enumerate(((inv_q, acc_q), (inv_k, acc_k))):
-                    inv_l, st_l = inv[sl], st[sl]
-                    for h in range(heads):
-                        hs = slice(h * HEAD_DIM, (h + 1) * HEAD_DIM)
-                        grad = inv_l * (fbuf[slot, 2 * m, :, hs] - (fbuf[slot, 2 * m + 1, :, hs] * inv_l) * st_l)
-                        gbuf[slot, :, m * cols + h * HEAD_DIM:m * cols + (h + 1) * HEAD_DIM] = grad.astype(BF16)
-                store(i, slot).start()
-                return 0
-
-            lax.fori_loop(0, nb * per, body, 0)
-            for s in range(min(2, nb * per)):
-                store(0, s).wait()
-
-        pl.run_scoped(norm_grad, pltpu.VMEM((2, 4, rb, cols), F32), pltpu.VMEM((2, rb, 2 * cols), BF16))
-        trade.start()
+        for c in grad_loads(nb - 1, 0):
+            c.start()
+        grad_begin(nb - 1)
+
+        def last_row(i, _):
+            @pl.when(i > 0)
+            def _():
+                grad_store(0, 0).wait()
+                for c in grad_loads(nb - 1, i):
+                    c.start()
+
+            grad_block(nb - 1, i)
+            return 0
+
+        lax.fori_loop(0, per, last_row, 0)
+        grad_store(0, 0).wait()
+        trade(nb - 1).start()
 
         def weight_grad(turned, obuf, dbuf, wst):
             bn = min(512, dim)
@@ -1054,7 +1115,7 @@
 
             def chunk(c):
                 slot = lax.rem(c, 2)
-                return pltpu.make_async_copy(d_full.at[:, :, pl.ds(pl.multiple_of(c * bn, bn), bn)], dbuf.at[slot], go_sem.at[slot])
+                return pltpu.make_async_copy(d_full.at[:, :, pl.ds(pl.multiple_of(c * bn, bn), bn)], dbuf.at[slot], w_sem.at[slot, 1])
 
             def store(c):
                 slot = lax.rem(c, 2)
@@ -1091,7 +1152,8 @@
         bn = min(512, dim)
         pl.run_scoped(weight_grad, pltpu.VMEM((cols, nb * tokens), BF16), pltpu.VMEM((nb, tokens, cols), BF16),
                       pltpu.VMEM((2, nb, tokens, bn), BF16), pltpu.VMEM((2, cols, bn), BF16))
-        trade.wait_recv()
+        for b in range(nb):
+            trade(b).wait_recv()
         for j in range(2):
             trade_w(j).wait_recv()
 
@@ -1137,7 +1199,8 @@
         pl.run_scoped(first_dy, pltpu.VMEM((4 * nb * rows, 6 * cols), BF16), pltpu.VMEM((2, CHUNK, 6 * cols), BF16),
                       pltpu.VMEM((4, nb * rows, CHUNK), BF16))
         scatter_end(scatter, proj_out, out_sem, nc)
-        trade.wait_send()
+        for b in range(nb):
+            trade(b).wait_send()
         for j in range(2):
             trade_w(j).wait_send()
         for j in range(n_dy):
@@ -1176,8 +1239,10 @@
         out_specs=[any_spec] * 10 + [out_vec, out_vec],
         scratch_shapes=Scatter.scratch(nb * rows, dim) + [lane_tile] * 4 + [pltpu.VMEM((tokens, tokens), BF16)] * 2 + [
             lane_tile, pltpu.VMEM((2, tokens, HEAD_DIM), F32), pltpu.VMEM((2, tokens, HEAD_DIM), F32),
-            pltpu.VMEM((2, tokens, HEAD_DIM), BF16), pltpu.VMEM(ss.shape, F32), pltpu.VMEM(ss.shape, F32), pltpu.VMEM((n,) + ss.shape, F32),
-            dma((2,)), dma((2, 2)), dma((2, 3)), dma((2, 4)), dma((2,)), dma((nb,)), dma((n,)), dma((n,)), dma((2,)), dma((2,)),
+            pltpu.VMEM((2, tokens, HEAD_DIM), BF16), pltpu.VMEM((nb, 8, tokens), F32), pltpu.VMEM((8, tokens), F32),
+            pltpu.VMEM((nb, n, 8, tokens), F32), pltpu.VMEM((4, min(256, tokens), cols), F32), pltpu.VMEM((min(256, tokens), 2 * cols), BF16),
+            pltpu.VMEM((4, tokens, HEAD_DIM), F32),
+            dma((2,)), dma((2, 2)), dma((2, 3)), dma((4,)), dma((2,)), dma((nb,)), dma((nb, n)), dma((nb, n)), dma((2,)), dma((2,)),
             dma((nb, n // 2)), dma((nb, n // 2)), dma((2, 6)), dma((n_dy, 6)), dma((n_dy, 6))],
         compiler_params=params("arbitrary", collective_id=2, has_side_effects=True),
         cost_estimate=cost(4 * nb * tokens * dim * cols + 36 * nb * tokens * tokens * cols, 30 * nb * tokens * cols),
@@ -1200,14 +1265,17 @@
     load_g = pltpu.make_async_copy(g_hbm, g, ld_sem.at[4])
 
     def chain(lhs, wbuf):
-        for c in stored:
-            c.start()
         loads = pair_rows(place, nb, rows, g_hbm, g_p, lhs, ld_sem)
         dy = DyChunks(lhs, wbuf, (wq_hbm, wk_hbm, wv_hbm, wq_p, wk_p, wv_p), w_sem)
         if early < nc:
-            for c in loads:
+            for c in dy.loads(early):
                 c.start()
-            for c in dy.loads(early):
+            for c in loads[:len(loads) // 2]:
+                c.start()
+        for c in stored:
+            c.start()
+        if early < nc:
+            for c in loads[len(loads) // 2:]:
                 c.start()
         place.barrier(place.near()[:2])
         for c in stored:

time: 489 us -> 478 us (0.978)
  Pallas kernels: 485 us -> 474 us
    pallas_call x1, Pallas kernels: 107 us -> 90.3 us  [gather_attn_call(): pl.pallas_call(functools.partial(gather_attn_kernel, n, nb, heads, dim),...]
    pallas_call x1, Pallas kernels: 114 us -> 122 us  [attn_bwd_call(): pl.pallas_call(functools.partial(attn_bwd_kernel, n, nb, heads, dim), nam...]
where the time goes in v8:
time: 478 us; the launch traced here: 477 us
  Pallas kernels  474 us (99%)
    pallas_call x1, Pallas kernels, gather_qkv_call(): pl.pallas_call(functools.partial(gather_qkv_kernel, n), name='gather_qkv'...  130 us
    pallas_call x1, Pallas kernels, attn_bwd_call(): pl.pallas_call(functools.partial(attn_bwd_kernel, n, nb, heads, dim), nam...  122 us
    pallas_call x1, Pallas kernels, dy_dw_call(): pl.pallas_call(functools.partial(dy_dw_kernel, n, nb, dim), name='dy_dw',...  94.2 us
    pallas_call x1, Pallas kernels, gather_attn_call(): pl.pallas_call(functools.partial(gather_attn_kernel, n, nb, heads, dim),...  90.3 us
    pallas_call x1, Pallas kernels, token_call(): pl.pallas_call(functools.partial(token_kernel, n_copies), name='tokens',...  27 us
    pallas_call x1, Pallas kernels, all_sum_call(): pl.pallas_call(functools.partial(all_sum_kernel, n), name='all_sum', out_...  10.8 us

profile of v8, /device:TPU:81, one launch (start us, length us, event | category | flops | bytes accessed | tf_op | source)
XLA Modules:
  0.0 476.9 jit_solution(17058233365918183973)
XLA Ops:
  0.6 129.8 %gather_qkv.1 = (bf16[3,768,5120]{2,1,0:T(8,128)(2,1)}, bf16[3,768,5120]{2,1,0:T(8,128)(2,1)}, f32[3,768,640]{2,1,0:T(8,128)}, f32[3,768,640]{2,1,0:T(8,128)}, b...) custom-call(bf16[3,96,5120]{2,1,0:T(8,128)(2,1)} %x_ref.3, ...), custom_call_target="tpu_custom_call" | custom-call | flops 45298483200 | bytes 40304640 | tf_op jit(solution)/shard_map/gather_qkv/pallas_call | solution.py:457
  130.5 90.3 %gather_attn.1 = (bf16[3,768,5120]{2,1,0:T(8,128)(2,1)}, bf16[3,768,640]{2,1,0:T(8,128)(2,1)}, bf16[3,768,640]{2,1,0:T(8,128)(2,1)}, bf16[3,768,640]{2,1,0:T(8,1...) custom-call(f32[3,768,640]{2,1,0:T(8,128)} %get-tuple-element.54.q_r, ...), custom_call_target="tpu_custom_call", output_to_operand_aliasing={{0}: (11, {})} | custom-call | flops 34728837120 | bytes 94371840 | tf_op jit(solution)/shard_map/gather_attn/pallas_call | solution.py:861
  220.8 122.2 %attn_bwd.1 = (bf16[3,96,5120]{2,1,0:T(8,128)(2,1)}, bf16[3,768,1920]{2,1,0:T(8,128)(2,1)}, bf16[3,768,1920]{2,1,0:T(8,128)(2,1)}, f32[3,768,640]{2,1,0:T(8,128)...) custom-call(f32[3,768,640]{2,1,0:T(8,128)} %get-tuple-element.54.q_r, ...), custom_call_target="tpu_custom_call" | custom-call | flops 70967623680 | bytes 44236800 | tf_op jit(solution)/shard_map/attn_bwd/pallas_call | solution.py:1232
  343.0 94.2 %dy_dw.1 = (bf16[3,96,5120]{2,1,0:T(8,128)(2,1)}, bf16[5120,640]{1,0:T(8,128)(2,1)}, bf16[5120,640]{1,0:T(8,128)(2,1)}, bf16[5120,640]{1,0:T(8,128)(2,1)}) custom-call(bf16[3,768,1920]{2,1,0:T(8,128)(2,1)} %get-tuple-element.75.g_hbm, bf16[3,768,1920]{2,1,0:T(8,128)(2,1)} %get-tuple-element.76.g_p, bf16[5120,640]{1,0:T(8,128)(2,1)} %wq_hbm.3, ...), custom_call_target="tpu_custom_call" | custom-call | flops 90596966400 | bytes 44236800 | tf_op jit(solution)/shard_map/dy_dw/pallas_call | solution.py:1375
  437.3 27.0 %tokens.1 = (bf16[3,96,5120]{2,1,0:T(8,128)(2,1)}, bf16[3,96,5120]{2,1,0:T(8,128)(2,1)}, f32[3,3,5120]{2,1,0:T(4,128)}, f32[640]{0:T(1024)}, f32[640]{0:T(1024)}...) custom-call(bf16[3,96,5120]{2,1,0:T(8,128)(2,1)} %x_ref.3, ...), custom_call_target="tpu_custom_call" | custom-call | flops 44236800 | bytes 17694720 | tf_op jit(solution)/shard_map/tokens/pallas_call | solution.py:1475
  464.2 1.1 reshape.26.x_ref
  465.3 10.8 %all_sum.1 = f32[8,45,128]{2,1,0:T(8,128)S(1)} custom-call(f32[8,45,128]{2,1,0:T(8,128)S(1)} %reshape.26.x_ref), custom_call_target="tpu_custom_call" | custom-call | flops 4000000000 | bytes 368640 | tf_op jit(solution)/shard_map/all_sum/pallas_call | solution.py:512
  476.1 0.1 reshape.27
  476.2 0.0 copy-start
  476.2 0.7 reduce_sum.9
  476.9 0.0 copy-done
Async XLA Ops:
  476.2 0.7 copy-start

commit v9 on v8

--- a/solution.py
+++ b/solution.py
@@ -647,7 +647,7 @@
 
 def gather_attn_kernel(n, nb, heads, dim, q_ref, k_ref, v_ref, gain_ref, cos_ref, sin_ref, ss_ref,
                        wq_ref, wo_ref, wo_p, wo_t, d_in,
-                       d_full, o_out, o_p, da_out, wq_p, part_out, far_in, qr_ref, kr_ref, lse_ref, o32_ref,
+                       d_full, o_out, o_p, da_out, wq_p, part_out, far_in, dwo_part, qr_ref, kr_ref, lse_ref, o32_ref,
                        inv_q, inv_k, o_all, wo, xbuf, ast,
                        w_sem, ld_sem, out_sem, o_sem, p_sem, l_sem, g_send, g_recv, t_send, t_recv, r_send, r_recv, s_send, s_recv):
     step = pl.program_id(0)
@@ -785,6 +785,47 @@
             lax.fori_loop(0, nc, body, 0)
             stored(nc - 1)
 
+        def first_dwo(turned, dbuf, fst):
+            bn = min(512, dim)
+            n_chunks = dim // bn
+
+            def chunk(c):
+                slot = lax.rem(c, 2)
+                cs = pl.ds(pl.multiple_of(c * bn, bn), bn)
+                return pltpu.make_async_copy(d_full.at[pl.ds(0, nb - 1), :, cs], dbuf.at[slot], p_sem.at[slot, 0])
+
+            def store(c):
+                slot = lax.rem(c, 2)
+                return pltpu.make_async_copy(fst.at[slot], dwo_part.at[:, pl.ds(pl.multiple_of(c * bn, bn), bn)], p_sem.at[slot, 1])
+
+            chunk(0).start()
+            for b in range(nb - 1):
+                turned[:, b * tokens:(b + 1) * tokens] = o_all[b].T
+
+            def body(c, _):
+                slot = lax.rem(c, 2)
+
+                @pl.when(c + 1 < n_chunks)
+                def _():
+                    chunk(c + 1).start()
+
+                @pl.when(c == n_chunks // 2)
+                def _():
+                    gather.arrive(4 * nb - 1, nb)
+
+                @pl.when(c >= 2)
+                def _():
+                    store(c).wait()
+
+                chunk(c).wait()
+                fst[slot] = jnp.dot(turned[...], dbuf[slot].reshape((nb - 1) * tokens, bn), preferred_element_type=F32)
+                store(c).start()
+                return 0
+
+            lax.fori_loop(0, n_chunks, body, 0)
+            for c in range(min(2, n_chunks)):
+                store(c).wait()
+
         def fetch(i):
             b, row0 = gather.ready(i, nb)
             load(b, row0, lax.rem(i, 2)).start()
@@ -795,11 +836,11 @@
         def item(i, _):
             slot = lax.rem(i, 2)
 
-            @pl.when((i + 2 != 3 * nb - 2) & (i + 2 != 3 * nb - 1) & (i + 2 < 4 * nb))
+            @pl.when((i + 2 != 3 * nb - 2) & (i + 2 != 3 * nb - 1) & (i + 2 < 4 * nb - 1))
             def _():
                 gather.arrive(i + 2, nb)
 
-            @pl.when((i + 1 != 3 * nb - 2) & (i + 1 < 4 * nb))
+            @pl.when((i + 1 != 3 * nb - 2) & (i + 1 < 4 * nb - 1))
             def _():
                 fetch(i + 1)
 
@@ -822,6 +863,13 @@
                 trade_o.wait_recv()
                 pl.run_scoped(project, pltpu.VMEM((4 * nb * rows, 2 * cols), BF16), pltpu.VMEM((2, 2 * cols, CHUNK), BF16),
                               pltpu.VMEM((2, 4, nb * rows, CHUNK), BF16))
+                fetch(i + 1)
+
+            @pl.when(i + 1 == 4 * nb - 1)
+            def _():
+                bn = min(512, dim)
+                pl.run_scoped(first_dwo, pltpu.VMEM((cols, (nb - 1) * tokens), BF16), pltpu.VMEM((2, nb - 1, tokens, bn), BF16),
+                              pltpu.VMEM((2, cols, bn), F32))
                 fetch(i + 1)
 
             return 0
@@ -861,10 +909,10 @@
     return pl.pallas_call(
         functools.partial(gather_attn_kernel, n, nb, heads, dim), name="gather_attn", grid=(nb * heads + 1,),
         out_shape=[shape(d_full.shape, BF16), head_arr, head_arr, head_arr, shape(w_q.shape, BF16)]
-        + [shape((nc, 4, nb * rows, CHUNK), BF16), shape((early, 2, nb * rows // 2, CHUNK), BF16), head_arr, head_arr,
+        + [shape((nc, 4, nb * rows, CHUNK), BF16), shape((early, 2, nb * rows // 2, CHUNK), BF16), shape((cols, dim), F32), head_arr, head_arr,
            shape((nb, tokens, cols), F32), shape((nb, tokens, cols), F32)],
         in_specs=[blk, blk, blk, vec, tab, tab, pl.BlockSpec(ss.shape, lambda i: (0, 0))] + [any_spec] * 5,
-        out_specs=[any_spec] * 7 + [blk] * 4,
+        out_specs=[any_spec] * 8 + [blk] * 4,
         scratch_shapes=[
             pltpu.VMEM((tokens, HEAD_DIM), F32), pltpu.VMEM((tokens, HEAD_DIM), F32), pltpu.VMEM((nb, tokens, cols), BF16),
             pltpu.VMEM((dim, cols), BF16), pltpu.VMEM((2, 2 * rows, dim), BF16), pltpu.VMEM((2, 2 * rows, cols), BF16),
@@ -893,7 +941,7 @@
 
 
 def attn_bwd_kernel(n, nb, heads, dim, q_ref, k_ref, qr_ref, kr_ref, v_ref, do_ref, o_ref, lse_ref, gain_ref, cos_ref, sin_ref, ss_ref,
-                    q_hbm, k_hbm, o_hbm, part_in, far_in, d_full, wq_hbm, wk_hbm, wv_hbm, wq_p,
+                    q_hbm, k_hbm, o_hbm, part_in, far_in, d_full, dwo_part, wq_hbm, wk_hbm, wv_hbm, wq_p,
                     proj_out, g_out, g_p, dqs_out, dks_out, dwo_out, wk_p, wv_p, part_dy, far_dy, dgq_ref, dgk_ref,
                     part, recv_far, recv_side, s_send, s_recv,
                     inv_q, inv_k, acc_q, acc_k, p_all, ds_all, dq_all, qs_st, ks_st, v_st, st_row, st_sum, slots, fbuf, gbuf, lanes_s,
@@ -914,16 +962,20 @@
         return [pltpu.make_async_copy(part_in, part, ld_sem.at[0]),
                 pltpu.make_async_copy(far_in, recv_far.at[pl.ds(0, early)], ld_sem.at[1])]
 
+    n_pieces = 8
+
     def trade_w(j):
-        return place.to_partner((wk_hbm, wv_hbm)[j], (wk_p, wv_p)[j], t_send.at[j], t_recv.at[j])
+        m = j % (n_pieces // 2)
+        size = dim // (n_pieces // 2)
+        src, dst = ((wk_hbm, wk_p), (wv_hbm, wv_p))[j // (n_pieces // 2)]
+        return place.to_partner(src.at[pl.ds(m * size, size)], dst.at[pl.ds(m * size, size)], t_send.at[j], t_recv.at[j])
+
 
     @pl.when(step == 0)
     def _():
         place.barrier(place.everyone())
         for c in stored():
             c.start()
-        for j in range(2):
-            trade_w(j).start()
 
     @pl.when(step == 1)
     def _():
@@ -936,6 +988,9 @@
         return [pltpu.make_async_copy(qs_st.at[slot], dqs_out.at[b, :, lanes], fl_sem.at[slot, 0]),
                 pltpu.make_async_copy(ks_st.at[slot], dks_out.at[b, :, lanes], fl_sem.at[slot, 1]),
                 pltpu.make_async_copy(v_st.at[slot], g_out.at[b, :, v_lanes], fl_sem.at[slot, 2])]
+
+    for j in range(n_pieces):
+        pl.when(step == j * (steps - 1) // n_pieces + 1)(lambda j=j: trade_w(j).start())
 
     mid = early
     events = []
@@ -988,6 +1043,7 @@
             lanes_s[2 * m + 1] = lanes_of(st_sum[m:m + 1] / dim)
 
     first = heads - per
+    assert first >= 2
     b_old = step // heads - 1
     i_old = lax.rem(step, heads) - first
 
@@ -1109,39 +1165,42 @@
         grad_store(0, 0).wait()
         trade(nb - 1).start()
 
-        def weight_grad(turned, obuf, dbuf, wst):
+        def weight_grad(turned, obuf, dbuf, fst, wst):
             bn = min(512, dim)
             n_chunks = dim // bn
 
             def chunk(c):
                 slot = lax.rem(c, 2)
-                return pltpu.make_async_copy(d_full.at[:, :, pl.ds(pl.multiple_of(c * bn, bn), bn)], dbuf.at[slot], w_sem.at[slot, 1])
+                cs = pl.ds(pl.multiple_of(c * bn, bn), bn)
+                return [pltpu.make_async_copy(d_full.at[nb - 1, :, cs], dbuf.at[slot], w_sem.at[slot, 1]),
+                        pltpu.make_async_copy(dwo_part.at[:, cs], fst.at[slot], w_sem.at[slot, 2])]
 
             def store(c):
                 slot = lax.rem(c, 2)
                 return pltpu.make_async_copy(wst.at[slot], dwo_out.at[:, pl.ds(pl.multiple_of(c * bn, bn), bn)], w_sem.at[slot, 0])
 
-            load_o = pltpu.make_async_copy(o_hbm, obuf, ld_sem.at[0])
+            load_o = pltpu.make_async_copy(o_hbm.at[nb - 1], obuf, ld_sem.at[0])
             load_o.start()
-            chunk(0).start()
+            for c in chunk(0):
+                c.start()
             load_o.wait()
-            for b in range(nb):
-                turned[:, b * tokens:(b + 1) * tokens] = obuf[b].T
+            turned[...] = obuf[...].T
 
             def body(c, _):
                 slot = lax.rem(c, 2)
 
                 @pl.when(c + 1 < n_chunks)
                 def _():
-                    chunk(c + 1).start()
+                    for m in chunk(c + 1):
+                        m.start()
 
                 @pl.when(c >= 2)
                 def _():
                     store(c).wait()
 
-                chunk(c).wait()
-                d = dbuf[slot].reshape(nb * tokens, bn)
-                wst[slot] = jnp.dot(turned[...], d, preferred_element_type=F32).astype(BF16)
+                for m in chunk(c):
+                    m.wait()
+                wst[slot] = (fst[slot] + jnp.dot(turned[...], dbuf[slot], preferred_element_type=F32)).astype(BF16)
                 store(c).start()
                 return 0
 
@@ -1150,11 +1209,11 @@
                 store(s).wait()
 
         bn = min(512, dim)
-        pl.run_scoped(weight_grad, pltpu.VMEM((cols, nb * tokens), BF16), pltpu.VMEM((nb, tokens, cols), BF16),
-                      pltpu.VMEM((2, nb, tokens, bn), BF16), pltpu.VMEM((2, cols, bn), BF16))
+        pl.run_scoped(weight_grad, pltpu.VMEM((cols, tokens), BF16), pltpu.VMEM((tokens, cols), BF16),
+                      pltpu.VMEM((2, tokens, bn), BF16), pltpu.VMEM((2, cols, bn), F32), pltpu.VMEM((2, cols, bn), BF16))
         for b in range(nb):
             trade(b).wait_recv()
-        for j in range(2):
+        for j in range(n_pieces):
             trade_w(j).wait_recv()
 
         n_dy = part_dy.shape[0]
@@ -1201,14 +1260,14 @@
         scatter_end(scatter, proj_out, out_sem, nc)
         for b in range(nb):
             trade(b).wait_send()
-        for j in range(2):
+        for j in range(n_pieces):
             trade_w(j).wait_send()
         for j in range(n_dy):
             for idx in (0, 1):
                 scatter_y.message(j, idx).wait()
 
 
-def attn_bwd_call(n, q, k, q_rot, k_rot, v, d_attn, o, o32, lse, gains, cos_tab, sin_tab, ss, part, far, d_full, w_q, w_k, w_v, wq_p):
+def attn_bwd_call(n, q, k, q_rot, k_rot, v, d_attn, o, o32, lse, gains, cos_tab, sin_tab, ss, part, far, d_full, dwo_part, w_q, w_k, w_v, wq_p):
     nb, tokens, cols = q.shape
     dim = d_full.shape[2]
     heads = cols // HEAD_DIM
@@ -1235,18 +1294,18 @@
                    shape(whole, F32), shape(whole, F32), shape((cols, dim), BF16),
                    shape(w_k.shape, BF16), shape(w_v.shape, BF16), shape((n_dy,) + part.shape[1:], BF16), shape((n_dy,) + far.shape[1:], BF16),
                    shape((nb, 1, cols), F32), shape((nb, 1, cols), F32)],
-        in_specs=[blk] * 8 + [vec, tab, tab, pl.BlockSpec(ss.shape, lambda i: (0, 0))] + [any_spec] * 10,
+        in_specs=[blk] * 8 + [vec, tab, tab, pl.BlockSpec(ss.shape, lambda i: (0, 0))] + [any_spec] * 11,
         out_specs=[any_spec] * 10 + [out_vec, out_vec],
         scratch_shapes=Scatter.scratch(nb * rows, dim) + [lane_tile] * 4 + [pltpu.VMEM((tokens, tokens), BF16)] * 2 + [
             lane_tile, pltpu.VMEM((2, tokens, HEAD_DIM), F32), pltpu.VMEM((2, tokens, HEAD_DIM), F32),
             pltpu.VMEM((2, tokens, HEAD_DIM), BF16), pltpu.VMEM((nb, 8, tokens), F32), pltpu.VMEM((8, tokens), F32),
             pltpu.VMEM((nb, n, 8, tokens), F32), pltpu.VMEM((4, min(256, tokens), cols), F32), pltpu.VMEM((min(256, tokens), 2 * cols), BF16),
             pltpu.VMEM((4, tokens, HEAD_DIM), F32),
-            dma((2,)), dma((2, 2)), dma((2, 3)), dma((4,)), dma((2,)), dma((nb,)), dma((nb, n)), dma((nb, n)), dma((2,)), dma((2,)),
+            dma((2,)), dma((2, 3)), dma((2, 3)), dma((4,)), dma((2,)), dma((nb,)), dma((nb, n)), dma((nb, n)), dma((8,)), dma((8,)),
             dma((nb, n // 2)), dma((nb, n // 2)), dma((2, 6)), dma((n_dy, 6)), dma((n_dy, 6))],
         compiler_params=params("arbitrary", collective_id=2, has_side_effects=True),
         cost_estimate=cost(4 * nb * tokens * dim * cols + 36 * nb * tokens * tokens * cols, 30 * nb * tokens * cols),
-    )(q, k, q_rot, k_rot, v, d_attn, o32, lse, gains, cos_tab, sin_tab, ss, q, k, o, part, far, d_full, w_q, w_k, w_v, wq_p)
+    )(q, k, q_rot, k_rot, v, d_attn, o32, lse, gains, cos_tab, sin_tab, ss, q, k, o, part, far, d_full, dwo_part, w_q, w_k, w_v, wq_p)
 
 
 def dy_dw_kernel(n, nb, dim, g_hbm, g_p, wq_hbm, wk_hbm, wv_hbm, wq_p, wk_p, wv_p, y_full, part_in, far_in,
@@ -1492,10 +1551,10 @@
         nb, _, dim = x_loc.shape
         y_full, d_own, q, k, v, wo_p, wo_t, ss, cos_tab, sin_tab, gains = gather_qkv_call(
             tp_size, x_loc, dy_loc, m_block, e_loc, w_q, w_k, w_v, w_o, b_q, b_k, b_v, g_q, g_k, pos_part)
-        d_full, o, _, d_attn, wq_p, part, far, q_rot, k_rot, lse, o32 = gather_attn_call(
+        d_full, o, _, d_attn, wq_p, part, far, dwo_part, q_rot, k_rot, lse, o32 = gather_attn_call(
             tp_size, q, k, v, gains, cos_tab, sin_tab, ss, w_q, w_o, wo_p, wo_t, d_own)
         proj, g, g_p, _, _, d_wo, wk_p, wv_p, part, far, d_gq, d_gk = attn_bwd_call(
-            tp_size, q, k, q_rot, k_rot, v, d_attn, o, o32, lse, gains, cos_tab, sin_tab, ss, part, far, d_full, w_q, w_k, w_v, wq_p)
+            tp_size, q, k, q_rot, k_rot, v, d_attn, o, o32, lse, gains, cos_tab, sin_tab, ss, part, far, d_full, dwo_part, w_q, w_k, w_v, wq_p)
         d_y, d_wq, d_wk, d_wv = dy_dw_call(tp_size, g, g_p, w_q, w_k, w_v, wq_p, wk_p, wv_p, y_full, part, far)
         x_out, d_x, d_mod, d_gq, d_gk, d_wq, d_wk, d_wv, d_wo = token_call(
             x_loc, dy_loc, proj, d_y, m_block, e_loc, b_o, d_gq, d_gk, (d_wq, d_wk, d_wv, d_wo))

time: 478 us -> 488 us (1.021)
  Pallas kernels: 474 us -> 484 us
    pallas_call x1, Pallas kernels: 90.3 us -> 100 us  [gather_attn_call(): pl.pallas_call(functools.partial(gather_attn_kernel, n, nb, heads, dim),...]
where the time goes in v9:
time: 488 us; the launch traced here: 487 us
  Pallas kernels  484 us (99%)
    pallas_call x1, Pallas kernels, gather_qkv_call(): pl.pallas_call(functools.partial(gather_qkv_kernel, n), name='gather_qkv'...  130 us
    pallas_call x1, Pallas kernels, attn_bwd_call(): pl.pallas_call(functools.partial(attn_bwd_kernel, n, nb, heads, dim), nam...  121 us
    pallas_call x1, Pallas kernels, gather_attn_call(): pl.pallas_call(functools.partial(gather_attn_kernel, n, nb, heads, dim),...  100 us
    pallas_call x1, Pallas kernels, dy_dw_call(): pl.pallas_call(functools.partial(dy_dw_kernel, n, nb, dim), name='dy_dw',...  94.2 us
    pallas_call x1, Pallas kernels, token_call(): pl.pallas_call(functools.partial(token_kernel, n_copies), name='tokens',...  27.1 us
    pallas_call x1, Pallas kernels, all_sum_call(): pl.pallas_call(functools.partial(all_sum_kernel, n), name='all_sum', out_...  10.9 us

profile of v9, /device:TPU:81, one launch (start us, length us, event | category | flops | bytes accessed | tf_op | source)
XLA Modules:
  0.0 486.6 jit_solution(16741857885174650155)
XLA Ops:
  0.6 129.9 %gather_qkv.1 = (bf16[3,768,5120]{2,1,0:T(8,128)(2,1)}, bf16[3,768,5120]{2,1,0:T(8,128)(2,1)}, f32[3,768,640]{2,1,0:T(8,128)}, f32[3,768,640]{2,1,0:T(8,128)}, b...) custom-call(bf16[3,96,5120]{2,1,0:T(8,128)(2,1)} %x_ref.3, ...), custom_call_target="tpu_custom_call" | custom-call | flops 45298483200 | bytes 40304640 | tf_op jit(solution)/shard_map/gather_qkv/pallas_call | solution.py:457
  130.5 100.4 %gather_attn.1 = (bf16[3,768,5120]{2,1,0:T(8,128)(2,1)}, bf16[3,768,640]{2,1,0:T(8,128)(2,1)}, bf16[3,768,640]{2,1,0:T(8,128)(2,1)}, bf16[3,768,640]{2,1,0:T(8,1...) custom-call(f32[3,768,640]{2,1,0:T(8,128)} %get-tuple-element.55.q_r, ...), custom_call_target="tpu_custom_call", output_to_operand_aliasing={{0}: (11, {})} | custom-call | flops 34728837120 | bytes 94371840 | tf_op jit(solution)/shard_map/gather_attn/pallas_call | solution.py:909
  230.9 121.5 %attn_bwd.1 = (bf16[3,96,5120]{2,1,0:T(8,128)(2,1)}, bf16[3,768,1920]{2,1,0:T(8,128)(2,1)}, bf16[3,768,1920]{2,1,0:T(8,128)(2,1)}, f32[3,768,640]{2,1,0:T(8,128)...) custom-call(f32[3,768,640]{2,1,0:T(8,128)} %get-tuple-element.55.q_r, ...), custom_call_target="tpu_custom_call" | custom-call | flops 70967623680 | bytes 44236800 | tf_op jit(solution)/shard_map/attn_bwd/pallas_call | solution.py:1291
  352.4 94.2 %dy_dw.1 = (bf16[3,96,5120]{2,1,0:T(8,128)(2,1)}, bf16[5120,640]{1,0:T(8,128)(2,1)}, bf16[5120,640]{1,0:T(8,128)(2,1)}, bf16[5120,640]{1,0:T(8,128)(2,1)}) custom-call(bf16[3,768,1920]{2,1,0:T(8,128)(2,1)} %get-tuple-element.77.g_hbm, bf16[3,768,1920]{2,1,0:T(8,128)(2,1)} %get-tuple-element.78.g_p, bf16[5120,640]{1,0:T(8,128)(2,1)} %wq_hbm.3, ...), custom_call_target="tpu_custom_call" | custom-call | flops 90596966400 | bytes 44236800 | tf_op jit(solution)/shard_map/dy_dw/pallas_call | solution.py:1434
  446.7 27.1 %tokens.1 = (bf16[3,96,5120]{2,1,0:T(8,128)(2,1)}, bf16[3,96,5120]{2,1,0:T(8,128)(2,1)}, f32[3,3,5120]{2,1,0:T(4,128)}, f32[640]{0:T(1024)}, f32[640]{0:T(1024)}...) custom-call(bf16[3,96,5120]{2,1,0:T(8,128)(2,1)} %x_ref.3, ...), custom_call_target="tpu_custom_call" | custom-call | flops 44236800 | bytes 17694720 | tf_op jit(solution)/shard_map/tokens/pallas_call | solution.py:1534
  473.8 1.1 reshape.26.x_ref
  474.9 10.9 %all_sum.1 = f32[8,45,128]{2,1,0:T(8,128)S(1)} custom-call(f32[8,45,128]{2,1,0:T(8,128)S(1)} %reshape.26.x_ref), custom_call_target="tpu_custom_call" | custom-call | flops 4000000000 | bytes 368640 | tf_op jit(solution)/shard_map/all_sum/pallas_call | solution.py:512
  485.8 0.1 reshape.27
  485.8 0.0 copy-start
  485.9 0.7 reduce_sum.9
  486.6 0.0 copy-done
Async XLA Ops:
  485.8 0.7 copy-start

commit v10 on v8

--- a/solution.py
+++ b/solution.py
@@ -538,69 +538,48 @@
 
 
 class Scatter:
-    def __init__(self, place, part, recv_far, recv_side, send, recv, far_src=None, early=0):
+    def __init__(self, place, part, recv_far, recv_side, send, recv, far_src=None):
         self.at, self.part, self.far, self.side, self.send, self.recv = place, part, recv_far, recv_side, send, recv
-        self.far_src, self.early = part if far_src is None else far_src, early
+        self.far_src = part if far_src is None else far_src
         self.rows = part.shape[2]
         self.half = self.rows // 2
 
-    def copy(self, j, idx, src, dst, target):
+    def message(self, idx, j, count=1):
+        js, p = pl.ds(j, count), self.at
+        rows = pl.ds(0, self.half) if idx in (0, 3, 4) else pl.ds(self.half, self.rows - self.half)
+        src = (self.far_src if idx < 2 else self.part).at[js, (0, 0, 1, 2, 1, 2)[idx], rows]
+        dst = self.far.at[js, idx] if idx < 2 else self.side.at[js, idx % 2, rows]
         return pltpu.make_async_remote_copy(src_ref=src, dst_ref=dst, send_sem=self.send.at[j, idx], recv_sem=self.recv.at[j, idx],
-                                            device_id={'tp': target}, device_id_type=MESH_ID)
-
-    def message(self, j, idx):
-        p, part, far, side = self.at, self.part, self.far, self.side
-        first, second = pl.ds(0, self.half), pl.ds(self.half, self.rows - self.half)
-        src, dst, target = (
-            lambda: (self.far_src.at[j, 0, first], far.at[j, 0], p.right),
-            lambda: (self.far_src.at[j, 0, second], far.at[j, 1], p.left),
-            lambda: (part.at[j, 1, second], side.at[j, 0, second], p.right),
-            lambda: (part.at[j, 2, first], side.at[j, 1, first], p.left),
-            lambda: (part.at[j, 1, first], side.at[j, 0, first], p.right),
-            lambda: (part.at[j, 2, second], side.at[j, 1, second], p.left))[idx]()
-        return self.copy(j, idx, src, dst, target)
-
-    def start_far(self, j, _=0):
-        for idx in (0, 1):
-            self.message(j, idx).start()
-        return 0
-
-    def start_side(self, j, _):
-        for idx in (2, 3):
-            self.message(j, idx).start()
-        return 0
-
-    def sums(self, j):
+                                            device_id={'tp': p.left if idx % 2 else p.right}, device_id_type=MESH_ID)
+
+    def start(self, kind, j, count=1):
+        for idx in (2 * kind, 2 * kind + 1):
+            self.message(idx, j, count).start()
+
+    def wait_recv(self, kind, j, count=1):
+        for idx in (2 * kind, 2 * kind + 1):
+            self.message(idx, j, count).wait_recv()
+
+    def wait_send(self, kind, j, count=1):
+        for idx in (2 * kind, 2 * kind + 1):
+            self.message(idx, j, count).wait_send()
+
+    def add(self, j):
         h = self.half
-
-        @pl.when(j >= self.early)
-        def _():
-            self.message(j, 0).wait_recv()
-            self.message(j, 1).wait_recv()
-
         self.part[j, 1, :h] = (self.part[j, 1, :h].astype(F32) + self.far[j, 0].astype(F32)).astype(BF16)
         self.part[j, 2, h:] = (self.part[j, 2, h:].astype(F32) + self.far[j, 1].astype(F32)).astype(BF16)
-        self.message(j, 4).start()
-        self.message(j, 5).start()
-
-    def sums_step(self, j, _):
-        self.sums(j)
-        return 0
+
+    def sums(self, j, count=1):
+        def step(m, _):
+            self.add(j + m)
+            return 0
+
+        lax.fori_loop(0, count, step, 0)
+        self.start(SUMS, j, count)
 
     def final(self, j):
-        for idx in range(2, 6):
-            self.message(j, idx).wait_recv()
         total = self.part[j, 3].astype(F32) + self.side[j, 0].astype(F32) + self.side[j, 1].astype(F32)
         self.part[j, 3] = total.astype(BF16)
-
-    def finish(self, j):
-        @pl.when(j >= self.early)
-        def _():
-            for idx in range(2):
-                self.message(j, idx).wait_send()
-
-        for idx in range(2, 6):
-            self.message(j, idx).wait_send()
 
     @staticmethod
     def scratch(rows, dim):
@@ -615,22 +594,41 @@
     return [pltpu.make_async_copy(part.at[j, 3, pl.ds(b * rows, rows)], out.at[b, :, cs], sem.at[b]) for b in range(nb)]
 
 
-def scatter_end(scatter, out, sem, nc):
-    def last(j, _):
-        scatter.final(j)
-        for c in scatter_outputs(scatter.part, out, sem, j):
-            c.start()
-        return 0
-
-    lax.fori_loop(0, nc, last, 0)
+FAR, SIDES, SUMS = range(3)
+
+
+def halves_of(nc):
+    return [(0, nc // 2), (nc // 2, nc - nc // 2)] if nc > 1 else [(0, nc)]
+
+
+def scatter_end(scatter, out, sem, nc, far_groups, sum_groups):
+    waiting = list(sum_groups)
+    for lo, count in halves_of(nc):
+        scatter.wait_recv(SIDES, lo, count)
+        while waiting and waiting[0][0] < lo + count:
+            scatter.wait_recv(SUMS, *waiting.pop(0))
+
+        def last(j, _):
+            scatter.final(j)
+            for c in scatter_outputs(scatter.part, out, sem, j):
+                c.start()
+            return 0
+
+        lax.fori_loop(lo, lo + count, last, 0)
 
     def drain(j, _):
         for c in scatter_outputs(scatter.part, out, sem, j):
             c.wait()
-        scatter.finish(j)
         return 0
 
     lax.fori_loop(0, nc, drain, 0)
+    for kind, groups in ((FAR, far_groups), (SIDES, halves_of(nc)), (SUMS, sum_groups)):
+        for group in groups:
+            scatter.wait_send(kind, *group)
+
+
+def pairs_of(lo, hi, size=2):
+    return [(j, min(size, hi - j)) for j in range(lo, hi, size)]
 
 
 def pair_rows(place, nb, rows, mine, theirs, lhs, sem):
@@ -658,8 +656,8 @@
     gather = Gather(place, d_full, rows, g_send, g_recv, early=EARLY_ROWS)
     cols = heads * HEAD_DIM
     nc = dim // CHUNK
-    early_chunks = min(EARLY_CHUNKS, nc)
     mid = nc // 2
+    early_chunks = min(EARLY_CHUNKS, mid)
     scatter = Scatter(place, part_out, far_in, None, s_send, s_recv)
     trade_o = RowTrade(place, o_out, o_p, rows, r_send, r_recv)
 
@@ -744,10 +742,6 @@
             def stored(j):
                 store(j).wait()
 
-                @pl.when((j < early_chunks) & (j >= mid))
-                def _():
-                    scatter.start_far(j)
-
             for c in chunk(0):
                 c.start()
             for c in loads:
@@ -778,7 +772,7 @@
                 def _():
                     gather.arrive(3 * nb - 2, nb)
                     gather.arrive(3 * nb - 1, nb)
-                    lax.fori_loop(0, min(early_chunks, mid), scatter.start_far, 0)
+                    scatter.start(FAR, 0, early_chunks)
 
                 return 0
 
@@ -833,9 +827,8 @@
             gather.finish(b)
         trade_o.wait_send()
         trade_w().wait()
-        for j in range(early_chunks):
-            for idx in (0, 1):
-                scatter.message(j, idx).wait()
+        scatter.wait_recv(FAR, 0, early_chunks)
+        scatter.wait_send(FAR, 0, early_chunks)
 
 
 def gather_attn_call(n, q, k, v, gains, cos_tab, sin_tab, ss, w_q, w_o, wo_p, wo_t, d_full):
@@ -845,7 +838,7 @@
     rows = tokens // n
     last = nb * heads - 1
     nc = dim // CHUNK
-    early = min(EARLY_CHUNKS, nc)
+    early = min(EARLY_CHUNKS, nc // 2)
     shape = jax.ShapeDtypeStruct
     dma = pltpu.SemaphoreType.DMA
     any_spec = pl.BlockSpec(memory_space=pl.ANY)
@@ -908,22 +901,25 @@
     scale = HEAD_DIM ** -0.5
     place = Place(n)
     early = far_in.shape[0]
-    scatter = Scatter(place, part, recv_far, recv_side, s_send, s_recv, far_src=part_in, early=early)
+    scatter = Scatter(place, part, recv_far, recv_side, s_send, s_recv, far_src=part_in)
 
     def stored():
         return [pltpu.make_async_copy(part_in, part, ld_sem.at[0]),
                 pltpu.make_async_copy(far_in, recv_far.at[pl.ds(0, early)], ld_sem.at[1])]
 
+    n_pieces = 8
+
     def trade_w(j):
-        return place.to_partner((wk_hbm, wv_hbm)[j], (wk_p, wv_p)[j], t_send.at[j], t_recv.at[j])
+        m = j % (n_pieces // 2)
+        size = dim // (n_pieces // 2)
+        src, dst = ((wk_hbm, wk_p), (wv_hbm, wv_p))[j // (n_pieces // 2)]
+        return place.to_partner(src.at[pl.ds(m * size, size)], dst.at[pl.ds(m * size, size)], t_send.at[j], t_recv.at[j])
 
     @pl.when(step == 0)
     def _():
         place.barrier(place.everyone())
         for c in stored():
             c.start()
-        for j in range(2):
-            trade_w(j).start()
 
     @pl.when(step == 1)
     def _():
@@ -937,18 +933,26 @@
                 pltpu.make_async_copy(ks_st.at[slot], dks_out.at[b, :, lanes], fl_sem.at[slot, 1]),
                 pltpu.make_async_copy(v_st.at[slot], g_out.at[b, :, v_lanes], fl_sem.at[slot, 2])]
 
-    mid = early
+    for j in range(n_pieces):
+        pl.when(step == j * (steps - 1) // n_pieces + 1)(lambda j=j: trade_w(j).start())
+
+    far_groups = pairs_of(early, nc)
+    early_sums = [(0, early - early // 2)] + ([(early - early // 2, early // 2)] if early > 1 else [])
+    late_sums = pairs_of(early, nc, 4)
     events = []
-    late = list(range(mid))
-    for m, j in enumerate(range(early, nc)):
-        events.append(functools.partial(scatter.start_far, j))
-        if m >= 2 and m % 2 == 0 and late:
-            events.append(functools.partial(scatter.sums, late.pop(0)))
-    events += [functools.partial(scatter.sums, j) for j in late]
-    for m, event in enumerate(events):
-        @pl.when(step == m * (steps - 1) // len(events))
+    for m, group in enumerate(far_groups):
+        events.append((group[1], functools.partial(scatter.start, FAR, *group)))
+        if m >= 1 and m - 1 < len(early_sums):
+            events.append((early_sums[m - 1][1], functools.partial(scatter.sums, *early_sums[m - 1])))
+    for group in early_sums[max(len(far_groups) - 1, 0):]:
+        events.append((group[1], functools.partial(scatter.sums, *group)))
+    total, done = sum(size for size, _ in events), 0
+    for size, event in events:
+        @pl.when(step == max(done * (steps - 1) // total, 0 if done == 0 else 2))
         def _(event=event):
             event()
+
+        done += size
 
     rb = min(256, tokens)
     per = tokens // rb
@@ -988,6 +992,7 @@
             lanes_s[2 * m + 1] = lanes_of(st_sum[m:m + 1] / dim)
 
     first = heads - per
+    assert first >= 2
     b_old = step // heads - 1
     i_old = lax.rem(step, heads) - first
 
@@ -1089,8 +1094,12 @@
         for s in range(2):
             for c in flush(0, 0, s):
                 c.wait()
-        lax.fori_loop(mid, nc, scatter.sums_step, 0)
-        lax.fori_loop(0, nc, scatter.start_side, 0)
+        for group in far_groups:
+            scatter.wait_recv(FAR, *group)
+        for group in late_sums:
+            scatter.sums(*group)
+        for group in halves_of(nc):
+            scatter.start(SIDES, *group)
         for c in grad_loads(nb - 1, 0):
             c.start()
         grad_begin(nb - 1)
@@ -1154,10 +1163,11 @@
                       pltpu.VMEM((2, nb, tokens, bn), BF16), pltpu.VMEM((2, cols, bn), BF16))
         for b in range(nb):
             trade(b).wait_recv()
-        for j in range(2):
+        for j in range(n_pieces):
             trade_w(j).wait_recv()
 
         n_dy = part_dy.shape[0]
+        dy_groups = pairs_of(0, n_dy)
         scatter_y = Scatter(place, part_dy, far_dy, None, y_send, y_recv)
 
         def first_dy(lhs, wbuf, pst):
@@ -1183,7 +1193,9 @@
                 @pl.when(j >= 1)
                 def _():
                     store.wait()
-                    scatter_y.start_far(j - 1)
+
+                for lo, count in dy_groups:
+                    pl.when(j == lo + count)(functools.partial(scatter_y.start, FAR, lo, count))
 
                 for d in range(2):
                     z = dy.dot(j, d)
@@ -1194,18 +1206,18 @@
 
             lax.fori_loop(0, n_dy, body, 0)
             pltpu.make_async_copy(pst, part_dy.at[n_dy - 1], go_sem.at[0]).wait()
-            scatter_y.start_far(n_dy - 1)
+            scatter_y.start(FAR, *dy_groups[-1])
 
         pl.run_scoped(first_dy, pltpu.VMEM((4 * nb * rows, 6 * cols), BF16), pltpu.VMEM((2, CHUNK, 6 * cols), BF16),
                       pltpu.VMEM((4, nb * rows, CHUNK), BF16))
-        scatter_end(scatter, proj_out, out_sem, nc)
+        scatter_end(scatter, proj_out, out_sem, nc, far_groups, early_sums + late_sums)
         for b in range(nb):
             trade(b).wait_send()
-        for j in range(2):
+        for j in range(n_pieces):
             trade_w(j).wait_send()
-        for j in range(n_dy):
-            for idx in (0, 1):
-                scatter_y.message(j, idx).wait()
+        for group in dy_groups:
+            scatter_y.wait_recv(FAR, *group)
+            scatter_y.wait_send(FAR, *group)
 
 
 def attn_bwd_call(n, q, k, q_rot, k_rot, v, d_attn, o, o32, lse, gains, cos_tab, sin_tab, ss, part, far, d_full, w_q, w_k, w_v, wq_p):
@@ -1242,7 +1254,7 @@
             pltpu.VMEM((2, tokens, HEAD_DIM), BF16), pltpu.VMEM((nb, 8, tokens), F32), pltpu.VMEM((8, tokens), F32),
             pltpu.VMEM((nb, n, 8, tokens), F32), pltpu.VMEM((4, min(256, tokens), cols), F32), pltpu.VMEM((min(256, tokens), 2 * cols), BF16),
             pltpu.VMEM((4, tokens, HEAD_DIM), F32),
-            dma((2,)), dma((2, 2)), dma((2, 3)), dma((4,)), dma((2,)), dma((nb,)), dma((nb, n)), dma((nb, n)), dma((2,)), dma((2,)),
+            dma((2,)), dma((2, 2)), dma((2, 3)), dma((4,)), dma((2,)), dma((nb,)), dma((nb, n)), dma((nb, n)), dma((8,)), dma((8,)),
             dma((nb, n // 2)), dma((nb, n // 2)), dma((2, 6)), dma((n_dy, 6)), dma((n_dy, 6))],
         compiler_params=params("arbitrary", collective_id=2, has_side_effects=True),
         cost_estimate=cost(4 * nb * tokens * dim * cols + 36 * nb * tokens * tokens * cols, 30 * nb * tokens * cols),
@@ -1259,7 +1271,10 @@
     early = far_in.shape[0]
     lag = 3
     place = Place(n)
-    scatter = Scatter(place, part, recv_far, recv_side, s_send, s_recv, early=early)
+    scatter = Scatter(place, part, recv_far, recv_side, s_send, s_recv)
+    far_groups = pairs_of(early, nc, 1)
+    in_loop = max(nc - lag - early, 0)
+    sum_groups = [(0, early)] + pairs_of(early, early + in_loop, 1) + [(early + in_loop, nc - early - in_loop)]
     stored = [pltpu.make_async_copy(part_in, part.at[pl.ds(0, early)], ld_sem.at[2]),
               pltpu.make_async_copy(far_in, recv_far.at[pl.ds(0, early)], ld_sem.at[3])]
     load_g = pltpu.make_async_copy(g_hbm, g, ld_sem.at[4])
@@ -1280,7 +1295,7 @@
         place.barrier(place.near()[:2])
         for c in stored:
             c.wait()
-        lax.fori_loop(0, early, scatter.sums_step, 0)
+        scatter.sums(0, early)
         load_g.start()
 
         def body(j, _):
@@ -1301,16 +1316,18 @@
                 part[j, 2 * d] = z[:nb * rows]
                 part[j, 2 * d + 1] = z[nb * rows:]
                 if d == 0:
-                    scatter.start_far(j)
+                    scatter.start(FAR, j)
 
             @pl.when(j >= early + lag)
             def _():
+                scatter.wait_recv(FAR, j - lag)
                 scatter.sums(j - lag)
 
             return 0
 
         lax.fori_loop(early, nc, body, 0)
-        lax.fori_loop(0, nc, scatter.start_side, 0)
+        for group in halves_of(nc):
+            scatter.start(SIDES, *group)
 
     pl.run_scoped(chain, pltpu.VMEM((4 * nb * rows, 6 * cols), BF16), pltpu.VMEM((2, CHUNK, 6 * cols), BF16))
 
@@ -1344,10 +1361,12 @@
                     s.wait()
 
             chunk(c).wait()
-            for m in range(lag):
-                late = max(nc - lag, early) + m
-                if late < nc:
-                    pl.when(c == min(m, n_chunks - 1))(functools.partial(scatter.sums, late))
+            @pl.when(c == min(1, n_chunks - 1))
+            def _():
+                for group in far_groups[in_loop:]:
+                    scatter.wait_recv(FAR, *group)
+                scatter.sums(*sum_groups[-1])
+
             wst[slot] = lax.dot_general(ybuf[slot].reshape(nb * tokens, bm), g[...].reshape(nb * tokens, 3 * cols), TN,
                                         preferred_element_type=F32).astype(BF16)
             for s in store(c):
@@ -1361,7 +1380,7 @@
 
     bm = min(512, dim)
     pl.run_scoped(weight_grad, pltpu.VMEM((2, nb, tokens, bm), BF16), pltpu.VMEM((2, bm, 3 * cols), BF16))
-    scatter_end(scatter, dy_out, out_sem, nc)
+    scatter_end(scatter, dy_out, out_sem, nc, far_groups, sum_groups)
 
 
 def dy_dw_call(n, g, g_p, w_q, w_k, w_v, wq_p, wk_p, wv_p, y_full, part, far):

time: 478 us -> 480 us (level)
  no operation moved by 1% of the time
where the time goes in v10:
time: 480 us; the launch traced here: 479 us
  Pallas kernels  476 us (99%)
    pallas_call x1, Pallas kernels, gather_qkv_call(): pl.pallas_call(functools.partial(gather_qkv_kernel, n), name='gather_qkv'...  130 us
    pallas_call x1, Pallas kernels, attn_bwd_call(): pl.pallas_call(functools.partial(attn_bwd_kernel, n, nb, heads, dim), nam...  121 us
    pallas_call x1, Pallas kernels, dy_dw_call(): pl.pallas_call(functools.partial(dy_dw_kernel, n, nb, dim), name='dy_dw',...  95.9 us
    pallas_call x1, Pallas kernels, gather_attn_call(): pl.pallas_call(functools.partial(gather_attn_kernel, n, nb, heads, dim),...  90.3 us
    pallas_call x1, Pallas kernels, token_call(): pl.pallas_call(functools.partial(token_kernel, n_copies), name='tokens',...  27 us
    pallas_call x1, Pallas kernels, all_sum_call(): pl.pallas_call(functools.partial(all_sum_kernel, n), name='all_sum', out_...  12.3 us

profile of v10, /device:TPU:81, one launch (start us, length us, event | category | flops | bytes accessed | tf_op | source)
XLA Modules:
  0.0 479.0 jit_solution(15003473029225390991)
XLA Ops:
  0.6 129.8 %gather_qkv.1 = (bf16[3,768,5120]{2,1,0:T(8,128)(2,1)}, bf16[3,768,5120]{2,1,0:T(8,128)(2,1)}, f32[3,768,640]{2,1,0:T(8,128)}, f32[3,768,640]{2,1,0:T(8,128)}, b...) custom-call(bf16[3,96,5120]{2,1,0:T(8,128)(2,1)} %x_ref.3, ...), custom_call_target="tpu_custom_call" | custom-call | flops 45298483200 | bytes 40304640 | tf_op jit(solution)/shard_map/gather_qkv/pallas_call | solution.py:457
  130.5 90.3 %gather_attn.1 = (bf16[3,768,5120]{2,1,0:T(8,128)(2,1)}, bf16[3,768,640]{2,1,0:T(8,128)(2,1)}, bf16[3,768,640]{2,1,0:T(8,128)(2,1)}, bf16[3,768,640]{2,1,0:T(8,1...) custom-call(f32[3,768,640]{2,1,0:T(8,128)} %get-tuple-element.54.q_r, ...), custom_call_target="tpu_custom_call", output_to_operand_aliasing={{0}: (11, {})} | custom-call | flops 34728837120 | bytes 94371840 | tf_op jit(solution)/shard_map/gather_attn/pallas_call | solution.py:854
  220.8 121.1 %attn_bwd.1 = (bf16[3,96,5120]{2,1,0:T(8,128)(2,1)}, bf16[3,768,1920]{2,1,0:T(8,128)(2,1)}, bf16[3,768,1920]{2,1,0:T(8,128)(2,1)}, f32[3,768,640]{2,1,0:T(8,128)...) custom-call(f32[3,768,640]{2,1,0:T(8,128)} %get-tuple-element.54.q_r, ...), custom_call_target="tpu_custom_call" | custom-call | flops 70967623680 | bytes 44236800 | tf_op jit(solution)/shard_map/attn_bwd/pallas_call | solution.py:1244
  341.9 95.9 %dy_dw.1 = (bf16[3,96,5120]{2,1,0:T(8,128)(2,1)}, bf16[5120,640]{1,0:T(8,128)(2,1)}, bf16[5120,640]{1,0:T(8,128)(2,1)}, bf16[5120,640]{1,0:T(8,128)(2,1)}) custom-call(bf16[3,768,1920]{2,1,0:T(8,128)(2,1)} %get-tuple-element.75.g_hbm, bf16[3,768,1920]{2,1,0:T(8,128)(2,1)} %get-tuple-element.76.g_p, bf16[5120,640]{1,0:T(8,128)(2,1)} %wq_hbm.3, ...), custom_call_target="tpu_custom_call" | custom-call | flops 90596966400 | bytes 44236800 | tf_op jit(solution)/shard_map/dy_dw/pallas_call | solution.py:1394
  437.9 27.0 %tokens.1 = (bf16[3,96,5120]{2,1,0:T(8,128)(2,1)}, bf16[3,96,5120]{2,1,0:T(8,128)(2,1)}, f32[3,3,5120]{2,1,0:T(4,128)}, f32[640]{0:T(1024)}, f32[640]{0:T(1024)}...) custom-call(bf16[3,96,5120]{2,1,0:T(8,128)(2,1)} %x_ref.3, ...), custom_call_target="tpu_custom_call" | custom-call | flops 44236800 | bytes 17694720 | tf_op jit(solution)/shard_map/tokens/pallas_call | solution.py:1494
  464.8 1.1 reshape.26.x_ref
  465.9 12.3 %all_sum.1 = f32[8,45,128]{2,1,0:T(8,128)S(1)} custom-call(f32[8,45,128]{2,1,0:T(8,128)S(1)} %reshape.26.x_ref), custom_call_target="tpu_custom_call" | custom-call | flops 4000000000 | bytes 368640 | tf_op jit(solution)/shard_map/all_sum/pallas_call | solution.py:512
  478.2 0.1 reshape.27
  478.3 0.0 copy-start
  478.3 0.7 reduce_sum.9
  479.0 0.0 copy-done
Async XLA Ops:
  478.3 0.7 copy-start

commit v11 on v8

--- a/solution.py
+++ b/solution.py
@@ -223,7 +223,7 @@
 
 GATHER_SEMS = 9
 EARLY_ROWS = 1
-EARLY_CHUNKS = 3
+EARLY_CHUNKS = 1
 EARLY_DY = 4
 
 
@@ -647,7 +647,7 @@
 
 def gather_attn_kernel(n, nb, heads, dim, q_ref, k_ref, v_ref, gain_ref, cos_ref, sin_ref, ss_ref,
                        wq_ref, wo_ref, wo_p, wo_t, d_in,
-                       d_full, o_out, o_p, da_out, wq_p, part_out, far_in, qr_ref, kr_ref, lse_ref, o32_ref,
+                       d_full, o_out, o_p, da_out, wq_p, part_out, far_in, o_t, qr_ref, kr_ref, lse_ref, o32_ref,
                        inv_q, inv_k, o_all, wo, xbuf, ast,
                        w_sem, ld_sem, out_sem, o_sem, p_sem, l_sem, g_send, g_recv, t_send, t_recv, r_send, r_recv, s_send, s_recv):
     step = pl.program_id(0)
@@ -824,6 +824,13 @@
                               pltpu.VMEM((2, 4, nb * rows, CHUNK), BF16))
                 fetch(i + 1)
 
+                def turn(turned):
+                    for b in range(nb):
+                        turned[:, b * tokens:(b + 1) * tokens] = o_all[b].T
+                    pltpu.sync_copy(turned, o_t)
+
+                pl.run_scoped(turn, pltpu.VMEM((cols, nb * tokens), BF16))
+
             return 0
 
         lax.fori_loop(0, 4 * nb, item, 0)
@@ -861,10 +868,10 @@
     return pl.pallas_call(
         functools.partial(gather_attn_kernel, n, nb, heads, dim), name="gather_attn", grid=(nb * heads + 1,),
         out_shape=[shape(d_full.shape, BF16), head_arr, head_arr, head_arr, shape(w_q.shape, BF16)]
-        + [shape((nc, 4, nb * rows, CHUNK), BF16), shape((early, 2, nb * rows // 2, CHUNK), BF16), head_arr, head_arr,
+        + [shape((nc, 4, nb * rows, CHUNK), BF16), shape((early, 2, nb * rows // 2, CHUNK), BF16), shape((cols, nb * tokens), BF16), head_arr, head_arr,
            shape((nb, tokens, cols), F32), shape((nb, tokens, cols), F32)],
         in_specs=[blk, blk, blk, vec, tab, tab, pl.BlockSpec(ss.shape, lambda i: (0, 0))] + [any_spec] * 5,
-        out_specs=[any_spec] * 7 + [blk] * 4,
+        out_specs=[any_spec] * 8 + [blk] * 4,
         scratch_shapes=[
             pltpu.VMEM((tokens, HEAD_DIM), F32), pltpu.VMEM((tokens, HEAD_DIM), F32), pltpu.VMEM((nb, tokens, cols), BF16),
             pltpu.VMEM((dim, cols), BF16), pltpu.VMEM((2, 2 * rows, dim), BF16), pltpu.VMEM((2, 2 * rows, cols), BF16),
@@ -893,7 +900,7 @@
 
 
 def attn_bwd_kernel(n, nb, heads, dim, q_ref, k_ref, qr_ref, kr_ref, v_ref, do_ref, o_ref, lse_ref, gain_ref, cos_ref, sin_ref, ss_ref,
-                    q_hbm, k_hbm, o_hbm, part_in, far_in, d_full, wq_hbm, wk_hbm, wv_hbm, wq_p,
+                    q_hbm, k_hbm, o_t, part_in, far_in, d_full, wq_hbm, wk_hbm, wv_hbm, wq_p,
                     proj_out, g_out, g_p, dqs_out, dks_out, dwo_out, wk_p, wv_p, part_dy, far_dy, dgq_ref, dgk_ref,
                     part, recv_far, recv_side, s_send, s_recv,
                     inv_q, inv_k, acc_q, acc_k, p_all, ds_all, dq_all, qs_st, ks_st, v_st, st_row, st_sum, slots, fbuf, gbuf, lanes_s,
@@ -914,16 +921,19 @@
         return [pltpu.make_async_copy(part_in, part, ld_sem.at[0]),
                 pltpu.make_async_copy(far_in, recv_far.at[pl.ds(0, early)], ld_sem.at[1])]
 
+    n_pieces = 8
+
     def trade_w(j):
-        return place.to_partner((wk_hbm, wv_hbm)[j], (wk_p, wv_p)[j], t_send.at[j], t_recv.at[j])
+        m = j % (n_pieces // 2)
+        size = dim // (n_pieces // 2)
+        src, dst = ((wk_hbm, wk_p), (wv_hbm, wv_p))[j // (n_pieces // 2)]
+        return place.to_partner(src.at[pl.ds(m * size, size)], dst.at[pl.ds(m * size, size)], t_send.at[j], t_recv.at[j])
 
     @pl.when(step == 0)
     def _():
         place.barrier(place.everyone())
         for c in stored():
             c.start()
-        for j in range(2):
-            trade_w(j).start()
 
     @pl.when(step == 1)
     def _():
@@ -936,6 +946,9 @@
         return [pltpu.make_async_copy(qs_st.at[slot], dqs_out.at[b, :, lanes], fl_sem.at[slot, 0]),
                 pltpu.make_async_copy(ks_st.at[slot], dks_out.at[b, :, lanes], fl_sem.at[slot, 1]),
                 pltpu.make_async_copy(v_st.at[slot], g_out.at[b, :, v_lanes], fl_sem.at[slot, 2])]
+
+    for j in range(n_pieces):
+        pl.when(step == j * (steps - 1) // n_pieces + 1)(lambda j=j: trade_w(j).start())
 
     mid = early
     events = []
@@ -988,6 +1001,7 @@
             lanes_s[2 * m + 1] = lanes_of(st_sum[m:m + 1] / dim)
 
     first = heads - per
+    assert first >= 2
     b_old = step // heads - 1
     i_old = lax.rem(step, heads) - first
 
@@ -1093,23 +1107,25 @@
         lax.fori_loop(0, nc, scatter.start_side, 0)
         for c in grad_loads(nb - 1, 0):
             c.start()
-        grad_begin(nb - 1)
-
-        def last_row(i, _):
-            @pl.when(i > 0)
-            def _():
-                grad_store(0, 0).wait()
-                for c in grad_loads(nb - 1, i):
-                    c.start()
-
-            grad_block(nb - 1, i)
-            return 0
-
-        lax.fori_loop(0, per, last_row, 0)
-        grad_store(0, 0).wait()
-        trade(nb - 1).start()
-
-        def weight_grad(turned, obuf, dbuf, wst):
+
+        def last_grad():
+            grad_begin(nb - 1)
+
+            def last_row(i, _):
+                @pl.when(i > 0)
+                def _():
+                    grad_store(0, 0).wait()
+                    for c in grad_loads(nb - 1, i):
+                        c.start()
+
+                grad_block(nb - 1, i)
+                return 0
+
+            lax.fori_loop(0, per, last_row, 0)
+            grad_store(0, 0).wait()
+            trade(nb - 1).start()
+
+        def weight_grad(turned, dbuf, wst):
             bn = min(512, dim)
             n_chunks = dim // bn
 
@@ -1121,12 +1137,10 @@
                 slot = lax.rem(c, 2)
                 return pltpu.make_async_copy(wst.at[slot], dwo_out.at[:, pl.ds(pl.multiple_of(c * bn, bn), bn)], w_sem.at[slot, 0])
 
-            load_o = pltpu.make_async_copy(o_hbm, obuf, ld_sem.at[0])
+            load_o = pltpu.make_async_copy(o_t, turned, ld_sem.at[0])
             load_o.start()
             chunk(0).start()
             load_o.wait()
-            for b in range(nb):
-                turned[:, b * tokens:(b + 1) * tokens] = obuf[b].T
 
             def body(c, _):
                 slot = lax.rem(c, 2)
@@ -1143,6 +1157,7 @@
                 d = dbuf[slot].reshape(nb * tokens, bn)
                 wst[slot] = jnp.dot(turned[...], d, preferred_element_type=F32).astype(BF16)
                 store(c).start()
+                pl.when(c == max(n_chunks // 2 - 2, 0))(last_grad)
                 return 0
 
             lax.fori_loop(0, n_chunks, body, 0)
@@ -1150,11 +1165,11 @@
                 store(s).wait()
 
         bn = min(512, dim)
-        pl.run_scoped(weight_grad, pltpu.VMEM((cols, nb * tokens), BF16), pltpu.VMEM((nb, tokens, cols), BF16),
-                      pltpu.VMEM((2, nb, tokens, bn), BF16), pltpu.VMEM((2, cols, bn), BF16))
+        pl.run_scoped(weight_grad, pltpu.VMEM((cols, nb * tokens), BF16), pltpu.VMEM((2, nb, tokens, bn), BF16),
+                      pltpu.VMEM((2, cols, bn), BF16))
         for b in range(nb):
             trade(b).wait_recv()
-        for j in range(2):
+        for j in range(n_pieces):
             trade_w(j).wait_recv()
 
         n_dy = part_dy.shape[0]
@@ -1201,14 +1216,14 @@
         scatter_end(scatter, proj_out, out_sem, nc)
         for b in range(nb):
             trade(b).wait_send()
-        for j in range(2):
+        for j in range(n_pieces):
             trade_w(j).wait_send()
         for j in range(n_dy):
             for idx in (0, 1):
                 scatter_y.message(j, idx).wait()
 
 
-def attn_bwd_call(n, q, k, q_rot, k_rot, v, d_attn, o, o32, lse, gains, cos_tab, sin_tab, ss, part, far, d_full, w_q, w_k, w_v, wq_p):
+def attn_bwd_call(n, q, k, q_rot, k_rot, v, d_attn, o_t, o32, lse, gains, cos_tab, sin_tab, ss, part, far, d_full, w_q, w_k, w_v, wq_p):
     nb, tokens, cols = q.shape
     dim = d_full.shape[2]
     heads = cols // HEAD_DIM
@@ -1242,11 +1257,11 @@
             pltpu.VMEM((2, tokens, HEAD_DIM), BF16), pltpu.VMEM((nb, 8, tokens), F32), pltpu.VMEM((8, tokens), F32),
             pltpu.VMEM((nb, n, 8, tokens), F32), pltpu.VMEM((4, min(256, tokens), cols), F32), pltpu.VMEM((min(256, tokens), 2 * cols), BF16),
             pltpu.VMEM((4, tokens, HEAD_DIM), F32),
-            dma((2,)), dma((2, 2)), dma((2, 3)), dma((4,)), dma((2,)), dma((nb,)), dma((nb, n)), dma((nb, n)), dma((2,)), dma((2,)),
+            dma((2,)), dma((2, 2)), dma((2, 3)), dma((4,)), dma((2,)), dma((nb,)), dma((nb, n)), dma((nb, n)), dma((8,)), dma((8,)),
             dma((nb, n // 2)), dma((nb, n // 2)), dma((2, 6)), dma((n_dy, 6)), dma((n_dy, 6))],
         compiler_params=params("arbitrary", collective_id=2, has_side_effects=True),
         cost_estimate=cost(4 * nb * tokens * dim * cols + 36 * nb * tokens * tokens * cols, 30 * nb * tokens * cols),
-    )(q, k, q_rot, k_rot, v, d_attn, o32, lse, gains, cos_tab, sin_tab, ss, q, k, o, part, far, d_full, w_q, w_k, w_v, wq_p)
+    )(q, k, q_rot, k_rot, v, d_attn, o32, lse, gains, cos_tab, sin_tab, ss, q, k, o_t, part, far, d_full, w_q, w_k, w_v, wq_p)
 
 
 def dy_dw_kernel(n, nb, dim, g_hbm, g_p, wq_hbm, wk_hbm, wv_hbm, wq_p, wk_p, wv_p, y_full, part_in, far_in,
@@ -1492,10 +1507,10 @@
         nb, _, dim = x_loc.shape
         y_full, d_own, q, k, v, wo_p, wo_t, ss, cos_tab, sin_tab, gains = gather_qkv_call(
             tp_size, x_loc, dy_loc, m_block, e_loc, w_q, w_k, w_v, w_o, b_q, b_k, b_v, g_q, g_k, pos_part)
-        d_full, o, _, d_attn, wq_p, part, far, q_rot, k_rot, lse, o32 = gather_attn_call(
+        d_full, _, _, d_attn, wq_p, part, far, o_t, q_rot, k_rot, lse, o32 = gather_attn_call(
             tp_size, q, k, v, gains, cos_tab, sin_tab, ss, w_q, w_o, wo_p, wo_t, d_own)
         proj, g, g_p, _, _, d_wo, wk_p, wv_p, part, far, d_gq, d_gk = attn_bwd_call(
-            tp_size, q, k, q_rot, k_rot, v, d_attn, o, o32, lse, gains, cos_tab, sin_tab, ss, part, far, d_full, w_q, w_k, w_v, wq_p)
+            tp_size, q, k, q_rot, k_rot, v, d_attn, o_t, o32, lse, gains, cos_tab, sin_tab, ss, part, far, d_full, w_q, w_k, w_v, wq_p)
         d_y, d_wq, d_wk, d_wv = dy_dw_call(tp_size, g, g_p, w_q, w_k, w_v, wq_p, wk_p, wv_p, y_full, part, far)
         x_out, d_x, d_mod, d_gq, d_gk, d_wq, d_wk, d_wv, d_wo = token_call(
             x_loc, dy_loc, proj, d_y, m_block, e_loc, b_o, d_gq, d_gk, (d_wq, d_wk, d_wv, d_wo))

time: 478 us -> 482 us (level)
  no operation moved by 1% of the time
where the time goes in v11:
time: 482 us; the launch traced here: 480 us
  Pallas kernels  478 us (99%)
    pallas_call x1, Pallas kernels, gather_qkv_call(): pl.pallas_call(functools.partial(gather_qkv_kernel, n), name='gather_qkv'...  130 us
    pallas_call x1, Pallas kernels, attn_bwd_call(): pl.pallas_call(functools.partial(attn_bwd_kernel, n, nb, heads, dim), nam...  127 us
    pallas_call x1, Pallas kernels, dy_dw_call(): pl.pallas_call(functools.partial(dy_dw_kernel, n, nb, dim), name='dy_dw',...  94.2 us
    pallas_call x1, Pallas kernels, gather_attn_call(): pl.pallas_call(functools.partial(gather_attn_kernel, n, nb, heads, dim),...  88.8 us
    pallas_call x1, Pallas kernels, token_call(): pl.pallas_call(functools.partial(token_kernel, n_copies), name='tokens',...  27 us
    pallas_call x1, Pallas kernels, all_sum_call(): pl.pallas_call(functools.partial(all_sum_kernel, n), name='all_sum', out_...  11.4 us

profile of v11, /device:TPU:81, one launch (start us, length us, event | category | flops | bytes accessed | tf_op | source)
XLA Modules:
  0.0 480.4 jit_solution(5138549895421583068)
XLA Ops:
  0.6 129.8 %gather_qkv.1 = (bf16[3,768,5120]{2,1,0:T(8,128)(2,1)}, bf16[3,768,5120]{2,1,0:T(8,128)(2,1)}, f32[3,768,640]{2,1,0:T(8,128)}, f32[3,768,640]{2,1,0:T(8,128)}, b...) custom-call(bf16[3,96,5120]{2,1,0:T(8,128)(2,1)} %x_ref.3, ...), custom_call_target="tpu_custom_call" | custom-call | flops 45298483200 | bytes 40304640 | tf_op jit(solution)/shard_map/gather_qkv/pallas_call | solution.py:457
  130.5 88.8 %gather_attn.1 = (bf16[3,768,5120]{2,1,0:T(8,128)(2,1)}, bf16[3,768,640]{2,1,0:T(8,128)(2,1)}, bf16[3,768,640]{2,1,0:T(8,128)(2,1)}, bf16[3,768,640]{2,1,0:T(8,1...) custom-call(f32[3,768,640]{2,1,0:T(8,128)} %get-tuple-element.54.q_r, ...), custom_call_target="tpu_custom_call", output_to_operand_aliasing={{0}: (11, {})} | custom-call | flops 34728837120 | bytes 94371840 | tf_op jit(solution)/shard_map/gather_attn/pallas_call | solution.py:868
  219.3 126.7 %attn_bwd.1 = (bf16[3,96,5120]{2,1,0:T(8,128)(2,1)}, bf16[3,768,1920]{2,1,0:T(8,128)(2,1)}, bf16[3,768,1920]{2,1,0:T(8,128)(2,1)}, f32[3,768,640]{2,1,0:T(8,128)...) custom-call(f32[3,768,640]{2,1,0:T(8,128)} %get-tuple-element.54.q_r, ...), custom_call_target="tpu_custom_call" | custom-call | flops 70967623680 | bytes 44236800 | tf_op jit(solution)/shard_map/attn_bwd/pallas_call | solution.py:1247
  346.0 94.2 %dy_dw.1 = (bf16[3,96,5120]{2,1,0:T(8,128)(2,1)}, bf16[5120,640]{1,0:T(8,128)(2,1)}, bf16[5120,640]{1,0:T(8,128)(2,1)}, bf16[5120,640]{1,0:T(8,128)(2,1)}) custom-call(bf16[3,768,1920]{2,1,0:T(8,128)(2,1)} %get-tuple-element.75.g_hbm, bf16[3,768,1920]{2,1,0:T(8,128)(2,1)} %get-tuple-element.76.g_p, bf16[5120,640]{1,0:T(8,128)(2,1)} %wq_hbm.3, ...), custom_call_target="tpu_custom_call" | custom-call | flops 90596966400 | bytes 44236800 | tf_op jit(solution)/shard_map/dy_dw/pallas_call | solution.py:1390
  440.2 27.0 %tokens.1 = (bf16[3,96,5120]{2,1,0:T(8,128)(2,1)}, bf16[3,96,5120]{2,1,0:T(8,128)(2,1)}, f32[3,3,5120]{2,1,0:T(4,128)}, f32[640]{0:T(1024)}, f32[640]{0:T(1024)}...) custom-call(bf16[3,96,5120]{2,1,0:T(8,128)(2,1)} %x_ref.3, ...), custom_call_target="tpu_custom_call" | custom-call | flops 44236800 | bytes 17694720 | tf_op jit(solution)/shard_map/tokens/pallas_call | solution.py:1490
  467.2 1.1 reshape.26.x_ref
  468.2 11.4 %all_sum.1 = f32[8,45,128]{2,1,0:T(8,128)S(1)} custom-call(f32[8,45,128]{2,1,0:T(8,128)S(1)} %reshape.26.x_ref), custom_call_target="tpu_custom_call" | custom-call | flops 4000000000 | bytes 368640 | tf_op jit(solution)/shard_map/all_sum/pallas_call | solution.py:512
  479.6 0.1 reshape.27
  479.7 0.0 copy-start
  479.7 0.7 reduce_sum.9
  480.4 0.0 copy-done
Async XLA Ops:
  479.7 0.7 copy-start

commit v12 on v11

--- a/solution.py
+++ b/solution.py
@@ -223,8 +223,8 @@
 
 GATHER_SEMS = 9
 EARLY_ROWS = 1
-EARLY_CHUNKS = 1
-EARLY_DY = 4
+EARLY_CHUNKS = 3
+EARLY_DY = 5
 
 
 def chunks_of(width, step):
@@ -950,12 +950,12 @@
     for j in range(n_pieces):
         pl.when(step == j * (steps - 1) // n_pieces + 1)(lambda j=j: trade_w(j).start())
 
-    mid = early
+    mid = min(early + 2, nc)
     events = []
     late = list(range(mid))
     for m, j in enumerate(range(early, nc)):
         events.append(functools.partial(scatter.start_far, j))
-        if m >= 2 and m % 2 == 0 and late:
+        if m >= 2 and late:
             events.append(functools.partial(scatter.sums, late.pop(0)))
     events += [functools.partial(scatter.sums, j) for j in late]
     for m, event in enumerate(events):

time: 482 us -> 478 us (level)
  no operation moved by 1% of the time
where the time goes in v12:
time: 478 us; the launch traced here: 477 us
  Pallas kernels  474 us (99%)
    pallas_call x1, Pallas kernels, gather_qkv_call(): pl.pallas_call(functools.partial(gather_qkv_kernel, n), name='gather_qkv'...  130 us
    pallas_call x1, Pallas kernels, attn_bwd_call(): pl.pallas_call(functools.partial(attn_bwd_kernel, n, nb, heads, dim), nam...  125 us
    pallas_call x1, Pallas kernels, gather_attn_call(): pl.pallas_call(functools.partial(gather_attn_kernel, n, nb, heads, dim),...  90.3 us
    pallas_call x1, Pallas kernels, dy_dw_call(): pl.pallas_call(functools.partial(dy_dw_kernel, n, nb, dim), name='dy_dw',...  90.1 us
    pallas_call x1, Pallas kernels, token_call(): pl.pallas_call(functools.partial(token_kernel, n_copies), name='tokens',...  27 us
    pallas_call x1, Pallas kernels, all_sum_call(): pl.pallas_call(functools.partial(all_sum_kernel, n), name='all_sum', out_...  12.5 us

profile of v12, /device:TPU:81, one launch (start us, length us, event | category | flops | bytes accessed | tf_op | source)
XLA Modules:
  0.0 476.9 jit_solution(2646104766962025145)
XLA Ops:
  0.6 129.8 %gather_qkv.1 = (bf16[3,768,5120]{2,1,0:T(8,128)(2,1)}, bf16[3,768,5120]{2,1,0:T(8,128)(2,1)}, f32[3,768,640]{2,1,0:T(8,128)}, f32[3,768,640]{2,1,0:T(8,128)}, b...) custom-call(bf16[3,96,5120]{2,1,0:T(8,128)(2,1)} %x_ref.3, ...), custom_call_target="tpu_custom_call" | custom-call | flops 45298483200 | bytes 40304640 | tf_op jit(solution)/shard_map/gather_qkv/pallas_call | solution.py:457
  130.5 90.3 %gather_attn.1 = (bf16[3,768,5120]{2,1,0:T(8,128)(2,1)}, bf16[3,768,640]{2,1,0:T(8,128)(2,1)}, bf16[3,768,640]{2,1,0:T(8,128)(2,1)}, bf16[3,768,640]{2,1,0:T(8,1...) custom-call(f32[3,768,640]{2,1,0:T(8,128)} %get-tuple-element.54.q_r, ...), custom_call_target="tpu_custom_call", output_to_operand_aliasing={{0}: (11, {})} | custom-call | flops 34728837120 | bytes 94371840 | tf_op jit(solution)/shard_map/gather_attn/pallas_call | solution.py:868
  220.8 124.7 %attn_bwd.1 = (bf16[3,96,5120]{2,1,0:T(8,128)(2,1)}, bf16[3,768,1920]{2,1,0:T(8,128)(2,1)}, bf16[3,768,1920]{2,1,0:T(8,128)(2,1)}, f32[3,768,640]{2,1,0:T(8,128)...) custom-call(f32[3,768,640]{2,1,0:T(8,128)} %get-tuple-element.54.q_r, ...), custom_call_target="tpu_custom_call" | custom-call | flops 70967623680 | bytes 44236800 | tf_op jit(solution)/shard_map/attn_bwd/pallas_call | solution.py:1247
  345.5 90.1 %dy_dw.1 = (bf16[3,96,5120]{2,1,0:T(8,128)(2,1)}, bf16[5120,640]{1,0:T(8,128)(2,1)}, bf16[5120,640]{1,0:T(8,128)(2,1)}, bf16[5120,640]{1,0:T(8,128)(2,1)}) custom-call(bf16[3,768,1920]{2,1,0:T(8,128)(2,1)} %get-tuple-element.75.g_hbm, bf16[3,768,1920]{2,1,0:T(8,128)(2,1)} %get-tuple-element.76.g_p, bf16[5120,640]{1,0:T(8,128)(2,1)} %wq_hbm.3, ...), custom_call_target="tpu_custom_call" | custom-call | flops 90596966400 | bytes 44236800 | tf_op jit(solution)/shard_map/dy_dw/pallas_call | solution.py:1390
  435.6 27.0 %tokens.1 = (bf16[3,96,5120]{2,1,0:T(8,128)(2,1)}, bf16[3,96,5120]{2,1,0:T(8,128)(2,1)}, f32[3,3,5120]{2,1,0:T(4,128)}, f32[640]{0:T(1024)}, f32[640]{0:T(1024)}...) custom-call(bf16[3,96,5120]{2,1,0:T(8,128)(2,1)} %x_ref.3, ...), custom_call_target="tpu_custom_call" | custom-call | flops 44236800 | bytes 17694720 | tf_op jit(solution)/shard_map/tokens/pallas_call | solution.py:1490
  462.5 1.1 reshape.26.x_ref
  463.6 12.5 %all_sum.1 = f32[8,45,128]{2,1,0:T(8,128)S(1)} custom-call(f32[8,45,128]{2,1,0:T(8,128)S(1)} %reshape.26.x_ref), custom_call_target="tpu_custom_call" | custom-call | flops 4000000000 | bytes 368640 | tf_op jit(solution)/shard_map/all_sum/pallas_call | solution.py:512
  476.1 0.1 reshape.27
  476.1 0.0 copy-start
  476.2 0.7 reduce_sum.9
  476.9 0.0 copy-done
Async XLA Ops:
  476.1 0.7 copy-start
